TPU v7x, 256 devices: a whole 4x4x8 slice. The times are simulated.
256 devices in a mesh: gx: 4 (over z_lo), gy: 8 (over y, core), gz: 8 (over z_hi, x).
Axes of the slice: x: 4, y: 4, z: 8 (z_hi: 2, z_lo: 4; z = z_hi * 4 + z_lo), core: 2. Of those that a mesh axis runs over, the one named last changes fastest.
Arguments:
- rhs: float32 [128, 256, 1024], P('gx', 'gy', 'gz'), may hold values from -8 to 8
- accumulation: float32 [128, 256, 1024], P('gx', 'gy', 'gz'), may hold values from 0.05 to 0.5
- permeability: float32 [3, 128, 256, 1024], P(None, 'gx', 'gy', 'gz'), may hold values from 0.1 to 10
- nnc_cell: int32 [4, 8, 8, 512], P('gx', 'gy', 'gz'), may hold values from 0 to 4095, as said below
- nnc_remote: int32 [4, 8, 8, 512], P('gx', 'gy', 'gz'), may hold values from 0 to 32767, as said below
- nnc_mask: int32 [4, 8, 8, 512], P('gx', 'gy', 'gz'), may hold values from 0 to 1, as said below
- nnc_trans: float32 [4, 8, 8, 512], P('gx', 'gy', 'gz'), may hold values from 0.5 to 4
Outputs:
- correction: float32 [128, 256, 1024], P('gx', 'gy', 'gz')
Inputs may be any that keep to these rules, and one draw needn't show every extreme that they name: `nnc_cell`: x * 128 + z of a cell with local x and local layer z on the device's first y layer. `nnc_remote`: x * 1024 + z2, with x the same local x as nnc_cell and z2 a global layer, naming a cell on the last y layer of the device below in y. `nnc_mask`: each device's live slots come first, then zeros; every slot is 0 on devices of the first gy index; the device last along every axis has all slots live.
All inputs are finite; a program needn't handle non-finite values.
Results may differ from a plain program's by a relative error of at most 0.00002.
Values sent between devices are 32-bit elements; how exact they have to be, the bound alone decides.
No kernel may reach another device: no remote copies, remote signals or barrier semaphores. Data moves between devices by JAX's collectives and lax.ppermute only.
A program may use at most 64 MiB of HBM per device.

v0:
```python
import jax
import jax.numpy as jnp
from jax import lax
from jax.experimental import pallas as pl
from jax.experimental.pallas import tpu as pltpu
from jax.sharding import PartitionSpec as P

SWEEPS = 6
lam_low = 0.1
lam_high = 2.0
theta = (lam_high + lam_low) / 2.0
delta = (lam_high - lam_low) / 2.0
sigma = theta / delta

H = 8
f32 = jnp.float32
bf16 = jnp.bfloat16


def harmonic(left, right):
    total = left + right
    live = total > 0.0
    return jnp.where(live, 2.0 * (left * right) / jnp.where(live, total, 1.0), 0.0)


def split3(v):
    hi = v.astype(bf16).astype(f32)
    rest = v - hi
    mid = rest.astype(bf16).astype(f32)
    return hi, mid, rest - mid


def dot(a, b, dims):
    return lax.dot_general(a, b, (dims, ((), ())), preferred_element_type=f32)


def lane_iota(shape):
    return lax.broadcasted_iota(jnp.int32, shape, len(shape) - 1)


def hits(col_ref, q, which):
    codes = col_ref[q, :, which : which + 1]
    return lane_iota((codes.shape[0], 128)).astype(f32) == codes


def rows_hit(row_ref, q, which, count):
    codes = row_ref[q, which : which + 1, :]
    rows = lax.broadcasted_iota(jnp.int32, (count, codes.shape[1]), 0).astype(f32)
    return jnp.where(rows == codes, 1.0, 0.0).astype(bf16)


def scatter(u, lane_hit, row_hit):
    parts = [jnp.where(lane_hit, p, 0.0).astype(bf16) for p in split3(u)]
    out = dot(row_hit, jnp.concatenate(parts, axis=1), ((1,), (0,)))
    return out[:, :128] + out[:, 128:256] + out[:, 256:]


def gather(table, lane_hit, codes):
    rows = table.shape[0]
    pick = jnp.where(lane_hit, 1.0, 0.0).astype(bf16)
    parts = [p.astype(bf16) for p in split3(table)]
    if rows % 128 == 0:
        got = sum(dot(pick, p, ((1,), (1,))) for p in parts)
        lanes = lane_iota(got.shape)
    else:
        got = dot(pick, jnp.concatenate(parts, axis=0), ((1,), (1,)))
        lanes = lane_iota(got.shape) % rows
    return jnp.sum(jnp.where(lanes.astype(f32) == codes, got, 0.0), axis=1, keepdims=True)


def pack_faces(faces, slab, x):
    cx, half = 32, faces.shape[0]
    lane = lane_iota(faces.shape)
    for part in range(2):
        rows = slab[part * half : (part + 1) * half]
        faces = jnp.where(lane == 2 * cx * part + x, rows[:, 0:1], faces)
        faces = jnp.where(lane == 2 * cx * part + cx + x, rows[:, 127:128], faces)
    return faces


def unpacked(low_faces, high_faces, slab, x):
    cx = 32
    lane = lane_iota(slab.shape)

    def column(faces, first, to):
        return jnp.concatenate(
            [pltpu.roll(faces, (to - first - 2 * cx * part - x) % 128, 1) for part in range(2)],
            axis=0,
        )

    low = jnp.where(lane == 0, column(low_faces, cx, 128), pltpu.roll(slab, 1, 1))
    high = jnp.where(lane == 127, column(high_faces, 0, 127 + 128), pltpu.roll(slab, 127, 1))
    return low, high


def put_partials(out_ref, base, tiles, q, col_ref, row_ref, u, cx):
    sums = scatter(u, hits(col_ref, q, 2), rows_hit(row_ref, q, 1, tiles * cx))
    for t in range(tiles):
        out_ref[t, base + q * cx : base + (q + 1) * cx, :] = sums[t * cx : (t + 1) * cx]


def first_kernel(own_k, before, after, col_ref, row_ref, out_ref):
    tiles = out_ref.shape[0]
    cx = own_k.shape[1]

    def body(x, faces):
        at = pl.multiple_of((4 * cx + x) * H, H)
        slab = jnp.concatenate([before[pl.ds(at, H), :], own_k[2, x], after[pl.ds(at, H), :]], axis=0)
        return pack_faces(faces, slab, x)

    half = (own_k.shape[2] + 2 * H) // 2
    faces = lax.fori_loop(0, cx, body, jnp.zeros((half, 128), f32))
    for t in range(tiles):
        out_ref[t, 0:half, :] = faces
    for q in range(2):
        put_partials(out_ref, half, tiles, q, col_ref, row_ref, col_ref[q, :, 4:5], cx)


def emit(a8_ref, planes, faces, col_ref, row_ref):
    tiles = a8_ref.shape[0]
    cx = planes.shape[1]
    half = faces.shape[0]
    for t in range(tiles):
        a8_ref[t, 0:cx, :] = planes[0]
        a8_ref[t, cx : 2 * cx, :] = planes[2]
        a8_ref[t, 2 * cx : 2 * cx + half, :] = faces
    for q in range(2):
        near = gather(planes[1 + 2 * q], hits(col_ref, q, 0), col_ref[q, :, 1:2])
        put_partials(a8_ref, 2 * cx + half, tiles, q, col_ref, row_ref, col_ref[q, :, 4:5] * near, cx)


def keep_planes(planes, slab, x):
    last = slab.shape[0] - H - 1
    for n, y in enumerate((H - 1, H, last, last + 1)):
        planes[n, pl.ds(x, 1), :] = slab[y : y + 1, :]


def with_fault(total, fault, x):
    y = lax.broadcasted_iota(jnp.int32, total.shape, 0)
    last = total.shape[0] - H - 1
    extra = jnp.zeros_like(total)
    for n, at in enumerate((H - 1, H, last, last + 1)):
        extra = jnp.where(y == at, fault[n, pl.ds(x, 1), :], extra)
    return total + extra


def neighbour_faces(l_ref, a8, base, half):
    tiles = a8.shape[0]
    l = l_ref[0]
    low = a8[jnp.maximum(l - 1, 0), base : base + half, :]
    high = a8[jnp.minimum(l + 1, tiles - 1), base : base + half, :]
    return low, high


def setup_kernel(l_ref, rhs, acc, perm, before, after, kx_low, kx_high, a8, col_ref, row_ref,
                 inv, z_out, d_out, tx, tym, typ, tzm, tzp, xf, a8_out, planes, fault):
    cx, cy = rhs.shape[0], rhs.shape[1]
    ye = cy + 2 * H
    half = ye // 2
    tiles = a8.shape[0]
    l = l_ref[0]
    low_faces, high_faces = neighbour_faces(l_ref, a8, 0, half)
    low_faces = jnp.where(l > 0, low_faces, 0.0)
    high_faces = jnp.where(l < tiles - 1, high_faces, 0.0)
    for q in range(2):
        base = half + q * cx
        far = a8[0, base : base + cx, :]
        for t in range(1, tiles):
            far = far + a8[t, base : base + cx, :]
        fault[2 * q] = far
        near = scatter(col_ref[q, :, 4:5], hits(col_ref, q, 0), rows_hit(row_ref, q, 0, cx))
        fault[2 * q + 1] = near

    def ext(a, own, x):
        at = pl.multiple_of((a * cx + x) * H, H)
        return jnp.concatenate([before[pl.ds(at, H), :], own, after[pl.ds(at, H), :]], axis=0)

    def body(x, carry):
        faces, t_low, kx = carry
        nxt = jnp.minimum(x + 1, cx - 1)
        kx_next = jnp.where(x == cx - 1, kx_high[...], ext(2, perm[0, nxt], nxt))
        ky = ext(3, perm[1, x], x)
        kz = ext(4, perm[2, x], x)
        t_high = harmonic(kx, kx_next)
        ym = harmonic(ky, pltpu.roll(ky, 1, 0))
        yp = harmonic(ky, pltpu.roll(ky, ye - 1, 0))
        kz_low, kz_high = unpacked(low_faces, high_faces, kz, x)
        zm = harmonic(kz, kz_low)
        zp = harmonic(kz, kz_high)
        diag = ext(1, acc[x], x) + t_low + t_high + ym + yp + zm + zp
        diag = with_fault(diag, fault, x)
        live = diag > 0.0
        inverse = jnp.where(live, 1.0 / jnp.where(live, diag, 1.0), 0.0)
        z = inverse * ext(0, rhs[x], x)
        d = z / theta
        inv[x] = inverse
        z_out[x] = z
        d_out[x] = d
        tx[x] = t_low
        tx[x + 1] = t_high
        tym[x] = ym
        typ[x] = yp
        tzm[x] = zm
        tzp[x] = zp
        keep_planes(planes, d, x)
        return pack_faces(faces, d, x), t_high, kx_next

    kx0 = ext(2, perm[0, 0], 0)
    init = (jnp.zeros((half, 128), f32), harmonic(kx_low[...], kx0), kx0)
    faces, _, _ = lax.fori_loop(0, cx, body, init)
    xf[0] = d_out[0]
    xf[1] = d_out[cx - 1]
    emit(a8_out, planes, faces, col_ref, row_ref)


def sweep_kernel(c1, c2, first, last, l_ref, d_in, z_in, *refs):
    refs = list(refs)
    corr_in = None if first else refs.pop(0)
    xlow, xhigh, a8, inv, tx, tym, typ, tzm, tzp, col_ref, row_ref = refs[:11]
    outs = refs[11:]
    if last:
        corr_out, fault = outs
    else:
        d_out, z_out, corr_out, xf, a8_out, planes, fault = outs
    cx, ye = d_in.shape[0], d_in.shape[1]
    cy = ye - 2 * H
    half = ye // 2
    tiles = a8.shape[0]
    low_faces, high_faces = neighbour_faces(l_ref, a8, 2 * cx, half)
    for q in range(2):
        base = 2 * cx + half + q * cx
        far = a8[0, base : base + cx, :]
        for t in range(1, tiles):
            far = far + a8[t, base : base + cx, :]
        fault[2 * q] = far
        table = jnp.concatenate([a8[t, q * cx : (q + 1) * cx, :] for t in range(tiles)], axis=0)
        got = gather(table, hits(col_ref, q, 2), col_ref[q, :, 3:4])
        fault[2 * q + 1] = scatter(
            col_ref[q, :, 4:5] * got, hits(col_ref, q, 0), rows_hit(row_ref, q, 0, cx)
        )

    def body(x, carry):
        faces, d_prev, d = carry
        d_next = jnp.where(x == cx - 1, xhigh[...], d_in[jnp.minimum(x + 1, cx - 1)])
        z_low, z_high = unpacked(low_faces, high_faces, d, x)
        flow = tx[x] * d_prev + tx[x + 1] * d_next
        flow = flow + (tym[x] * pltpu.roll(d, 1, 0) + typ[x] * pltpu.roll(d, ye - 1, 0))
        flow = flow + (tzm[x] * z_low + tzp[x] * z_high)
        flow = with_fault(flow, fault, x)
        z = z_in[x] - d + inv[x] * flow
        new = c1 * d + c2 * z
        before = d[H : H + cy] if first else corr_in[x]
        corr_out[x] = before + new[H : H + cy]
        if last:
            return faces, d, d_next
        d_out[x] = new
        z_out[x] = z
        keep_planes(planes, new, x)
        return pack_faces(faces, new, x), d, d_next

    init = (jnp.zeros((half, 128), f32), xlow[...], d_in[0])
    faces, _, _ = lax.fori_loop(0, cx, body, init)
    if not last:
        xf[0] = d_out[0]
        xf[1] = d_out[cx - 1]
        emit(a8_out, planes, faces, col_ref, row_ref)


VMEM = pl.BlockSpec(memory_space=pltpu.VMEM)
SMEM = pl.BlockSpec(memory_space=pltpu.SMEM)


def steps(axis):
    peers = lax.axis_size(axis)
    up = [(i, i + 1) for i in range(peers - 1)]
    return up, [(j, i) for i, j in up]


def local(rhs, accumulation, permeability, nnc_cell, nnc_remote, nnc_mask, nnc_trans):
    cx, cy, cz = rhs.shape
    tiles = lax.axis_size("gz")
    slots = nnc_cell.shape[-1]
    ye = cy + 2 * H
    half = ye // 2
    up_y, down_y = steps("gy")
    up_x, down_x = steps("gx")

    def struct(*shape):
        return jax.ShapeDtypeStruct(shape, f32)

    weight = nnc_trans.reshape(-1) * nnc_mask.reshape(-1).astype(f32)
    mine = jnp.stack([nnc_cell.reshape(-1).astype(f32), nnc_remote.reshape(-1).astype(f32), weight])
    bottom = [rhs[None, :, :H], accumulation[None, :, :H], permeability[:, :, :H]]
    top = [rhs[None, :, cy - H :], accumulation[None, :, cy - H :], permeability[:, :, cy - H :]]
    bottom = jnp.concatenate(bottom, axis=0).reshape(-1, cz)
    top = jnp.concatenate(top, axis=0).reshape(-1, cz)
    flat = jnp.pad(mine.reshape(-1, cz), ((0, 4), (0, 0)))
    before = lax.ppermute(top, "gy", up_y)
    after = lax.ppermute(jnp.concatenate([bottom, flat], axis=0), "gy", down_y)
    count = bottom.shape[0]
    above = after[count : count + 3 * slots // cz].reshape(3, slots)
    lists = jnp.stack([mine, above])
    cell = lists[:, 0].astype(jnp.int32)
    remote = lists[:, 1].astype(jnp.int32)
    column = cz * tiles
    far_z = remote % column
    own_x = (cell // cz).astype(f32)
    far_code = ((far_z // cz) * cx + remote // column).astype(f32)
    col = jnp.stack(
        [(cell % cz).astype(f32), own_x, (far_z % cz).astype(f32), far_code, lists[:, 2]], axis=-1
    )
    row = jnp.stack([own_x, far_code], axis=1)

    l = lax.axis_index("gz").reshape(1).astype(jnp.int32)
    a8 = pl.pallas_call(
        first_kernel, out_shape=struct(tiles, half + 2 * cx, cz), in_specs=[VMEM] * 5, out_specs=VMEM
    )(permeability, before, after, col, row)

    def kx_face(x):
        at = (2 * cx + x) * H
        return jnp.concatenate([before[at : at + H], permeability[0, x], after[at : at + H]], axis=0)

    kx_low = lax.ppermute(kx_face(cx - 1), "gx", up_x)
    kx_high = lax.ppermute(kx_face(0), "gx", down_x)
    a8 = lax.all_to_all(a8, "gz", 0, 0, tiled=True)

    big = struct(cx, ye, cz)
    tall = struct(cx + 1, ye, cz)
    sent = struct(tiles, 4 * cx + half, cz)
    edge = struct(2, ye, cz)
    scratch = [pltpu.VMEM((4, cx, cz), f32)]
    inv, z, d, tx, tym, typ, tzm, tzp, xf, a8 = pl.pallas_call(
        setup_kernel,
        out_shape=(big, big, big, tall, big, big, big, big, edge, sent),
        in_specs=[SMEM] + [VMEM] * 10,
        out_specs=(VMEM,) * 10,
        scratch_shapes=scratch * 2,
    )(l, rhs, accumulation, permeability, before, after, kx_low, kx_high, a8, col, row)

    rho = 1.0 / sigma
    corr = None
    for sweep in range(1, SWEEPS):
        first, last = sweep == 1, sweep == SWEEPS - 1
        rho_next = 1.0 / (2.0 * sigma - rho)
        c1, c2 = rho_next * rho, 2.0 * rho_next / delta
        rho = rho_next
        xlow = lax.ppermute(xf[1], "gx", up_x)
        xhigh = lax.ppermute(xf[0], "gx", down_x)
        a8 = lax.all_to_all(a8, "gz", 0, 0, tiled=True)
        args = [l, d, z] + ([] if first else [corr])
        args += [xlow, xhigh, a8, inv, tx, tym, typ, tzm, tzp, col, row]

        def kernel(*refs, c1=c1, c2=c2, first=first, last=last):
            sweep_kernel(c1, c2, first, last, *refs)

        small = struct(cx, cy, cz)
        out = pl.pallas_call(
            kernel,
            out_shape=small if last else (big, big, small, edge, sent),
            in_specs=[SMEM] + [VMEM] * (len(args) - 1),
            out_specs=VMEM if last else (VMEM,) * 5,
            scratch_shapes=scratch if last else scratch * 2,
        )(*args)
        if last:
            corr = out
        else:
            d, z, corr, xf, a8 = out
    return corr


def solution(mesh):
    split = P("gx", "gy", "gz")
    slots = P("gx", "gy", "gz", None)
    return jax.shard_map(
        local,
        mesh=mesh,
        in_specs=(split, split, P(None, "gx", "gy", "gz"), slots, slots, slots, slots),
        out_specs=split,
        check_vma=False,
    )
```

profile of v0, /device:TPU:40, one launch (start us, length us, event | category | flops | bytes accessed | tf_op | source)
XLA Modules:
  0.0 252.5 jit_solution(817383202195836449)
XLA Ops:
  8.0 5.0 %collective-permute-done.1.after = f32[1296,128]{1,0:T(8,128)S(1)} collective-permute-done((f32[1296,128]{1,0:T(8,128)S(1)}, f32[1296,128]{1,0:T(8,128)S(1)}, u32[]{:S(2)}, u32[]{:S(2)}) %collective-permute-start.1) | collective-permute-done | bytes 663584 | tf_op jit(solution)/shard_map/ppermute | solution.py:299
  17.7 6.0 %shard_map.73 = f32[8,88,128]{2,1,0:T(8,128)} custom-call(f32[3,32,32,128]{3,2,1,0:T(8,128)} %perm.1, f32[1280,128]{1,0:T(8,128)} %copy-done.1, f32[1296,128]{1,0:T(8,128)} %copy-done, f32[2,512,5]{2,1,0:T(8,128)} %copy.8.col_ref.refs_12_.refs_13_, f32[2,2,512]{2,1,0:T(2,128)} %pad_maximum_fusion.5.row_ref.refs_13_.refs_14_), custom_call_target="tpu_custom_call" | custom-call | tf_op jit(solution)/shard_map/pallas_call | solution.py:315
  23.7 10.0 %all-to-all-start = ((f32[8,88,128]{2,1,0:T(8,128)}), f32[8,88,128]{2,1,0:T(8,128)S(1)}, u32[]{:S(2)}, u32[]{:S(2)}) async-start(f32[8,88,128]{2,1,0:T(8,128)} %shard_map.73), calls=%async_computation | async-start | bytes 720896 | tf_op jit(solution)/shard_map/all_to_all | solution.py:325
  43.7 6.3 %all-to-all-done.a8 = f32[8,88,128]{2,1,0:T(8,128)S(1)} async-done(((f32[8,88,128]{2,1,0:T(8,128)}), f32[8,88,128]{2,1,0:T(8,128)S(1)}, u32[]{:S(2)}, u32[]{:S(2)}) %all-to-all-start) | async-done | bytes 360480 | tf_op jit(solution)/shard_map/all_to_all | solution.py:325
  50.8 12.1 %shard_map.74 = (f32[32,48,128]{2,1,0:T(8,128)}, f32[32,48,128]{2,1,0:T(8,128)}, f32[32,48,128]{2,1,0:T(8,128)}, f32[33,48,128]{2,1,0:T(8,128)}, f32[32,48,128]{...) custom-call(s32[1]{0:T(128)} %bitcast.l_ref.refs_0_, ...), custom_call_target="tpu_custom_call" | custom-call | tf_op jit(solution)/shard_map/pallas_call | solution.py:332
  62.8 3.5 %all-to-all-start.1 = ((f32[8,152,128]{2,1,0:T(8,128)}), f32[8,152,128]{2,1,0:T(8,128)S(1)}, u32[]{:S(2)}, u32[]{:S(2)}) async-start(f32[8,152,128]{2,1,0:T(8,128)} %get-tuple-element.38), calls=%async_computation.1 | async-start | bytes 1245184 | tf_op jit(solution)/shard_map/all_to_all | solution.py:349
  73.0 6.4 %collective-permute-done.5.refs_4_ = f32[48,128]{1,0:T(8,128)S(1)} collective-permute-done((f32[48,128]{1,0:T(8,128)S(1)}, f32[48,128]{1,0:T(8,128)S(1)}, u32[]{:S(2)}, u32[]{:S(2)}) %collective-permute-start.5) | collective-permute-done | bytes 24608 | tf_op jit(solution)/shard_map/ppermute | solution.py:348
  79.4 6.7 %all-to-all-done.1.refs_5_ = f32[8,152,128]{2,1,0:T(8,128)S(1)} async-done(((f32[8,152,128]{2,1,0:T(8,128)}), f32[8,152,128]{2,1,0:T(8,128)S(1)}, u32[]{:S(2)}, u32[]{:S(2)}) %all-to-all-start.1) | async-done | bytes 622624 | tf_op jit(solution)/shard_map/all_to_all | solution.py:349
  86.9 13.7 %shard_map.75 = (f32[32,48,128]{2,1,0:T(8,128)}, f32[32,48,128]{2,1,0:T(8,128)}, f32[32,32,128]{2,1,0:T(8,128)}, f32[2,48,128]{2,1,0:T(8,128)}, f32[8,152,128]{2,1,0:T(8,128)}) custom-call(s32[1]{0:T(128)} %bitcast.l_ref.refs_0_, f32[32,48,128]{2,1,0:T(8,128)} %get-tuple-element.35.refs_1_, f32[32,48,128]{2,1,0:T(8,128)} %get-tuple-element.36.refs_2_, ...), custom_call_target="tpu_custom_call" | custom-call | tf_op jit(solution)/shard_map/pallas_call | solution.py:357
  100.6 3.7 %all-to-all-start.2 = ((f32[8,152,128]{2,1,0:T(8,128)}), f32[8,152,128]{2,1,0:T(8,128)S(1)}, u32[]{:S(2)}, u32[]{:S(2)}) async-start(f32[8,152,128]{2,1,0:T(8,128)} %get-tuple-element.49), calls=%async_computation.2 | async-start | bytes 1245184 | tf_op jit(solution)/shard_map/all_to_all | solution.py:349
  110.9 7.6 %collective-permute-done.7.refs_5_ = f32[48,128]{1,0:T(8,128)S(1)} collective-permute-done((f32[48,128]{1,0:T(8,128)S(1)}, f32[48,128]{1,0:T(8,128)S(1)}, u32[]{:S(2)}, u32[]{:S(2)}) %collective-permute-start.7) | collective-permute-done | bytes 24608 | tf_op jit(solution)/shard_map/ppermute | solution.py:348
  118.5 7.1 %all-to-all-done.2.refs_6_ = f32[8,152,128]{2,1,0:T(8,128)S(1)} async-done(((f32[8,152,128]{2,1,0:T(8,128)}), f32[8,152,128]{2,1,0:T(8,128)S(1)}, u32[]{:S(2)}, u32[]{:S(2)}) %all-to-all-start.2) | async-done | bytes 622624 | tf_op jit(solution)/shard_map/all_to_all | solution.py:349
  126.4 13.8 %shard_map.76 = (f32[32,48,128]{2,1,0:T(8,128)}, f32[32,48,128]{2,1,0:T(8,128)}, f32[32,32,128]{2,1,0:T(8,128)}, f32[2,48,128]{2,1,0:T(8,128)}, f32[8,152,128]{2,1,0:T(8,128)}) custom-call(s32[1]{0:T(128)} %bitcast.l_ref.refs_0_, f32[32,48,128]{2,1,0:T(8,128)} %get-tuple-element.45.refs_1_, f32[32,48,128]{2,1,0:T(8,128)} %get-tuple-element.46.refs_2_, ...), custom_call_target="tpu_custom_call" | custom-call | tf_op jit(solution)/shard_map/pallas_call | solution.py:357
  150.5 7.1 %collective-permute-done.9.refs_5_ = f32[48,128]{1,0:T(8,128)S(1)} collective-permute-done((f32[48,128]{1,0:T(8,128)S(1)}, f32[48,128]{1,0:T(8,128)S(1)}, u32[]{:S(2)}, u32[]{:S(2)}) %collective-permute-start.9) | collective-permute-done | bytes 24608 | tf_op jit(solution)/shard_map/ppermute | solution.py:348
  157.7 6.3 %all-to-all-done.3.refs_6_ = f32[8,152,128]{2,1,0:T(8,128)S(1)} async-done(((f32[8,152,128]{2,1,0:T(8,128)}), f32[8,152,128]{2,1,0:T(8,128)S(1)}, u32[]{:S(2)}, u32[]{:S(2)}) %all-to-all-start.3) | async-done | bytes 622624 | tf_op jit(solution)/shard_map/all_to_all | solution.py:349
  164.8 13.8 %shard_map.77 = (f32[32,48,128]{2,1,0:T(8,128)}, f32[32,48,128]{2,1,0:T(8,128)}, f32[32,32,128]{2,1,0:T(8,128)}, f32[2,48,128]{2,1,0:T(8,128)}, f32[8,152,128]{2,1,0:T(8,128)}) custom-call(s32[1]{0:T(128)} %bitcast.l_ref.refs_0_, f32[32,48,128]{2,1,0:T(8,128)} %get-tuple-element.50.refs_1_, f32[32,48,128]{2,1,0:T(8,128)} %get-tuple-element.51.refs_2_, ...), custom_call_target="tpu_custom_call" | custom-call | tf_op jit(solution)/shard_map/pallas_call | solution.py:357
  178.5 4.1 %all-to-all-start.4 = ((f32[8,152,128]{2,1,0:T(8,128)}), f32[8,152,128]{2,1,0:T(8,128)S(1)}, u32[]{:S(2)}, u32[]{:S(2)}) async-start(f32[8,152,128]{2,1,0:T(8,128)} %get-tuple-element.59), calls=%async_computation.4 | async-start | bytes 1245184 | tf_op jit(solution)/shard_map/all_to_all | solution.py:349
  189.2 7.6 %collective-permute-done.11.refs_5_ = f32[48,128]{1,0:T(8,128)S(1)} collective-permute-done((f32[48,128]{1,0:T(8,128)S(1)}, f32[48,128]{1,0:T(8,128)S(1)}, u32[]{:S(2)}, u32[]{:S(2)}) %collective-permute-start.11) | collective-permute-done | bytes 24608 | tf_op jit(solution)/shard_map/ppermute | solution.py:348
  196.8 7.1 %all-to-all-done.4.refs_6_ = f32[8,152,128]{2,1,0:T(8,128)S(1)} async-done(((f32[8,152,128]{2,1,0:T(8,128)}), f32[8,152,128]{2,1,0:T(8,128)S(1)}, u32[]{:S(2)}, u32[]{:S(2)}) %all-to-all-start.4) | async-done | bytes 622624 | tf_op jit(solution)/shard_map/all_to_all | solution.py:349
  204.7 13.8 %shard_map.78 = (f32[32,48,128]{2,1,0:T(8,128)}, f32[32,48,128]{2,1,0:T(8,128)}, f32[32,32,128]{2,1,0:T(8,128)}, f32[2,48,128]{2,1,0:T(8,128)}, f32[8,152,128]{2,1,0:T(8,128)}) custom-call(s32[1]{0:T(128)} %bitcast.l_ref.refs_0_, f32[32,48,128]{2,1,0:T(8,128)} %get-tuple-element.55.refs_1_, f32[32,48,128]{2,1,0:T(8,128)} %get-tuple-element.56.refs_2_, ...), custom_call_target="tpu_custom_call" | custom-call | tf_op jit(solution)/shard_map/pallas_call | solution.py:357
  218.5 3.5 %all-to-all-start.5 = ((f32[8,152,128]{2,1,0:T(8,128)}), f32[8,152,128]{2,1,0:T(8,128)S(1)}, u32[]{:S(2)}, u32[]{:S(2)}) async-start(f32[8,152,128]{2,1,0:T(8,128)} %get-tuple-element.64), calls=%async_computation.5 | async-start | bytes 1245184 | tf_op jit(solution)/shard_map/all_to_all | solution.py:349
  228.7 7.3 %collective-permute-done.13.refs_5_ = f32[48,128]{1,0:T(8,128)S(1)} collective-permute-done((f32[48,128]{1,0:T(8,128)S(1)}, f32[48,128]{1,0:T(8,128)S(1)}, u32[]{:S(2)}, u32[]{:S(2)}) %collective-permute-start.13) | collective-permute-done | bytes 24608 | tf_op jit(solution)/shard_map/ppermute | solution.py:348
  235.9 6.2 %all-to-all-done.5.refs_6_ = f32[8,152,128]{2,1,0:T(8,128)S(1)} async-done(((f32[8,152,128]{2,1,0:T(8,128)}), f32[8,152,128]{2,1,0:T(8,128)S(1)}, u32[]{:S(2)}, u32[]{:S(2)}) %all-to-all-start.5) | async-done | bytes 622624 | tf_op jit(solution)/shard_map/all_to_all | solution.py:349
  242.9 9.5 %shard_map.79 = f32[32,32,128]{2,1,0:T(8,128)} custom-call(s32[1]{0:T(128)} %bitcast.l_ref.refs_0_, f32[32,48,128]{2,1,0:T(8,128)} %get-tuple-element.60.refs_1_, f32[32,48,128]{2,1,0:T(8,128)} %get-tuple-element.61.refs_2_, f32[32,32,128]{2,1,0:T(8,128)} %get-tuple-element.62.refs_3_, f32[48,128]{1,0:T(8,128)} %copy-done.16, f32[48,128]{1,0:T(8,128)} %copy-done.12, ...), custom_call_target="tpu_custom_call" | custom-call | tf_op jit(solution)/shard_map/pallas_call | solution.py:357
  (97 shorter events, 64.2 us)
Async XLA Ops:
  2.9 10.1 %collective-permute-start.1 = (f32[1296,128]{1,0:T(8,128)S(1)}, f32[1296,128]{1,0:T(8,128)S(1)}, u32[]{:S(2)}, u32[]{:S(2)}) collective-permute-start(f32[1296,128]{1,0:T(8,128)S(1)} %select_maximum_fusion), channel_id=1, source_target_pairs={{8,0},{16,8},{24,16},{32,24},{40,32},{48,40},{56,48},{9,1},{17,9},... | collective-permute-start | bytes 1990664 | tf_op jit(solution)/shard_map/ppermute | solution.py:299
  4.9 11.9 %collective-permute-start = (f32[1280,128]{1,0:T(8,128)S(1)}, f32[1280,128]{1,0:T(8,128)S(1)}, u32[]{:S(2)}, u32[]{:S(2)}) collective-permute-start(f32[1280,128]{1,0:T(8,128)S(1)} %bitcast.78), channel_id=1, source_target_pairs={{0,8},{8,16},{16,24},{24,32},{32,40},{40,48},{48,56},{1,9},{9,17},... | collective-permute-start | bytes 1966088 | tf_op jit(solution)/shard_map/ppermute | solution.py:298
  23.7 26.4 %all-to-all-start = ((f32[8,88,128]{2,1,0:T(8,128)}), f32[8,88,128]{2,1,0:T(8,128)S(1)}, u32[]{:S(2)}, u32[]{:S(2)}) async-start(f32[8,88,128]{2,1,0:T(8,128)} %shard_map.73), calls=%async_computation | async-start | bytes 720896 | tf_op jit(solution)/shard_map/all_to_all | solution.py:325
  35.1 6.2 %collective-permute-start.2 = (f32[48,128]{1,0:T(8,128)S(1)}, f32[48,128]{1,0:T(8,128)S(1)}, u32[]{:S(2)}, u32[]{:S(2)}) collective-permute-start(f32[48,128]{1,0:T(8,128)S(1)} %pad_maximum_fusion.2), channel_id=1, source_target_pairs={{0,64},{64,128},{128,192},{1,65},{65,129},{129,193},{2,66},{66,130... | collective-permute-start | bytes 73736 | tf_op jit(solution)/shard_map/ppermute | solution.py:323
  38.0 5.7 %collective-permute-start.3 = (f32[48,128]{1,0:T(8,128)S(1)}, f32[48,128]{1,0:T(8,128)S(1)}, u32[]{:S(2)}, u32[]{:S(2)}) collective-permute-start(f32[48,128]{1,0:T(8,128)S(1)} %pad_maximum_fusion.3), channel_id=1, source_target_pairs={{64,0},{128,64},{192,128},{65,1},{129,65},{193,129},{66,2},{130,66... | collective-permute-start | bytes 73736 | tf_op jit(solution)/shard_map/ppermute | solution.py:324
  41.2 8.8 %copy-start.10 = (f32[48,128]{1,0:T(8,128)}, f32[48,128]{1,0:T(8,128)S(1)}, u32[]{:S(2)}) copy-start(f32[48,128]{1,0:T(8,128)S(1)} %collective-permute-done.2.kx_low) | copy-start | bytes 73732
  62.8 23.3 %all-to-all-start.1 = ((f32[8,152,128]{2,1,0:T(8,128)}), f32[8,152,128]{2,1,0:T(8,128)S(1)}, u32[]{:S(2)}, u32[]{:S(2)}) async-start(f32[8,152,128]{2,1,0:T(8,128)} %get-tuple-element.38), calls=%async_computation.1 | async-start | bytes 1245184 | tf_op jit(solution)/shard_map/all_to_all | solution.py:349
  67.2 12.3 %collective-permute-start.5 = (f32[48,128]{1,0:T(8,128)S(1)}, f32[48,128]{1,0:T(8,128)S(1)}, u32[]{:S(2)}, u32[]{:S(2)}) collective-permute-start(f32[48,128]{1,0:T(8,128)S(1)} %get-tuple-element.93), channel_id=1, source_target_pairs={{64,0},{128,64},{192,128},{65,1},{129,65},{193,129},{66,2},{130,66... | collective-permute-start | bytes 73736 | tf_op jit(solution)/shard_map/ppermute | solution.py:348
  69.9 9.6 %collective-permute-start.4 = (f32[48,128]{1,0:T(8,128)S(1)}, f32[48,128]{1,0:T(8,128)S(1)}, u32[]{:S(2)}, u32[]{:S(2)}) collective-permute-start(f32[48,128]{1,0:T(8,128)S(1)} %get-tuple-element.94), channel_id=1, source_target_pairs={{0,64},{64,128},{128,192},{1,65},{65,129},{129,193},{2,66},{66,130... | collective-permute-start | bytes 73736 | tf_op jit(solution)/shard_map/ppermute | solution.py:347
  100.6 25.0 %all-to-all-start.2 = ((f32[8,152,128]{2,1,0:T(8,128)}), f32[8,152,128]{2,1,0:T(8,128)S(1)}, u32[]{:S(2)}, u32[]{:S(2)}) async-start(f32[8,152,128]{2,1,0:T(8,128)} %get-tuple-element.49), calls=%async_computation.2 | async-start | bytes 1245184 | tf_op jit(solution)/shard_map/all_to_all | solution.py:349
  105.1 13.4 %collective-permute-start.7 = (f32[48,128]{1,0:T(8,128)S(1)}, f32[48,128]{1,0:T(8,128)S(1)}, u32[]{:S(2)}, u32[]{:S(2)}) collective-permute-start(f32[48,128]{1,0:T(8,128)S(1)} %get-tuple-element.91), channel_id=1, source_target_pairs={{64,0},{128,64},{192,128},{65,1},{129,65},{193,129},{66,2},{130,66... | collective-permute-start | bytes 73736 | tf_op jit(solution)/shard_map/ppermute | solution.py:348
  108.4 10.1 %collective-permute-start.6 = (f32[48,128]{1,0:T(8,128)S(1)}, f32[48,128]{1,0:T(8,128)S(1)}, u32[]{:S(2)}, u32[]{:S(2)}) collective-permute-start(f32[48,128]{1,0:T(8,128)S(1)} %get-tuple-element.92), channel_id=1, source_target_pairs={{0,64},{64,128},{128,192},{1,65},{65,129},{129,193},{2,66},{66,130... | collective-permute-start | bytes 73736 | tf_op jit(solution)/shard_map/ppermute | solution.py:347
  118.5 7.1 %copy-start.13 = (f32[48,128]{1,0:T(8,128)}, f32[48,128]{1,0:T(8,128)S(1)}, u32[]{:S(2)}) copy-start(f32[48,128]{1,0:T(8,128)S(1)} %collective-permute-done.7.refs_5_) | copy-start | bytes 73732
  140.2 23.7 %all-to-all-start.3 = ((f32[8,152,128]{2,1,0:T(8,128)}), f32[8,152,128]{2,1,0:T(8,128)S(1)}, u32[]{:S(2)}, u32[]{:S(2)}) async-start(f32[8,152,128]{2,1,0:T(8,128)} %get-tuple-element.54), calls=%async_computation.3 | async-start | bytes 1245184 | tf_op jit(solution)/shard_map/all_to_all | solution.py:349
  144.5 13.2 %collective-permute-start.9 = (f32[48,128]{1,0:T(8,128)S(1)}, f32[48,128]{1,0:T(8,128)S(1)}, u32[]{:S(2)}, u32[]{:S(2)}) collective-permute-start(f32[48,128]{1,0:T(8,128)S(1)} %get-tuple-element.89), channel_id=1, source_target_pairs={{64,0},{128,64},{192,128},{65,1},{129,65},{193,129},{66,2},{130,66... | collective-permute-start | bytes 73736 | tf_op jit(solution)/shard_map/ppermute | solution.py:348
  147.6 10.1 %collective-permute-start.8 = (f32[48,128]{1,0:T(8,128)S(1)}, f32[48,128]{1,0:T(8,128)S(1)}, u32[]{:S(2)}, u32[]{:S(2)}) collective-permute-start(f32[48,128]{1,0:T(8,128)S(1)} %get-tuple-element.90), channel_id=1, source_target_pairs={{0,64},{64,128},{128,192},{1,65},{65,129},{129,193},{2,66},{66,130... | collective-permute-start | bytes 73736 | tf_op jit(solution)/shard_map/ppermute | solution.py:347
  178.5 25.4 %all-to-all-start.4 = ((f32[8,152,128]{2,1,0:T(8,128)}), f32[8,152,128]{2,1,0:T(8,128)S(1)}, u32[]{:S(2)}, u32[]{:S(2)}) async-start(f32[8,152,128]{2,1,0:T(8,128)} %get-tuple-element.59), calls=%async_computation.4 | async-start | bytes 1245184 | tf_op jit(solution)/shard_map/all_to_all | solution.py:349
  183.4 13.4 %collective-permute-start.11 = (f32[48,128]{1,0:T(8,128)S(1)}, f32[48,128]{1,0:T(8,128)S(1)}, u32[]{:S(2)}, u32[]{:S(2)}) collective-permute-start(f32[48,128]{1,0:T(8,128)S(1)} %get-tuple-element.87), channel_id=1, source_target_pairs={{64,0},{128,64},{192,128},{65,1},{129,65},{193,129},{66,2},{130,66... | collective-permute-start | bytes 73736 | tf_op jit(solution)/shard_map/ppermute | solution.py:348
  186.7 10.1 %collective-permute-start.10 = (f32[48,128]{1,0:T(8,128)S(1)}, f32[48,128]{1,0:T(8,128)S(1)}, u32[]{:S(2)}, u32[]{:S(2)}) collective-permute-start(f32[48,128]{1,0:T(8,128)S(1)} %get-tuple-element.88), channel_id=1, source_target_pairs={{0,64},{64,128},{128,192},{1,65},{65,129},{129,193},{2,66},{66,130... | collective-permute-start | bytes 73736 | tf_op jit(solution)/shard_map/ppermute | solution.py:347
  196.8 7.1 %copy-start.15 = (f32[48,128]{1,0:T(8,128)}, f32[48,128]{1,0:T(8,128)S(1)}, u32[]{:S(2)}) copy-start(f32[48,128]{1,0:T(8,128)S(1)} %collective-permute-done.11.refs_5_) | copy-start | bytes 73732
  196.8 7.1 %copy-start.20 = (f32[48,128]{1,0:T(8,128)}, f32[48,128]{1,0:T(8,128)S(1)}, u32[]{:S(2)}) copy-start(f32[48,128]{1,0:T(8,128)S(1)} %collective-permute-done.10.refs_4_) | copy-start | bytes 73732
  218.5 23.6 %all-to-all-start.5 = ((f32[8,152,128]{2,1,0:T(8,128)}), f32[8,152,128]{2,1,0:T(8,128)S(1)}, u32[]{:S(2)}, u32[]{:S(2)}) async-start(f32[8,152,128]{2,1,0:T(8,128)} %get-tuple-element.64), calls=%async_computation.5 | async-start | bytes 1245184 | tf_op jit(solution)/shard_map/all_to_all | solution.py:349
  222.8 13.1 %collective-permute-start.13 = (f32[48,128]{1,0:T(8,128)S(1)}, f32[48,128]{1,0:T(8,128)S(1)}, u32[]{:S(2)}, u32[]{:S(2)}) collective-permute-start(f32[48,128]{1,0:T(8,128)S(1)} %get-tuple-element.85), channel_id=1, source_target_pairs={{64,0},{128,64},{192,128},{65,1},{129,65},{193,129},{66,2},{130,66... | collective-permute-start | bytes 73736 | tf_op jit(solution)/shard_map/ppermute | solution.py:348
  225.9 10.0 %collective-permute-start.12 = (f32[48,128]{1,0:T(8,128)S(1)}, f32[48,128]{1,0:T(8,128)S(1)}, u32[]{:S(2)}, u32[]{:S(2)}) collective-permute-start(f32[48,128]{1,0:T(8,128)S(1)} %get-tuple-element.86), channel_id=1, source_target_pairs={{0,64},{64,128},{128,192},{1,65},{65,129},{129,193},{2,66},{66,130... | collective-permute-start | bytes 73736 | tf_op jit(solution)/shard_map/ppermute | solution.py:347
  (18 other events, 66.7 us)
where the time goes:
time: 254 us; the launch traced here: 252 us
  waiting for transfers between devices  85.2 us (34%)
  Pallas kernels  82.5 us (32%)
  starting transfers between devices  68 us (27%)
  local copies, waits for them, and re-layouts  14.1 us (6%)
    pallas_call x5, Pallas kernels, local(): pl.pallas_call(kernel, out_shape=small if last else (big, big, small, edg...  64.5 us
    all_to_all x6, waiting for transfers between devices, local(): a8 = lax.all_to_all(a8, 'gz', 0, 0, tiled=True)  39.6 us
    ppermute x5, waiting for transfers between devices, local(): xhigh = lax.ppermute(xf[0], 'gx', down_x)  36 us
    all_to_all x6, starting transfers between devices, local(): a8 = lax.all_to_all(a8, 'gz', 0, 0, tiled=True)  28.5 us
    ppermute x5, starting transfers between devices, local(): xhigh = lax.ppermute(xf[0], 'gx', down_x)  15.6 us
    ppermute x5, starting transfers between devices, local(): xlow = lax.ppermute(xf[1], 'gx', up_x)  13.8 us
    pallas_call x1, Pallas kernels, local(): pl.pallas_call(setup_kernel, out_shape=(big, big, big, tall, big, big, bi...  12.1 us
    pallas_call x1, Pallas kernels, local(): pl.pallas_call(first_kernel, out_shape=struct(tiles, half + 2 * cx, cz),...  6 us
  transfers between devices with their start and end apart: 20, of which 15 were waited for; matrix products, arithmetic and copies ran while one was open for 3% of the time, Pallas kernels for 0%

commit v1 on v0

--- a/solution.py
+++ b/solution.py
@@ -99,7 +99,7 @@
         out_ref[t, base + q * cx : base + (q + 1) * cx, :] = sums[t * cx : (t + 1) * cx]
 
 
-def first_kernel(own_k, before, after, col_ref, row_ref, out_ref):
+def first_kernel(own_k, before, after, col_ref, row_ref, out_ref, kx_first, kx_last):
     tiles = out_ref.shape[0]
     cx = own_k.shape[1]
 
@@ -108,8 +108,11 @@
         slab = jnp.concatenate([before[pl.ds(at, H), :], own_k[2, x], after[pl.ds(at, H), :]], axis=0)
         return pack_faces(faces, slab, x)
 
+    for x, face in ((0, kx_first), (cx - 1, kx_last)):
+        at = (2 * cx + x) * H
+        face[...] = jnp.concatenate([before[at : at + H, :], own_k[0, x], after[at : at + H, :]], axis=0)
     half = (own_k.shape[2] + 2 * H) // 2
-    faces = lax.fori_loop(0, cx, body, jnp.zeros((half, 128), f32))
+    faces = lax.fori_loop(0, cx, body, jnp.zeros((half, 128), f32), unroll=4)
     for t in range(tiles):
         out_ref[t, 0:half, :] = faces
     for q in range(2):
@@ -153,7 +156,7 @@
 
 
 def setup_kernel(l_ref, rhs, acc, perm, before, after, kx_low, kx_high, a8, col_ref, row_ref,
-                 inv, z_out, d_out, tx, tym, typ, tzm, tzp, xf, a8_out, planes, fault):
+                 inv, z_out, d_out, tx, tym, typ, tzm, tzp, d_first, d_last, a8_out, planes, fault):
     cx, cy = rhs.shape[0], rhs.shape[1]
     ye = cy + 2 * H
     half = ye // 2
@@ -207,9 +210,9 @@
 
     kx0 = ext(2, perm[0, 0], 0)
     init = (jnp.zeros((half, 128), f32), harmonic(kx_low[...], kx0), kx0)
-    faces, _, _ = lax.fori_loop(0, cx, body, init)
-    xf[0] = d_out[0]
-    xf[1] = d_out[cx - 1]
+    faces, _, _ = lax.fori_loop(0, cx, body, init, unroll=4)
+    d_first[...] = d_out[0]
+    d_last[...] = d_out[cx - 1]
     emit(a8_out, planes, faces, col_ref, row_ref)
 
 
@@ -221,7 +224,7 @@
     if last:
         corr_out, fault = outs
     else:
-        d_out, z_out, corr_out, xf, a8_out, planes, fault = outs
+        d_out, z_out, corr_out, d_first, d_last, a8_out, planes, fault = outs
     cx, ye = d_in.shape[0], d_in.shape[1]
     cy = ye - 2 * H
     half = ye // 2
@@ -259,15 +262,16 @@
         return pack_faces(faces, new, x), d, d_next
 
     init = (jnp.zeros((half, 128), f32), xlow[...], d_in[0])
-    faces, _, _ = lax.fori_loop(0, cx, body, init)
+    faces, _, _ = lax.fori_loop(0, cx, body, init, unroll=4)
     if not last:
-        xf[0] = d_out[0]
-        xf[1] = d_out[cx - 1]
+        d_first[...] = d_out[0]
+        d_last[...] = d_out[cx - 1]
         emit(a8_out, planes, faces, col_ref, row_ref)
 
 
 VMEM = pl.BlockSpec(memory_space=pltpu.VMEM)
 SMEM = pl.BlockSpec(memory_space=pltpu.SMEM)
+PARAMS = pltpu.CompilerParams(vmem_limit_bytes=24 << 20)
 
 
 def steps(axis):
@@ -311,30 +315,31 @@
     )
     row = jnp.stack([own_x, far_code], axis=1)
 
+    edge = struct(ye, cz)
+    a8, kx_first, kx_last = pl.pallas_call(
+        first_kernel,
+        out_shape=(struct(tiles, half + 2 * cx, cz), edge, edge),
+        in_specs=[VMEM] * 5,
+        out_specs=(VMEM,) * 3,
+        compiler_params=PARAMS,
+    )(permeability, before, after, col, row)
+    kx_low = lax.ppermute(kx_last, "gx", up_x)
+    kx_high = lax.ppermute(kx_first, "gx", down_x)
     l = lax.axis_index("gz").reshape(1).astype(jnp.int32)
-    a8 = pl.pallas_call(
-        first_kernel, out_shape=struct(tiles, half + 2 * cx, cz), in_specs=[VMEM] * 5, out_specs=VMEM
-    )(permeability, before, after, col, row)
-
-    def kx_face(x):
-        at = (2 * cx + x) * H
-        return jnp.concatenate([before[at : at + H], permeability[0, x], after[at : at + H]], axis=0)
-
-    kx_low = lax.ppermute(kx_face(cx - 1), "gx", up_x)
-    kx_high = lax.ppermute(kx_face(0), "gx", down_x)
+    l, a8, kx_low, kx_high = lax.optimization_barrier((l, a8, kx_low, kx_high))
     a8 = lax.all_to_all(a8, "gz", 0, 0, tiled=True)
 
     big = struct(cx, ye, cz)
     tall = struct(cx + 1, ye, cz)
     sent = struct(tiles, 4 * cx + half, cz)
-    edge = struct(2, ye, cz)
     scratch = [pltpu.VMEM((4, cx, cz), f32)]
-    inv, z, d, tx, tym, typ, tzm, tzp, xf, a8 = pl.pallas_call(
+    inv, z, d, tx, tym, typ, tzm, tzp, d_first, d_last, a8 = pl.pallas_call(
         setup_kernel,
-        out_shape=(big, big, big, tall, big, big, big, big, edge, sent),
+        out_shape=(big, big, big, tall, big, big, big, big, edge, edge, sent),
         in_specs=[SMEM] + [VMEM] * 10,
-        out_specs=(VMEM,) * 10,
+        out_specs=(VMEM,) * 11,
         scratch_shapes=scratch * 2,
+        compiler_params=PARAMS,
     )(l, rhs, accumulation, permeability, before, after, kx_low, kx_high, a8, col, row)
 
     rho = 1.0 / sigma
@@ -344,8 +349,9 @@
         rho_next = 1.0 / (2.0 * sigma - rho)
         c1, c2 = rho_next * rho, 2.0 * rho_next / delta
         rho = rho_next
-        xlow = lax.ppermute(xf[1], "gx", up_x)
-        xhigh = lax.ppermute(xf[0], "gx", down_x)
+        xlow = lax.ppermute(d_last, "gx", up_x)
+        xhigh = lax.ppermute(d_first, "gx", down_x)
+        a8, xlow, xhigh = lax.optimization_barrier((a8, xlow, xhigh))
         a8 = lax.all_to_all(a8, "gz", 0, 0, tiled=True)
         args = [l, d, z] + ([] if first else [corr])
         args += [xlow, xhigh, a8, inv, tx, tym, typ, tzm, tzp, col, row]
@@ -356,15 +362,16 @@
         small = struct(cx, cy, cz)
         out = pl.pallas_call(
             kernel,
-            out_shape=small if last else (big, big, small, edge, sent),
+            out_shape=small if last else (big, big, small, edge, edge, sent),
             in_specs=[SMEM] + [VMEM] * (len(args) - 1),
-            out_specs=VMEM if last else (VMEM,) * 5,
+            out_specs=VMEM if last else (VMEM,) * 6,
             scratch_shapes=scratch if last else scratch * 2,
+            compiler_params=PARAMS,
         )(*args)
         if last:
             corr = out
         else:
-            d, z, corr, xf, a8 = out
+            d, z, corr, d_first, d_last, a8 = out
     return corr
 
 

time: 254 us -> 232 us (0.913)
  the two profiles are of different devices: /device:TPU:40 before, /device:TPU:2 now
where the time goes in v1:
time: 232 us; the launch traced here: 231 us
  blocking collectives  117 us (50%)
  starting transfers between devices  41.7 us (18%)
  Pallas kernels  37.1 us (16%)
  waiting for transfers between devices  28.2 us (12%)
  local copies, waits for them, and re-layouts  4.32 us (2%)
  other arithmetic  2.71 us (1%)
    all_to_all x6, blocking collectives, local(): a8 = lax.all_to_all(a8, 'gz', 0, 0, tiled=True)  117 us
    pallas_call x5, Pallas kernels, local(): pl.pallas_call(kernel, out_shape=small if last else (big, big, small, edg...  30.3 us
    ppermute x5, starting transfers between devices, local(): xlow = lax.ppermute(d_last, 'gx', up_x)  25.6 us
    ppermute x5, waiting for transfers between devices, local(): xhigh = lax.ppermute(d_first, 'gx', down_x)  21.5 us
    ppermute x5, starting transfers between devices, local(): xhigh = lax.ppermute(d_first, 'gx', down_x)  6.46 us
    pallas_call x1, Pallas kernels, local(): pl.pallas_call(setup_kernel, out_shape=(big, big, big, tall, big, big, bi...  4.96 us
  transfers between devices with their start and end apart: 14, of which 13 were waited for; matrix products, arithmetic and copies ran while one was open for 1% of the time, Pallas kernels for 0%

profile of v1, /device:TPU:2, one launch (start us, length us, event | category | flops | bytes accessed | tf_op | source)
XLA Modules:
  0.0 231.3 jit_solution(6452582508865258396)
XLA Ops:
  5.2 3.1 %collective-permute-start = (f32[1280,128]{1,0:T(8,128)}, f32[1280,128]{1,0:T(8,128)S(1)}, u32[]{:S(2)}, u32[]{:S(2)}) collective-permute-start(f32[1280,128]{1,0:T(8,128)} %bitcast.3), channel_id=1, source_target_pairs={{0,8},{8,16},{16,24},{24,32},{32,40},{40,48},{48,56},{1,9},{9,17},... | collective-permute-start | bytes 1966088 | tf_op jit(solution)/shard_map/ppermute | solution.py:302
  12.7 3.8 %collective-permute-start.2 = (f32[48,128]{1,0:T(8,128)S(1)}, f32[48,128]{1,0:T(8,128)S(1)}, u32[]{:S(2)}, u32[]{:S(2)}) collective-permute-start(f32[48,128]{1,0:T(8,128)S(1)} %get-tuple-element.63), channel_id=1, source_target_pairs={{0,64},{64,128},{128,192},{1,65},{65,129},{129,193},{2,66},{66,130... | collective-permute-start | bytes 73736 | tf_op jit(solution)/shard_map/ppermute | solution.py:326
  18.0 4.2 %collective-permute-done.3.kx_high = f32[48,128]{1,0:T(8,128)S(1)} collective-permute-done((f32[48,128]{1,0:T(8,128)S(1)}, f32[48,128]{1,0:T(8,128)S(1)}, u32[]{:S(2)}, u32[]{:S(2)}) %collective-permute-start.3) | collective-permute-done | bytes 24608 | tf_op jit(solution)/shard_map/ppermute | solution.py:327
  22.2 20.9 %all_to_all.30.a8 = f32[8,88,128]{2,1,0:T(8,128)S(1)} all-to-all(f32[8,88,128]{2,1,0:T(8,128)} %copy-done.5), channel_id=1, replica_groups=mesh['gx'=4,'gy'=8,'gz'=8] {'gz'}, dimensions={0} | all-to-all | bytes 720896 | tf_op jit(solution)/shard_map/all_to_all | solution.py:330
  45.3 5.0 %shard_map.74 = (f32[32,48,128]{2,1,0:T(8,128)S(1)}, f32[32,48,128]{2,1,0:T(8,128)S(1)}, f32[32,48,128]{2,1,0:T(8,128)S(1)}, f32[33,48,128]{2,1,0:T(8,128)S(1)},...) custom-call(s32[1]{0:T(128)} %bitcast.l_ref.refs_0_, ...), custom_call_target="tpu_custom_call" | custom-call | tf_op jit(solution)/shard_map/pallas_call | solution.py:336
  50.2 4.4 %collective-permute-start.4 = (f32[48,128]{1,0:T(8,128)S(1)}, f32[48,128]{1,0:T(8,128)S(1)}, u32[]{:S(2)}, u32[]{:S(2)}) collective-permute-start(f32[48,128]{1,0:T(8,128)S(1)} %get-tuple-element.72), channel_id=1, source_target_pairs={{0,64},{64,128},{128,192},{1,65},{65,129},{129,193},{2,66},{66,130... | collective-permute-start | bytes 73736 | tf_op jit(solution)/shard_map/ppermute | solution.py:352
  56.1 4.2 %collective-permute-done.5.refs_4_ = f32[48,128]{1,0:T(8,128)S(1)} collective-permute-done((f32[48,128]{1,0:T(8,128)S(1)}, f32[48,128]{1,0:T(8,128)S(1)}, u32[]{:S(2)}, u32[]{:S(2)}) %collective-permute-start.5) | collective-permute-done | bytes 24608 | tf_op jit(solution)/shard_map/ppermute | solution.py:353
  60.3 18.5 %all_to_all.31.refs_5_ = f32[8,152,128]{2,1,0:T(8,128)S(1)} all-to-all(f32[8,152,128]{2,1,0:T(8,128)S(1)} %get-tuple-element.76), channel_id=1, replica_groups=mesh['gx'=4,'gy'=8,'gz'=8] {'gz'}, dimensions={0} | all-to-all | bytes 1245184 | tf_op jit(solution)/shard_map/all_to_all | solution.py:355
  78.8 6.5 %shard_map.75 = (f32[32,48,128]{2,1,0:T(8,128)S(1)}, f32[32,48,128]{2,1,0:T(8,128)S(1)}, f32[32,32,128]{2,1,0:T(8,128)S(1)}, f32[48,128]{1,0:T(8,128)S(1)}, f32[...) custom-call(s32[1]{0:T(128)} %bitcast.l_ref.refs_0_, f32[32,48,128]{2,1,0:T(8,128)S(1)} %get-tuple-element.69.refs_1_, ...), custom_call_target="tpu_custom_call" | custom-call | tf_op jit(solution)/shard_map/pallas_call | solution.py:363
  85.3 8.6 %collective-permute-start.6 = (f32[48,128]{1,0:T(8,128)S(1)}, f32[48,128]{1,0:T(8,128)S(1)}, u32[]{:S(2)}, u32[]{:S(2)}) collective-permute-start(f32[48,128]{1,0:T(8,128)S(1)} %get-tuple-element.87), channel_id=1, source_target_pairs={{0,64},{64,128},{128,192},{1,65},{65,129},{129,193},{2,66},{66,130... | collective-permute-start | bytes 73736 | tf_op jit(solution)/shard_map/ppermute | solution.py:352
  95.4 4.2 %collective-permute-done.7.refs_5_ = f32[48,128]{1,0:T(8,128)S(1)} collective-permute-done((f32[48,128]{1,0:T(8,128)S(1)}, f32[48,128]{1,0:T(8,128)S(1)}, u32[]{:S(2)}, u32[]{:S(2)}) %collective-permute-start.7) | collective-permute-done | bytes 24608 | tf_op jit(solution)/shard_map/ppermute | solution.py:353
  99.7 18.1 %all_to_all.32.refs_6_ = f32[8,152,128]{2,1,0:T(8,128)S(1)} all-to-all(f32[8,152,128]{2,1,0:T(8,128)S(1)} %get-tuple-element.91), channel_id=1, replica_groups=mesh['gx'=4,'gy'=8,'gz'=8] {'gz'}, dimensions={0} | all-to-all | bytes 1245184 | tf_op jit(solution)/shard_map/all_to_all | solution.py:355
  117.8 6.5 %shard_map.76 = (f32[32,48,128]{2,1,0:T(8,128)S(1)}, f32[32,48,128]{2,1,0:T(8,128)S(1)}, f32[32,32,128]{2,1,0:T(8,128)S(1)}, f32[48,128]{1,0:T(8,128)S(1)}, f32[...) custom-call(s32[1]{0:T(128)} %bitcast.l_ref.refs_0_, f32[32,48,128]{2,1,0:T(8,128)S(1)} %get-tuple-element.83.refs_1_, ...), custom_call_target="tpu_custom_call" | custom-call | tf_op jit(solution)/shard_map/pallas_call | solution.py:363
  124.3 7.5 %collective-permute-start.8 = (f32[48,128]{1,0:T(8,128)S(1)}, f32[48,128]{1,0:T(8,128)S(1)}, u32[]{:S(2)}, u32[]{:S(2)}) collective-permute-start(f32[48,128]{1,0:T(8,128)S(1)} %get-tuple-element.96), channel_id=1, source_target_pairs={{0,64},{64,128},{128,192},{1,65},{65,129},{129,193},{2,66},{66,130... | collective-permute-start | bytes 73736 | tf_op jit(solution)/shard_map/ppermute | solution.py:352
  133.3 4.2 %collective-permute-done.9.refs_5_ = f32[48,128]{1,0:T(8,128)S(1)} collective-permute-done((f32[48,128]{1,0:T(8,128)S(1)}, f32[48,128]{1,0:T(8,128)S(1)}, u32[]{:S(2)}, u32[]{:S(2)}) %collective-permute-start.9) | collective-permute-done | bytes 24608 | tf_op jit(solution)/shard_map/ppermute | solution.py:353
  137.5 21.2 %all_to_all.33.refs_6_ = f32[8,152,128]{2,1,0:T(8,128)S(1)} all-to-all(f32[8,152,128]{2,1,0:T(8,128)S(1)} %get-tuple-element.100), channel_id=1, replica_groups=mesh['gx'=4,'gy'=8,'gz'=8] {'gz'}, dimensions={0} | all-to-all | bytes 1245184 | tf_op jit(solution)/shard_map/all_to_all | solution.py:355
  158.7 6.5 %shard_map.77 = (f32[32,48,128]{2,1,0:T(8,128)S(1)}, f32[32,48,128]{2,1,0:T(8,128)S(1)}, f32[32,32,128]{2,1,0:T(8,128)S(1)}, f32[48,128]{1,0:T(8,128)S(1)}, f32[...) custom-call(s32[1]{0:T(128)} %bitcast.l_ref.refs_0_, f32[32,48,128]{2,1,0:T(8,128)S(1)} %get-tuple-element.92.refs_1_, ...), custom_call_target="tpu_custom_call" | custom-call | tf_op jit(solution)/shard_map/pallas_call | solution.py:363
  165.2 3.3 %collective-permute-start.10 = (f32[48,128]{1,0:T(8,128)S(1)}, f32[48,128]{1,0:T(8,128)S(1)}, u32[]{:S(2)}, u32[]{:S(2)}) collective-permute-start(f32[48,128]{1,0:T(8,128)S(1)} %get-tuple-element.105), channel_id=1, source_target_pairs={{0,64},{64,128},{128,192},{1,65},{65,129},{129,193},{2,66},{66,130... | collective-permute-start | bytes 73736 | tf_op jit(solution)/shard_map/ppermute | solution.py:352
  170.0 4.2 %collective-permute-done.11.refs_5_ = f32[48,128]{1,0:T(8,128)S(1)} collective-permute-done((f32[48,128]{1,0:T(8,128)S(1)}, f32[48,128]{1,0:T(8,128)S(1)}, u32[]{:S(2)}, u32[]{:S(2)}) %collective-permute-start.11) | collective-permute-done | bytes 24608 | tf_op jit(solution)/shard_map/ppermute | solution.py:353
  174.2 20.5 %all_to_all.34.refs_6_ = f32[8,152,128]{2,1,0:T(8,128)S(1)} all-to-all(f32[8,152,128]{2,1,0:T(8,128)S(1)} %get-tuple-element.109), channel_id=1, replica_groups=mesh['gx'=4,'gy'=8,'gz'=8] {'gz'}, dimensions={0} | all-to-all | bytes 1245184 | tf_op jit(solution)/shard_map/all_to_all | solution.py:355
  194.8 6.5 %shard_map.78 = (f32[32,48,128]{2,1,0:T(8,128)S(1)}, f32[32,48,128]{2,1,0:T(8,128)S(1)}, f32[32,32,128]{2,1,0:T(8,128)S(1)}, f32[48,128]{1,0:T(8,128)S(1)}, f32[...) custom-call(s32[1]{0:T(128)} %bitcast.l_ref.refs_0_, f32[32,48,128]{2,1,0:T(8,128)S(1)} %get-tuple-element.101.refs_1_, ...), custom_call_target="tpu_custom_call" | custom-call | tf_op jit(solution)/shard_map/pallas_call | solution.py:363
  204.6 4.6 %collective-permute-done.13.refs_5_ = f32[48,128]{1,0:T(8,128)S(1)} collective-permute-done((f32[48,128]{1,0:T(8,128)S(1)}, f32[48,128]{1,0:T(8,128)S(1)}, u32[]{:S(2)}, u32[]{:S(2)}) %collective-permute-start.13) | collective-permute-done | bytes 24608 | tf_op jit(solution)/shard_map/ppermute | solution.py:353
  209.1 17.8 %all_to_all.35.refs_6_ = f32[8,152,128]{2,1,0:T(8,128)S(1)} all-to-all(f32[8,152,128]{2,1,0:T(8,128)S(1)} %get-tuple-element.118), channel_id=1, replica_groups=mesh['gx'=4,'gy'=8,'gz'=8] {'gz'}, dimensions={0} | all-to-all | bytes 1245184 | tf_op jit(solution)/shard_map/all_to_all | solution.py:355
  226.9 4.4 %shard_map.79 = f32[32,32,128]{2,1,0:T(8,128)} custom-call(s32[1]{0:T(128)} %bitcast.l_ref.refs_0_, f32[32,48,128]{2,1,0:T(8,128)S(1)} %get-tuple-element.110.refs_1_, f32[32,48,128]{2,1,0:T(8,128)S(1)} %get-tuple-element.111.refs_2_, f32[32,32,128]{2,1,0:T(8,128)S(1)} %get-tuple-element.112.refs_3_, f32[48,128]{1,0:T(8,128)S(1)} %collective-permute-done.12.refs_4_, ...), custom_call_target="tpu_custom_call" | custom-call | tf_op jit(solution)/shard_map/pallas_call | solution.py:363
  (49 shorter events, 22.3 us)
Async XLA Ops:
  0.0 2.7 %copy-start.3 = (f32[32,32,128]{2,1,0:T(8,128)S(1)}, f32[32,32,128]{2,1,0:T(8,128)}, u32[]{:S(2)}) copy-start(f32[32,32,128]{2,1,0:T(8,128)} %acc.1) | copy-start | bytes 1572868
  0.0 2.7 %copy-start.1 = (f32[32,32,128]{2,1,0:T(8,128)S(1)}, f32[32,32,128]{2,1,0:T(8,128)}, u32[]{:S(2)}) copy-start(f32[32,32,128]{2,1,0:T(8,128)} %rhs.1) | copy-start | bytes 1572868
  2.8 7.3 %copy-start = (f32[3,32,32,128]{3,2,1,0:T(8,128)S(1)}, f32[3,32,32,128]{3,2,1,0:T(8,128)}, u32[]{:S(2)}) copy-start(f32[3,32,32,128]{3,2,1,0:T(8,128)} %perm.1) | copy-start | bytes 4718596
  2.9 5.4 %collective-permute-start.1 = (f32[1296,128]{1,0:T(8,128)S(1)}, f32[1296,128]{1,0:T(8,128)S(1)}, u32[]{:S(2)}, u32[]{:S(2)}) collective-permute-start(f32[1296,128]{1,0:T(8,128)S(1)} %select_maximum_fusion), channel_id=1, source_target_pairs={{8,0},{16,8},{24,16},{32,24},{40,32},{48,40},{56,48},{9,1},{17,9},... | collective-permute-start | bytes 1990664 | tf_op jit(solution)/shard_map/ppermute | solution.py:303
  5.2 4.9 %collective-permute-start = (f32[1280,128]{1,0:T(8,128)}, f32[1280,128]{1,0:T(8,128)S(1)}, u32[]{:S(2)}, u32[]{:S(2)}) collective-permute-start(f32[1280,128]{1,0:T(8,128)} %bitcast.3), channel_id=1, source_target_pairs={{0,8},{8,16},{16,24},{24,32},{32,40},{40,48},{48,56},{1,9},{9,17},... | collective-permute-start | bytes 1966088 | tf_op jit(solution)/shard_map/ppermute | solution.py:302
  11.9 0.7 copy-start.5
  12.7 5.3 %collective-permute-start.2 = (f32[48,128]{1,0:T(8,128)S(1)}, f32[48,128]{1,0:T(8,128)S(1)}, u32[]{:S(2)}, u32[]{:S(2)}) collective-permute-start(f32[48,128]{1,0:T(8,128)S(1)} %get-tuple-element.63), channel_id=1, source_target_pairs={{0,64},{64,128},{128,192},{1,65},{65,129},{129,193},{2,66},{66,130... | collective-permute-start | bytes 73736 | tf_op jit(solution)/shard_map/ppermute | solution.py:326
  16.5 5.7 %collective-permute-start.3 = (f32[48,128]{1,0:T(8,128)S(1)}, f32[48,128]{1,0:T(8,128)S(1)}, u32[]{:S(2)}, u32[]{:S(2)}) collective-permute-start(f32[48,128]{1,0:T(8,128)S(1)} %get-tuple-element.64), channel_id=1, source_target_pairs={{64,0},{128,64},{192,128},{65,1},{129,65},{193,129},{66,2},{130,66... | collective-permute-start | bytes 73736 | tf_op jit(solution)/shard_map/ppermute | solution.py:327
  43.2 1.0 copy-start.2
  44.2 1.0 copy-start.4
  50.2 5.9 %collective-permute-start.4 = (f32[48,128]{1,0:T(8,128)S(1)}, f32[48,128]{1,0:T(8,128)S(1)}, u32[]{:S(2)}, u32[]{:S(2)}) collective-permute-start(f32[48,128]{1,0:T(8,128)S(1)} %get-tuple-element.72), channel_id=1, source_target_pairs={{0,64},{64,128},{128,192},{1,65},{65,129},{129,193},{2,66},{66,130... | collective-permute-start | bytes 73736 | tf_op jit(solution)/shard_map/ppermute | solution.py:352
  54.6 5.7 %collective-permute-start.5 = (f32[48,128]{1,0:T(8,128)S(1)}, f32[48,128]{1,0:T(8,128)S(1)}, u32[]{:S(2)}, u32[]{:S(2)}) collective-permute-start(f32[48,128]{1,0:T(8,128)S(1)} %get-tuple-element.73), channel_id=1, source_target_pairs={{64,0},{128,64},{192,128},{65,1},{129,65},{193,129},{66,2},{130,66... | collective-permute-start | bytes 73736 | tf_op jit(solution)/shard_map/ppermute | solution.py:353
  85.3 10.2 %collective-permute-start.6 = (f32[48,128]{1,0:T(8,128)S(1)}, f32[48,128]{1,0:T(8,128)S(1)}, u32[]{:S(2)}, u32[]{:S(2)}) collective-permute-start(f32[48,128]{1,0:T(8,128)S(1)} %get-tuple-element.87), channel_id=1, source_target_pairs={{0,64},{64,128},{128,192},{1,65},{65,129},{129,193},{2,66},{66,130... | collective-permute-start | bytes 73736 | tf_op jit(solution)/shard_map/ppermute | solution.py:352
  93.9 5.7 %collective-permute-start.7 = (f32[48,128]{1,0:T(8,128)S(1)}, f32[48,128]{1,0:T(8,128)S(1)}, u32[]{:S(2)}, u32[]{:S(2)}) collective-permute-start(f32[48,128]{1,0:T(8,128)S(1)} %get-tuple-element.88), channel_id=1, source_target_pairs={{64,0},{128,64},{192,128},{65,1},{129,65},{193,129},{66,2},{130,66... | collective-permute-start | bytes 73736 | tf_op jit(solution)/shard_map/ppermute | solution.py:353
  124.3 9.0 %collective-permute-start.8 = (f32[48,128]{1,0:T(8,128)S(1)}, f32[48,128]{1,0:T(8,128)S(1)}, u32[]{:S(2)}, u32[]{:S(2)}) collective-permute-start(f32[48,128]{1,0:T(8,128)S(1)} %get-tuple-element.96), channel_id=1, source_target_pairs={{0,64},{64,128},{128,192},{1,65},{65,129},{129,193},{2,66},{66,130... | collective-permute-start | bytes 73736 | tf_op jit(solution)/shard_map/ppermute | solution.py:352
  131.8 5.7 %collective-permute-start.9 = (f32[48,128]{1,0:T(8,128)S(1)}, f32[48,128]{1,0:T(8,128)S(1)}, u32[]{:S(2)}, u32[]{:S(2)}) collective-permute-start(f32[48,128]{1,0:T(8,128)S(1)} %get-tuple-element.97), channel_id=1, source_target_pairs={{64,0},{128,64},{192,128},{65,1},{129,65},{193,129},{66,2},{130,66... | collective-permute-start | bytes 73736 | tf_op jit(solution)/shard_map/ppermute | solution.py:353
  165.2 4.8 %collective-permute-start.10 = (f32[48,128]{1,0:T(8,128)S(1)}, f32[48,128]{1,0:T(8,128)S(1)}, u32[]{:S(2)}, u32[]{:S(2)}) collective-permute-start(f32[48,128]{1,0:T(8,128)S(1)} %get-tuple-element.105), channel_id=1, source_target_pairs={{0,64},{64,128},{128,192},{1,65},{65,129},{129,193},{2,66},{66,130... | collective-permute-start | bytes 73736 | tf_op jit(solution)/shard_map/ppermute | solution.py:352
  168.5 5.7 %collective-permute-start.11 = (f32[48,128]{1,0:T(8,128)S(1)}, f32[48,128]{1,0:T(8,128)S(1)}, u32[]{:S(2)}, u32[]{:S(2)}) collective-permute-start(f32[48,128]{1,0:T(8,128)S(1)} %get-tuple-element.106), channel_id=1, source_target_pairs={{64,0},{128,64},{192,128},{65,1},{129,65},{193,129},{66,2},{130,66... | collective-permute-start | bytes 73736 | tf_op jit(solution)/shard_map/ppermute | solution.py:353
  201.3 3.3 %collective-permute-start.12 = (f32[48,128]{1,0:T(8,128)S(1)}, f32[48,128]{1,0:T(8,128)S(1)}, u32[]{:S(2)}, u32[]{:S(2)}) collective-permute-start(f32[48,128]{1,0:T(8,128)S(1)} %get-tuple-element.114), channel_id=1, source_target_pairs={{0,64},{64,128},{128,192},{1,65},{65,129},{129,193},{2,66},{66,130... | collective-permute-start | bytes 73736 | tf_op jit(solution)/shard_map/ppermute | solution.py:352
  203.0 6.1 %collective-permute-start.13 = (f32[48,128]{1,0:T(8,128)S(1)}, f32[48,128]{1,0:T(8,128)S(1)}, u32[]{:S(2)}, u32[]{:S(2)}) collective-permute-start(f32[48,128]{1,0:T(8,128)S(1)} %get-tuple-element.115), channel_id=1, source_target_pairs={{64,0},{128,64},{192,128},{65,1},{129,65},{193,129},{66,2},{130,66... | collective-permute-start | bytes 73736 | tf_op jit(solution)/shard_map/ppermute | solution.py:353

commit v2 on v1

--- a/solution.py
+++ b/solution.py
@@ -99,7 +99,14 @@
         out_ref[t, base + q * cx : base + (q + 1) * cx, :] = sums[t * cx : (t + 1) * cx]
 
 
-def first_kernel(own_k, before, after, col_ref, row_ref, out_ref, kx_first, kx_last):
+def first_kernel(own_k, before, after, col_ref, row_ref, rhs, acc,
+                 out_ref, kx_first, kx_last, rhs_out, acc_out, sem):
+    moves = [
+        pltpu.make_async_copy(rhs, rhs_out, sem.at[0]),
+        pltpu.make_async_copy(acc, acc_out, sem.at[1]),
+    ]
+    for move in moves:
+        move.start()
     tiles = out_ref.shape[0]
     cx = own_k.shape[1]
 
@@ -117,6 +124,8 @@
         out_ref[t, 0:half, :] = faces
     for q in range(2):
         put_partials(out_ref, half, tiles, q, col_ref, row_ref, col_ref[q, :, 4:5], cx)
+    for move in moves:
+        move.wait()
 
 
 def emit(a8_ref, planes, faces, col_ref, row_ref):
@@ -155,8 +164,37 @@
     return low, high
 
 
-def setup_kernel(l_ref, rhs, acc, perm, before, after, kx_low, kx_high, a8, col_ref, row_ref,
-                 inv, z_out, d_out, tx, tym, typ, tzm, tzp, d_first, d_last, a8_out, planes, fault):
+def weights_kernel(a8, col_ref, row_ref, fault):
+    tiles, rows = a8.shape[0], a8.shape[1]
+    cx = fault.shape[1]
+    for q in range(2):
+        base = rows - (2 - q) * cx
+        far = a8[0, base : base + cx, :]
+        for t in range(1, tiles):
+            far = far + a8[t, base : base + cx, :]
+        fault[2 * q] = far
+        near = scatter(col_ref[q, :, 4:5], hits(col_ref, q, 0), rows_hit(row_ref, q, 0, cx))
+        fault[2 * q + 1] = near
+
+
+def fault_kernel(a8, col_ref, row_ref, fault):
+    tiles, rows = a8.shape[0], a8.shape[1]
+    cx = fault.shape[1]
+    for q in range(2):
+        base = rows - (2 - q) * cx
+        far = a8[0, base : base + cx, :]
+        for t in range(1, tiles):
+            far = far + a8[t, base : base + cx, :]
+        fault[2 * q] = far
+        table = jnp.concatenate([a8[t, q * cx : (q + 1) * cx, :] for t in range(tiles)], axis=0)
+        got = gather(table, hits(col_ref, q, 2), col_ref[q, :, 3:4])
+        fault[2 * q + 1] = scatter(
+            col_ref[q, :, 4:5] * got, hits(col_ref, q, 0), rows_hit(row_ref, q, 0, cx)
+        )
+
+
+def setup_kernel(l_ref, rhs, acc, perm, before, after, kx_low, kx_high, a8, fault, col_ref, row_ref,
+                 inv, z_out, d_out, tx, tym, typ, tzm, tzp, d_first, d_last, a8_out, planes):
     cx, cy = rhs.shape[0], rhs.shape[1]
     ye = cy + 2 * H
     half = ye // 2
@@ -165,14 +203,6 @@
     low_faces, high_faces = neighbour_faces(l_ref, a8, 0, half)
     low_faces = jnp.where(l > 0, low_faces, 0.0)
     high_faces = jnp.where(l < tiles - 1, high_faces, 0.0)
-    for q in range(2):
-        base = half + q * cx
-        far = a8[0, base : base + cx, :]
-        for t in range(1, tiles):
-            far = far + a8[t, base : base + cx, :]
-        fault[2 * q] = far
-        near = scatter(col_ref[q, :, 4:5], hits(col_ref, q, 0), rows_hit(row_ref, q, 0, cx))
-        fault[2 * q + 1] = near
 
     def ext(a, own, x):
         at = pl.multiple_of((a * cx + x) * H, H)
@@ -219,28 +249,16 @@
 def sweep_kernel(c1, c2, first, last, l_ref, d_in, z_in, *refs):
     refs = list(refs)
     corr_in = None if first else refs.pop(0)
-    xlow, xhigh, a8, inv, tx, tym, typ, tzm, tzp, col_ref, row_ref = refs[:11]
-    outs = refs[11:]
+    xlow, xhigh, a8, fault, inv, tx, tym, typ, tzm, tzp, col_ref, row_ref = refs[:12]
+    outs = refs[12:]
     if last:
-        corr_out, fault = outs
+        (corr_out,) = outs
     else:
-        d_out, z_out, corr_out, d_first, d_last, a8_out, planes, fault = outs
+        d_out, z_out, corr_out, d_first, d_last, a8_out, planes = outs
     cx, ye = d_in.shape[0], d_in.shape[1]
     cy = ye - 2 * H
     half = ye // 2
-    tiles = a8.shape[0]
     low_faces, high_faces = neighbour_faces(l_ref, a8, 2 * cx, half)
-    for q in range(2):
-        base = 2 * cx + half + q * cx
-        far = a8[0, base : base + cx, :]
-        for t in range(1, tiles):
-            far = far + a8[t, base : base + cx, :]
-        fault[2 * q] = far
-        table = jnp.concatenate([a8[t, q * cx : (q + 1) * cx, :] for t in range(tiles)], axis=0)
-        got = gather(table, hits(col_ref, q, 2), col_ref[q, :, 3:4])
-        fault[2 * q + 1] = scatter(
-            col_ref[q, :, 4:5] * got, hits(col_ref, q, 0), rows_hit(row_ref, q, 0, cx)
-        )
 
     def body(x, carry):
         faces, d_prev, d = carry
@@ -280,6 +298,21 @@
     return up, [(j, i) for i, j in up]
 
 
+def exchange(step, a8, first, last, col, row, cx):
+    up_x, down_x = steps("gx")
+    low = lax.ppermute(last, "gx", up_x)
+    high = lax.ppermute(first, "gx", down_x)
+    a8 = lax.all_to_all(a8, "gz", 0, 0, tiled=True)
+    fault = pl.pallas_call(
+        fault_kernel if step else weights_kernel,
+        out_shape=jax.ShapeDtypeStruct((4, cx, a8.shape[-1]), f32),
+        in_specs=[VMEM] * 3,
+        out_specs=VMEM,
+        compiler_params=PARAMS,
+    )(a8, col, row)
+    return a8, low, high, fault
+
+
 def local(rhs, accumulation, permeability, nnc_cell, nnc_remote, nnc_mask, nnc_trans):
     cx, cy, cz = rhs.shape
     tiles = lax.axis_size("gz")
@@ -287,7 +320,6 @@
     ye = cy + 2 * H
     half = ye // 2
     up_y, down_y = steps("gy")
-    up_x, down_x = steps("gx")
 
     def struct(*shape):
         return jax.ShapeDtypeStruct(shape, f32)
@@ -316,18 +348,18 @@
     row = jnp.stack([own_x, far_code], axis=1)
 
     edge = struct(ye, cz)
-    a8, kx_first, kx_last = pl.pallas_call(
+    l = lax.axis_index("gz").reshape(1).astype(jnp.int32)
+    l, col, row = lax.optimization_barrier((l, col, row))
+    small = struct(cx, cy, cz)
+    a8, kx_first, kx_last, rhs, accumulation = pl.pallas_call(
         first_kernel,
-        out_shape=(struct(tiles, half + 2 * cx, cz), edge, edge),
-        in_specs=[VMEM] * 5,
-        out_specs=(VMEM,) * 3,
+        out_shape=(struct(tiles, half + 2 * cx, cz), edge, edge, small, small),
+        in_specs=[VMEM] * 5 + [pl.BlockSpec(memory_space=pltpu.HBM)] * 2,
+        out_specs=(VMEM,) * 5,
+        scratch_shapes=[pltpu.SemaphoreType.DMA((2,))],
         compiler_params=PARAMS,
-    )(permeability, before, after, col, row)
-    kx_low = lax.ppermute(kx_last, "gx", up_x)
-    kx_high = lax.ppermute(kx_first, "gx", down_x)
-    l = lax.axis_index("gz").reshape(1).astype(jnp.int32)
-    l, a8, kx_low, kx_high = lax.optimization_barrier((l, a8, kx_low, kx_high))
-    a8 = lax.all_to_all(a8, "gz", 0, 0, tiled=True)
+    )(permeability, before, after, col, row, rhs, accumulation)
+    a8, kx_low, kx_high, fault = exchange(0, a8, kx_first, kx_last, col, row, cx)
 
     big = struct(cx, ye, cz)
     tall = struct(cx + 1, ye, cz)
@@ -336,11 +368,11 @@
     inv, z, d, tx, tym, typ, tzm, tzp, d_first, d_last, a8 = pl.pallas_call(
         setup_kernel,
         out_shape=(big, big, big, tall, big, big, big, big, edge, edge, sent),
-        in_specs=[SMEM] + [VMEM] * 10,
+        in_specs=[SMEM] + [VMEM] * 11,
         out_specs=(VMEM,) * 11,
-        scratch_shapes=scratch * 2,
+        scratch_shapes=scratch,
         compiler_params=PARAMS,
-    )(l, rhs, accumulation, permeability, before, after, kx_low, kx_high, a8, col, row)
+    )(l, rhs, accumulation, permeability, before, after, kx_low, kx_high, a8, fault, col, row)
 
     rho = 1.0 / sigma
     corr = None
@@ -349,23 +381,19 @@
         rho_next = 1.0 / (2.0 * sigma - rho)
         c1, c2 = rho_next * rho, 2.0 * rho_next / delta
         rho = rho_next
-        xlow = lax.ppermute(d_last, "gx", up_x)
-        xhigh = lax.ppermute(d_first, "gx", down_x)
-        a8, xlow, xhigh = lax.optimization_barrier((a8, xlow, xhigh))
-        a8 = lax.all_to_all(a8, "gz", 0, 0, tiled=True)
+        a8, xlow, xhigh, fault = exchange(sweep, a8, d_first, d_last, col, row, cx)
         args = [l, d, z] + ([] if first else [corr])
-        args += [xlow, xhigh, a8, inv, tx, tym, typ, tzm, tzp, col, row]
+        args += [xlow, xhigh, a8, fault, inv, tx, tym, typ, tzm, tzp, col, row]
 
         def kernel(*refs, c1=c1, c2=c2, first=first, last=last):
             sweep_kernel(c1, c2, first, last, *refs)
 
-        small = struct(cx, cy, cz)
         out = pl.pallas_call(
             kernel,
             out_shape=small if last else (big, big, small, edge, edge, sent),
             in_specs=[SMEM] + [VMEM] * (len(args) - 1),
             out_specs=VMEM if last else (VMEM,) * 6,
-            scratch_shapes=scratch if last else scratch * 2,
+            scratch_shapes=[] if last else scratch,
             compiler_params=PARAMS,
         )(*args)
         if last:

time: 232 us -> 265 us (1.14)
  the two profiles are of different devices: /device:TPU:2 before, /device:TPU:40 now
where the time goes in v2:
time: 265 us; the launch traced here: 263 us
  waiting for transfers between devices  83.5 us (32%)
  starting transfers between devices  70.8 us (27%)
  local copies, waits for them, and re-layouts  63.4 us (24%)
  Pallas kernels  40.8 us (15%)
  other arithmetic  3.53 us (1%)
    all_to_all x6, waiting for transfers between devices, exchange(): a8 = lax.all_to_all(a8, 'gz', 0, 0, tiled=True)  74.3 us
    unnamed x152, local copies, waits for them, and re-layouts  61.9 us
    all_to_all x6, starting transfers between devices, exchange(): a8 = lax.all_to_all(a8, 'gz', 0, 0, tiled=True)  28.4 us
    pallas_call x5, Pallas kernels, local(): pl.pallas_call(kernel, out_shape=small if last else (big, big, small, edg...  22.7 us
    ppermute x6, starting transfers between devices, exchange(): high = lax.ppermute(first, 'gx', down_x)  19.9 us
    ppermute x6, starting transfers between devices, exchange(): low = lax.ppermute(last, 'gx', up_x)  18.2 us
    pallas_call x6, Pallas kernels, exchange(): pl.pallas_call(fault_kernel if step else weights_kernel, out_shape=jax.Sh...  11.8 us
  transfers between devices with their start and end apart: 20, of which 8 were waited for; matrix products, arithmetic and copies ran while one was open for 1% of the time, Pallas kernels for 4%

profile of v2, /device:TPU:40, one launch (start us, length us, event | category | flops | bytes accessed | tf_op | source)
XLA Modules:
  0.0 262.7 jit_solution(5476404886733591432)
XLA Ops:
  8.9 5.2 %collective-permute-done.after = f32[1296,128]{1,0:T(8,128)S(1)} collective-permute-done((f32[1296,128]{1,0:T(8,128)}, f32[1296,128]{1,0:T(8,128)S(1)}, u32[]{:S(2)}, u32[]{:S(2)}) %collective-permute-start) | collective-permute-done | bytes 663584 | tf_op jit(solution)/shard_map/ppermute | solution.py:335
  14.7 4.0 %collective-permute-done.1.before = f32[1280,128]{1,0:T(8,128)S(1)} collective-permute-done((f32[1280,128]{1,0:T(8,128)}, f32[1280,128]{1,0:T(8,128)S(1)}, u32[]{:S(2)}, u32[]{:S(2)}) %collective-permute-start.1) | collective-permute-done | bytes 655392 | tf_op jit(solution)/shard_map/ppermute | solution.py:334
  24.9 10.0 %all-to-all-start = ((f32[8,88,128]{2,1,0:T(8,128)}), f32[8,88,128]{2,1,0:T(8,128)S(1)}, u32[]{:S(2)}, u32[]{:S(2)}) async-start(f32[8,88,128]{2,1,0:T(8,128)} %copy-done.65), calls=%async_computation | async-start | bytes 720896 | tf_op jit(solution)/shard_map/all_to_all | solution.py:305
  40.8 9.5 %all-to-all-done.a8 = f32[8,88,128]{2,1,0:T(8,128)S(1)} async-done(((f32[8,88,128]{2,1,0:T(8,128)}), f32[8,88,128]{2,1,0:T(8,128)S(1)}, u32[]{:S(2)}, u32[]{:S(2)}) %all-to-all-start) | async-done | bytes 360480 | tf_op jit(solution)/shard_map/all_to_all | solution.py:305
  56.6 4.4 %shard_map.75 = (f32[32,48,128]{2,1,0:T(8,128)S(1)}, f32[32,48,128]{2,1,0:T(8,128)S(1)}, f32[32,48,128]{2,1,0:T(8,128)S(1)}, f32[33,48,128]{2,1,0:T(8,128)S(1)},...) custom-call(s32[1]{0:T(128)} %bitcast.l_ref.refs_0_, ...), custom_call_target="tpu_custom_call" | custom-call | tf_op jit(solution)/shard_map/pallas_call | solution.py:368
  67.5 3.5 %all-to-all-start.1 = ((f32[8,152,128]{2,1,0:T(8,128)}), f32[8,152,128]{2,1,0:T(8,128)S(1)}, u32[]{:S(2)}, u32[]{:S(2)}) async-start(f32[8,152,128]{2,1,0:T(8,128)} %copy-done.48), calls=%async_computation.1 | async-start | bytes 1245184 | tf_op jit(solution)/shard_map/all_to_all | solution.py:305
  74.0 3.5 %collective-permute-start.5 = (f32[48,128]{1,0:T(8,128)}, f32[48,128]{1,0:T(8,128)}, u32[]{:S(2)}, u32[]{:S(2)}) collective-permute-start(f32[48,128]{1,0:T(8,128)} %copy-done.66), channel_id=1, source_target_pairs={{64,0},{128,64},{192,128},{65,1},{129,65},{193,129},{66,2},{130,66... | collective-permute-start | bytes 73736 | tf_op jit(solution)/shard_map/ppermute | solution.py:304
  77.5 12.6 %all-to-all-done.1.a8.refs_5_ = f32[8,152,128]{2,1,0:T(8,128)S(1)} async-done(((f32[8,152,128]{2,1,0:T(8,128)}), f32[8,152,128]{2,1,0:T(8,128)S(1)}, u32[]{:S(2)}, u32[]{:S(2)}) %all-to-all-start.1) | async-done | bytes 622624 | tf_op jit(solution)/shard_map/all_to_all | solution.py:305
  96.9 5.0 %shard_map.77 = (f32[32,48,128]{2,1,0:T(8,128)S(1)}, f32[32,48,128]{2,1,0:T(8,128)S(1)}, f32[32,32,128]{2,1,0:T(8,128)S(1)}, f32[48,128]{1,0:T(8,128)S(1)}, f32[...) custom-call(s32[1]{0:T(128)} %bitcast.l_ref.refs_0_, f32[32,48,128]{2,1,0:T(8,128)S(1)} %copy-done.31, ...), custom_call_target="tpu_custom_call" | custom-call | tf_op jit(solution)/shard_map/pallas_call | solution.py:391
  106.5 3.5 %all-to-all-start.2 = ((f32[8,152,128]{2,1,0:T(8,128)}), f32[8,152,128]{2,1,0:T(8,128)S(1)}, u32[]{:S(2)}, u32[]{:S(2)}) async-start(f32[8,152,128]{2,1,0:T(8,128)} %copy-done.52), calls=%async_computation.2 | async-start | bytes 1245184 | tf_op jit(solution)/shard_map/all_to_all | solution.py:305
  113.1 3.4 %collective-permute-start.7 = (f32[48,128]{1,0:T(8,128)}, f32[48,128]{1,0:T(8,128)}, u32[]{:S(2)}, u32[]{:S(2)}) collective-permute-start(f32[48,128]{1,0:T(8,128)} %copy-done.71), channel_id=1, source_target_pairs={{64,0},{128,64},{192,128},{65,1},{129,65},{193,129},{66,2},{130,66... | collective-permute-start | bytes 73736 | tf_op jit(solution)/shard_map/ppermute | solution.py:304
  116.5 11.6 %all-to-all-done.2.a8.refs_6_ = f32[8,152,128]{2,1,0:T(8,128)S(1)} async-done(((f32[8,152,128]{2,1,0:T(8,128)}), f32[8,152,128]{2,1,0:T(8,128)S(1)}, u32[]{:S(2)}, u32[]{:S(2)}) %all-to-all-start.2) | async-done | bytes 622624 | tf_op jit(solution)/shard_map/all_to_all | solution.py:305
  136.0 5.0 %shard_map.79 = (f32[32,48,128]{2,1,0:T(8,128)S(1)}, f32[32,48,128]{2,1,0:T(8,128)S(1)}, f32[32,32,128]{2,1,0:T(8,128)S(1)}, f32[48,128]{1,0:T(8,128)S(1)}, f32[...) custom-call(s32[1]{0:T(128)} %bitcast.l_ref.refs_0_, f32[32,48,128]{2,1,0:T(8,128)S(1)} %copy-done.45, ...), custom_call_target="tpu_custom_call" | custom-call | tf_op jit(solution)/shard_map/pallas_call | solution.py:391
  145.6 3.8 %all-to-all-start.3 = ((f32[8,152,128]{2,1,0:T(8,128)}), f32[8,152,128]{2,1,0:T(8,128)S(1)}, u32[]{:S(2)}, u32[]{:S(2)}) async-start(f32[8,152,128]{2,1,0:T(8,128)} %copy-done.49), calls=%async_computation.3 | async-start | bytes 1245184 | tf_op jit(solution)/shard_map/all_to_all | solution.py:305
  149.4 3.6 %collective-permute-start.8 = (f32[48,128]{1,0:T(8,128)}, f32[48,128]{1,0:T(8,128)}, u32[]{:S(2)}, u32[]{:S(2)}) collective-permute-start(f32[48,128]{1,0:T(8,128)} %copy-done.72), channel_id=1, source_target_pairs={{0,64},{64,128},{128,192},{1,65},{65,129},{129,193},{2,66},{66,130... | collective-permute-start | bytes 73736 | tf_op jit(solution)/shard_map/ppermute | solution.py:303
  156.0 13.8 %all-to-all-done.3.a8.refs_6_ = f32[8,152,128]{2,1,0:T(8,128)S(1)} async-done(((f32[8,152,128]{2,1,0:T(8,128)}), f32[8,152,128]{2,1,0:T(8,128)S(1)}, u32[]{:S(2)}, u32[]{:S(2)}) %all-to-all-start.3) | async-done | bytes 622624 | tf_op jit(solution)/shard_map/all_to_all | solution.py:305
  177.7 5.0 %shard_map.81 = (f32[32,48,128]{2,1,0:T(8,128)S(1)}, f32[32,48,128]{2,1,0:T(8,128)S(1)}, f32[32,32,128]{2,1,0:T(8,128)S(1)}, f32[48,128]{1,0:T(8,128)S(1)}, f32[...) custom-call(s32[1]{0:T(128)} %bitcast.l_ref.refs_0_, f32[32,48,128]{2,1,0:T(8,128)S(1)} %copy-done.37, ...), custom_call_target="tpu_custom_call" | custom-call | tf_op jit(solution)/shard_map/pallas_call | solution.py:391
  187.3 3.7 %all-to-all-start.4 = ((f32[8,152,128]{2,1,0:T(8,128)}), f32[8,152,128]{2,1,0:T(8,128)S(1)}, u32[]{:S(2)}, u32[]{:S(2)}) async-start(f32[8,152,128]{2,1,0:T(8,128)} %copy-done.50), calls=%async_computation.4 | async-start | bytes 1245184 | tf_op jit(solution)/shard_map/all_to_all | solution.py:305
  193.7 3.8 %collective-permute-start.11 = (f32[48,128]{1,0:T(8,128)}, f32[48,128]{1,0:T(8,128)}, u32[]{:S(2)}, u32[]{:S(2)}) collective-permute-start(f32[48,128]{1,0:T(8,128)} %copy-done.69), channel_id=1, source_target_pairs={{64,0},{128,64},{192,128},{65,1},{129,65},{193,129},{66,2},{130,66... | collective-permute-start | bytes 73736 | tf_op jit(solution)/shard_map/ppermute | solution.py:304
  197.5 13.1 %all-to-all-done.4.a8.refs_6_ = f32[8,152,128]{2,1,0:T(8,128)S(1)} async-done(((f32[8,152,128]{2,1,0:T(8,128)}), f32[8,152,128]{2,1,0:T(8,128)S(1)}, u32[]{:S(2)}, u32[]{:S(2)}) %all-to-all-start.4) | async-done | bytes 622624 | tf_op jit(solution)/shard_map/all_to_all | solution.py:305
  218.5 5.0 %shard_map.83 = (f32[32,48,128]{2,1,0:T(8,128)S(1)}, f32[32,48,128]{2,1,0:T(8,128)S(1)}, f32[32,32,128]{2,1,0:T(8,128)S(1)}, f32[48,128]{1,0:T(8,128)S(1)}, f32[...) custom-call(s32[1]{0:T(128)} %bitcast.l_ref.refs_0_, f32[32,48,128]{2,1,0:T(8,128)S(1)} %copy-done.41, ...), custom_call_target="tpu_custom_call" | custom-call | tf_op jit(solution)/shard_map/pallas_call | solution.py:391
  228.1 3.7 %all-to-all-start.5 = ((f32[8,152,128]{2,1,0:T(8,128)}), f32[8,152,128]{2,1,0:T(8,128)S(1)}, u32[]{:S(2)}, u32[]{:S(2)}) async-start(f32[8,152,128]{2,1,0:T(8,128)} %copy-done.51), calls=%async_computation.5 | async-start | bytes 1245184 | tf_op jit(solution)/shard_map/all_to_all | solution.py:305
  235.1 3.2 %collective-permute-start.13 = (f32[48,128]{1,0:T(8,128)}, f32[48,128]{1,0:T(8,128)}, u32[]{:S(2)}, u32[]{:S(2)}) collective-permute-start(f32[48,128]{1,0:T(8,128)} %copy-done.70), channel_id=1, source_target_pairs={{64,0},{128,64},{192,128},{65,1},{129,65},{193,129},{66,2},{130,66... | collective-permute-start | bytes 73736 | tf_op jit(solution)/shard_map/ppermute | solution.py:304
  238.3 13.7 %all-to-all-done.5.a8.refs_6_ = f32[8,152,128]{2,1,0:T(8,128)S(1)} async-done(((f32[8,152,128]{2,1,0:T(8,128)}), f32[8,152,128]{2,1,0:T(8,128)S(1)}, u32[]{:S(2)}, u32[]{:S(2)}) %all-to-all-start.5) | async-done | bytes 622624 | tf_op jit(solution)/shard_map/all_to_all | solution.py:305
  (201 shorter events, 108.4 us)
Async XLA Ops:
  0.0 2.7 %copy-start.24 = (f32[32,32,128]{2,1,0:T(8,128)S(1)}, f32[32,32,128]{2,1,0:T(8,128)}, u32[]{:S(2)}) copy-start(f32[32,32,128]{2,1,0:T(8,128)} %acc.1) | copy-start | bytes 1572868
  0.0 2.7 %copy-start.26 = (f32[32,32,128]{2,1,0:T(8,128)S(1)}, f32[32,32,128]{2,1,0:T(8,128)}, u32[]{:S(2)}) copy-start(f32[32,32,128]{2,1,0:T(8,128)} %rhs.1) | copy-start | bytes 1572868
  2.8 15.8 %copy-start.18 = (f32[3,32,32,128]{3,2,1,0:T(8,128)S(1)}, f32[3,32,32,128]{3,2,1,0:T(8,128)}, u32[]{:S(2)}) copy-start(f32[3,32,32,128]{3,2,1,0:T(8,128)} %perm.1) | copy-start | bytes 4718596
  3.7 10.4 %collective-permute-start = (f32[1296,128]{1,0:T(8,128)}, f32[1296,128]{1,0:T(8,128)S(1)}, u32[]{:S(2)}, u32[]{:S(2)}) collective-permute-start(f32[1296,128]{1,0:T(8,128)} %select_maximum_fusion), channel_id=1, source_target_pairs={{8,0},{16,8},{24,16},{32,24},{40,32},{48,40},{56,48},{9,1},{17,9},... | collective-permute-start | bytes 1990664 | tf_op jit(solution)/shard_map/ppermute | solution.py:335
  6.5 12.1 %collective-permute-start.1 = (f32[1280,128]{1,0:T(8,128)}, f32[1280,128]{1,0:T(8,128)S(1)}, u32[]{:S(2)}, u32[]{:S(2)}) collective-permute-start(f32[1280,128]{1,0:T(8,128)} %bitcast.13), channel_id=1, source_target_pairs={{0,8},{8,16},{16,24},{24,32},{32,40},{40,48},{48,56},{1,9},{9,17},... | collective-permute-start | bytes 1966088 | tf_op jit(solution)/shard_map/ppermute | solution.py:334
  14.1 8.5 %copy-start.20 = (f32[1296,128]{1,0:T(8,128)}, f32[1296,128]{1,0:T(8,128)S(1)}, u32[]{:S(2)}) copy-start(f32[1296,128]{1,0:T(8,128)S(1)} %collective-permute-done.after) | copy-start | bytes 1990660
  24.9 25.4 %all-to-all-start = ((f32[8,88,128]{2,1,0:T(8,128)}), f32[8,88,128]{2,1,0:T(8,128)S(1)}, u32[]{:S(2)}, u32[]{:S(2)}) async-start(f32[8,88,128]{2,1,0:T(8,128)} %copy-done.65), calls=%async_computation | async-start | bytes 720896 | tf_op jit(solution)/shard_map/all_to_all | solution.py:305
  35.0 15.9 %collective-permute-start.2 = (f32[48,128]{1,0:T(8,128)S(1)}, f32[48,128]{1,0:T(8,128)S(1)}, u32[]{:S(2)}, u32[]{:S(2)}) collective-permute-start(f32[48,128]{1,0:T(8,128)S(1)} %get-tuple-element.53), channel_id=1, source_target_pairs={{0,64},{64,128},{128,192},{1,65},{65,129},{129,193},{2,66},{66,130... | collective-permute-start | bytes 73736 | tf_op jit(solution)/shard_map/ppermute | solution.py:303
  37.9 13.0 %collective-permute-start.3 = (f32[48,128]{1,0:T(8,128)S(1)}, f32[48,128]{1,0:T(8,128)S(1)}, u32[]{:S(2)}, u32[]{:S(2)}) collective-permute-start(f32[48,128]{1,0:T(8,128)S(1)} %get-tuple-element.54), channel_id=1, source_target_pairs={{64,0},{128,64},{192,128},{65,1},{129,65},{193,129},{66,2},{130,66... | collective-permute-start | bytes 73736 | tf_op jit(solution)/shard_map/ppermute | solution.py:304
  67.5 22.6 %all-to-all-start.1 = ((f32[8,152,128]{2,1,0:T(8,128)}), f32[8,152,128]{2,1,0:T(8,128)S(1)}, u32[]{:S(2)}, u32[]{:S(2)}) async-start(f32[8,152,128]{2,1,0:T(8,128)} %copy-done.48), calls=%async_computation.1 | async-start | bytes 1245184 | tf_op jit(solution)/shard_map/all_to_all | solution.py:305
  71.0 21.3 %collective-permute-start.4 = (f32[48,128]{1,0:T(8,128)}, f32[48,128]{1,0:T(8,128)}, u32[]{:S(2)}, u32[]{:S(2)}) collective-permute-start(f32[48,128]{1,0:T(8,128)} %copy-done.67), channel_id=1, source_target_pairs={{0,64},{64,128},{128,192},{1,65},{65,129},{129,193},{2,66},{66,130... | collective-permute-start | bytes 73736 | tf_op jit(solution)/shard_map/ppermute | solution.py:303
  74.0 18.4 %collective-permute-start.5 = (f32[48,128]{1,0:T(8,128)}, f32[48,128]{1,0:T(8,128)}, u32[]{:S(2)}, u32[]{:S(2)}) collective-permute-start(f32[48,128]{1,0:T(8,128)} %copy-done.66), channel_id=1, source_target_pairs={{64,0},{128,64},{192,128},{65,1},{129,65},{193,129},{66,2},{130,66... | collective-permute-start | bytes 73736 | tf_op jit(solution)/shard_map/ppermute | solution.py:304
  106.5 21.6 %all-to-all-start.2 = ((f32[8,152,128]{2,1,0:T(8,128)}), f32[8,152,128]{2,1,0:T(8,128)S(1)}, u32[]{:S(2)}, u32[]{:S(2)}) async-start(f32[8,152,128]{2,1,0:T(8,128)} %copy-done.52), calls=%async_computation.2 | async-start | bytes 1245184 | tf_op jit(solution)/shard_map/all_to_all | solution.py:305
  110.1 20.3 %collective-permute-start.6 = (f32[48,128]{1,0:T(8,128)}, f32[48,128]{1,0:T(8,128)}, u32[]{:S(2)}, u32[]{:S(2)}) collective-permute-start(f32[48,128]{1,0:T(8,128)} %copy-done.75), channel_id=1, source_target_pairs={{0,64},{64,128},{128,192},{1,65},{65,129},{129,193},{2,66},{66,130... | collective-permute-start | bytes 73736 | tf_op jit(solution)/shard_map/ppermute | solution.py:303
  113.1 17.3 %collective-permute-start.7 = (f32[48,128]{1,0:T(8,128)}, f32[48,128]{1,0:T(8,128)}, u32[]{:S(2)}, u32[]{:S(2)}) collective-permute-start(f32[48,128]{1,0:T(8,128)} %copy-done.71), channel_id=1, source_target_pairs={{64,0},{128,64},{192,128},{65,1},{129,65},{193,129},{66,2},{130,66... | collective-permute-start | bytes 73736 | tf_op jit(solution)/shard_map/ppermute | solution.py:304
  145.6 24.2 %all-to-all-start.3 = ((f32[8,152,128]{2,1,0:T(8,128)}), f32[8,152,128]{2,1,0:T(8,128)S(1)}, u32[]{:S(2)}, u32[]{:S(2)}) async-start(f32[8,152,128]{2,1,0:T(8,128)} %copy-done.49), calls=%async_computation.3 | async-start | bytes 1245184 | tf_op jit(solution)/shard_map/all_to_all | solution.py:305
  149.4 22.7 %collective-permute-start.8 = (f32[48,128]{1,0:T(8,128)}, f32[48,128]{1,0:T(8,128)}, u32[]{:S(2)}, u32[]{:S(2)}) collective-permute-start(f32[48,128]{1,0:T(8,128)} %copy-done.72), channel_id=1, source_target_pairs={{0,64},{64,128},{128,192},{1,65},{65,129},{129,193},{2,66},{66,130... | collective-permute-start | bytes 73736 | tf_op jit(solution)/shard_map/ppermute | solution.py:303
  153.0 19.1 %collective-permute-start.9 = (f32[48,128]{1,0:T(8,128)}, f32[48,128]{1,0:T(8,128)}, u32[]{:S(2)}, u32[]{:S(2)}) collective-permute-start(f32[48,128]{1,0:T(8,128)} %copy-done.68), channel_id=1, source_target_pairs={{64,0},{128,64},{192,128},{65,1},{129,65},{193,129},{66,2},{130,66... | collective-permute-start | bytes 73736 | tf_op jit(solution)/shard_map/ppermute | solution.py:304
  187.3 23.3 %all-to-all-start.4 = ((f32[8,152,128]{2,1,0:T(8,128)}), f32[8,152,128]{2,1,0:T(8,128)S(1)}, u32[]{:S(2)}, u32[]{:S(2)}) async-start(f32[8,152,128]{2,1,0:T(8,128)} %copy-done.50), calls=%async_computation.4 | async-start | bytes 1245184 | tf_op jit(solution)/shard_map/all_to_all | solution.py:305
  191.1 21.8 %collective-permute-start.10 = (f32[48,128]{1,0:T(8,128)}, f32[48,128]{1,0:T(8,128)}, u32[]{:S(2)}, u32[]{:S(2)}) collective-permute-start(f32[48,128]{1,0:T(8,128)} %copy-done.73), channel_id=1, source_target_pairs={{0,64},{64,128},{128,192},{1,65},{65,129},{129,193},{2,66},{66,130... | collective-permute-start | bytes 73736 | tf_op jit(solution)/shard_map/ppermute | solution.py:303
  193.7 19.2 %collective-permute-start.11 = (f32[48,128]{1,0:T(8,128)}, f32[48,128]{1,0:T(8,128)}, u32[]{:S(2)}, u32[]{:S(2)}) collective-permute-start(f32[48,128]{1,0:T(8,128)} %copy-done.69), channel_id=1, source_target_pairs={{64,0},{128,64},{192,128},{65,1},{129,65},{193,129},{66,2},{130,66... | collective-permute-start | bytes 73736 | tf_op jit(solution)/shard_map/ppermute | solution.py:304
  228.1 23.9 %all-to-all-start.5 = ((f32[8,152,128]{2,1,0:T(8,128)}), f32[8,152,128]{2,1,0:T(8,128)S(1)}, u32[]{:S(2)}, u32[]{:S(2)}) async-start(f32[8,152,128]{2,1,0:T(8,128)} %copy-done.51), calls=%async_computation.5 | async-start | bytes 1245184 | tf_op jit(solution)/shard_map/all_to_all | solution.py:305
  231.9 22.4 %collective-permute-start.12 = (f32[48,128]{1,0:T(8,128)}, f32[48,128]{1,0:T(8,128)}, u32[]{:S(2)}, u32[]{:S(2)}) collective-permute-start(f32[48,128]{1,0:T(8,128)} %copy-done.74), channel_id=1, source_target_pairs={{0,64},{64,128},{128,192},{1,65},{65,129},{129,193},{2,66},{66,130... | collective-permute-start | bytes 73736 | tf_op jit(solution)/shard_map/ppermute | solution.py:303
  235.1 19.2 %collective-permute-start.13 = (f32[48,128]{1,0:T(8,128)}, f32[48,128]{1,0:T(8,128)}, u32[]{:S(2)}, u32[]{:S(2)}) collective-permute-start(f32[48,128]{1,0:T(8,128)} %copy-done.70), channel_id=1, source_target_pairs={{64,0},{128,64},{192,128},{65,1},{129,65},{193,129},{66,2},{130,66... | collective-permute-start | bytes 73736 | tf_op jit(solution)/shard_map/ppermute | solution.py:304
  (72 other events, 75.3 us)

commit v3 on v2

--- a/solution.py
+++ b/solution.py
@@ -12,6 +12,7 @@
 delta = (lam_high - lam_low) / 2.0
 sigma = theta / delta
 
+SLOT_ROWS = 4
 H = 8
 f32 = jnp.float32
 bf16 = jnp.bfloat16
@@ -38,34 +39,45 @@
     return lax.broadcasted_iota(jnp.int32, shape, len(shape) - 1)
 
 
-def hits(col_ref, q, which):
-    codes = col_ref[q, :, which : which + 1]
-    return lane_iota((codes.shape[0], 128)).astype(f32) == codes
-
-
-def rows_hit(row_ref, q, which, count):
-    codes = row_ref[q, which : which + 1, :]
-    rows = lax.broadcasted_iota(jnp.int32, (count, codes.shape[1]), 0).astype(f32)
-    return jnp.where(rows == codes, 1.0, 0.0).astype(bf16)
-
-
-def scatter(u, lane_hit, row_hit):
-    parts = [jnp.where(lane_hit, p, 0.0).astype(bf16) for p in split3(u)]
-    out = dot(row_hit, jnp.concatenate(parts, axis=1), ((1,), (0,)))
-    return out[:, :128] + out[:, 128:256] + out[:, 256:]
-
-
-def gather(table, lane_hit, codes):
-    rows = table.shape[0]
-    pick = jnp.where(lane_hit, 1.0, 0.0).astype(bf16)
-    parts = [p.astype(bf16) for p in split3(table)]
-    if rows % 128 == 0:
-        got = sum(dot(pick, p, ((1,), (1,))) for p in parts)
-        lanes = lane_iota(got.shape)
-    else:
-        got = dot(pick, jnp.concatenate(parts, axis=0), ((1,), (1,)))
-        lanes = lane_iota(got.shape) % rows
-    return jnp.sum(jnp.where(lanes.astype(f32) == codes, got, 0.0), axis=1, keepdims=True)
+def rows_hit(codes, count):
+    shape = (count, codes.shape[1])
+    return lax.broadcasted_iota(jnp.int32, shape, 0).astype(f32) == codes
+
+
+def picks(codes):
+    return jnp.where(rows_hit(codes, 128), 1.0, 0.0).astype(bf16)
+
+
+def thirds(out):
+    n = out.shape[0] // 3
+    return out[:n] + out[n : 2 * n] + out[2 * n :]
+
+
+def gather(table, pick, x_hit):
+    parts = jnp.concatenate(split3(table), axis=0).astype(bf16)
+    got = thirds(dot(parts, pick, ((1,), (0,))))
+    return jnp.sum(jnp.where(x_hit, got, 0.0), axis=0, keepdims=True)
+
+
+def scatter(u, pick, x_hit):
+    parts = [jnp.where(x_hit, p, 0.0) for p in split3(u)]
+    return thirds(dot(jnp.concatenate(parts, axis=0).astype(bf16), pick, ((1,), (1,))))
+
+
+def get_rows(ref, t, base, count):
+    return jnp.concatenate([ref[t, base + k : base + k + 1, :] for k in range(count)], axis=1)
+
+
+def put_rows(ref, t, base, values):
+    for k in range(values.shape[1] // 128):
+        ref[t, base + k : base + k + 1, :] = values[:, 128 * k : 128 * (k + 1)]
+
+
+NEAR_Z, NEAR_X, WEIGHT, FAR_X, FAR_TILE, FAR_Z = range(6)
+
+
+def slot_row(row_ref, q, which):
+    return row_ref[q, which : which + 1, :]
 
 
 def pack_faces(faces, slab, x):
@@ -93,13 +105,7 @@
     return low, high
 
 
-def put_partials(out_ref, base, tiles, q, col_ref, row_ref, u, cx):
-    sums = scatter(u, hits(col_ref, q, 2), rows_hit(row_ref, q, 1, tiles * cx))
-    for t in range(tiles):
-        out_ref[t, base + q * cx : base + (q + 1) * cx, :] = sums[t * cx : (t + 1) * cx]
-
-
-def first_kernel(own_k, before, after, col_ref, row_ref, rhs, acc,
+def first_kernel(own_k, before, after, row_ref, rhs, acc,
                  out_ref, kx_first, kx_last, rhs_out, acc_out, sem):
     moves = [
         pltpu.make_async_copy(rhs, rhs_out, sem.at[0]),
@@ -123,22 +129,32 @@
     for t in range(tiles):
         out_ref[t, 0:half, :] = faces
     for q in range(2):
-        put_partials(out_ref, half, tiles, q, col_ref, row_ref, col_ref[q, :, 4:5], cx)
+        base = half + q * 4 * SLOT_ROWS
+        for n, which in enumerate((FAR_X, FAR_TILE, FAR_Z, WEIGHT)):
+            for t in range(tiles):
+                put_rows(out_ref, t, base + n * SLOT_ROWS, slot_row(row_ref, q, which))
     for move in moves:
         move.wait()
 
 
-def emit(a8_ref, planes, faces, col_ref, row_ref):
+def emit(a8_ref, planes, faces, row_ref, pick_ref, far_x):
     tiles = a8_ref.shape[0]
     cx = planes.shape[1]
     half = faces.shape[0]
+    slots = row_ref.shape[2]
     for t in range(tiles):
-        a8_ref[t, 0:cx, :] = planes[0]
-        a8_ref[t, cx : 2 * cx, :] = planes[2]
-        a8_ref[t, 2 * cx : 2 * cx + half, :] = faces
+        a8_ref[t, 0:half, :] = faces
     for q in range(2):
-        near = gather(planes[1 + 2 * q], hits(col_ref, q, 0), col_ref[q, :, 1:2])
-        put_partials(a8_ref, 2 * cx + half, tiles, q, col_ref, row_ref, col_ref[q, :, 4:5] * near, cx)
+        base = half + q * 2 * SLOT_ROWS
+        near = gather(
+            planes[2 * q + 1], picks(slot_row(row_ref, q, NEAR_Z)), rows_hit(slot_row(row_ref, q, NEAR_X), cx)
+        )
+        near = slot_row(row_ref, q, WEIGHT) * near
+        for t in range(tiles):
+            at = slice(t * slots, (t + 1) * slots)
+            far = gather(planes[2 * q], pick_ref[q, :, at], rows_hit(far_x[q : q + 1, at], cx))
+            put_rows(a8_ref, t, base, near)
+            put_rows(a8_ref, t, base + SLOT_ROWS, far)
 
 
 def keep_planes(planes, slab, x):
@@ -164,36 +180,50 @@
     return low, high
 
 
-def weights_kernel(a8, col_ref, row_ref, fault):
+def near_sum(row_ref, q, values, cx):
+    return scatter(
+        values, picks(slot_row(row_ref, q, NEAR_Z)), rows_hit(slot_row(row_ref, q, NEAR_X), cx)
+    )
+
+
+def weights_kernel(l_ref, a8, row_ref, fault, pick_ref, far_x):
     tiles, rows = a8.shape[0], a8.shape[1]
     cx = fault.shape[1]
+    slots = row_ref.shape[2]
+    here = l_ref[0].astype(f32)
     for q in range(2):
-        base = rows - (2 - q) * cx
-        far = a8[0, base : base + cx, :]
-        for t in range(1, tiles):
-            far = far + a8[t, base : base + cx, :]
+        base = rows - (2 - q) * 4 * SLOT_ROWS
+        far = jnp.zeros((cx, 128), f32)
+        for t in range(tiles):
+            at = slice(t * slots, (t + 1) * slots)
+            x, tile, z, weight = [get_rows(a8, t, base + n * SLOT_ROWS, SLOT_ROWS) for n in range(4)]
+            x = jnp.where(tile == here, x, -1.0)
+            pick = picks(z)
+            pick_ref[q, :, at] = pick
+            far_x[q : q + 1, at] = x
+            far = far + scatter(weight, pick, rows_hit(x, cx))
         fault[2 * q] = far
-        near = scatter(col_ref[q, :, 4:5], hits(col_ref, q, 0), rows_hit(row_ref, q, 0, cx))
-        fault[2 * q + 1] = near
-
-
-def fault_kernel(a8, col_ref, row_ref, fault):
+        fault[2 * q + 1] = near_sum(row_ref, q, slot_row(row_ref, q, WEIGHT), cx)
+
+
+def fault_kernel(a8, row_ref, pick_ref, far_x, fault):
     tiles, rows = a8.shape[0], a8.shape[1]
     cx = fault.shape[1]
+    slots = row_ref.shape[2]
     for q in range(2):
-        base = rows - (2 - q) * cx
-        far = a8[0, base : base + cx, :]
-        for t in range(1, tiles):
-            far = far + a8[t, base : base + cx, :]
+        base = rows - (2 - q) * 2 * SLOT_ROWS
+        far = jnp.zeros((cx, 128), f32)
+        near = jnp.zeros((1, slots), f32)
+        for t in range(tiles):
+            at = slice(t * slots, (t + 1) * slots)
+            values = get_rows(a8, t, base, SLOT_ROWS)
+            far = far + scatter(values, pick_ref[q, :, at], rows_hit(far_x[q : q + 1, at], cx))
+            near = near + get_rows(a8, t, base + SLOT_ROWS, SLOT_ROWS)
         fault[2 * q] = far
-        table = jnp.concatenate([a8[t, q * cx : (q + 1) * cx, :] for t in range(tiles)], axis=0)
-        got = gather(table, hits(col_ref, q, 2), col_ref[q, :, 3:4])
-        fault[2 * q + 1] = scatter(
-            col_ref[q, :, 4:5] * got, hits(col_ref, q, 0), rows_hit(row_ref, q, 0, cx)
-        )
-
-
-def setup_kernel(l_ref, rhs, acc, perm, before, after, kx_low, kx_high, a8, fault, col_ref, row_ref,
+        fault[2 * q + 1] = near_sum(row_ref, q, slot_row(row_ref, q, WEIGHT) * near, cx)
+
+
+def setup_kernel(l_ref, rhs, acc, perm, before, after, kx_low, kx_high, a8, fault, row_ref, pick_ref, far_x,
                  inv, z_out, d_out, tx, tym, typ, tzm, tzp, d_first, d_last, a8_out, planes):
     cx, cy = rhs.shape[0], rhs.shape[1]
     ye = cy + 2 * H
@@ -243,14 +273,18 @@
     faces, _, _ = lax.fori_loop(0, cx, body, init, unroll=4)
     d_first[...] = d_out[0]
     d_last[...] = d_out[cx - 1]
-    emit(a8_out, planes, faces, col_ref, row_ref)
+    emit(a8_out, planes, faces, row_ref, pick_ref, far_x)
 
 
 def sweep_kernel(c1, c2, first, last, l_ref, d_in, z_in, *refs):
     refs = list(refs)
     corr_in = None if first else refs.pop(0)
-    xlow, xhigh, a8, fault, inv, tx, tym, typ, tzm, tzp, col_ref, row_ref = refs[:12]
-    outs = refs[12:]
+    xlow, xhigh, a8, fault, inv, tx, tym, typ, tzm, tzp = refs[:10]
+    refs = refs[10:]
+    if not last:
+        row_ref, pick_ref, far_x = refs[:3]
+        refs = refs[3:]
+    outs = refs
     if last:
         (corr_out,) = outs
     else:
@@ -258,7 +292,7 @@
     cx, ye = d_in.shape[0], d_in.shape[1]
     cy = ye - 2 * H
     half = ye // 2
-    low_faces, high_faces = neighbour_faces(l_ref, a8, 2 * cx, half)
+    low_faces, high_faces = neighbour_faces(l_ref, a8, 0, half)
 
     def body(x, carry):
         faces, d_prev, d = carry
@@ -284,7 +318,7 @@
     if not last:
         d_first[...] = d_out[0]
         d_last[...] = d_out[cx - 1]
-        emit(a8_out, planes, faces, col_ref, row_ref)
+        emit(a8_out, planes, faces, row_ref, pick_ref, far_x)
 
 
 VMEM = pl.BlockSpec(memory_space=pltpu.VMEM)
@@ -298,18 +332,35 @@
     return up, [(j, i) for i, j in up]
 
 
-def exchange(step, a8, first, last, col, row, cx):
+def exchange(step, a8, first, last, operands, cx):
     up_x, down_x = steps("gx")
+    cz = a8.shape[-1]
+    fault = jax.ShapeDtypeStruct((4, cx, cz), f32)
     low = lax.ppermute(last, "gx", up_x)
     high = lax.ppermute(first, "gx", down_x)
     a8 = lax.all_to_all(a8, "gz", 0, 0, tiled=True)
-    fault = pl.pallas_call(
-        fault_kernel if step else weights_kernel,
-        out_shape=jax.ShapeDtypeStruct((4, cx, a8.shape[-1]), f32),
-        in_specs=[VMEM] * 3,
-        out_specs=VMEM,
-        compiler_params=PARAMS,
-    )(a8, col, row)
+    if step:
+        fault = pl.pallas_call(
+            fault_kernel,
+            out_shape=fault,
+            in_specs=[VMEM] * 4,
+            out_specs=VMEM,
+            compiler_params=PARAMS,
+        )(a8, *operands)
+    else:
+        l, row = operands
+        every = a8.shape[0] * row.shape[-1]
+        fault = pl.pallas_call(
+            weights_kernel,
+            out_shape=(
+                fault,
+                jax.ShapeDtypeStruct((2, cz, every), bf16),
+                jax.ShapeDtypeStruct((2, every), f32),
+            ),
+            in_specs=[SMEM, VMEM, VMEM],
+            out_specs=(VMEM,) * 3,
+            compiler_params=PARAMS,
+        )(l, a8, row)
     return a8, low, high, fault
 
 
@@ -340,39 +391,42 @@
     remote = lists[:, 1].astype(jnp.int32)
     column = cz * tiles
     far_z = remote % column
-    own_x = (cell // cz).astype(f32)
-    far_code = ((far_z // cz) * cx + remote // column).astype(f32)
-    col = jnp.stack(
-        [(cell % cz).astype(f32), own_x, (far_z % cz).astype(f32), far_code, lists[:, 2]], axis=-1
-    )
-    row = jnp.stack([own_x, far_code], axis=1)
+    table = [
+        (cell % cz).astype(f32),
+        (cell // cz).astype(f32),
+        lists[:, 2],
+        (remote // column).astype(f32),
+        (far_z // cz).astype(f32),
+        (far_z % cz).astype(f32),
+    ]
+    row = jnp.stack(table + [jnp.zeros_like(lists[:, 2])] * 2, axis=1)
 
     edge = struct(ye, cz)
     l = lax.axis_index("gz").reshape(1).astype(jnp.int32)
-    l, col, row = lax.optimization_barrier((l, col, row))
+    l, row = lax.optimization_barrier((l, row))
     small = struct(cx, cy, cz)
     a8, kx_first, kx_last, rhs, accumulation = pl.pallas_call(
         first_kernel,
-        out_shape=(struct(tiles, half + 2 * cx, cz), edge, edge, small, small),
-        in_specs=[VMEM] * 5 + [pl.BlockSpec(memory_space=pltpu.HBM)] * 2,
+        out_shape=(struct(tiles, half + 8 * SLOT_ROWS, cz), edge, edge, small, small),
+        in_specs=[VMEM] * 4 + [pl.BlockSpec(memory_space=pltpu.HBM)] * 2,
         out_specs=(VMEM,) * 5,
         scratch_shapes=[pltpu.SemaphoreType.DMA((2,))],
         compiler_params=PARAMS,
-    )(permeability, before, after, col, row, rhs, accumulation)
-    a8, kx_low, kx_high, fault = exchange(0, a8, kx_first, kx_last, col, row, cx)
+    )(permeability, before, after, row, rhs, accumulation)
+    a8, kx_low, kx_high, (fault, pick, far_x) = exchange(0, a8, kx_first, kx_last, (l, row), cx)
 
     big = struct(cx, ye, cz)
     tall = struct(cx + 1, ye, cz)
-    sent = struct(tiles, 4 * cx + half, cz)
+    sent = struct(tiles, half + 4 * SLOT_ROWS, cz)
     scratch = [pltpu.VMEM((4, cx, cz), f32)]
     inv, z, d, tx, tym, typ, tzm, tzp, d_first, d_last, a8 = pl.pallas_call(
         setup_kernel,
         out_shape=(big, big, big, tall, big, big, big, big, edge, edge, sent),
-        in_specs=[SMEM] + [VMEM] * 11,
+        in_specs=[SMEM] + [VMEM] * 12,
         out_specs=(VMEM,) * 11,
         scratch_shapes=scratch,
         compiler_params=PARAMS,
-    )(l, rhs, accumulation, permeability, before, after, kx_low, kx_high, a8, fault, col, row)
+    )(l, rhs, accumulation, permeability, before, after, kx_low, kx_high, a8, fault, row, pick, far_x)
 
     rho = 1.0 / sigma
     corr = None
@@ -381,9 +435,10 @@
         rho_next = 1.0 / (2.0 * sigma - rho)
         c1, c2 = rho_next * rho, 2.0 * rho_next / delta
         rho = rho_next
-        a8, xlow, xhigh, fault = exchange(sweep, a8, d_first, d_last, col, row, cx)
+        a8, xlow, xhigh, fault = exchange(sweep, a8, d_first, d_last, (row, pick, far_x), cx)
         args = [l, d, z] + ([] if first else [corr])
-        args += [xlow, xhigh, a8, fault, inv, tx, tym, typ, tzm, tzp, col, row]
+        args += [xlow, xhigh, a8, fault, inv, tx, tym, typ, tzm, tzp]
+        args += [] if last else [row, pick, far_x]
 
         def kernel(*refs, c1=c1, c2=c2, first=first, last=last):
             sweep_kernel(c1, c2, first, last, *refs)

time: 265 us -> 211 us (0.80)
  the two profiles are of different devices: /device:TPU:40 before, /device:TPU:24 now
where the time goes in v3:
time: 211 us; the launch traced here: 209 us
  starting transfers between devices  65.4 us (31%)
  local copies, waits for them, and re-layouts  57.3 us (27%)
  waiting for transfers between devices  51.9 us (25%)
  Pallas kernels  30.2 us (14%)
  other arithmetic  3.47 us (2%)
    unnamed x144, local copies, waits for them, and re-layouts  56 us
    all_to_all x6, waiting for transfers between devices, exchange(): a8 = lax.all_to_all(a8, 'gz', 0, 0, tiled=True)  42.2 us
    all_to_all x6, starting transfers between devices, exchange(): a8 = lax.all_to_all(a8, 'gz', 0, 0, tiled=True)  38.9 us
    pallas_call x5, Pallas kernels, local(): pl.pallas_call(kernel, out_shape=small if last else (big, big, small, edg...  19.2 us
    ppermute x6, starting transfers between devices, exchange(): low = lax.ppermute(last, 'gx', up_x)  14.5 us
    ppermute x6, starting transfers between devices, exchange(): high = lax.ppermute(first, 'gx', down_x)  7.75 us
    ppermute x1, waiting for transfers between devices, local(): after = lax.ppermute(jnp.concatenate([bottom, flat], axis=0), 'gy', down_y)  5.32 us
    pallas_call x1, Pallas kernels, local(): pl.pallas_call(setup_kernel, out_shape=(big, big, big, tall, big, big, bi...  4.45 us
  transfers between devices with their start and end apart: 20, of which 8 were waited for; matrix products, arithmetic and copies ran while one was open for 1% of the time, Pallas kernels for 3%

profile of v3, /device:TPU:24, one launch (start us, length us, event | category | flops | bytes accessed | tf_op | source)
XLA Modules:
  0.0 208.8 jit_solution(13373918566100330964)
XLA Ops:
  6.7 2.3 %collective-permute-start.1 = (f32[1280,128]{1,0:T(8,128)}, f32[1280,128]{1,0:T(8,128)S(1)}, u32[]{:S(2)}, u32[]{:S(2)}) collective-permute-start(f32[1280,128]{1,0:T(8,128)} %bitcast.10), channel_id=1, source_target_pairs={{0,8},{8,16},{16,24},{24,32},{32,40},{40,48},{48,56},{1,9},{9,17},... | collective-permute-start | bytes 1966088 | tf_op jit(solution)/shard_map/ppermute | solution.py:385
  9.0 5.3 %collective-permute-done.after = f32[1296,128]{1,0:T(8,128)S(1)} collective-permute-done((f32[1296,128]{1,0:T(8,128)}, f32[1296,128]{1,0:T(8,128)S(1)}, u32[]{:S(2)}, u32[]{:S(2)}) %collective-permute-start) | collective-permute-done | bytes 663584 | tf_op jit(solution)/shard_map/ppermute | solution.py:386
  14.6 4.3 %collective-permute-done.1.before = f32[1280,128]{1,0:T(8,128)S(1)} collective-permute-done((f32[1280,128]{1,0:T(8,128)}, f32[1280,128]{1,0:T(8,128)S(1)}, u32[]{:S(2)}, u32[]{:S(2)}) %collective-permute-start.1) | collective-permute-done | bytes 655392 | tf_op jit(solution)/shard_map/ppermute | solution.py:385
  23.4 10.9 %all-to-all-start = ((f32[8,56,128]{2,1,0:T(8,128)}), f32[8,56,128]{2,1,0:T(8,128)S(1)}, u32[]{:S(2)}, u32[]{:S(2)}) async-start(f32[8,56,128]{2,1,0:T(8,128)} %copy-done.71), calls=%async_computation | async-start | bytes 458752 | tf_op jit(solution)/shard_map/all_to_all | solution.py:341
  34.3 2.9 %collective-permute-start.2 = (f32[48,128]{1,0:T(8,128)S(1)}, f32[48,128]{1,0:T(8,128)S(1)}, u32[]{:S(2)}, u32[]{:S(2)}) collective-permute-start(f32[48,128]{1,0:T(8,128)S(1)} %get-tuple-element.54), channel_id=1, source_target_pairs={{0,64},{64,128},{128,192},{1,65},{65,129},{129,193},{2,66},{66,130... | collective-permute-start | bytes 73736 | tf_op jit(solution)/shard_map/ppermute | solution.py:339
  38.6 6.9 %all-to-all-done.a8 = f32[8,56,128]{2,1,0:T(8,128)S(1)} async-done(((f32[8,56,128]{2,1,0:T(8,128)}), f32[8,56,128]{2,1,0:T(8,128)S(1)}, u32[]{:S(2)}, u32[]{:S(2)}) %all-to-all-start) | async-done | bytes 229408 | tf_op jit(solution)/shard_map/all_to_all | solution.py:341
  52.2 4.4 %shard_map.75 = (f32[32,48,128]{2,1,0:T(8,128)S(1)}, f32[32,48,128]{2,1,0:T(8,128)S(1)}, f32[32,48,128]{2,1,0:T(8,128)S(1)}, f32[33,48,128]{2,1,0:T(8,128)S(1)},...) custom-call(s32[1]{0:T(128)} %bitcast.l_ref.refs_0_, ...), custom_call_target="tpu_custom_call" | custom-call | tf_op jit(solution)/shard_map/pallas_call | solution.py:422
  62.9 6.1 %all-to-all-start.1 = ((f32[8,40,128]{2,1,0:T(8,128)}), f32[8,40,128]{2,1,0:T(8,128)S(1)}, u32[]{:S(2)}, u32[]{:S(2)}) async-start(f32[8,40,128]{2,1,0:T(8,128)} %get-tuple-element.64), calls=%async_computation.1 | async-start | bytes 327680 | tf_op jit(solution)/shard_map/all_to_all | solution.py:341
  69.0 2.9 %collective-permute-start.4 = (f32[48,128]{1,0:T(8,128)S(1)}, f32[48,128]{1,0:T(8,128)S(1)}, u32[]{:S(2)}, u32[]{:S(2)}) collective-permute-start(f32[48,128]{1,0:T(8,128)S(1)} %get-tuple-element.62), channel_id=1, source_target_pairs={{0,64},{64,128},{128,192},{1,65},{65,129},{129,193},{2,66},{66,130... | collective-permute-start | bytes 73736 | tf_op jit(solution)/shard_map/ppermute | solution.py:339
  73.2 6.4 %all-to-all-done.1.a8.refs_5_ = f32[8,40,128]{2,1,0:T(8,128)S(1)} async-done(((f32[8,40,128]{2,1,0:T(8,128)}), f32[8,40,128]{2,1,0:T(8,128)S(1)}, u32[]{:S(2)}, u32[]{:S(2)}) %all-to-all-start.1) | async-done | bytes 163872 | tf_op jit(solution)/shard_map/all_to_all | solution.py:341
  85.8 4.3 %shard_map.77 = (f32[32,48,128]{2,1,0:T(8,128)S(1)}, f32[32,48,128]{2,1,0:T(8,128)S(1)}, f32[32,32,128]{2,1,0:T(8,128)S(1)}, f32[48,128]{1,0:T(8,128)S(1)}, f32[...) custom-call(s32[1]{0:T(128)} %bitcast.l_ref.refs_0_, f32[32,48,128]{2,1,0:T(8,128)S(1)} %copy-done.42, ...), custom_call_target="tpu_custom_call" | custom-call | tf_op jit(solution)/shard_map/pallas_call | solution.py:446
  92.7 6.0 %all-to-all-start.2 = ((f32[8,40,128]{2,1,0:T(8,128)}), f32[8,40,128]{2,1,0:T(8,128)S(1)}, u32[]{:S(2)}, u32[]{:S(2)}) async-start(f32[8,40,128]{2,1,0:T(8,128)} %get-tuple-element.76), calls=%async_computation.2 | async-start | bytes 327680 | tf_op jit(solution)/shard_map/all_to_all | solution.py:341
  98.7 2.9 %collective-permute-start.6 = (f32[48,128]{1,0:T(8,128)S(1)}, f32[48,128]{1,0:T(8,128)S(1)}, u32[]{:S(2)}, u32[]{:S(2)}) collective-permute-start(f32[48,128]{1,0:T(8,128)S(1)} %get-tuple-element.74), channel_id=1, source_target_pairs={{0,64},{64,128},{128,192},{1,65},{65,129},{129,193},{2,66},{66,130... | collective-permute-start | bytes 73736 | tf_op jit(solution)/shard_map/ppermute | solution.py:339
  102.9 6.5 %all-to-all-done.2.a8.refs_6_ = f32[8,40,128]{2,1,0:T(8,128)S(1)} async-done(((f32[8,40,128]{2,1,0:T(8,128)}), f32[8,40,128]{2,1,0:T(8,128)S(1)}, u32[]{:S(2)}, u32[]{:S(2)}) %all-to-all-start.2) | async-done | bytes 163872 | tf_op jit(solution)/shard_map/all_to_all | solution.py:341
  116.6 4.3 %shard_map.79 = (f32[32,48,128]{2,1,0:T(8,128)S(1)}, f32[32,48,128]{2,1,0:T(8,128)S(1)}, f32[32,32,128]{2,1,0:T(8,128)S(1)}, f32[48,128]{1,0:T(8,128)S(1)}, f32[...) custom-call(s32[1]{0:T(128)} %bitcast.l_ref.refs_0_, f32[32,48,128]{2,1,0:T(8,128)S(1)} %copy-done.56, ...), custom_call_target="tpu_custom_call" | custom-call | tf_op jit(solution)/shard_map/pallas_call | solution.py:446
  123.5 5.9 %all-to-all-start.3 = ((f32[8,40,128]{2,1,0:T(8,128)}), f32[8,40,128]{2,1,0:T(8,128)S(1)}, u32[]{:S(2)}, u32[]{:S(2)}) async-start(f32[8,40,128]{2,1,0:T(8,128)} %get-tuple-element.82), calls=%async_computation.3 | async-start | bytes 327680 | tf_op jit(solution)/shard_map/all_to_all | solution.py:341
  132.6 7.5 %all-to-all-done.3.a8.refs_6_ = f32[8,40,128]{2,1,0:T(8,128)S(1)} async-done(((f32[8,40,128]{2,1,0:T(8,128)}), f32[8,40,128]{2,1,0:T(8,128)S(1)}, u32[]{:S(2)}, u32[]{:S(2)}) %all-to-all-start.3) | async-done | bytes 163872 | tf_op jit(solution)/shard_map/all_to_all | solution.py:341
  147.3 4.3 %shard_map.81 = (f32[32,48,128]{2,1,0:T(8,128)S(1)}, f32[32,48,128]{2,1,0:T(8,128)S(1)}, f32[32,32,128]{2,1,0:T(8,128)S(1)}, f32[48,128]{1,0:T(8,128)S(1)}, f32[...) custom-call(s32[1]{0:T(128)} %bitcast.l_ref.refs_0_, f32[32,48,128]{2,1,0:T(8,128)S(1)} %copy-done.48, ...), custom_call_target="tpu_custom_call" | custom-call | tf_op jit(solution)/shard_map/pallas_call | solution.py:446
  154.2 5.0 %all-to-all-start.4 = ((f32[8,40,128]{2,1,0:T(8,128)}), f32[8,40,128]{2,1,0:T(8,128)S(1)}, u32[]{:S(2)}, u32[]{:S(2)}) async-start(f32[8,40,128]{2,1,0:T(8,128)} %get-tuple-element.88), calls=%async_computation.4 | async-start | bytes 327680 | tf_op jit(solution)/shard_map/all_to_all | solution.py:341
  162.3 7.5 %all-to-all-done.4.a8.refs_6_ = f32[8,40,128]{2,1,0:T(8,128)S(1)} async-done(((f32[8,40,128]{2,1,0:T(8,128)}), f32[8,40,128]{2,1,0:T(8,128)S(1)}, u32[]{:S(2)}, u32[]{:S(2)}) %all-to-all-start.4) | async-done | bytes 163872 | tf_op jit(solution)/shard_map/all_to_all | solution.py:341
  177.0 4.3 %shard_map.83 = (f32[32,48,128]{2,1,0:T(8,128)S(1)}, f32[32,48,128]{2,1,0:T(8,128)S(1)}, f32[32,32,128]{2,1,0:T(8,128)S(1)}, f32[48,128]{1,0:T(8,128)S(1)}, f32[...) custom-call(s32[1]{0:T(128)} %bitcast.l_ref.refs_0_, f32[32,48,128]{2,1,0:T(8,128)S(1)} %copy-done.52, ...), custom_call_target="tpu_custom_call" | custom-call | tf_op jit(solution)/shard_map/pallas_call | solution.py:446
  183.9 5.0 %all-to-all-start.5 = ((f32[8,40,128]{2,1,0:T(8,128)}), f32[8,40,128]{2,1,0:T(8,128)S(1)}, u32[]{:S(2)}, u32[]{:S(2)}) async-start(f32[8,40,128]{2,1,0:T(8,128)} %get-tuple-element.94), calls=%async_computation.5 | async-start | bytes 327680 | tf_op jit(solution)/shard_map/all_to_all | solution.py:341
  192.0 7.5 %all-to-all-done.5.a8.refs_6_ = f32[8,40,128]{2,1,0:T(8,128)S(1)} async-done(((f32[8,40,128]{2,1,0:T(8,128)}), f32[8,40,128]{2,1,0:T(8,128)S(1)}, u32[]{:S(2)}, u32[]{:S(2)}) %all-to-all-start.5) | async-done | bytes 163872 | tf_op jit(solution)/shard_map/all_to_all | solution.py:341
  206.7 2.1 %shard_map.85 = f32[32,32,128]{2,1,0:T(8,128)} custom-call(s32[1]{0:T(128)} %bitcast.l_ref.refs_0_, f32[32,48,128]{2,1,0:T(8,128)S(1)} %copy-done.44, f32[32,48,128]{2,1,0:T(8,128)S(1)} %copy-done.46, f32[32,32,128]{2,1,0:T(8,128)S(1)} %copy-done.60, f32[48,128]{1,0:T(8,128)S(1)} %collective-permute-done.12.refs_4_, ...), custom_call_target="tpu_custom_call" | custom-call | tf_op jit(solution)/shard_map/pallas_call | solution.py:446
  (191 shorter events, 83.0 us)
Async XLA Ops:
  0.0 2.7 %copy-start.36 = (f32[32,32,128]{2,1,0:T(8,128)S(1)}, f32[32,32,128]{2,1,0:T(8,128)}, u32[]{:S(2)}) copy-start(f32[32,32,128]{2,1,0:T(8,128)} %acc.1) | copy-start | bytes 1572868
  0.0 2.7 %copy-start.37 = (f32[32,32,128]{2,1,0:T(8,128)S(1)}, f32[32,32,128]{2,1,0:T(8,128)}, u32[]{:S(2)}) copy-start(f32[32,32,128]{2,1,0:T(8,128)} %rhs.1) | copy-start | bytes 1572868
  2.8 16.0 %copy-start.30 = (f32[3,32,32,128]{3,2,1,0:T(8,128)S(1)}, f32[3,32,32,128]{3,2,1,0:T(8,128)}, u32[]{:S(2)}) copy-start(f32[3,32,32,128]{3,2,1,0:T(8,128)} %perm.1) | copy-start | bytes 4718596
  3.7 10.6 %collective-permute-start = (f32[1296,128]{1,0:T(8,128)}, f32[1296,128]{1,0:T(8,128)S(1)}, u32[]{:S(2)}, u32[]{:S(2)}) collective-permute-start(f32[1296,128]{1,0:T(8,128)} %select_maximum_fusion), channel_id=1, source_target_pairs={{8,0},{16,8},{24,16},{32,24},{40,32},{48,40},{56,48},{9,1},{17,9},... | collective-permute-start | bytes 1990664 | tf_op jit(solution)/shard_map/ppermute | solution.py:386
  6.7 12.1 %collective-permute-start.1 = (f32[1280,128]{1,0:T(8,128)}, f32[1280,128]{1,0:T(8,128)S(1)}, u32[]{:S(2)}, u32[]{:S(2)}) collective-permute-start(f32[1280,128]{1,0:T(8,128)} %bitcast.10), channel_id=1, source_target_pairs={{0,8},{8,16},{16,24},{24,32},{32,40},{40,48},{48,56},{1,9},{9,17},... | collective-permute-start | bytes 1966088 | tf_op jit(solution)/shard_map/ppermute | solution.py:385
  14.3 6.8 %copy-start.32 = (f32[1296,128]{1,0:T(8,128)}, f32[1296,128]{1,0:T(8,128)S(1)}, u32[]{:S(2)}) copy-start(f32[1296,128]{1,0:T(8,128)S(1)} %collective-permute-done.after) | copy-start | bytes 1990660
  23.4 22.0 %all-to-all-start = ((f32[8,56,128]{2,1,0:T(8,128)}), f32[8,56,128]{2,1,0:T(8,128)S(1)}, u32[]{:S(2)}, u32[]{:S(2)}) async-start(f32[8,56,128]{2,1,0:T(8,128)} %copy-done.71), calls=%async_computation | async-start | bytes 458752 | tf_op jit(solution)/shard_map/all_to_all | solution.py:341
  34.3 12.2 %collective-permute-start.2 = (f32[48,128]{1,0:T(8,128)S(1)}, f32[48,128]{1,0:T(8,128)S(1)}, u32[]{:S(2)}, u32[]{:S(2)}) collective-permute-start(f32[48,128]{1,0:T(8,128)S(1)} %get-tuple-element.54), channel_id=1, source_target_pairs={{0,64},{64,128},{128,192},{1,65},{65,129},{129,193},{2,66},{66,130... | collective-permute-start | bytes 73736 | tf_op jit(solution)/shard_map/ppermute | solution.py:339
  37.3 9.2 %collective-permute-start.3 = (f32[48,128]{1,0:T(8,128)S(1)}, f32[48,128]{1,0:T(8,128)S(1)}, u32[]{:S(2)}, u32[]{:S(2)}) collective-permute-start(f32[48,128]{1,0:T(8,128)S(1)} %get-tuple-element.55), channel_id=1, source_target_pairs={{64,0},{128,64},{192,128},{65,1},{129,65},{193,129},{66,2},{130,66... | collective-permute-start | bytes 73736 | tf_op jit(solution)/shard_map/ppermute | solution.py:340
  62.9 16.7 %all-to-all-start.1 = ((f32[8,40,128]{2,1,0:T(8,128)}), f32[8,40,128]{2,1,0:T(8,128)S(1)}, u32[]{:S(2)}, u32[]{:S(2)}) async-start(f32[8,40,128]{2,1,0:T(8,128)} %get-tuple-element.64), calls=%async_computation.1 | async-start | bytes 327680 | tf_op jit(solution)/shard_map/all_to_all | solution.py:341
  69.0 11.5 %collective-permute-start.4 = (f32[48,128]{1,0:T(8,128)S(1)}, f32[48,128]{1,0:T(8,128)S(1)}, u32[]{:S(2)}, u32[]{:S(2)}) collective-permute-start(f32[48,128]{1,0:T(8,128)S(1)} %get-tuple-element.62), channel_id=1, source_target_pairs={{0,64},{64,128},{128,192},{1,65},{65,129},{129,193},{2,66},{66,130... | collective-permute-start | bytes 73736 | tf_op jit(solution)/shard_map/ppermute | solution.py:339
  71.9 8.6 %collective-permute-start.5 = (f32[48,128]{1,0:T(8,128)S(1)}, f32[48,128]{1,0:T(8,128)S(1)}, u32[]{:S(2)}, u32[]{:S(2)}) collective-permute-start(f32[48,128]{1,0:T(8,128)S(1)} %get-tuple-element.63), channel_id=1, source_target_pairs={{64,0},{128,64},{192,128},{65,1},{129,65},{193,129},{66,2},{130,66... | collective-permute-start | bytes 73736 | tf_op jit(solution)/shard_map/ppermute | solution.py:340
  92.7 16.7 %all-to-all-start.2 = ((f32[8,40,128]{2,1,0:T(8,128)}), f32[8,40,128]{2,1,0:T(8,128)S(1)}, u32[]{:S(2)}, u32[]{:S(2)}) async-start(f32[8,40,128]{2,1,0:T(8,128)} %get-tuple-element.76), calls=%async_computation.2 | async-start | bytes 327680 | tf_op jit(solution)/shard_map/all_to_all | solution.py:341
  98.7 11.6 %collective-permute-start.6 = (f32[48,128]{1,0:T(8,128)S(1)}, f32[48,128]{1,0:T(8,128)S(1)}, u32[]{:S(2)}, u32[]{:S(2)}) collective-permute-start(f32[48,128]{1,0:T(8,128)S(1)} %get-tuple-element.74), channel_id=1, source_target_pairs={{0,64},{64,128},{128,192},{1,65},{65,129},{129,193},{2,66},{66,130... | collective-permute-start | bytes 73736 | tf_op jit(solution)/shard_map/ppermute | solution.py:339
  101.6 8.7 %collective-permute-start.7 = (f32[48,128]{1,0:T(8,128)S(1)}, f32[48,128]{1,0:T(8,128)S(1)}, u32[]{:S(2)}, u32[]{:S(2)}) collective-permute-start(f32[48,128]{1,0:T(8,128)S(1)} %get-tuple-element.75), channel_id=1, source_target_pairs={{64,0},{128,64},{192,128},{65,1},{129,65},{193,129},{66,2},{130,66... | collective-permute-start | bytes 73736 | tf_op jit(solution)/shard_map/ppermute | solution.py:340
  123.5 16.6 %all-to-all-start.3 = ((f32[8,40,128]{2,1,0:T(8,128)}), f32[8,40,128]{2,1,0:T(8,128)S(1)}, u32[]{:S(2)}, u32[]{:S(2)}) async-start(f32[8,40,128]{2,1,0:T(8,128)} %get-tuple-element.82), calls=%async_computation.3 | async-start | bytes 327680 | tf_op jit(solution)/shard_map/all_to_all | solution.py:341
  129.4 11.6 %collective-permute-start.8 = (f32[48,128]{1,0:T(8,128)S(1)}, f32[48,128]{1,0:T(8,128)S(1)}, u32[]{:S(2)}, u32[]{:S(2)}) collective-permute-start(f32[48,128]{1,0:T(8,128)S(1)} %get-tuple-element.80), channel_id=1, source_target_pairs={{0,64},{64,128},{128,192},{1,65},{65,129},{129,193},{2,66},{66,130... | collective-permute-start | bytes 73736 | tf_op jit(solution)/shard_map/ppermute | solution.py:339
  131.3 9.7 %collective-permute-start.9 = (f32[48,128]{1,0:T(8,128)S(1)}, f32[48,128]{1,0:T(8,128)S(1)}, u32[]{:S(2)}, u32[]{:S(2)}) collective-permute-start(f32[48,128]{1,0:T(8,128)S(1)} %get-tuple-element.81), channel_id=1, source_target_pairs={{64,0},{128,64},{192,128},{65,1},{129,65},{193,129},{66,2},{130,66... | collective-permute-start | bytes 73736 | tf_op jit(solution)/shard_map/ppermute | solution.py:340
  154.2 15.7 %all-to-all-start.4 = ((f32[8,40,128]{2,1,0:T(8,128)}), f32[8,40,128]{2,1,0:T(8,128)S(1)}, u32[]{:S(2)}, u32[]{:S(2)}) async-start(f32[8,40,128]{2,1,0:T(8,128)} %get-tuple-element.88), calls=%async_computation.4 | async-start | bytes 327680 | tf_op jit(solution)/shard_map/all_to_all | solution.py:341
  159.1 11.6 %collective-permute-start.10 = (f32[48,128]{1,0:T(8,128)S(1)}, f32[48,128]{1,0:T(8,128)S(1)}, u32[]{:S(2)}, u32[]{:S(2)}) collective-permute-start(f32[48,128]{1,0:T(8,128)S(1)} %get-tuple-element.86), channel_id=1, source_target_pairs={{0,64},{64,128},{128,192},{1,65},{65,129},{129,193},{2,66},{66,130... | collective-permute-start | bytes 73736 | tf_op jit(solution)/shard_map/ppermute | solution.py:339
  161.0 9.7 %collective-permute-start.11 = (f32[48,128]{1,0:T(8,128)S(1)}, f32[48,128]{1,0:T(8,128)S(1)}, u32[]{:S(2)}, u32[]{:S(2)}) collective-permute-start(f32[48,128]{1,0:T(8,128)S(1)} %get-tuple-element.87), channel_id=1, source_target_pairs={{64,0},{128,64},{192,128},{65,1},{129,65},{193,129},{66,2},{130,66... | collective-permute-start | bytes 73736 | tf_op jit(solution)/shard_map/ppermute | solution.py:340
  183.9 15.7 %all-to-all-start.5 = ((f32[8,40,128]{2,1,0:T(8,128)}), f32[8,40,128]{2,1,0:T(8,128)S(1)}, u32[]{:S(2)}, u32[]{:S(2)}) async-start(f32[8,40,128]{2,1,0:T(8,128)} %get-tuple-element.94), calls=%async_computation.5 | async-start | bytes 327680 | tf_op jit(solution)/shard_map/all_to_all | solution.py:341
  188.8 11.6 %collective-permute-start.12 = (f32[48,128]{1,0:T(8,128)S(1)}, f32[48,128]{1,0:T(8,128)S(1)}, u32[]{:S(2)}, u32[]{:S(2)}) collective-permute-start(f32[48,128]{1,0:T(8,128)S(1)} %get-tuple-element.92), channel_id=1, source_target_pairs={{0,64},{64,128},{128,192},{1,65},{65,129},{129,193},{2,66},{66,130... | collective-permute-start | bytes 73736 | tf_op jit(solution)/shard_map/ppermute | solution.py:339
  190.7 9.7 %collective-permute-start.13 = (f32[48,128]{1,0:T(8,128)S(1)}, f32[48,128]{1,0:T(8,128)S(1)}, u32[]{:S(2)}, u32[]{:S(2)}) collective-permute-start(f32[48,128]{1,0:T(8,128)S(1)} %get-tuple-element.93), channel_id=1, source_target_pairs={{64,0},{128,64},{192,128},{65,1},{129,65},{193,129},{66,2},{130,66... | collective-permute-start | bytes 73736 | tf_op jit(solution)/shard_map/ppermute | solution.py:340
  (68 other events, 74.3 us)

commit v4 on v3

v4 whole, which is shorter than its diff:
```python
import jax
import jax.numpy as jnp
from jax import lax
from jax.experimental import pallas as pl
from jax.experimental.pallas import tpu as pltpu
from jax.sharding import PartitionSpec as P

SWEEPS = 6
lam_low = 0.1
lam_high = 2.0
theta = (lam_high + lam_low) / 2.0
delta = (lam_high - lam_low) / 2.0
sigma = theta / delta

SLOT_ROWS = 4
LIST_ROWS = 24
H = 8
f32 = jnp.float32
bf16 = jnp.bfloat16


def harmonic(left, right):
    total = left + right
    live = total > 0.0
    return jnp.where(live, 2.0 * (left * right) / jnp.where(live, total, 1.0), 0.0)


def split3(v):
    hi = v.astype(bf16).astype(f32)
    rest = v - hi
    mid = rest.astype(bf16).astype(f32)
    return hi, mid, rest - mid


def dot(a, b, dims):
    return lax.dot_general(a, b, (dims, ((), ())), preferred_element_type=f32)


def lane_iota(shape):
    return lax.broadcasted_iota(jnp.int32, shape, len(shape) - 1)


def rows_hit(codes, count):
    shape = (count, codes.shape[1])
    return lax.broadcasted_iota(jnp.int32, shape, 0).astype(f32) == codes


def picks(codes):
    return jnp.where(rows_hit(codes, 128), 1.0, 0.0).astype(bf16)


def thirds(out):
    n = out.shape[0] // 3
    return out[:n] + out[n : 2 * n] + out[2 * n :]


def gather(table, pick, x_hit):
    parts = jnp.concatenate(split3(table), axis=0).astype(bf16)
    got = thirds(dot(parts, pick, ((1,), (0,))))
    return jnp.sum(jnp.where(x_hit, got, 0.0), axis=0, keepdims=True)


def scatter(u, pick, x_hit):
    parts = [jnp.where(x_hit, p, 0.0) for p in split3(u)]
    return thirds(dot(jnp.concatenate(parts, axis=0).astype(bf16), pick, ((1,), (1,))))


def get_rows(ref, t, base, count):
    return jnp.concatenate([ref[t, base + k : base + k + 1, :] for k in range(count)], axis=1)


def put_rows(ref, t, base, values):
    for k in range(values.shape[1] // 128):
        ref[t, base + k : base + k + 1, :] = values[:, 128 * k : 128 * (k + 1)]


NEAR_Z, NEAR_X, WEIGHT, FAR_X, FAR_TILE, FAR_Z = range(6)


def slot_row(row_ref, q, which):
    return row_ref[q, which : which + 1, :]


FACE_ROWS = 16


def pack_faces(faces, slab, x, cx):
    low, high = faces
    lane = lane_iota(low.shape)
    for part in range(slab.shape[0] // FACE_ROWS):
        rows = slab[part * FACE_ROWS : (part + 1) * FACE_ROWS]
        here = lane == cx * part + x
        low = jnp.where(here, rows[:, 0:1], low)
        high = jnp.where(here, rows[:, 127:128], high)
    return low, high


def no_faces():
    return jnp.zeros((FACE_ROWS, 128), f32), jnp.zeros((FACE_ROWS, 128), f32)


def put_faces(l, ref, faces):
    for t in range(ref.shape[0]):
        ref[t, 0:FACE_ROWS, :] = jnp.where(t > l, faces[1], faces[0])


def get_faces(l, ref):
    tiles = ref.shape[0]
    low = ref[jnp.maximum(l - 1, 0), 0:FACE_ROWS, :]
    high = ref[jnp.minimum(l + 1, tiles - 1), 0:FACE_ROWS, :]
    return low, high


def unpacked(faces, slab, x, cx):
    lane = lane_iota(slab.shape)
    parts = slab.shape[0] // FACE_ROWS

    def column(packed, to):
        return jnp.concatenate(
            [pltpu.roll(packed, (to + 128 - cx * part - x) % 128, 1) for part in range(parts)], axis=0
        )

    low = jnp.where(lane == 0, column(faces[0], 0), pltpu.roll(slab, 1, 1))
    high = jnp.where(lane == 127, column(faces[1], 127), pltpu.roll(slab, 127, 1))
    return low, high


def pack_kernel(l_ref, rhs, acc, perm, cell, remote, mask, trans,
                top, bottom, a8, kx_first, kx_last, kz, sem):
    tiles = a8.shape[0]
    cx, cy = rhs.shape[0], rhs.shape[1]
    sources = [rhs, acc] + [perm.at[n] for n in range(3)]
    moves = [pltpu.make_async_copy(perm.at[2], kz, sem.at[0])]
    for n, source in enumerate(sources):
        moves.append(pltpu.make_async_copy(source.at[:, cy - H :, :], top.at[n], sem.at[1 + 2 * n]))
        moves.append(pltpu.make_async_copy(source.at[:, :H, :], bottom.at[n], sem.at[2 + 2 * n]))
    count = 2 * len(sources) + 1
    moves.append(pltpu.make_async_copy(perm.at[0, 0], kx_first, sem.at[count]))
    moves.append(pltpu.make_async_copy(perm.at[0, cx - 1], kx_last, sem.at[count + 1]))
    for move in moves:
        move.start()
    weight = trans[...] * mask[...].astype(f32)
    own, far = cell[...], remote[...]
    column = tiles * 128
    far_z = far & (column - 1)
    table = [
        (own & 127).astype(f32),
        (own >> 7).astype(f32),
        weight,
        (far >> (column.bit_length() - 1)).astype(f32),
        (far_z >> 7).astype(f32),
        (far_z & 127).astype(f32),
    ]
    for n, values in enumerate(table):
        for t in range(tiles):
            put_rows(a8, t, FACE_ROWS + n * SLOT_ROWS, values)
    moves[0].wait()

    def body(x, faces):
        return pack_faces(faces, kz[x], x, cx)

    put_faces(l_ref[0], a8, lax.fori_loop(0, cx, body, no_faces(), unroll=4))
    for move in moves[1:]:
        move.wait()


def relay_kernel(l_ref, a8, faces, lists):
    tiles = a8.shape[0]
    l = l_ref[0]
    low, high = get_faces(l, a8)
    faces[0:FACE_ROWS, :] = jnp.where(l > 0, low, 0.0)
    faces[FACE_ROWS:, :] = jnp.where(l < tiles - 1, high, 0.0)
    for t in range(tiles):
        lists[LIST_ROWS * t : LIST_ROWS * (t + 1), :] = a8[t, FACE_ROWS:, :]


def join_kernel(faces, lists, kx_low, kx_high, up, down):
    cy = kx_low.shape[0]
    base = 2 * FACE_ROWS
    for out in (up, down):
        out[0:base, :] = faces[...]
        out[base : base + cy, :] = kx_low[...]
        out[base + cy : base + 2 * cy, :] = kx_high[...]
    down[base + 2 * cy :, :] = lists[...]


def emit(l_ref, a8_ref, planes, faces, row_ref, pick_ref, far_x):
    tiles = a8_ref.shape[0]
    cx = planes.shape[1]
    slots = row_ref.shape[2]
    put_faces(l_ref[0], a8_ref, faces)
    for q in range(2):
        base = FACE_ROWS + q * 2 * SLOT_ROWS
        near = gather(
            planes[2 * q + 1], picks(slot_row(row_ref, q, NEAR_Z)), rows_hit(slot_row(row_ref, q, NEAR_X), cx)
        )
        near = slot_row(row_ref, q, WEIGHT) * near
        for t in range(tiles):
            at = slice(t * slots, (t + 1) * slots)
            far = gather(planes[2 * q], pick_ref[q, :, at], rows_hit(far_x[q : q + 1, at], cx))
            put_rows(a8_ref, t, base, near)
            put_rows(a8_ref, t, base + SLOT_ROWS, far)


def keep_planes(planes, slab, x):
    last = slab.shape[0] - H - 1
    for n, y in enumerate((H - 1, H, last, last + 1)):
        planes[n, pl.ds(x, 1), :] = slab[y : y + 1, :]


def with_fault(total, fault, x):
    tiles = [total[8 * n : 8 * (n + 1)] for n in range(total.shape[0] // 8)]
    y = lax.broadcasted_iota(jnp.int32, tiles[0].shape, 0)
    last = total.shape[0] - H - 1
    for n, at in enumerate((H - 1, H, last, last + 1)):
        tiles[at // 8] += jnp.where(y == at % 8, fault[n, pl.ds(x, 1), :], 0.0)
    return jnp.concatenate(tiles, axis=0)


def near_sum(row_ref, q, values, cx):
    return scatter(
        values, picks(slot_row(row_ref, q, NEAR_Z)), rows_hit(slot_row(row_ref, q, NEAR_X), cx)
    )


def weights(l, a8, above, row_ref, pick_ref, far_x, fault):
    tiles = a8.shape[0]
    cx = fault.shape[1]
    slots = row_ref.shape[2]
    first = above.shape[0] - tiles * LIST_ROWS

    def codes(block):
        parts = [block[n : n + 1] for n in range(LIST_ROWS)]
        return [
            jnp.concatenate(parts[SLOT_ROWS * n : SLOT_ROWS * (n + 1)], axis=1) for n in range(6)
        ]

    def block(q, t):
        if q == 0:
            return a8[t, FACE_ROWS : FACE_ROWS + LIST_ROWS, :]
        return above[pl.ds(pl.multiple_of(first + t * LIST_ROWS, 8), LIST_ROWS), :]

    for q in range(2):
        mine = codes(block(q, l))
        for n in range(3):
            row_ref[q, n : n + 1, :] = mine[n]
        far = jnp.zeros((cx, 128), f32)
        for t in range(tiles):
            at = slice(t * slots, (t + 1) * slots)
            table = codes(block(q, t))
            x = jnp.where(table[FAR_TILE] == l.astype(f32), table[FAR_X], -1.0)
            pick = picks(table[FAR_Z])
            pick_ref[q, :, at] = pick
            far_x[q : q + 1, at] = x
            far = far + scatter(table[WEIGHT], pick, rows_hit(x, cx))
        fault[2 * q] = far
        fault[2 * q + 1] = near_sum(row_ref, q, slot_row(row_ref, q, WEIGHT), cx)


def fault_kernel(a8, row_ref, pick_ref, far_x, fault):
    tiles, rows = a8.shape[0], a8.shape[1]
    cx = fault.shape[1]
    slots = row_ref.shape[2]
    for q in range(2):
        base = rows - (2 - q) * 2 * SLOT_ROWS
        far = jnp.zeros((cx, 128), f32)
        near = jnp.zeros((1, slots), f32)
        for t in range(tiles):
            at = slice(t * slots, (t + 1) * slots)
            values = get_rows(a8, t, base, SLOT_ROWS)
            far = far + scatter(values, pick_ref[q, :, at], rows_hit(far_x[q : q + 1, at], cx))
            near = near + get_rows(a8, t, base + SLOT_ROWS, SLOT_ROWS)
        fault[2 * q] = far
        fault[2 * q + 1] = near_sum(row_ref, q, slot_row(row_ref, q, WEIGHT) * near, cx)


def setup_kernel(l_ref, rhs, acc, perm, before, after, below, above, kx_low, kx_high, a8,
                 inv, z_out, d_out, tx, tym, typ, tzm, tzp, d_first, d_last, a8_out,
                 row_ref, pick_ref, far_x, planes, fault):
    cx, cy = rhs.shape[0], rhs.shape[1]
    ye = cy + 2 * H
    tiles = a8.shape[0]
    l = l_ref[0]
    weights(l, a8, above, row_ref, pick_ref, far_x, fault)
    low, high = get_faces(l, a8)
    faces_in = []
    for n, own in enumerate((jnp.where(l > 0, low, 0.0), jnp.where(l < tiles - 1, high, 0.0))):
        at = n * FACE_ROWS
        lane = lane_iota((8, 128))
        under, over = below[at + 8 : at + 16, :], above[at : at + 8, :]
        first = jnp.where(lane < cx, pltpu.roll(under, 128 - cx, 1), pltpu.roll(own[8:16], cx, 1))
        second = jnp.where(lane < 2 * cx, own[0:8], pltpu.roll(over, 2 * cx, 1))
        faces_in.append(jnp.concatenate([first, second], axis=0))

    def ext_face(n, own):
        at = 2 * FACE_ROWS + n * cy
        return jnp.concatenate([below[at + cy - H : at + cy, :], own[...], above[at : at + H, :]], axis=0)

    kx_under, kx_over = ext_face(0, kx_low), ext_face(1, kx_high)

    def ext(a, own, x):
        return jnp.concatenate([before[a, x], own, after[a, x]], axis=0)

    def body(x, carry):
        faces, t_low, kx = carry
        nxt = jnp.minimum(x + 1, cx - 1)
        kx_next = jnp.where(x == cx - 1, kx_over, ext(2, perm[0, nxt], nxt))
        ky = ext(3, perm[1, x], x)
        kz = ext(4, perm[2, x], x)
        t_high = harmonic(kx, kx_next)
        ym = harmonic(ky, pltpu.roll(ky, 1, 0))
        yp = harmonic(ky, pltpu.roll(ky, ye - 1, 0))
        kz_low, kz_high = unpacked(faces_in, kz, x, cx)
        zm = harmonic(kz, kz_low)
        zp = harmonic(kz, kz_high)
        diag = ext(1, acc[x], x) + t_low + t_high + ym + yp + zm + zp
        diag = with_fault(diag, fault, x)
        live = diag > 0.0
        inverse = jnp.where(live, 1.0 / jnp.where(live, diag, 1.0), 0.0)
        z = inverse * ext(0, rhs[x], x)
        d = z / theta
        inv[x] = inverse
        z_out[x] = z
        d_out[x] = d
        tx[x] = t_low
        tx[x + 1] = t_high
        tym[x] = ym
        typ[x] = yp
        tzm[x] = zm
        tzp[x] = zp
        keep_planes(planes, d, x)
        return pack_faces(faces, d, x, cx), t_high, kx_next

    kx0 = ext(2, perm[0, 0], 0)
    init = (no_faces(), harmonic(kx_under, kx0), kx0)
    faces, _, _ = lax.fori_loop(0, cx, body, init, unroll=4)
    d_first[...] = d_out[0]
    d_last[...] = d_out[cx - 1]
    emit(l_ref, a8_out, planes, faces, row_ref, pick_ref, far_x)


def sweep_kernel(c1, c2, first, last, l_ref, d_in, z_in, *refs):
    refs = list(refs)
    corr_in = None if first else refs.pop(0)
    xlow, xhigh, a8, fault, inv, tx, tym, typ, tzm, tzp = refs[:10]
    refs = refs[10:]
    if not last:
        row_ref, pick_ref, far_x = refs[:3]
        refs = refs[3:]
    outs = refs
    if last:
        (corr_out,) = outs
    else:
        d_out, z_out, corr_out, d_first, d_last, a8_out, planes = outs
    cx, ye = d_in.shape[0], d_in.shape[1]
    cy = ye - 2 * H
    faces_in = get_faces(l_ref[0], a8)

    def body(x, carry):
        faces, d_prev, d = carry
        d_next = jnp.where(x == cx - 1, xhigh[...], d_in[jnp.minimum(x + 1, cx - 1)])
        z_low, z_high = unpacked(faces_in, d, x, cx)
        flow = tx[x] * d_prev + tx[x + 1] * d_next
        flow = flow + (tym[x] * pltpu.roll(d, 1, 0) + typ[x] * pltpu.roll(d, ye - 1, 0))
        flow = flow + (tzm[x] * z_low + tzp[x] * z_high)
        flow = with_fault(flow, fault, x)
        z = z_in[x] - d + inv[x] * flow
        new = c1 * d + c2 * z
        before = d[H : H + cy] if first else corr_in[x]
        corr_out[x] = before + new[H : H + cy]
        if last:
            return faces, d, d_next
        d_out[x] = new
        z_out[x] = z
        keep_planes(planes, new, x)
        return pack_faces(faces, new, x, cx), d, d_next

    init = (no_faces(), xlow[...], d_in[0])
    faces, _, _ = lax.fori_loop(0, cx, body, init, unroll=4)
    if not last:
        d_first[...] = d_out[0]
        d_last[...] = d_out[cx - 1]
        emit(l_ref, a8_out, planes, faces, row_ref, pick_ref, far_x)


VMEM = pl.BlockSpec(memory_space=pltpu.VMEM)
SMEM = pl.BlockSpec(memory_space=pltpu.SMEM)
HBM = pl.BlockSpec(memory_space=pltpu.HBM)
PARAMS = pltpu.CompilerParams(vmem_limit_bytes=24 << 20)


def steps(axis):
    peers = lax.axis_size(axis)
    up = [(i, i + 1) for i in range(peers - 1)]
    return up, [(j, i) for i, j in up]


def local(rhs, accumulation, permeability, nnc_cell, nnc_remote, nnc_mask, nnc_trans):
    cx, cy, cz = rhs.shape
    tiles = lax.axis_size("gz")
    slots = nnc_cell.shape[-1]
    ye = cy + 2 * H
    up_y, down_y = steps("gy")
    up_x, down_x = steps("gx")

    def struct(*shape, dtype=f32):
        return jax.ShapeDtypeStruct(shape, dtype)

    l = lax.axis_index("gz").reshape(1).astype(jnp.int32)
    flats = [a.reshape(1, slots) for a in (nnc_cell, nnc_remote, nnc_mask, nnc_trans)]
    halo = struct(5, cx, H, cz)
    top, bottom, a8, kx_first, kx_last = pl.pallas_call(
        pack_kernel,
        out_shape=(halo, halo, struct(tiles, FACE_ROWS + LIST_ROWS, cz), struct(cy, cz), struct(cy, cz)),
        in_specs=[SMEM] + [HBM] * 3 + [VMEM] * 4,
        out_specs=(VMEM,) * 5,
        scratch_shapes=[pltpu.VMEM((cx, cy, cz), f32), pltpu.SemaphoreType.DMA((13,))],
    )(l, rhs, accumulation, permeability, *flats)
    kx_low = lax.ppermute(kx_last, "gx", up_x)
    kx_high = lax.ppermute(kx_first, "gx", down_x)
    before = lax.ppermute(top, "gy", up_y)
    after = lax.ppermute(bottom, "gy", down_y)
    a8 = lax.all_to_all(a8, "gz", 0, 0, tiled=True)
    faces, group = pl.pallas_call(
        relay_kernel,
        out_shape=(struct(2 * FACE_ROWS, cz), struct(tiles * LIST_ROWS, cz)),
        in_specs=[SMEM, VMEM],
        out_specs=(VMEM,) * 2,
        compiler_params=PARAMS,
    )(l, a8)
    small = 2 * FACE_ROWS + 2 * cy
    below, above = pl.pallas_call(
        join_kernel,
        out_shape=(struct(small, cz), struct(small + tiles * LIST_ROWS, cz)),
        in_specs=[VMEM] * 4,
        out_specs=(VMEM,) * 2,
        compiler_params=PARAMS,
    )(faces, group, kx_low, kx_high)
    below = lax.ppermute(below, "gy", up_y)
    above = lax.ppermute(above, "gy", down_y)

    big = struct(cx, ye, cz)
    tall = struct(cx + 1, ye, cz)
    edge = struct(ye, cz)
    small = struct(cx, cy, cz)
    sent = struct(tiles, FACE_ROWS + 4 * SLOT_ROWS, cz)
    scratch = [pltpu.VMEM((4, cx, cz), f32)]
    every = tiles * slots
    lists = (struct(2, 8, slots), struct(2, cz, every, dtype=bf16), struct(2, every))
    inv, z, d, tx, tym, typ, tzm, tzp, d_first, d_last, a8, row, pick, far_x = pl.pallas_call(
        setup_kernel,
        out_shape=(big, big, big, tall, big, big, big, big, edge, edge, sent) + lists,
        in_specs=[SMEM] + [VMEM] * 10,
        out_specs=(VMEM,) * 14,
        scratch_shapes=scratch * 2,
        compiler_params=PARAMS,
    )(l, rhs, accumulation, permeability, before, after, below, above, kx_low, kx_high, a8)

    rho = 1.0 / sigma
    corr = None
    for sweep in range(1, SWEEPS):
        first, last = sweep == 1, sweep == SWEEPS - 1
        rho_next = 1.0 / (2.0 * sigma - rho)
        c1, c2 = rho_next * rho, 2.0 * rho_next / delta
        rho = rho_next
        xlow = lax.ppermute(d_last, "gx", up_x)
        xhigh = lax.ppermute(d_first, "gx", down_x)
        a8 = lax.all_to_all(a8, "gz", 0, 0, tiled=True)
        fault = pl.pallas_call(
            fault_kernel,
            out_shape=struct(4, cx, cz),
            in_specs=[VMEM] * 4,
            out_specs=VMEM,
            compiler_params=PARAMS,
        )(a8, row, pick, far_x)
        args = [l, d, z] + ([] if first else [corr])
        args += [xlow, xhigh, a8, fault, inv, tx, tym, typ, tzm, tzp]
        args += [] if last else [row, pick, far_x]

        def kernel(*refs, c1=c1, c2=c2, first=first, last=last):
            sweep_kernel(c1, c2, first, last, *refs)

        out = pl.pallas_call(
            kernel,
            out_shape=small if last else (big, big, small, edge, edge, sent),
            in_specs=[SMEM] + [VMEM] * (len(args) - 1),
            out_specs=VMEM if last else (VMEM,) * 6,
            scratch_shapes=[] if last else scratch,
            compiler_params=PARAMS,
        )(*args)
        if last:
            corr = out
        else:
            d, z, corr, d_first, d_last, a8 = out
    return corr


def solution(mesh):
    split = P("gx", "gy", "gz")
    slots = P("gx", "gy", "gz", None)
    return jax.shard_map(
        local,
        mesh=mesh,
        in_specs=(split, split, P(None, "gx", "gy", "gz"), slots, slots, slots, slots),
        out_specs=split,
        check_vma=False,
    )
```

time: 211 us -> 208 us (0.986)
  the two profiles are of different devices: /device:TPU:24 before, /device:TPU:16 now
where the time goes in v4:
time: 208 us; the launch traced here: 205 us
  starting transfers between devices  73.1 us (35%)
  local copies, waits for them, and re-layouts  55.5 us (27%)
  waiting for transfers between devices  44.2 us (21%)
  Pallas kernels  31.9 us (15%)
    unnamed x138, local copies, waits for them, and re-layouts  55.5 us
    all_to_all x6, waiting for transfers between devices, local(): a8 = lax.all_to_all(a8, 'gz', 0, 0, tiled=True)  41.1 us
    all_to_all x6, starting transfers between devices, local(): a8 = lax.all_to_all(a8, 'gz', 0, 0, tiled=True)  41 us
    pallas_call x5, Pallas kernels, local(): pl.pallas_call(kernel, out_shape=small if last else (big, big, small, edg...  19.1 us
    ppermute x5, starting transfers between devices, local(): xlow = lax.ppermute(d_last, 'gx', up_x)  11.6 us
    ppermute x5, starting transfers between devices, local(): xhigh = lax.ppermute(d_first, 'gx', down_x)  6.46 us
    pallas_call x1, Pallas kernels, local(): pl.pallas_call(setup_kernel, out_shape=(big, big, big, tall, big, big, bi...  4.58 us
    pallas_call x5, Pallas kernels, local(): pl.pallas_call(fault_kernel, out_shape=struct(4, cx, cz), in_specs=[VMEM]...  4.25 us
  transfers between devices with their start and end apart: 22, of which 7 were waited for; matrix products, arithmetic and copies ran while one was open for 0% of the time, Pallas kernels for 2%

profile of v4, /device:TPU:16, one launch (start us, length us, event | category | flops | bytes accessed | tf_op | source)
XLA Modules:
  0.0 205.1 jit_solution(18271923986235581081)
XLA Ops:
  0.0 4.0 %shard_map.73 = (f32[5,32,8,128]{3,2,1,0:T(8,128)}, f32[5,32,8,128]{3,2,1,0:T(8,128)}, f32[8,40,128]{2,1,0:T(8,128)}, f32[32,128]{1,0:T(8,128)}, f32[32,128]{1,0:T(8,128)}) custom-call(s32[1]{0:T(128)} %bitcast.l_ref.refs_0_, f32[32,32,128]{2,1,0:T(8,128)} %rhs.3, f32[32,32,128]{2,1,0:T(8,128)} %acc.3, f32[3,32,32,128]{3,2,1,0:T(8,128)} %perm.3, ...), custom_call_target="tpu_custom_call" | custom-call | tf_op jit(solution)/shard_map/pallas_call | solution.py:412
  5.9 3.6 %collective-permute-start.1 = (f32[5,32,8,128]{3,2,1,0:T(8,128)}, f32[5,32,8,128]{3,2,1,0:T(8,128)S(1)}, u32[]{:S(2)}, u32[]{:S(2)}) collective-permute-start(f32[5,32,8,128]{3,2,1,0:T(8,128)} %get-tuple-element.53), channel_id=1, source_target_pairs={{8,0},{16,8},{24,16},{32,24},{40,32},{48,40},{56,48},{9,1},{17,9},... | collective-permute-start | bytes 1966088 | tf_op jit(solution)/shard_map/ppermute | solution.py:422
  9.6 10.9 %all-to-all-start = ((f32[8,40,128]{2,1,0:T(8,128)}), f32[8,40,128]{2,1,0:T(8,128)S(1)}, u32[]{:S(2)}, u32[]{:S(2)}) async-start(f32[8,40,128]{2,1,0:T(8,128)} %get-tuple-element.54), calls=%async_computation | async-start | bytes 327680 | tf_op jit(solution)/shard_map/all_to_all | solution.py:423
  20.5 2.9 %collective-permute-start.2 = (f32[32,128]{1,0:T(8,128)}, f32[32,128]{1,0:T(8,128)S(1)}, u32[]{:S(2)}, u32[]{:S(2)}) collective-permute-start(f32[32,128]{1,0:T(8,128)} %get-tuple-element.57), channel_id=1, source_target_pairs={{0,64},{64,128},{128,192},{1,65},{65,129},{129,193},{2,66},{66,130... | collective-permute-start | bytes 49160 | tf_op jit(solution)/shard_map/ppermute | solution.py:419
  24.7 6.5 %all-to-all-done.a8 = f32[8,40,128]{2,1,0:T(8,128)S(1)} async-done(((f32[8,40,128]{2,1,0:T(8,128)}), f32[8,40,128]{2,1,0:T(8,128)S(1)}, u32[]{:S(2)}, u32[]{:S(2)}) %all-to-all-start) | async-done | bytes 163872 | tf_op jit(solution)/shard_map/all_to_all | solution.py:423
  33.3 2.4 %collective-permute-start.4 = (f32[96,128]{1,0:T(8,128)S(1)}, f32[96,128]{1,0:T(8,128)S(1)}, u32[]{:S(2)}, u32[]{:S(2)}) collective-permute-start(f32[96,128]{1,0:T(8,128)S(1)} %get-tuple-element.59), channel_id=1, source_target_pairs={{0,8},{8,16},{16,24},{24,32},{32,40},{40,48},{48,56},{1,9},{9,17},... | collective-permute-start | bytes 147464 | tf_op jit(solution)/shard_map/ppermute | solution.py:439
  35.7 3.0 %collective-permute-done.4.below = f32[96,128]{1,0:T(8,128)S(1)} collective-permute-done((f32[96,128]{1,0:T(8,128)S(1)}, f32[96,128]{1,0:T(8,128)S(1)}, u32[]{:S(2)}, u32[]{:S(2)}) %collective-permute-start.4) | collective-permute-done | bytes 49184 | tf_op jit(solution)/shard_map/ppermute | solution.py:439
  46.0 4.6 %shard_map.76 = (f32[32,48,128]{2,1,0:T(8,128)S(1)}, f32[32,48,128]{2,1,0:T(8,128)S(1)}, f32[32,48,128]{2,1,0:T(8,128)S(1)}, f32[33,48,128]{2,1,0:T(8,128)S(1)},...) custom-call(s32[1]{0:T(128)} %bitcast.l_ref.refs_0_, ...), custom_call_target="tpu_custom_call" | custom-call | tf_op jit(solution)/shard_map/pallas_call | solution.py:450
  58.1 7.6 %all-to-all-start.1 = ((f32[8,32,128]{2,1,0:T(8,128)}), f32[8,32,128]{2,1,0:T(8,128)S(1)}, u32[]{:S(2)}, u32[]{:S(2)}) async-start(f32[8,32,128]{2,1,0:T(8,128)} %copy-done.67), calls=%async_computation.1 | async-start | bytes 262144 | tf_op jit(solution)/shard_map/all_to_all | solution.py:468
  65.6 2.9 %collective-permute-start.6 = (f32[48,128]{1,0:T(8,128)}, f32[48,128]{1,0:T(8,128)S(1)}, u32[]{:S(2)}, u32[]{:S(2)}) collective-permute-start(f32[48,128]{1,0:T(8,128)} %copy-done.68), channel_id=1, source_target_pairs={{0,64},{64,128},{128,192},{1,65},{65,129},{129,193},{2,66},{66,130... | collective-permute-start | bytes 73736 | tf_op jit(solution)/shard_map/ppermute | solution.py:466
  69.9 6.4 %all-to-all-done.1.a8.refs_5_ = f32[8,32,128]{2,1,0:T(8,128)S(1)} async-done(((f32[8,32,128]{2,1,0:T(8,128)}), f32[8,32,128]{2,1,0:T(8,128)S(1)}, u32[]{:S(2)}, u32[]{:S(2)}) %all-to-all-start.1) | async-done | bytes 131104 | tf_op jit(solution)/shard_map/all_to_all | solution.py:468
  82.4 4.2 %shard_map.78 = (f32[32,48,128]{2,1,0:T(8,128)S(1)}, f32[32,48,128]{2,1,0:T(8,128)S(1)}, f32[32,32,128]{2,1,0:T(8,128)S(1)}, f32[48,128]{1,0:T(8,128)S(1)}, f32[...) custom-call(s32[1]{0:T(128)} %bitcast.l_ref.refs_0_, f32[32,48,128]{2,1,0:T(8,128)S(1)} %copy-done.38, ...), custom_call_target="tpu_custom_call" | custom-call | tf_op jit(solution)/shard_map/pallas_call | solution.py:483
  89.2 6.1 %all-to-all-start.2 = ((f32[8,32,128]{2,1,0:T(8,128)}), f32[8,32,128]{2,1,0:T(8,128)S(1)}, u32[]{:S(2)}, u32[]{:S(2)}) async-start(f32[8,32,128]{2,1,0:T(8,128)} %get-tuple-element.80), calls=%async_computation.2 | async-start | bytes 262144 | tf_op jit(solution)/shard_map/all_to_all | solution.py:468
  95.2 2.9 %collective-permute-start.8 = (f32[48,128]{1,0:T(8,128)S(1)}, f32[48,128]{1,0:T(8,128)S(1)}, u32[]{:S(2)}, u32[]{:S(2)}) collective-permute-start(f32[48,128]{1,0:T(8,128)S(1)} %get-tuple-element.78), channel_id=1, source_target_pairs={{0,64},{64,128},{128,192},{1,65},{65,129},{129,193},{2,66},{66,130... | collective-permute-start | bytes 73736 | tf_op jit(solution)/shard_map/ppermute | solution.py:466
  99.5 6.3 %all-to-all-done.2.a8.refs_6_ = f32[8,32,128]{2,1,0:T(8,128)S(1)} async-done(((f32[8,32,128]{2,1,0:T(8,128)}), f32[8,32,128]{2,1,0:T(8,128)S(1)}, u32[]{:S(2)}, u32[]{:S(2)}) %all-to-all-start.2) | async-done | bytes 131104 | tf_op jit(solution)/shard_map/all_to_all | solution.py:468
  113.0 4.2 %shard_map.80 = (f32[32,48,128]{2,1,0:T(8,128)S(1)}, f32[32,48,128]{2,1,0:T(8,128)S(1)}, f32[32,32,128]{2,1,0:T(8,128)S(1)}, f32[48,128]{1,0:T(8,128)S(1)}, f32[...) custom-call(s32[1]{0:T(128)} %bitcast.l_ref.refs_0_, f32[32,48,128]{2,1,0:T(8,128)S(1)} %copy-done.52, ...), custom_call_target="tpu_custom_call" | custom-call | tf_op jit(solution)/shard_map/pallas_call | solution.py:483
  119.8 6.1 %all-to-all-start.3 = ((f32[8,32,128]{2,1,0:T(8,128)}), f32[8,32,128]{2,1,0:T(8,128)S(1)}, u32[]{:S(2)}, u32[]{:S(2)}) async-start(f32[8,32,128]{2,1,0:T(8,128)} %get-tuple-element.86), calls=%async_computation.3 | async-start | bytes 262144 | tf_op jit(solution)/shard_map/all_to_all | solution.py:468
  129.1 7.3 %all-to-all-done.3.a8.refs_6_ = f32[8,32,128]{2,1,0:T(8,128)S(1)} async-done(((f32[8,32,128]{2,1,0:T(8,128)}), f32[8,32,128]{2,1,0:T(8,128)S(1)}, u32[]{:S(2)}, u32[]{:S(2)}) %all-to-all-start.3) | async-done | bytes 131104 | tf_op jit(solution)/shard_map/all_to_all | solution.py:468
  143.6 4.2 %shard_map.82 = (f32[32,48,128]{2,1,0:T(8,128)S(1)}, f32[32,48,128]{2,1,0:T(8,128)S(1)}, f32[32,32,128]{2,1,0:T(8,128)S(1)}, f32[48,128]{1,0:T(8,128)S(1)}, f32[...) custom-call(s32[1]{0:T(128)} %bitcast.l_ref.refs_0_, f32[32,48,128]{2,1,0:T(8,128)S(1)} %copy-done.44, ...), custom_call_target="tpu_custom_call" | custom-call | tf_op jit(solution)/shard_map/pallas_call | solution.py:483
  150.4 5.1 %all-to-all-start.4 = ((f32[8,32,128]{2,1,0:T(8,128)}), f32[8,32,128]{2,1,0:T(8,128)S(1)}, u32[]{:S(2)}, u32[]{:S(2)}) async-start(f32[8,32,128]{2,1,0:T(8,128)} %get-tuple-element.92), calls=%async_computation.4 | async-start | bytes 262144 | tf_op jit(solution)/shard_map/all_to_all | solution.py:468
  158.8 7.3 %all-to-all-done.4.a8.refs_6_ = f32[8,32,128]{2,1,0:T(8,128)S(1)} async-done(((f32[8,32,128]{2,1,0:T(8,128)}), f32[8,32,128]{2,1,0:T(8,128)S(1)}, u32[]{:S(2)}, u32[]{:S(2)}) %all-to-all-start.4) | async-done | bytes 131104 | tf_op jit(solution)/shard_map/all_to_all | solution.py:468
  173.2 4.2 %shard_map.84 = (f32[32,48,128]{2,1,0:T(8,128)S(1)}, f32[32,48,128]{2,1,0:T(8,128)S(1)}, f32[32,32,128]{2,1,0:T(8,128)S(1)}, f32[48,128]{1,0:T(8,128)S(1)}, f32[...) custom-call(s32[1]{0:T(128)} %bitcast.l_ref.refs_0_, f32[32,48,128]{2,1,0:T(8,128)S(1)} %copy-done.48, ...), custom_call_target="tpu_custom_call" | custom-call | tf_op jit(solution)/shard_map/pallas_call | solution.py:483
  180.0 5.1 %all-to-all-start.5 = ((f32[8,32,128]{2,1,0:T(8,128)}), f32[8,32,128]{2,1,0:T(8,128)S(1)}, u32[]{:S(2)}, u32[]{:S(2)}) async-start(f32[8,32,128]{2,1,0:T(8,128)} %get-tuple-element.98), calls=%async_computation.5 | async-start | bytes 262144 | tf_op jit(solution)/shard_map/all_to_all | solution.py:468
  188.4 7.3 %all-to-all-done.5.a8.refs_6_ = f32[8,32,128]{2,1,0:T(8,128)S(1)} async-done(((f32[8,32,128]{2,1,0:T(8,128)}), f32[8,32,128]{2,1,0:T(8,128)S(1)}, u32[]{:S(2)}, u32[]{:S(2)}) %all-to-all-start.5) | async-done | bytes 131104 | tf_op jit(solution)/shard_map/all_to_all | solution.py:468
  (172 shorter events, 79.4 us)
Async XLA Ops:
  0.0 40.4 %copy-start.31 = (f32[32,32,128]{2,1,0:T(8,128)S(1)}, f32[32,32,128]{2,1,0:T(8,128)}, u32[]{:S(2)}) copy-start(f32[32,32,128]{2,1,0:T(8,128)} %rhs.3) | copy-start | bytes 1572868
  4.0 34.7 %collective-permute-start = (f32[5,32,8,128]{3,2,1,0:T(8,128)}, f32[5,32,8,128]{3,2,1,0:T(8,128)S(1)}, u32[]{:S(2)}, u32[]{:S(2)}) collective-permute-start(f32[5,32,8,128]{3,2,1,0:T(8,128)} %get-tuple-element.52), channel_id=1, source_target_pairs={{0,8},{8,16},{16,24},{24,32},{32,40},{40,48},{48,56},{1,9},{9,17},... | collective-permute-start | bytes 1966088 | tf_op jit(solution)/shard_map/ppermute | solution.py:421
  5.9 33.6 %collective-permute-start.1 = (f32[5,32,8,128]{3,2,1,0:T(8,128)}, f32[5,32,8,128]{3,2,1,0:T(8,128)S(1)}, u32[]{:S(2)}, u32[]{:S(2)}) collective-permute-start(f32[5,32,8,128]{3,2,1,0:T(8,128)} %get-tuple-element.53), channel_id=1, source_target_pairs={{8,0},{16,8},{24,16},{32,24},{40,32},{48,40},{56,48},{9,1},{17,9},... | collective-permute-start | bytes 1966088 | tf_op jit(solution)/shard_map/ppermute | solution.py:422
  9.6 21.7 %all-to-all-start = ((f32[8,40,128]{2,1,0:T(8,128)}), f32[8,40,128]{2,1,0:T(8,128)S(1)}, u32[]{:S(2)}, u32[]{:S(2)}) async-start(f32[8,40,128]{2,1,0:T(8,128)} %get-tuple-element.54), calls=%async_computation | async-start | bytes 327680 | tf_op jit(solution)/shard_map/all_to_all | solution.py:423
  20.5 10.8 %collective-permute-start.2 = (f32[32,128]{1,0:T(8,128)}, f32[32,128]{1,0:T(8,128)S(1)}, u32[]{:S(2)}, u32[]{:S(2)}) collective-permute-start(f32[32,128]{1,0:T(8,128)} %get-tuple-element.57), channel_id=1, source_target_pairs={{0,64},{64,128},{128,192},{1,65},{65,129},{129,193},{2,66},{66,130... | collective-permute-start | bytes 49160 | tf_op jit(solution)/shard_map/ppermute | solution.py:419
  23.4 7.9 %collective-permute-start.3 = (f32[32,128]{1,0:T(8,128)}, f32[32,128]{1,0:T(8,128)S(1)}, u32[]{:S(2)}, u32[]{:S(2)}) collective-permute-start(f32[32,128]{1,0:T(8,128)} %get-tuple-element.58), channel_id=1, source_target_pairs={{64,0},{128,64},{192,128},{65,1},{129,65},{193,129},{66,2},{130,66... | collective-permute-start | bytes 49160 | tf_op jit(solution)/shard_map/ppermute | solution.py:420
  31.3 7.4 %copy-start.33 = (f32[8,40,128]{2,1,0:T(8,128)}, f32[8,40,128]{2,1,0:T(8,128)S(1)}, u32[]{:S(2)}) copy-start(f32[8,40,128]{2,1,0:T(8,128)S(1)} %all-to-all-done.a8) | copy-start | bytes 491524
  31.4 7.3 %collective-permute-start.5 = (f32[288,128]{1,0:T(8,128)S(1)}, f32[288,128]{1,0:T(8,128)S(1)}, u32[]{:S(2)}, u32[]{:S(2)}) collective-permute-start(f32[288,128]{1,0:T(8,128)S(1)} %get-tuple-element.60), channel_id=1, source_target_pairs={{8,0},{16,8},{24,16},{32,24},{40,32},{48,40},{56,48},{9,1},{17,9},... | collective-permute-start | bytes 442376 | tf_op jit(solution)/shard_map/ppermute | solution.py:440
  33.3 5.4 %collective-permute-start.4 = (f32[96,128]{1,0:T(8,128)S(1)}, f32[96,128]{1,0:T(8,128)S(1)}, u32[]{:S(2)}, u32[]{:S(2)}) collective-permute-start(f32[96,128]{1,0:T(8,128)S(1)} %get-tuple-element.59), channel_id=1, source_target_pairs={{0,8},{8,16},{16,24},{24,32},{32,40},{40,48},{48,56},{1,9},{9,17},... | collective-permute-start | bytes 147464 | tf_op jit(solution)/shard_map/ppermute | solution.py:439
  58.1 18.1 %all-to-all-start.1 = ((f32[8,32,128]{2,1,0:T(8,128)}), f32[8,32,128]{2,1,0:T(8,128)S(1)}, u32[]{:S(2)}, u32[]{:S(2)}) async-start(f32[8,32,128]{2,1,0:T(8,128)} %copy-done.67), calls=%async_computation.1 | async-start | bytes 262144 | tf_op jit(solution)/shard_map/all_to_all | solution.py:468
  65.6 11.5 %collective-permute-start.6 = (f32[48,128]{1,0:T(8,128)}, f32[48,128]{1,0:T(8,128)S(1)}, u32[]{:S(2)}, u32[]{:S(2)}) collective-permute-start(f32[48,128]{1,0:T(8,128)} %copy-done.68), channel_id=1, source_target_pairs={{0,64},{64,128},{128,192},{1,65},{65,129},{129,193},{2,66},{66,130... | collective-permute-start | bytes 73736 | tf_op jit(solution)/shard_map/ppermute | solution.py:466
  68.6 8.6 %collective-permute-start.7 = (f32[48,128]{1,0:T(8,128)S(1)}, f32[48,128]{1,0:T(8,128)S(1)}, u32[]{:S(2)}, u32[]{:S(2)}) collective-permute-start(f32[48,128]{1,0:T(8,128)S(1)} %get-tuple-element.64), channel_id=1, source_target_pairs={{64,0},{128,64},{192,128},{65,1},{129,65},{193,129},{66,2},{130,66... | collective-permute-start | bytes 73736 | tf_op jit(solution)/shard_map/ppermute | solution.py:467
  89.2 16.6 %all-to-all-start.2 = ((f32[8,32,128]{2,1,0:T(8,128)}), f32[8,32,128]{2,1,0:T(8,128)S(1)}, u32[]{:S(2)}, u32[]{:S(2)}) async-start(f32[8,32,128]{2,1,0:T(8,128)} %get-tuple-element.80), calls=%async_computation.2 | async-start | bytes 262144 | tf_op jit(solution)/shard_map/all_to_all | solution.py:468
  95.2 11.4 %collective-permute-start.8 = (f32[48,128]{1,0:T(8,128)S(1)}, f32[48,128]{1,0:T(8,128)S(1)}, u32[]{:S(2)}, u32[]{:S(2)}) collective-permute-start(f32[48,128]{1,0:T(8,128)S(1)} %get-tuple-element.78), channel_id=1, source_target_pairs={{0,64},{64,128},{128,192},{1,65},{65,129},{129,193},{2,66},{66,130... | collective-permute-start | bytes 73736 | tf_op jit(solution)/shard_map/ppermute | solution.py:466
  98.2 8.5 %collective-permute-start.9 = (f32[48,128]{1,0:T(8,128)S(1)}, f32[48,128]{1,0:T(8,128)S(1)}, u32[]{:S(2)}, u32[]{:S(2)}) collective-permute-start(f32[48,128]{1,0:T(8,128)S(1)} %get-tuple-element.79), channel_id=1, source_target_pairs={{64,0},{128,64},{192,128},{65,1},{129,65},{193,129},{66,2},{130,66... | collective-permute-start | bytes 73736 | tf_op jit(solution)/shard_map/ppermute | solution.py:467
  119.8 16.6 %all-to-all-start.3 = ((f32[8,32,128]{2,1,0:T(8,128)}), f32[8,32,128]{2,1,0:T(8,128)S(1)}, u32[]{:S(2)}, u32[]{:S(2)}) async-start(f32[8,32,128]{2,1,0:T(8,128)} %get-tuple-element.86), calls=%async_computation.3 | async-start | bytes 262144 | tf_op jit(solution)/shard_map/all_to_all | solution.py:468
  125.9 11.4 %collective-permute-start.10 = (f32[48,128]{1,0:T(8,128)S(1)}, f32[48,128]{1,0:T(8,128)S(1)}, u32[]{:S(2)}, u32[]{:S(2)}) collective-permute-start(f32[48,128]{1,0:T(8,128)S(1)} %get-tuple-element.84), channel_id=1, source_target_pairs={{0,64},{64,128},{128,192},{1,65},{65,129},{129,193},{2,66},{66,130... | collective-permute-start | bytes 73736 | tf_op jit(solution)/shard_map/ppermute | solution.py:466
  127.8 9.5 %collective-permute-start.11 = (f32[48,128]{1,0:T(8,128)S(1)}, f32[48,128]{1,0:T(8,128)S(1)}, u32[]{:S(2)}, u32[]{:S(2)}) collective-permute-start(f32[48,128]{1,0:T(8,128)S(1)} %get-tuple-element.85), channel_id=1, source_target_pairs={{64,0},{128,64},{192,128},{65,1},{129,65},{193,129},{66,2},{130,66... | collective-permute-start | bytes 73736 | tf_op jit(solution)/shard_map/ppermute | solution.py:467
  150.4 15.6 %all-to-all-start.4 = ((f32[8,32,128]{2,1,0:T(8,128)}), f32[8,32,128]{2,1,0:T(8,128)S(1)}, u32[]{:S(2)}, u32[]{:S(2)}) async-start(f32[8,32,128]{2,1,0:T(8,128)} %get-tuple-element.92), calls=%async_computation.4 | async-start | bytes 262144 | tf_op jit(solution)/shard_map/all_to_all | solution.py:468
  155.5 11.4 %collective-permute-start.12 = (f32[48,128]{1,0:T(8,128)S(1)}, f32[48,128]{1,0:T(8,128)S(1)}, u32[]{:S(2)}, u32[]{:S(2)}) collective-permute-start(f32[48,128]{1,0:T(8,128)S(1)} %get-tuple-element.90), channel_id=1, source_target_pairs={{0,64},{64,128},{128,192},{1,65},{65,129},{129,193},{2,66},{66,130... | collective-permute-start | bytes 73736 | tf_op jit(solution)/shard_map/ppermute | solution.py:466
  157.5 9.5 %collective-permute-start.13 = (f32[48,128]{1,0:T(8,128)S(1)}, f32[48,128]{1,0:T(8,128)S(1)}, u32[]{:S(2)}, u32[]{:S(2)}) collective-permute-start(f32[48,128]{1,0:T(8,128)S(1)} %get-tuple-element.91), channel_id=1, source_target_pairs={{64,0},{128,64},{192,128},{65,1},{129,65},{193,129},{66,2},{130,66... | collective-permute-start | bytes 73736 | tf_op jit(solution)/shard_map/ppermute | solution.py:467
  180.0 15.7 %all-to-all-start.5 = ((f32[8,32,128]{2,1,0:T(8,128)}), f32[8,32,128]{2,1,0:T(8,128)S(1)}, u32[]{:S(2)}, u32[]{:S(2)}) async-start(f32[8,32,128]{2,1,0:T(8,128)} %get-tuple-element.98), calls=%async_computation.5 | async-start | bytes 262144 | tf_op jit(solution)/shard_map/all_to_all | solution.py:468
  185.2 11.4 %collective-permute-start.14 = (f32[48,128]{1,0:T(8,128)S(1)}, f32[48,128]{1,0:T(8,128)S(1)}, u32[]{:S(2)}, u32[]{:S(2)}) collective-permute-start(f32[48,128]{1,0:T(8,128)S(1)} %get-tuple-element.96), channel_id=1, source_target_pairs={{0,64},{64,128},{128,192},{1,65},{65,129},{129,193},{2,66},{66,130... | collective-permute-start | bytes 73736 | tf_op jit(solution)/shard_map/ppermute | solution.py:466
  187.1 9.5 %collective-permute-start.15 = (f32[48,128]{1,0:T(8,128)S(1)}, f32[48,128]{1,0:T(8,128)S(1)}, u32[]{:S(2)}, u32[]{:S(2)}) collective-permute-start(f32[48,128]{1,0:T(8,128)S(1)} %get-tuple-element.97), channel_id=1, source_target_pairs={{64,0},{128,64},{192,128},{65,1},{129,65},{193,129},{66,2},{130,66... | collective-permute-start | bytes 73736 | tf_op jit(solution)/shard_map/ppermute | solution.py:467
  (67 other events, 72.5 us)

commit v5 on v4

--- a/solution.py
+++ b/solution.py
@@ -81,51 +81,56 @@
     return row_ref[q, which : which + 1, :]
 
 
-FACE_ROWS = 16
-
-
-def pack_faces(faces, slab, x, cx):
-    low, high = faces
-    lane = lane_iota(low.shape)
-    for part in range(slab.shape[0] // FACE_ROWS):
-        rows = slab[part * FACE_ROWS : (part + 1) * FACE_ROWS]
-        here = lane == cx * part + x
-        low = jnp.where(here, rows[:, 0:1], low)
-        high = jnp.where(here, rows[:, 127:128], high)
-    return low, high
+FACE_ROWS = 24
+
+
+def pack_faces(faces, tiles, x):
+    faces = list(faces)
+    lane = lane_iota((8, 128))
+    for half in range(2):
+        at = 64 * half + 2 * x + 2
+        here = ((lane - (at - 1)) & 127) < 2
+        for n in range(3):
+            tile = tiles[3 * half + n]
+            if tile is not None:
+                faces[n] = jnp.where(here, pltpu.roll(tile, at % 128, 1), faces[n])
+    return tuple(faces)
 
 
 def no_faces():
-    return jnp.zeros((FACE_ROWS, 128), f32), jnp.zeros((FACE_ROWS, 128), f32)
-
-
-def put_faces(l, ref, faces):
+    return (jnp.zeros((8, 128), f32),) * 3
+
+
+def y_tiles(slab):
+    return [slab[8 * n : 8 * (n + 1)] for n in range(slab.shape[0] // 8)]
+
+
+def put_faces(ref, faces):
+    packed = jnp.concatenate(faces, axis=0)
     for t in range(ref.shape[0]):
-        ref[t, 0:FACE_ROWS, :] = jnp.where(t > l, faces[1], faces[0])
+        ref[t, 0:FACE_ROWS, :] = packed
 
 
 def get_faces(l, ref):
     tiles = ref.shape[0]
-    low = ref[jnp.maximum(l - 1, 0), 0:FACE_ROWS, :]
-    high = ref[jnp.minimum(l + 1, tiles - 1), 0:FACE_ROWS, :]
-    return low, high
-
-
-def unpacked(faces, slab, x, cx):
-    lane = lane_iota(slab.shape)
-    parts = slab.shape[0] // FACE_ROWS
-
-    def column(packed, to):
-        return jnp.concatenate(
-            [pltpu.roll(packed, (to + 128 - cx * part - x) % 128, 1) for part in range(parts)], axis=0
-        )
-
-    low = jnp.where(lane == 0, column(faces[0], 0), pltpu.roll(slab, 1, 1))
-    high = jnp.where(lane == 127, column(faces[1], 127), pltpu.roll(slab, 127, 1))
-    return low, high
-
-
-def pack_kernel(l_ref, rhs, acc, perm, cell, remote, mask, trans,
+    low = jnp.where(l > 0, ref[jnp.maximum(l - 1, 0), 0:FACE_ROWS, :], 0.0)
+    high = jnp.where(l < tiles - 1, ref[jnp.minimum(l + 1, tiles - 1), 0:FACE_ROWS, :], 0.0)
+    odd = (lane_iota(low.shape) & 1) == 1
+    return jnp.where(odd, low, pltpu.roll(high, 126, 1))
+
+
+def unpacked(faces, slab, x):
+    lane = lane_iota((8, 128))
+    lows, highs = [], []
+    for n, tile in enumerate(y_tiles(slab)):
+        packed = faces[8 * (n % 3) : 8 * (n % 3) + 8]
+        outer = pltpu.roll(packed, (127 - 64 * (n // 3) - 2 * x) % 128, 1)
+        lows.append(jnp.where(lane == 0, outer, pltpu.roll(tile, 1, 1)))
+        highs.append(jnp.where(lane == 127, outer, pltpu.roll(tile, 127, 1)))
+    return jnp.concatenate(lows, axis=0), jnp.concatenate(highs, axis=0)
+
+
+def pack_kernel(rhs, acc, perm, cell, remote, mask, trans,
                 top, bottom, a8, kx_first, kx_last, kz, sem):
     tiles = a8.shape[0]
     cx, cy = rhs.shape[0], rhs.shape[1]
@@ -157,9 +162,9 @@
     moves[0].wait()
 
     def body(x, faces):
-        return pack_faces(faces, kz[x], x, cx)
-
-    put_faces(l_ref[0], a8, lax.fori_loop(0, cx, body, no_faces(), unroll=4))
+        return pack_faces(faces, [None] + y_tiles(kz[x]) + [None], x)
+
+    put_faces(a8, lax.fori_loop(0, cx, body, no_faces(), unroll=4))
     for move in moves[1:]:
         move.wait()
 
@@ -167,16 +172,14 @@
 def relay_kernel(l_ref, a8, faces, lists):
     tiles = a8.shape[0]
     l = l_ref[0]
-    low, high = get_faces(l, a8)
-    faces[0:FACE_ROWS, :] = jnp.where(l > 0, low, 0.0)
-    faces[FACE_ROWS:, :] = jnp.where(l < tiles - 1, high, 0.0)
+    faces[...] = get_faces(l, a8)
     for t in range(tiles):
         lists[LIST_ROWS * t : LIST_ROWS * (t + 1), :] = a8[t, FACE_ROWS:, :]
 
 
 def join_kernel(faces, lists, kx_low, kx_high, up, down):
     cy = kx_low.shape[0]
-    base = 2 * FACE_ROWS
+    base = FACE_ROWS
     for out in (up, down):
         out[0:base, :] = faces[...]
         out[base : base + cy, :] = kx_low[...]
@@ -184,11 +187,11 @@
     down[base + 2 * cy :, :] = lists[...]
 
 
-def emit(l_ref, a8_ref, planes, faces, row_ref, pick_ref, far_x):
+def emit(a8_ref, planes, faces, row_ref, pick_ref, far_x):
     tiles = a8_ref.shape[0]
     cx = planes.shape[1]
     slots = row_ref.shape[2]
-    put_faces(l_ref[0], a8_ref, faces)
+    put_faces(a8_ref, faces)
     for q in range(2):
         base = FACE_ROWS + q * 2 * SLOT_ROWS
         near = gather(
@@ -209,7 +212,7 @@
 
 
 def with_fault(total, fault, x):
-    tiles = [total[8 * n : 8 * (n + 1)] for n in range(total.shape[0] // 8)]
+    tiles = y_tiles(total)
     y = lax.broadcasted_iota(jnp.int32, tiles[0].shape, 0)
     last = total.shape[0] - H - 1
     for n, at in enumerate((H - 1, H, last, last + 1)):
@@ -279,21 +282,21 @@
                  row_ref, pick_ref, far_x, planes, fault):
     cx, cy = rhs.shape[0], rhs.shape[1]
     ye = cy + 2 * H
-    tiles = a8.shape[0]
     l = l_ref[0]
     weights(l, a8, above, row_ref, pick_ref, far_x, fault)
-    low, high = get_faces(l, a8)
-    faces_in = []
-    for n, own in enumerate((jnp.where(l > 0, low, 0.0), jnp.where(l < tiles - 1, high, 0.0))):
-        at = n * FACE_ROWS
-        lane = lane_iota((8, 128))
-        under, over = below[at + 8 : at + 16, :], above[at : at + 8, :]
-        first = jnp.where(lane < cx, pltpu.roll(under, 128 - cx, 1), pltpu.roll(own[8:16], cx, 1))
-        second = jnp.where(lane < 2 * cx, own[0:8], pltpu.roll(over, 2 * cx, 1))
-        faces_in.append(jnp.concatenate([first, second], axis=0))
+    own = get_faces(l, a8)
+    left = lane_iota((8, 128)) < 64
+    faces_in = jnp.concatenate(
+        [
+            jnp.where(left, pltpu.roll(below[8:16, :], 64, 1), own[0:8]),
+            own[8:16],
+            jnp.where(left, own[16:24], pltpu.roll(above[8:16, :], 64, 1)),
+        ],
+        axis=0,
+    )
 
     def ext_face(n, own):
-        at = 2 * FACE_ROWS + n * cy
+        at = FACE_ROWS + n * cy
         return jnp.concatenate([below[at + cy - H : at + cy, :], own[...], above[at : at + H, :]], axis=0)
 
     kx_under, kx_over = ext_face(0, kx_low), ext_face(1, kx_high)
@@ -310,7 +313,7 @@
         t_high = harmonic(kx, kx_next)
         ym = harmonic(ky, pltpu.roll(ky, 1, 0))
         yp = harmonic(ky, pltpu.roll(ky, ye - 1, 0))
-        kz_low, kz_high = unpacked(faces_in, kz, x, cx)
+        kz_low, kz_high = unpacked(faces_in, kz, x)
         zm = harmonic(kz, kz_low)
         zp = harmonic(kz, kz_high)
         diag = ext(1, acc[x], x) + t_low + t_high + ym + yp + zm + zp
@@ -329,14 +332,14 @@
         tzm[x] = zm
         tzp[x] = zp
         keep_planes(planes, d, x)
-        return pack_faces(faces, d, x, cx), t_high, kx_next
+        return pack_faces(faces, y_tiles(d), x), t_high, kx_next
 
     kx0 = ext(2, perm[0, 0], 0)
     init = (no_faces(), harmonic(kx_under, kx0), kx0)
     faces, _, _ = lax.fori_loop(0, cx, body, init, unroll=4)
     d_first[...] = d_out[0]
     d_last[...] = d_out[cx - 1]
-    emit(l_ref, a8_out, planes, faces, row_ref, pick_ref, far_x)
+    emit(a8_out, planes, faces, row_ref, pick_ref, far_x)
 
 
 def sweep_kernel(c1, c2, first, last, l_ref, d_in, z_in, *refs):
@@ -359,7 +362,7 @@
     def body(x, carry):
         faces, d_prev, d = carry
         d_next = jnp.where(x == cx - 1, xhigh[...], d_in[jnp.minimum(x + 1, cx - 1)])
-        z_low, z_high = unpacked(faces_in, d, x, cx)
+        z_low, z_high = unpacked(faces_in, d, x)
         flow = tx[x] * d_prev + tx[x + 1] * d_next
         flow = flow + (tym[x] * pltpu.roll(d, 1, 0) + typ[x] * pltpu.roll(d, ye - 1, 0))
         flow = flow + (tzm[x] * z_low + tzp[x] * z_high)
@@ -373,14 +376,14 @@
         d_out[x] = new
         z_out[x] = z
         keep_planes(planes, new, x)
-        return pack_faces(faces, new, x, cx), d, d_next
+        return pack_faces(faces, y_tiles(new), x), d, d_next
 
     init = (no_faces(), xlow[...], d_in[0])
     faces, _, _ = lax.fori_loop(0, cx, body, init, unroll=4)
     if not last:
         d_first[...] = d_out[0]
         d_last[...] = d_out[cx - 1]
-        emit(l_ref, a8_out, planes, faces, row_ref, pick_ref, far_x)
+        emit(a8_out, planes, faces, row_ref, pick_ref, far_x)
 
 
 VMEM = pl.BlockSpec(memory_space=pltpu.VMEM)
@@ -408,14 +411,15 @@
 
     l = lax.axis_index("gz").reshape(1).astype(jnp.int32)
     flats = [a.reshape(1, slots) for a in (nnc_cell, nnc_remote, nnc_mask, nnc_trans)]
+    l, *flats = lax.optimization_barrier((l, *flats))
     halo = struct(5, cx, H, cz)
     top, bottom, a8, kx_first, kx_last = pl.pallas_call(
         pack_kernel,
         out_shape=(halo, halo, struct(tiles, FACE_ROWS + LIST_ROWS, cz), struct(cy, cz), struct(cy, cz)),
-        in_specs=[SMEM] + [HBM] * 3 + [VMEM] * 4,
+        in_specs=[HBM] * 3 + [VMEM] * 4,
         out_specs=(VMEM,) * 5,
         scratch_shapes=[pltpu.VMEM((cx, cy, cz), f32), pltpu.SemaphoreType.DMA((13,))],
-    )(l, rhs, accumulation, permeability, *flats)
+    )(rhs, accumulation, permeability, *flats)
     kx_low = lax.ppermute(kx_last, "gx", up_x)
     kx_high = lax.ppermute(kx_first, "gx", down_x)
     before = lax.ppermute(top, "gy", up_y)
@@ -423,12 +427,12 @@
     a8 = lax.all_to_all(a8, "gz", 0, 0, tiled=True)
     faces, group = pl.pallas_call(
         relay_kernel,
-        out_shape=(struct(2 * FACE_ROWS, cz), struct(tiles * LIST_ROWS, cz)),
+        out_shape=(struct(FACE_ROWS, cz), struct(tiles * LIST_ROWS, cz)),
         in_specs=[SMEM, VMEM],
         out_specs=(VMEM,) * 2,
         compiler_params=PARAMS,
     )(l, a8)
-    small = 2 * FACE_ROWS + 2 * cy
+    small = FACE_ROWS + 2 * cy
     below, above = pl.pallas_call(
         join_kernel,
         out_shape=(struct(small, cz), struct(small + tiles * LIST_ROWS, cz)),

time: 208 us -> 203 us (0.976)
  the two profiles are of different devices: /device:TPU:16 before, /device:TPU:8 now
where the time goes in v5:
time: 203 us; the launch traced here: 200 us
  starting transfers between devices  72.2 us (36%)
  local copies, waits for them, and re-layouts  55.5 us (27%)
  waiting for transfers between devices  45.1 us (22%)
  Pallas kernels  27.1 us (13%)
    unnamed x138, local copies, waits for them, and re-layouts  55.5 us
    all_to_all x6, waiting for transfers between devices, local(): a8 = lax.all_to_all(a8, 'gz', 0, 0, tiled=True)  42.1 us
    all_to_all x6, starting transfers between devices, local(): a8 = lax.all_to_all(a8, 'gz', 0, 0, tiled=True)  40.1 us
    pallas_call x5, Pallas kernels, local(): pl.pallas_call(kernel, out_shape=small if last else (big, big, small, edg...  14.9 us
    ppermute x5, starting transfers between devices, local(): xlow = lax.ppermute(d_last, 'gx', up_x)  11.6 us
    ppermute x5, starting transfers between devices, local(): xhigh = lax.ppermute(d_first, 'gx', down_x)  6.46 us
    pallas_call x5, Pallas kernels, local(): pl.pallas_call(fault_kernel, out_shape=struct(4, cx, cz), in_specs=[VMEM]...  4.25 us
  transfers between devices with their start and end apart: 22, of which 7 were waited for; matrix products, arithmetic and copies ran while one was open for 0% of the time, Pallas kernels for 2%

profile of v5, /device:TPU:8, one launch (start us, length us, event | category | flops | bytes accessed | tf_op | source)
XLA Modules:
  0.0 200.3 jit_solution(613667861070110723)
XLA Ops:
  0.0 3.8 %shard_map.73 = (f32[5,32,8,128]{3,2,1,0:T(8,128)}, f32[5,32,8,128]{3,2,1,0:T(8,128)}, f32[8,48,128]{2,1,0:T(8,128)}, f32[32,128]{1,0:T(8,128)}, f32[32,128]{1,0:T(8,128)}) custom-call(f32[32,32,128]{2,1,0:T(8,128)} %rhs.3, f32[32,32,128]{2,1,0:T(8,128)} %acc.3, f32[3,32,32,128]{3,2,1,0:T(8,128)} %perm.3, s32[1,512]{1,0:T(1,128)} %bitcast.5, ...), custom_call_target="tpu_custom_call" | custom-call | tf_op jit(solution)/shard_map/pallas_call | solution.py:416
  5.7 3.6 %collective-permute-start.1 = (f32[5,32,8,128]{3,2,1,0:T(8,128)}, f32[5,32,8,128]{3,2,1,0:T(8,128)S(1)}, u32[]{:S(2)}, u32[]{:S(2)}) collective-permute-start(f32[5,32,8,128]{3,2,1,0:T(8,128)} %get-tuple-element.63), channel_id=1, source_target_pairs={{8,0},{16,8},{24,16},{32,24},{40,32},{48,40},{56,48},{9,1},{17,9},... | collective-permute-start | bytes 1966088 | tf_op jit(solution)/shard_map/ppermute | solution.py:426
  9.4 10.9 %all-to-all-start = ((f32[8,48,128]{2,1,0:T(8,128)}), f32[8,48,128]{2,1,0:T(8,128)S(1)}, u32[]{:S(2)}, u32[]{:S(2)}) async-start(f32[8,48,128]{2,1,0:T(8,128)} %get-tuple-element.64), calls=%async_computation | async-start | bytes 393216 | tf_op jit(solution)/shard_map/all_to_all | solution.py:427
  20.3 2.9 %collective-permute-start.2 = (f32[32,128]{1,0:T(8,128)}, f32[32,128]{1,0:T(8,128)S(1)}, u32[]{:S(2)}, u32[]{:S(2)}) collective-permute-start(f32[32,128]{1,0:T(8,128)} %get-tuple-element.67), channel_id=1, source_target_pairs={{0,64},{64,128},{128,192},{1,65},{65,129},{129,193},{2,66},{66,130... | collective-permute-start | bytes 49160 | tf_op jit(solution)/shard_map/ppermute | solution.py:423
  24.6 6.6 %all-to-all-done.a8 = f32[8,48,128]{2,1,0:T(8,128)S(1)} async-done(((f32[8,48,128]{2,1,0:T(8,128)}), f32[8,48,128]{2,1,0:T(8,128)S(1)}, u32[]{:S(2)}, u32[]{:S(2)}) %all-to-all-start) | async-done | bytes 196640 | tf_op jit(solution)/shard_map/all_to_all | solution.py:427
  33.2 2.4 %collective-permute-start.4 = (f32[88,128]{1,0:T(8,128)S(1)}, f32[88,128]{1,0:T(8,128)S(1)}, u32[]{:S(2)}, u32[]{:S(2)}) collective-permute-start(f32[88,128]{1,0:T(8,128)S(1)} %get-tuple-element.69), channel_id=1, source_target_pairs={{0,8},{8,16},{16,24},{24,32},{32,40},{40,48},{48,56},{1,9},{9,17},... | collective-permute-start | bytes 135176 | tf_op jit(solution)/shard_map/ppermute | solution.py:443
  35.6 3.0 %collective-permute-done.4.below = f32[88,128]{1,0:T(8,128)S(1)} collective-permute-done((f32[88,128]{1,0:T(8,128)S(1)}, f32[88,128]{1,0:T(8,128)S(1)}, u32[]{:S(2)}, u32[]{:S(2)}) %collective-permute-start.4) | collective-permute-done | bytes 45088 | tf_op jit(solution)/shard_map/ppermute | solution.py:443
  45.9 4.0 %shard_map.76 = (f32[32,48,128]{2,1,0:T(8,128)S(1)}, f32[32,48,128]{2,1,0:T(8,128)S(1)}, f32[32,48,128]{2,1,0:T(8,128)S(1)}, f32[33,48,128]{2,1,0:T(8,128)S(1)},...) custom-call(s32[1]{0:T(128)} %bitcast.l_ref.refs_0_, ...), custom_call_target="tpu_custom_call" | custom-call | tf_op jit(solution)/shard_map/pallas_call | solution.py:454
  57.4 7.4 %all-to-all-start.1 = ((f32[8,40,128]{2,1,0:T(8,128)}), f32[8,40,128]{2,1,0:T(8,128)S(1)}, u32[]{:S(2)}, u32[]{:S(2)}) async-start(f32[8,40,128]{2,1,0:T(8,128)} %copy-done.67), calls=%async_computation.1 | async-start | bytes 327680 | tf_op jit(solution)/shard_map/all_to_all | solution.py:472
  64.8 2.9 %collective-permute-start.6 = (f32[48,128]{1,0:T(8,128)}, f32[48,128]{1,0:T(8,128)S(1)}, u32[]{:S(2)}, u32[]{:S(2)}) collective-permute-start(f32[48,128]{1,0:T(8,128)} %copy-done.68), channel_id=1, source_target_pairs={{0,64},{64,128},{128,192},{1,65},{65,129},{129,193},{2,66},{66,130... | collective-permute-start | bytes 73736 | tf_op jit(solution)/shard_map/ppermute | solution.py:470
  69.0 6.6 %all-to-all-done.1.a8.refs_5_ = f32[8,40,128]{2,1,0:T(8,128)S(1)} async-done(((f32[8,40,128]{2,1,0:T(8,128)}), f32[8,40,128]{2,1,0:T(8,128)S(1)}, u32[]{:S(2)}, u32[]{:S(2)}) %all-to-all-start.1) | async-done | bytes 163872 | tf_op jit(solution)/shard_map/all_to_all | solution.py:472
  81.7 3.2 %shard_map.78 = (f32[32,48,128]{2,1,0:T(8,128)S(1)}, f32[32,48,128]{2,1,0:T(8,128)S(1)}, f32[32,32,128]{2,1,0:T(8,128)S(1)}, f32[48,128]{1,0:T(8,128)S(1)}, f32[...) custom-call(s32[1]{0:T(128)} %bitcast.l_ref.refs_0_, f32[32,48,128]{2,1,0:T(8,128)S(1)} %copy-done.38, ...), custom_call_target="tpu_custom_call" | custom-call | tf_op jit(solution)/shard_map/pallas_call | solution.py:487
  87.6 5.9 %all-to-all-start.2 = ((f32[8,40,128]{2,1,0:T(8,128)}), f32[8,40,128]{2,1,0:T(8,128)S(1)}, u32[]{:S(2)}, u32[]{:S(2)}) async-start(f32[8,40,128]{2,1,0:T(8,128)} %get-tuple-element.90), calls=%async_computation.2 | async-start | bytes 327680 | tf_op jit(solution)/shard_map/all_to_all | solution.py:472
  93.4 2.9 %collective-permute-start.8 = (f32[48,128]{1,0:T(8,128)S(1)}, f32[48,128]{1,0:T(8,128)S(1)}, u32[]{:S(2)}, u32[]{:S(2)}) collective-permute-start(f32[48,128]{1,0:T(8,128)S(1)} %get-tuple-element.88), channel_id=1, source_target_pairs={{0,64},{64,128},{128,192},{1,65},{65,129},{129,193},{2,66},{66,130... | collective-permute-start | bytes 73736 | tf_op jit(solution)/shard_map/ppermute | solution.py:470
  97.6 6.5 %all-to-all-done.2.a8.refs_6_ = f32[8,40,128]{2,1,0:T(8,128)S(1)} async-done(((f32[8,40,128]{2,1,0:T(8,128)}), f32[8,40,128]{2,1,0:T(8,128)S(1)}, u32[]{:S(2)}, u32[]{:S(2)}) %all-to-all-start.2) | async-done | bytes 163872 | tf_op jit(solution)/shard_map/all_to_all | solution.py:472
  111.3 3.3 %shard_map.80 = (f32[32,48,128]{2,1,0:T(8,128)S(1)}, f32[32,48,128]{2,1,0:T(8,128)S(1)}, f32[32,32,128]{2,1,0:T(8,128)S(1)}, f32[48,128]{1,0:T(8,128)S(1)}, f32[...) custom-call(s32[1]{0:T(128)} %bitcast.l_ref.refs_0_, f32[32,48,128]{2,1,0:T(8,128)S(1)} %copy-done.52, ...), custom_call_target="tpu_custom_call" | custom-call | tf_op jit(solution)/shard_map/pallas_call | solution.py:487
  117.2 5.9 %all-to-all-start.3 = ((f32[8,40,128]{2,1,0:T(8,128)}), f32[8,40,128]{2,1,0:T(8,128)S(1)}, u32[]{:S(2)}, u32[]{:S(2)}) async-start(f32[8,40,128]{2,1,0:T(8,128)} %get-tuple-element.96), calls=%async_computation.3 | async-start | bytes 327680 | tf_op jit(solution)/shard_map/all_to_all | solution.py:472
  126.3 7.5 %all-to-all-done.3.a8.refs_6_ = f32[8,40,128]{2,1,0:T(8,128)S(1)} async-done(((f32[8,40,128]{2,1,0:T(8,128)}), f32[8,40,128]{2,1,0:T(8,128)S(1)}, u32[]{:S(2)}, u32[]{:S(2)}) %all-to-all-start.3) | async-done | bytes 163872 | tf_op jit(solution)/shard_map/all_to_all | solution.py:472
  141.0 3.3 %shard_map.82 = (f32[32,48,128]{2,1,0:T(8,128)S(1)}, f32[32,48,128]{2,1,0:T(8,128)S(1)}, f32[32,32,128]{2,1,0:T(8,128)S(1)}, f32[48,128]{1,0:T(8,128)S(1)}, f32[...) custom-call(s32[1]{0:T(128)} %bitcast.l_ref.refs_0_, f32[32,48,128]{2,1,0:T(8,128)S(1)} %copy-done.44, ...), custom_call_target="tpu_custom_call" | custom-call | tf_op jit(solution)/shard_map/pallas_call | solution.py:487
  146.8 5.0 %all-to-all-start.4 = ((f32[8,40,128]{2,1,0:T(8,128)}), f32[8,40,128]{2,1,0:T(8,128)S(1)}, u32[]{:S(2)}, u32[]{:S(2)}) async-start(f32[8,40,128]{2,1,0:T(8,128)} %get-tuple-element.102), calls=%async_computation.4 | async-start | bytes 327680 | tf_op jit(solution)/shard_map/all_to_all | solution.py:472
  155.0 7.5 %all-to-all-done.4.a8.refs_6_ = f32[8,40,128]{2,1,0:T(8,128)S(1)} async-done(((f32[8,40,128]{2,1,0:T(8,128)}), f32[8,40,128]{2,1,0:T(8,128)S(1)}, u32[]{:S(2)}, u32[]{:S(2)}) %all-to-all-start.4) | async-done | bytes 163872 | tf_op jit(solution)/shard_map/all_to_all | solution.py:472
  169.6 3.3 %shard_map.84 = (f32[32,48,128]{2,1,0:T(8,128)S(1)}, f32[32,48,128]{2,1,0:T(8,128)S(1)}, f32[32,32,128]{2,1,0:T(8,128)S(1)}, f32[48,128]{1,0:T(8,128)S(1)}, f32[...) custom-call(s32[1]{0:T(128)} %bitcast.l_ref.refs_0_, f32[32,48,128]{2,1,0:T(8,128)S(1)} %copy-done.48, ...), custom_call_target="tpu_custom_call" | custom-call | tf_op jit(solution)/shard_map/pallas_call | solution.py:487
  175.5 5.0 %all-to-all-start.5 = ((f32[8,40,128]{2,1,0:T(8,128)}), f32[8,40,128]{2,1,0:T(8,128)S(1)}, u32[]{:S(2)}, u32[]{:S(2)}) async-start(f32[8,40,128]{2,1,0:T(8,128)} %get-tuple-element.108), calls=%async_computation.5 | async-start | bytes 327680 | tf_op jit(solution)/shard_map/all_to_all | solution.py:472
  183.7 7.5 %all-to-all-done.5.a8.refs_6_ = f32[8,40,128]{2,1,0:T(8,128)S(1)} async-done(((f32[8,40,128]{2,1,0:T(8,128)}), f32[8,40,128]{2,1,0:T(8,128)S(1)}, u32[]{:S(2)}, u32[]{:S(2)}) %all-to-all-start.5) | async-done | bytes 163872 | tf_op jit(solution)/shard_map/all_to_all | solution.py:472
  (172 shorter events, 79.2 us)
Async XLA Ops:
  0.0 40.3 %copy-start.31 = (f32[32,32,128]{2,1,0:T(8,128)S(1)}, f32[32,32,128]{2,1,0:T(8,128)}, u32[]{:S(2)}) copy-start(f32[32,32,128]{2,1,0:T(8,128)} %rhs.3) | copy-start | bytes 1572868
  3.8 34.8 %collective-permute-start = (f32[5,32,8,128]{3,2,1,0:T(8,128)}, f32[5,32,8,128]{3,2,1,0:T(8,128)S(1)}, u32[]{:S(2)}, u32[]{:S(2)}) collective-permute-start(f32[5,32,8,128]{3,2,1,0:T(8,128)} %get-tuple-element.62), channel_id=1, source_target_pairs={{0,8},{8,16},{16,24},{24,32},{32,40},{40,48},{48,56},{1,9},{9,17},... | collective-permute-start | bytes 1966088 | tf_op jit(solution)/shard_map/ppermute | solution.py:425
  5.7 33.7 %collective-permute-start.1 = (f32[5,32,8,128]{3,2,1,0:T(8,128)}, f32[5,32,8,128]{3,2,1,0:T(8,128)S(1)}, u32[]{:S(2)}, u32[]{:S(2)}) collective-permute-start(f32[5,32,8,128]{3,2,1,0:T(8,128)} %get-tuple-element.63), channel_id=1, source_target_pairs={{8,0},{16,8},{24,16},{32,24},{40,32},{48,40},{56,48},{9,1},{17,9},... | collective-permute-start | bytes 1966088 | tf_op jit(solution)/shard_map/ppermute | solution.py:426
  9.4 21.8 %all-to-all-start = ((f32[8,48,128]{2,1,0:T(8,128)}), f32[8,48,128]{2,1,0:T(8,128)S(1)}, u32[]{:S(2)}, u32[]{:S(2)}) async-start(f32[8,48,128]{2,1,0:T(8,128)} %get-tuple-element.64), calls=%async_computation | async-start | bytes 393216 | tf_op jit(solution)/shard_map/all_to_all | solution.py:427
  20.3 10.9 %collective-permute-start.2 = (f32[32,128]{1,0:T(8,128)}, f32[32,128]{1,0:T(8,128)S(1)}, u32[]{:S(2)}, u32[]{:S(2)}) collective-permute-start(f32[32,128]{1,0:T(8,128)} %get-tuple-element.67), channel_id=1, source_target_pairs={{0,64},{64,128},{128,192},{1,65},{65,129},{129,193},{2,66},{66,130... | collective-permute-start | bytes 49160 | tf_op jit(solution)/shard_map/ppermute | solution.py:423
  23.3 8.0 %collective-permute-start.3 = (f32[32,128]{1,0:T(8,128)}, f32[32,128]{1,0:T(8,128)S(1)}, u32[]{:S(2)}, u32[]{:S(2)}) collective-permute-start(f32[32,128]{1,0:T(8,128)} %get-tuple-element.68), channel_id=1, source_target_pairs={{64,0},{128,64},{192,128},{65,1},{129,65},{193,129},{66,2},{130,66... | collective-permute-start | bytes 49160 | tf_op jit(solution)/shard_map/ppermute | solution.py:424
  31.2 7.4 %copy-start.33 = (f32[8,48,128]{2,1,0:T(8,128)}, f32[8,48,128]{2,1,0:T(8,128)S(1)}, u32[]{:S(2)}) copy-start(f32[8,48,128]{2,1,0:T(8,128)S(1)} %all-to-all-done.a8) | copy-start | bytes 589828
  31.3 7.3 %collective-permute-start.5 = (f32[280,128]{1,0:T(8,128)S(1)}, f32[280,128]{1,0:T(8,128)S(1)}, u32[]{:S(2)}, u32[]{:S(2)}) collective-permute-start(f32[280,128]{1,0:T(8,128)S(1)} %get-tuple-element.70), channel_id=1, source_target_pairs={{8,0},{16,8},{24,16},{32,24},{40,32},{48,40},{56,48},{9,1},{17,9},... | collective-permute-start | bytes 430088 | tf_op jit(solution)/shard_map/ppermute | solution.py:444
  33.2 5.4 %collective-permute-start.4 = (f32[88,128]{1,0:T(8,128)S(1)}, f32[88,128]{1,0:T(8,128)S(1)}, u32[]{:S(2)}, u32[]{:S(2)}) collective-permute-start(f32[88,128]{1,0:T(8,128)S(1)} %get-tuple-element.69), channel_id=1, source_target_pairs={{0,8},{8,16},{16,24},{24,32},{32,40},{40,48},{48,56},{1,9},{9,17},... | collective-permute-start | bytes 135176 | tf_op jit(solution)/shard_map/ppermute | solution.py:443
  57.4 18.2 %all-to-all-start.1 = ((f32[8,40,128]{2,1,0:T(8,128)}), f32[8,40,128]{2,1,0:T(8,128)S(1)}, u32[]{:S(2)}, u32[]{:S(2)}) async-start(f32[8,40,128]{2,1,0:T(8,128)} %copy-done.67), calls=%async_computation.1 | async-start | bytes 327680 | tf_op jit(solution)/shard_map/all_to_all | solution.py:472
  64.8 11.7 %collective-permute-start.6 = (f32[48,128]{1,0:T(8,128)}, f32[48,128]{1,0:T(8,128)S(1)}, u32[]{:S(2)}, u32[]{:S(2)}) collective-permute-start(f32[48,128]{1,0:T(8,128)} %copy-done.68), channel_id=1, source_target_pairs={{0,64},{64,128},{128,192},{1,65},{65,129},{129,193},{2,66},{66,130... | collective-permute-start | bytes 73736 | tf_op jit(solution)/shard_map/ppermute | solution.py:470
  67.7 8.8 %collective-permute-start.7 = (f32[48,128]{1,0:T(8,128)S(1)}, f32[48,128]{1,0:T(8,128)S(1)}, u32[]{:S(2)}, u32[]{:S(2)}) collective-permute-start(f32[48,128]{1,0:T(8,128)S(1)} %get-tuple-element.74), channel_id=1, source_target_pairs={{64,0},{128,64},{192,128},{65,1},{129,65},{193,129},{66,2},{130,66... | collective-permute-start | bytes 73736 | tf_op jit(solution)/shard_map/ppermute | solution.py:471
  87.6 16.6 %all-to-all-start.2 = ((f32[8,40,128]{2,1,0:T(8,128)}), f32[8,40,128]{2,1,0:T(8,128)S(1)}, u32[]{:S(2)}, u32[]{:S(2)}) async-start(f32[8,40,128]{2,1,0:T(8,128)} %get-tuple-element.90), calls=%async_computation.2 | async-start | bytes 327680 | tf_op jit(solution)/shard_map/all_to_all | solution.py:472
  93.4 11.6 %collective-permute-start.8 = (f32[48,128]{1,0:T(8,128)S(1)}, f32[48,128]{1,0:T(8,128)S(1)}, u32[]{:S(2)}, u32[]{:S(2)}) collective-permute-start(f32[48,128]{1,0:T(8,128)S(1)} %get-tuple-element.88), channel_id=1, source_target_pairs={{0,64},{64,128},{128,192},{1,65},{65,129},{129,193},{2,66},{66,130... | collective-permute-start | bytes 73736 | tf_op jit(solution)/shard_map/ppermute | solution.py:470
  96.3 8.7 %collective-permute-start.9 = (f32[48,128]{1,0:T(8,128)S(1)}, f32[48,128]{1,0:T(8,128)S(1)}, u32[]{:S(2)}, u32[]{:S(2)}) collective-permute-start(f32[48,128]{1,0:T(8,128)S(1)} %get-tuple-element.89), channel_id=1, source_target_pairs={{64,0},{128,64},{192,128},{65,1},{129,65},{193,129},{66,2},{130,66... | collective-permute-start | bytes 73736 | tf_op jit(solution)/shard_map/ppermute | solution.py:471
  117.2 16.6 %all-to-all-start.3 = ((f32[8,40,128]{2,1,0:T(8,128)}), f32[8,40,128]{2,1,0:T(8,128)S(1)}, u32[]{:S(2)}, u32[]{:S(2)}) async-start(f32[8,40,128]{2,1,0:T(8,128)} %get-tuple-element.96), calls=%async_computation.3 | async-start | bytes 327680 | tf_op jit(solution)/shard_map/all_to_all | solution.py:472
  123.1 11.6 %collective-permute-start.10 = (f32[48,128]{1,0:T(8,128)S(1)}, f32[48,128]{1,0:T(8,128)S(1)}, u32[]{:S(2)}, u32[]{:S(2)}) collective-permute-start(f32[48,128]{1,0:T(8,128)S(1)} %get-tuple-element.94), channel_id=1, source_target_pairs={{0,64},{64,128},{128,192},{1,65},{65,129},{129,193},{2,66},{66,130... | collective-permute-start | bytes 73736 | tf_op jit(solution)/shard_map/ppermute | solution.py:470
  125.0 9.7 %collective-permute-start.11 = (f32[48,128]{1,0:T(8,128)S(1)}, f32[48,128]{1,0:T(8,128)S(1)}, u32[]{:S(2)}, u32[]{:S(2)}) collective-permute-start(f32[48,128]{1,0:T(8,128)S(1)} %get-tuple-element.95), channel_id=1, source_target_pairs={{64,0},{128,64},{192,128},{65,1},{129,65},{193,129},{66,2},{130,66... | collective-permute-start | bytes 73736 | tf_op jit(solution)/shard_map/ppermute | solution.py:471
  146.8 15.7 %all-to-all-start.4 = ((f32[8,40,128]{2,1,0:T(8,128)}), f32[8,40,128]{2,1,0:T(8,128)S(1)}, u32[]{:S(2)}, u32[]{:S(2)}) async-start(f32[8,40,128]{2,1,0:T(8,128)} %get-tuple-element.102), calls=%async_computation.4 | async-start | bytes 327680 | tf_op jit(solution)/shard_map/all_to_all | solution.py:472
  151.8 11.6 %collective-permute-start.12 = (f32[48,128]{1,0:T(8,128)S(1)}, f32[48,128]{1,0:T(8,128)S(1)}, u32[]{:S(2)}, u32[]{:S(2)}) collective-permute-start(f32[48,128]{1,0:T(8,128)S(1)} %get-tuple-element.100), channel_id=1, source_target_pairs={{0,64},{64,128},{128,192},{1,65},{65,129},{129,193},{2,66},{66,130... | collective-permute-start | bytes 73736 | tf_op jit(solution)/shard_map/ppermute | solution.py:470
  153.7 9.7 %collective-permute-start.13 = (f32[48,128]{1,0:T(8,128)S(1)}, f32[48,128]{1,0:T(8,128)S(1)}, u32[]{:S(2)}, u32[]{:S(2)}) collective-permute-start(f32[48,128]{1,0:T(8,128)S(1)} %get-tuple-element.101), channel_id=1, source_target_pairs={{64,0},{128,64},{192,128},{65,1},{129,65},{193,129},{66,2},{130,66... | collective-permute-start | bytes 73736 | tf_op jit(solution)/shard_map/ppermute | solution.py:471
  175.5 15.7 %all-to-all-start.5 = ((f32[8,40,128]{2,1,0:T(8,128)}), f32[8,40,128]{2,1,0:T(8,128)S(1)}, u32[]{:S(2)}, u32[]{:S(2)}) async-start(f32[8,40,128]{2,1,0:T(8,128)} %get-tuple-element.108), calls=%async_computation.5 | async-start | bytes 327680 | tf_op jit(solution)/shard_map/all_to_all | solution.py:472
  180.5 11.6 %collective-permute-start.14 = (f32[48,128]{1,0:T(8,128)S(1)}, f32[48,128]{1,0:T(8,128)S(1)}, u32[]{:S(2)}, u32[]{:S(2)}) collective-permute-start(f32[48,128]{1,0:T(8,128)S(1)} %get-tuple-element.106), channel_id=1, source_target_pairs={{0,64},{64,128},{128,192},{1,65},{65,129},{129,193},{2,66},{66,130... | collective-permute-start | bytes 73736 | tf_op jit(solution)/shard_map/ppermute | solution.py:470
  182.4 9.7 %collective-permute-start.15 = (f32[48,128]{1,0:T(8,128)S(1)}, f32[48,128]{1,0:T(8,128)S(1)}, u32[]{:S(2)}, u32[]{:S(2)}) collective-permute-start(f32[48,128]{1,0:T(8,128)S(1)} %get-tuple-element.107), channel_id=1, source_target_pairs={{64,0},{128,64},{192,128},{65,1},{129,65},{193,129},{66,2},{130,66... | collective-permute-start | bytes 73736 | tf_op jit(solution)/shard_map/ppermute | solution.py:471
  (67 other events, 72.5 us)

commit v6 on v5

--- a/solution.py
+++ b/solution.py
@@ -81,7 +81,8 @@
     return row_ref[q, which : which + 1, :]
 
 
-FACE_ROWS = 24
+FACE_ROWS = 16
+BOTH_ROWS = 24
 
 
 def pack_faces(faces, tiles, x):
@@ -105,18 +106,26 @@
     return [slab[8 * n : 8 * (n + 1)] for n in range(slab.shape[0] // 8)]
 
 
-def put_faces(ref, faces):
-    packed = jnp.concatenate(faces, axis=0)
+def put_faces(l, ref, faces):
+    odd = (lane_iota((8, 128)) & 1) == 1
+    first, second, third = faces
+    above = jnp.where(odd, first, pltpu.roll(second, 127, 1))
+    below = jnp.where(odd, pltpu.roll(second, 1, 1), first)
     for t in range(ref.shape[0]):
-        ref[t, 0:FACE_ROWS, :] = packed
+        ref[t, 0:8, :] = jnp.where(t > l, above, below)
+        ref[t, 8:16, :] = third
 
 
 def get_faces(l, ref):
     tiles = ref.shape[0]
-    low = jnp.where(l > 0, ref[jnp.maximum(l - 1, 0), 0:FACE_ROWS, :], 0.0)
-    high = jnp.where(l < tiles - 1, ref[jnp.minimum(l + 1, tiles - 1), 0:FACE_ROWS, :], 0.0)
-    odd = (lane_iota(low.shape) & 1) == 1
-    return jnp.where(odd, low, pltpu.roll(high, 126, 1))
+    low = jnp.where(l > 0, ref[jnp.maximum(l - 1, 0), 0:16, :], 0.0)
+    high = jnp.where(l < tiles - 1, ref[jnp.minimum(l + 1, tiles - 1), 0:16, :], 0.0)
+    odd = (lane_iota((8, 128)) & 1) == 1
+    high = pltpu.roll(high, 126, 1)
+    first = jnp.where(odd, low[0:8], high[0:8])
+    second = jnp.where(odd, pltpu.roll(low[0:8], 1, 1), pltpu.roll(high[0:8], 127, 1))
+    third = jnp.where(odd, low[8:16], high[8:16])
+    return jnp.concatenate([first, second, third], axis=0)
 
 
 def unpacked(faces, slab, x):
@@ -130,7 +139,7 @@
     return jnp.concatenate(lows, axis=0), jnp.concatenate(highs, axis=0)
 
 
-def pack_kernel(rhs, acc, perm, cell, remote, mask, trans,
+def pack_kernel(l_ref, rhs, acc, perm, cell, remote, mask, trans,
                 top, bottom, a8, kx_first, kx_last, kz, sem):
     tiles = a8.shape[0]
     cx, cy = rhs.shape[0], rhs.shape[1]
@@ -164,7 +173,7 @@
     def body(x, faces):
         return pack_faces(faces, [None] + y_tiles(kz[x]) + [None], x)
 
-    put_faces(a8, lax.fori_loop(0, cx, body, no_faces(), unroll=4))
+    put_faces(l_ref[0], a8, lax.fori_loop(0, cx, body, no_faces(), unroll=4))
     for move in moves[1:]:
         move.wait()
 
@@ -179,7 +188,7 @@
 
 def join_kernel(faces, lists, kx_low, kx_high, up, down):
     cy = kx_low.shape[0]
-    base = FACE_ROWS
+    base = BOTH_ROWS
     for out in (up, down):
         out[0:base, :] = faces[...]
         out[base : base + cy, :] = kx_low[...]
@@ -187,11 +196,11 @@
     down[base + 2 * cy :, :] = lists[...]
 
 
-def emit(a8_ref, planes, faces, row_ref, pick_ref, far_x):
+def emit(l_ref, a8_ref, planes, faces, row_ref, pick_ref, far_x):
     tiles = a8_ref.shape[0]
     cx = planes.shape[1]
     slots = row_ref.shape[2]
-    put_faces(a8_ref, faces)
+    put_faces(l_ref[0], a8_ref, faces)
     for q in range(2):
         base = FACE_ROWS + q * 2 * SLOT_ROWS
         near = gather(
@@ -296,7 +305,7 @@
     )
 
     def ext_face(n, own):
-        at = FACE_ROWS + n * cy
+        at = BOTH_ROWS + n * cy
         return jnp.concatenate([below[at + cy - H : at + cy, :], own[...], above[at : at + H, :]], axis=0)
 
     kx_under, kx_over = ext_face(0, kx_low), ext_face(1, kx_high)
@@ -339,7 +348,7 @@
     faces, _, _ = lax.fori_loop(0, cx, body, init, unroll=4)
     d_first[...] = d_out[0]
     d_last[...] = d_out[cx - 1]
-    emit(a8_out, planes, faces, row_ref, pick_ref, far_x)
+    emit(l_ref, a8_out, planes, faces, row_ref, pick_ref, far_x)
 
 
 def sweep_kernel(c1, c2, first, last, l_ref, d_in, z_in, *refs):
@@ -360,10 +369,11 @@
     faces_in = get_faces(l_ref[0], a8)
 
     def body(x, carry):
-        faces, d_prev, d = carry
+        faces, d_prev, d, t_low = carry
+        t_high = tx[x + 1]
         d_next = jnp.where(x == cx - 1, xhigh[...], d_in[jnp.minimum(x + 1, cx - 1)])
         z_low, z_high = unpacked(faces_in, d, x)
-        flow = tx[x] * d_prev + tx[x + 1] * d_next
+        flow = t_low * d_prev + t_high * d_next
         flow = flow + (tym[x] * pltpu.roll(d, 1, 0) + typ[x] * pltpu.roll(d, ye - 1, 0))
         flow = flow + (tzm[x] * z_low + tzp[x] * z_high)
         flow = with_fault(flow, fault, x)
@@ -372,18 +382,18 @@
         before = d[H : H + cy] if first else corr_in[x]
         corr_out[x] = before + new[H : H + cy]
         if last:
-            return faces, d, d_next
+            return faces, d, d_next, t_high
         d_out[x] = new
         z_out[x] = z
         keep_planes(planes, new, x)
-        return pack_faces(faces, y_tiles(new), x), d, d_next
-
-    init = (no_faces(), xlow[...], d_in[0])
-    faces, _, _ = lax.fori_loop(0, cx, body, init, unroll=4)
+        return pack_faces(faces, y_tiles(new), x), d, d_next, t_high
+
+    init = (no_faces(), xlow[...], d_in[0], tx[0])
+    faces, _, _, _ = lax.fori_loop(0, cx, body, init, unroll=4)
     if not last:
         d_first[...] = d_out[0]
         d_last[...] = d_out[cx - 1]
-        emit(a8_out, planes, faces, row_ref, pick_ref, far_x)
+        emit(l_ref, a8_out, planes, faces, row_ref, pick_ref, far_x)
 
 
 VMEM = pl.BlockSpec(memory_space=pltpu.VMEM)
@@ -416,10 +426,10 @@
     top, bottom, a8, kx_first, kx_last = pl.pallas_call(
         pack_kernel,
         out_shape=(halo, halo, struct(tiles, FACE_ROWS + LIST_ROWS, cz), struct(cy, cz), struct(cy, cz)),
-        in_specs=[HBM] * 3 + [VMEM] * 4,
+        in_specs=[SMEM] + [HBM] * 3 + [VMEM] * 4,
         out_specs=(VMEM,) * 5,
         scratch_shapes=[pltpu.VMEM((cx, cy, cz), f32), pltpu.SemaphoreType.DMA((13,))],
-    )(rhs, accumulation, permeability, *flats)
+    )(l, rhs, accumulation, permeability, *flats)
     kx_low = lax.ppermute(kx_last, "gx", up_x)
     kx_high = lax.ppermute(kx_first, "gx", down_x)
     before = lax.ppermute(top, "gy", up_y)
@@ -427,12 +437,12 @@
     a8 = lax.all_to_all(a8, "gz", 0, 0, tiled=True)
     faces, group = pl.pallas_call(
         relay_kernel,
-        out_shape=(struct(FACE_ROWS, cz), struct(tiles * LIST_ROWS, cz)),
+        out_shape=(struct(BOTH_ROWS, cz), struct(tiles * LIST_ROWS, cz)),
         in_specs=[SMEM, VMEM],
         out_specs=(VMEM,) * 2,
         compiler_params=PARAMS,
     )(l, a8)
-    small = FACE_ROWS + 2 * cy
+    small = BOTH_ROWS + 2 * cy
     below, above = pl.pallas_call(
         join_kernel,
         out_shape=(struct(small, cz), struct(small + tiles * LIST_ROWS, cz)),

time: 203 us -> 203 us (level)
  no operation moved by 1% of the time
where the time goes in v6:
time: 203 us; the launch traced here: 200 us
  starting transfers between devices  73.1 us (36%)
  local copies, waits for them, and re-layouts  55.5 us (27%)
  waiting for transfers between devices  44.1 us (22%)
  Pallas kernels  27.4 us (13%)
    unnamed x138, local copies, waits for them, and re-layouts  55.5 us
    all_to_all x6, waiting for transfers between devices, local(): a8 = lax.all_to_all(a8, 'gz', 0, 0, tiled=True)  41 us
    all_to_all x6, starting transfers between devices, local(): a8 = lax.all_to_all(a8, 'gz', 0, 0, tiled=True)  41 us
    pallas_call x5, Pallas kernels, local(): pl.pallas_call(kernel, out_shape=small if last else (big, big, small, edg...  15.2 us
    ppermute x5, starting transfers between devices, local(): xlow = lax.ppermute(d_last, 'gx', up_x)  11.6 us
    ppermute x5, starting transfers between devices, local(): xhigh = lax.ppermute(d_first, 'gx', down_x)  6.46 us
    pallas_call x5, Pallas kernels, local(): pl.pallas_call(fault_kernel, out_shape=struct(4, cx, cz), in_specs=[VMEM]...  4.25 us
  transfers between devices with their start and end apart: 22, of which 7 were waited for; matrix products, arithmetic and copies ran while one was open for 0% of the time, Pallas kernels for 2%

profile of v6, /device:TPU:8, one launch (start us, length us, event | category | flops | bytes accessed | tf_op | source)
XLA Modules:
  0.0 200.4 jit_solution(10208683143638923144)
XLA Ops:
  0.0 3.9 %shard_map.73 = (f32[5,32,8,128]{3,2,1,0:T(8,128)}, f32[5,32,8,128]{3,2,1,0:T(8,128)}, f32[8,40,128]{2,1,0:T(8,128)}, f32[32,128]{1,0:T(8,128)}, f32[32,128]{1,0:T(8,128)}) custom-call(s32[1]{0:T(128)} %bitcast.l_ref.refs_0_, f32[32,32,128]{2,1,0:T(8,128)} %rhs.3, f32[32,32,128]{2,1,0:T(8,128)} %acc.3, f32[3,32,32,128]{3,2,1,0:T(8,128)} %perm.3, ...), custom_call_target="tpu_custom_call" | custom-call | tf_op jit(solution)/shard_map/pallas_call | solution.py:426
  5.8 3.6 %collective-permute-start.1 = (f32[5,32,8,128]{3,2,1,0:T(8,128)}, f32[5,32,8,128]{3,2,1,0:T(8,128)S(1)}, u32[]{:S(2)}, u32[]{:S(2)}) collective-permute-start(f32[5,32,8,128]{3,2,1,0:T(8,128)} %get-tuple-element.63), channel_id=1, source_target_pairs={{8,0},{16,8},{24,16},{32,24},{40,32},{48,40},{56,48},{9,1},{17,9},... | collective-permute-start | bytes 1966088 | tf_op jit(solution)/shard_map/ppermute | solution.py:436
  9.5 10.9 %all-to-all-start = ((f32[8,40,128]{2,1,0:T(8,128)}), f32[8,40,128]{2,1,0:T(8,128)S(1)}, u32[]{:S(2)}, u32[]{:S(2)}) async-start(f32[8,40,128]{2,1,0:T(8,128)} %get-tuple-element.64), calls=%async_computation | async-start | bytes 327680 | tf_op jit(solution)/shard_map/all_to_all | solution.py:437
  20.4 2.9 %collective-permute-start.2 = (f32[32,128]{1,0:T(8,128)}, f32[32,128]{1,0:T(8,128)S(1)}, u32[]{:S(2)}, u32[]{:S(2)}) collective-permute-start(f32[32,128]{1,0:T(8,128)} %get-tuple-element.67), channel_id=1, source_target_pairs={{0,64},{64,128},{128,192},{1,65},{65,129},{129,193},{2,66},{66,130... | collective-permute-start | bytes 49160 | tf_op jit(solution)/shard_map/ppermute | solution.py:433
  24.6 6.4 %all-to-all-done.a8 = f32[8,40,128]{2,1,0:T(8,128)S(1)} async-done(((f32[8,40,128]{2,1,0:T(8,128)}), f32[8,40,128]{2,1,0:T(8,128)S(1)}, u32[]{:S(2)}, u32[]{:S(2)}) %all-to-all-start) | async-done | bytes 163872 | tf_op jit(solution)/shard_map/all_to_all | solution.py:437
  33.2 2.4 %collective-permute-start.4 = (f32[88,128]{1,0:T(8,128)S(1)}, f32[88,128]{1,0:T(8,128)S(1)}, u32[]{:S(2)}, u32[]{:S(2)}) collective-permute-start(f32[88,128]{1,0:T(8,128)S(1)} %get-tuple-element.69), channel_id=1, source_target_pairs={{0,8},{8,16},{16,24},{24,32},{32,40},{40,48},{48,56},{1,9},{9,17},... | collective-permute-start | bytes 135176 | tf_op jit(solution)/shard_map/ppermute | solution.py:453
  35.6 3.0 %collective-permute-done.4.below = f32[88,128]{1,0:T(8,128)S(1)} collective-permute-done((f32[88,128]{1,0:T(8,128)S(1)}, f32[88,128]{1,0:T(8,128)S(1)}, u32[]{:S(2)}, u32[]{:S(2)}) %collective-permute-start.4) | collective-permute-done | bytes 45088 | tf_op jit(solution)/shard_map/ppermute | solution.py:453
  45.8 3.9 %shard_map.76 = (f32[32,48,128]{2,1,0:T(8,128)S(1)}, f32[32,48,128]{2,1,0:T(8,128)S(1)}, f32[32,48,128]{2,1,0:T(8,128)S(1)}, f32[33,48,128]{2,1,0:T(8,128)S(1)},...) custom-call(s32[1]{0:T(128)} %bitcast.l_ref.refs_0_, ...), custom_call_target="tpu_custom_call" | custom-call | tf_op jit(solution)/shard_map/pallas_call | solution.py:464
  57.3 7.6 %all-to-all-start.1 = ((f32[8,32,128]{2,1,0:T(8,128)}), f32[8,32,128]{2,1,0:T(8,128)S(1)}, u32[]{:S(2)}, u32[]{:S(2)}) async-start(f32[8,32,128]{2,1,0:T(8,128)} %copy-done.67), calls=%async_computation.1 | async-start | bytes 262144 | tf_op jit(solution)/shard_map/all_to_all | solution.py:482
  64.8 2.9 %collective-permute-start.6 = (f32[48,128]{1,0:T(8,128)}, f32[48,128]{1,0:T(8,128)S(1)}, u32[]{:S(2)}, u32[]{:S(2)}) collective-permute-start(f32[48,128]{1,0:T(8,128)} %copy-done.68), channel_id=1, source_target_pairs={{0,64},{64,128},{128,192},{1,65},{65,129},{129,193},{2,66},{66,130... | collective-permute-start | bytes 73736 | tf_op jit(solution)/shard_map/ppermute | solution.py:480
  69.1 6.4 %all-to-all-done.1.a8.refs_5_ = f32[8,32,128]{2,1,0:T(8,128)S(1)} async-done(((f32[8,32,128]{2,1,0:T(8,128)}), f32[8,32,128]{2,1,0:T(8,128)S(1)}, u32[]{:S(2)}, u32[]{:S(2)}) %all-to-all-start.1) | async-done | bytes 131104 | tf_op jit(solution)/shard_map/all_to_all | solution.py:482
  81.6 3.3 %shard_map.78 = (f32[32,48,128]{2,1,0:T(8,128)S(1)}, f32[32,48,128]{2,1,0:T(8,128)S(1)}, f32[32,32,128]{2,1,0:T(8,128)S(1)}, f32[48,128]{1,0:T(8,128)S(1)}, f32[...) custom-call(s32[1]{0:T(128)} %bitcast.l_ref.refs_0_, f32[32,48,128]{2,1,0:T(8,128)S(1)} %copy-done.38, ...), custom_call_target="tpu_custom_call" | custom-call | tf_op jit(solution)/shard_map/pallas_call | solution.py:497
  87.4 6.1 %all-to-all-start.2 = ((f32[8,32,128]{2,1,0:T(8,128)}), f32[8,32,128]{2,1,0:T(8,128)S(1)}, u32[]{:S(2)}, u32[]{:S(2)}) async-start(f32[8,32,128]{2,1,0:T(8,128)} %get-tuple-element.90), calls=%async_computation.2 | async-start | bytes 262144 | tf_op jit(solution)/shard_map/all_to_all | solution.py:482
  93.5 2.9 %collective-permute-start.8 = (f32[48,128]{1,0:T(8,128)S(1)}, f32[48,128]{1,0:T(8,128)S(1)}, u32[]{:S(2)}, u32[]{:S(2)}) collective-permute-start(f32[48,128]{1,0:T(8,128)S(1)} %get-tuple-element.88), channel_id=1, source_target_pairs={{0,64},{64,128},{128,192},{1,65},{65,129},{129,193},{2,66},{66,130... | collective-permute-start | bytes 73736 | tf_op jit(solution)/shard_map/ppermute | solution.py:480
  97.7 6.3 %all-to-all-done.2.a8.refs_6_ = f32[8,32,128]{2,1,0:T(8,128)S(1)} async-done(((f32[8,32,128]{2,1,0:T(8,128)}), f32[8,32,128]{2,1,0:T(8,128)S(1)}, u32[]{:S(2)}, u32[]{:S(2)}) %all-to-all-start.2) | async-done | bytes 131104 | tf_op jit(solution)/shard_map/all_to_all | solution.py:482
  111.2 3.3 %shard_map.80 = (f32[32,48,128]{2,1,0:T(8,128)S(1)}, f32[32,48,128]{2,1,0:T(8,128)S(1)}, f32[32,32,128]{2,1,0:T(8,128)S(1)}, f32[48,128]{1,0:T(8,128)S(1)}, f32[...) custom-call(s32[1]{0:T(128)} %bitcast.l_ref.refs_0_, f32[32,48,128]{2,1,0:T(8,128)S(1)} %copy-done.52, ...), custom_call_target="tpu_custom_call" | custom-call | tf_op jit(solution)/shard_map/pallas_call | solution.py:497
  117.1 6.1 %all-to-all-start.3 = ((f32[8,32,128]{2,1,0:T(8,128)}), f32[8,32,128]{2,1,0:T(8,128)S(1)}, u32[]{:S(2)}, u32[]{:S(2)}) async-start(f32[8,32,128]{2,1,0:T(8,128)} %get-tuple-element.96), calls=%async_computation.3 | async-start | bytes 262144 | tf_op jit(solution)/shard_map/all_to_all | solution.py:482
  126.4 7.3 %all-to-all-done.3.a8.refs_6_ = f32[8,32,128]{2,1,0:T(8,128)S(1)} async-done(((f32[8,32,128]{2,1,0:T(8,128)}), f32[8,32,128]{2,1,0:T(8,128)S(1)}, u32[]{:S(2)}, u32[]{:S(2)}) %all-to-all-start.3) | async-done | bytes 131104 | tf_op jit(solution)/shard_map/all_to_all | solution.py:482
  140.9 3.3 %shard_map.82 = (f32[32,48,128]{2,1,0:T(8,128)S(1)}, f32[32,48,128]{2,1,0:T(8,128)S(1)}, f32[32,32,128]{2,1,0:T(8,128)S(1)}, f32[48,128]{1,0:T(8,128)S(1)}, f32[...) custom-call(s32[1]{0:T(128)} %bitcast.l_ref.refs_0_, f32[32,48,128]{2,1,0:T(8,128)S(1)} %copy-done.44, ...), custom_call_target="tpu_custom_call" | custom-call | tf_op jit(solution)/shard_map/pallas_call | solution.py:497
  146.8 5.1 %all-to-all-start.4 = ((f32[8,32,128]{2,1,0:T(8,128)}), f32[8,32,128]{2,1,0:T(8,128)S(1)}, u32[]{:S(2)}, u32[]{:S(2)}) async-start(f32[8,32,128]{2,1,0:T(8,128)} %get-tuple-element.102), calls=%async_computation.4 | async-start | bytes 262144 | tf_op jit(solution)/shard_map/all_to_all | solution.py:482
  155.2 7.3 %all-to-all-done.4.a8.refs_6_ = f32[8,32,128]{2,1,0:T(8,128)S(1)} async-done(((f32[8,32,128]{2,1,0:T(8,128)}), f32[8,32,128]{2,1,0:T(8,128)S(1)}, u32[]{:S(2)}, u32[]{:S(2)}) %all-to-all-start.4) | async-done | bytes 131104 | tf_op jit(solution)/shard_map/all_to_all | solution.py:482
  169.7 3.3 %shard_map.84 = (f32[32,48,128]{2,1,0:T(8,128)S(1)}, f32[32,48,128]{2,1,0:T(8,128)S(1)}, f32[32,32,128]{2,1,0:T(8,128)S(1)}, f32[48,128]{1,0:T(8,128)S(1)}, f32[...) custom-call(s32[1]{0:T(128)} %bitcast.l_ref.refs_0_, f32[32,48,128]{2,1,0:T(8,128)S(1)} %copy-done.48, ...), custom_call_target="tpu_custom_call" | custom-call | tf_op jit(solution)/shard_map/pallas_call | solution.py:497
  175.5 5.1 %all-to-all-start.5 = ((f32[8,32,128]{2,1,0:T(8,128)}), f32[8,32,128]{2,1,0:T(8,128)S(1)}, u32[]{:S(2)}, u32[]{:S(2)}) async-start(f32[8,32,128]{2,1,0:T(8,128)} %get-tuple-element.108), calls=%async_computation.5 | async-start | bytes 262144 | tf_op jit(solution)/shard_map/all_to_all | solution.py:482
  183.9 7.3 %all-to-all-done.5.a8.refs_6_ = f32[8,32,128]{2,1,0:T(8,128)S(1)} async-done(((f32[8,32,128]{2,1,0:T(8,128)}), f32[8,32,128]{2,1,0:T(8,128)S(1)}, u32[]{:S(2)}, u32[]{:S(2)}) %all-to-all-start.5) | async-done | bytes 131104 | tf_op jit(solution)/shard_map/all_to_all | solution.py:482
  (172 shorter events, 79.3 us)
Async XLA Ops:
  0.0 40.2 %copy-start.31 = (f32[32,32,128]{2,1,0:T(8,128)S(1)}, f32[32,32,128]{2,1,0:T(8,128)}, u32[]{:S(2)}) copy-start(f32[32,32,128]{2,1,0:T(8,128)} %rhs.3) | copy-start | bytes 1572868
  3.9 34.7 %collective-permute-start = (f32[5,32,8,128]{3,2,1,0:T(8,128)}, f32[5,32,8,128]{3,2,1,0:T(8,128)S(1)}, u32[]{:S(2)}, u32[]{:S(2)}) collective-permute-start(f32[5,32,8,128]{3,2,1,0:T(8,128)} %get-tuple-element.62), channel_id=1, source_target_pairs={{0,8},{8,16},{16,24},{24,32},{32,40},{40,48},{48,56},{1,9},{9,17},... | collective-permute-start | bytes 1966088 | tf_op jit(solution)/shard_map/ppermute | solution.py:435
  5.8 33.6 %collective-permute-start.1 = (f32[5,32,8,128]{3,2,1,0:T(8,128)}, f32[5,32,8,128]{3,2,1,0:T(8,128)S(1)}, u32[]{:S(2)}, u32[]{:S(2)}) collective-permute-start(f32[5,32,8,128]{3,2,1,0:T(8,128)} %get-tuple-element.63), channel_id=1, source_target_pairs={{8,0},{16,8},{24,16},{32,24},{40,32},{48,40},{56,48},{9,1},{17,9},... | collective-permute-start | bytes 1966088 | tf_op jit(solution)/shard_map/ppermute | solution.py:436
  9.5 21.6 %all-to-all-start = ((f32[8,40,128]{2,1,0:T(8,128)}), f32[8,40,128]{2,1,0:T(8,128)S(1)}, u32[]{:S(2)}, u32[]{:S(2)}) async-start(f32[8,40,128]{2,1,0:T(8,128)} %get-tuple-element.64), calls=%async_computation | async-start | bytes 327680 | tf_op jit(solution)/shard_map/all_to_all | solution.py:437
  20.4 10.8 %collective-permute-start.2 = (f32[32,128]{1,0:T(8,128)}, f32[32,128]{1,0:T(8,128)S(1)}, u32[]{:S(2)}, u32[]{:S(2)}) collective-permute-start(f32[32,128]{1,0:T(8,128)} %get-tuple-element.67), channel_id=1, source_target_pairs={{0,64},{64,128},{128,192},{1,65},{65,129},{129,193},{2,66},{66,130... | collective-permute-start | bytes 49160 | tf_op jit(solution)/shard_map/ppermute | solution.py:433
  23.3 7.9 %collective-permute-start.3 = (f32[32,128]{1,0:T(8,128)}, f32[32,128]{1,0:T(8,128)S(1)}, u32[]{:S(2)}, u32[]{:S(2)}) collective-permute-start(f32[32,128]{1,0:T(8,128)} %get-tuple-element.68), channel_id=1, source_target_pairs={{64,0},{128,64},{192,128},{65,1},{129,65},{193,129},{66,2},{130,66... | collective-permute-start | bytes 49160 | tf_op jit(solution)/shard_map/ppermute | solution.py:434
  31.1 7.5 %copy-start.33 = (f32[8,40,128]{2,1,0:T(8,128)}, f32[8,40,128]{2,1,0:T(8,128)S(1)}, u32[]{:S(2)}) copy-start(f32[8,40,128]{2,1,0:T(8,128)S(1)} %all-to-all-done.a8) | copy-start | bytes 491524
  31.2 7.3 %collective-permute-start.5 = (f32[280,128]{1,0:T(8,128)S(1)}, f32[280,128]{1,0:T(8,128)S(1)}, u32[]{:S(2)}, u32[]{:S(2)}) collective-permute-start(f32[280,128]{1,0:T(8,128)S(1)} %get-tuple-element.70), channel_id=1, source_target_pairs={{8,0},{16,8},{24,16},{32,24},{40,32},{48,40},{56,48},{9,1},{17,9},... | collective-permute-start | bytes 430088 | tf_op jit(solution)/shard_map/ppermute | solution.py:454
  33.2 5.4 %collective-permute-start.4 = (f32[88,128]{1,0:T(8,128)S(1)}, f32[88,128]{1,0:T(8,128)S(1)}, u32[]{:S(2)}, u32[]{:S(2)}) collective-permute-start(f32[88,128]{1,0:T(8,128)S(1)} %get-tuple-element.69), channel_id=1, source_target_pairs={{0,8},{8,16},{16,24},{24,32},{32,40},{40,48},{48,56},{1,9},{9,17},... | collective-permute-start | bytes 135176 | tf_op jit(solution)/shard_map/ppermute | solution.py:453
  57.3 18.1 %all-to-all-start.1 = ((f32[8,32,128]{2,1,0:T(8,128)}), f32[8,32,128]{2,1,0:T(8,128)S(1)}, u32[]{:S(2)}, u32[]{:S(2)}) async-start(f32[8,32,128]{2,1,0:T(8,128)} %copy-done.67), calls=%async_computation.1 | async-start | bytes 262144 | tf_op jit(solution)/shard_map/all_to_all | solution.py:482
  64.8 11.5 %collective-permute-start.6 = (f32[48,128]{1,0:T(8,128)}, f32[48,128]{1,0:T(8,128)S(1)}, u32[]{:S(2)}, u32[]{:S(2)}) collective-permute-start(f32[48,128]{1,0:T(8,128)} %copy-done.68), channel_id=1, source_target_pairs={{0,64},{64,128},{128,192},{1,65},{65,129},{129,193},{2,66},{66,130... | collective-permute-start | bytes 73736 | tf_op jit(solution)/shard_map/ppermute | solution.py:480
  67.8 8.5 %collective-permute-start.7 = (f32[48,128]{1,0:T(8,128)S(1)}, f32[48,128]{1,0:T(8,128)S(1)}, u32[]{:S(2)}, u32[]{:S(2)}) collective-permute-start(f32[48,128]{1,0:T(8,128)S(1)} %get-tuple-element.74), channel_id=1, source_target_pairs={{64,0},{128,64},{192,128},{65,1},{129,65},{193,129},{66,2},{130,66... | collective-permute-start | bytes 73736 | tf_op jit(solution)/shard_map/ppermute | solution.py:481
  87.4 16.6 %all-to-all-start.2 = ((f32[8,32,128]{2,1,0:T(8,128)}), f32[8,32,128]{2,1,0:T(8,128)S(1)}, u32[]{:S(2)}, u32[]{:S(2)}) async-start(f32[8,32,128]{2,1,0:T(8,128)} %get-tuple-element.90), calls=%async_computation.2 | async-start | bytes 262144 | tf_op jit(solution)/shard_map/all_to_all | solution.py:482
  93.5 11.4 %collective-permute-start.8 = (f32[48,128]{1,0:T(8,128)S(1)}, f32[48,128]{1,0:T(8,128)S(1)}, u32[]{:S(2)}, u32[]{:S(2)}) collective-permute-start(f32[48,128]{1,0:T(8,128)S(1)} %get-tuple-element.88), channel_id=1, source_target_pairs={{0,64},{64,128},{128,192},{1,65},{65,129},{129,193},{2,66},{66,130... | collective-permute-start | bytes 73736 | tf_op jit(solution)/shard_map/ppermute | solution.py:480
  96.4 8.5 %collective-permute-start.9 = (f32[48,128]{1,0:T(8,128)S(1)}, f32[48,128]{1,0:T(8,128)S(1)}, u32[]{:S(2)}, u32[]{:S(2)}) collective-permute-start(f32[48,128]{1,0:T(8,128)S(1)} %get-tuple-element.89), channel_id=1, source_target_pairs={{64,0},{128,64},{192,128},{65,1},{129,65},{193,129},{66,2},{130,66... | collective-permute-start | bytes 73736 | tf_op jit(solution)/shard_map/ppermute | solution.py:481
  117.1 16.6 %all-to-all-start.3 = ((f32[8,32,128]{2,1,0:T(8,128)}), f32[8,32,128]{2,1,0:T(8,128)S(1)}, u32[]{:S(2)}, u32[]{:S(2)}) async-start(f32[8,32,128]{2,1,0:T(8,128)} %get-tuple-element.96), calls=%async_computation.3 | async-start | bytes 262144 | tf_op jit(solution)/shard_map/all_to_all | solution.py:482
  123.2 11.4 %collective-permute-start.10 = (f32[48,128]{1,0:T(8,128)S(1)}, f32[48,128]{1,0:T(8,128)S(1)}, u32[]{:S(2)}, u32[]{:S(2)}) collective-permute-start(f32[48,128]{1,0:T(8,128)S(1)} %get-tuple-element.94), channel_id=1, source_target_pairs={{0,64},{64,128},{128,192},{1,65},{65,129},{129,193},{2,66},{66,130... | collective-permute-start | bytes 73736 | tf_op jit(solution)/shard_map/ppermute | solution.py:480
  125.1 9.5 %collective-permute-start.11 = (f32[48,128]{1,0:T(8,128)S(1)}, f32[48,128]{1,0:T(8,128)S(1)}, u32[]{:S(2)}, u32[]{:S(2)}) collective-permute-start(f32[48,128]{1,0:T(8,128)S(1)} %get-tuple-element.95), channel_id=1, source_target_pairs={{64,0},{128,64},{192,128},{65,1},{129,65},{193,129},{66,2},{130,66... | collective-permute-start | bytes 73736 | tf_op jit(solution)/shard_map/ppermute | solution.py:481
  146.8 15.7 %all-to-all-start.4 = ((f32[8,32,128]{2,1,0:T(8,128)}), f32[8,32,128]{2,1,0:T(8,128)S(1)}, u32[]{:S(2)}, u32[]{:S(2)}) async-start(f32[8,32,128]{2,1,0:T(8,128)} %get-tuple-element.102), calls=%async_computation.4 | async-start | bytes 262144 | tf_op jit(solution)/shard_map/all_to_all | solution.py:482
  152.0 11.4 %collective-permute-start.12 = (f32[48,128]{1,0:T(8,128)S(1)}, f32[48,128]{1,0:T(8,128)S(1)}, u32[]{:S(2)}, u32[]{:S(2)}) collective-permute-start(f32[48,128]{1,0:T(8,128)S(1)} %get-tuple-element.100), channel_id=1, source_target_pairs={{0,64},{64,128},{128,192},{1,65},{65,129},{129,193},{2,66},{66,130... | collective-permute-start | bytes 73736 | tf_op jit(solution)/shard_map/ppermute | solution.py:480
  153.9 9.5 %collective-permute-start.13 = (f32[48,128]{1,0:T(8,128)S(1)}, f32[48,128]{1,0:T(8,128)S(1)}, u32[]{:S(2)}, u32[]{:S(2)}) collective-permute-start(f32[48,128]{1,0:T(8,128)S(1)} %get-tuple-element.101), channel_id=1, source_target_pairs={{64,0},{128,64},{192,128},{65,1},{129,65},{193,129},{66,2},{130,66... | collective-permute-start | bytes 73736 | tf_op jit(solution)/shard_map/ppermute | solution.py:481
  175.5 15.7 %all-to-all-start.5 = ((f32[8,32,128]{2,1,0:T(8,128)}), f32[8,32,128]{2,1,0:T(8,128)S(1)}, u32[]{:S(2)}, u32[]{:S(2)}) async-start(f32[8,32,128]{2,1,0:T(8,128)} %get-tuple-element.108), calls=%async_computation.5 | async-start | bytes 262144 | tf_op jit(solution)/shard_map/all_to_all | solution.py:482
  180.7 11.4 %collective-permute-start.14 = (f32[48,128]{1,0:T(8,128)S(1)}, f32[48,128]{1,0:T(8,128)S(1)}, u32[]{:S(2)}, u32[]{:S(2)}) collective-permute-start(f32[48,128]{1,0:T(8,128)S(1)} %get-tuple-element.106), channel_id=1, source_target_pairs={{0,64},{64,128},{128,192},{1,65},{65,129},{129,193},{2,66},{66,130... | collective-permute-start | bytes 73736 | tf_op jit(solution)/shard_map/ppermute | solution.py:480
  182.6 9.5 %collective-permute-start.15 = (f32[48,128]{1,0:T(8,128)S(1)}, f32[48,128]{1,0:T(8,128)S(1)}, u32[]{:S(2)}, u32[]{:S(2)}) collective-permute-start(f32[48,128]{1,0:T(8,128)S(1)} %get-tuple-element.107), channel_id=1, source_target_pairs={{64,0},{128,64},{192,128},{65,1},{129,65},{193,129},{66,2},{130,66... | collective-permute-start | bytes 73736 | tf_op jit(solution)/shard_map/ppermute | solution.py:481
  (67 other events, 72.5 us)

commit v7 on v6

--- a/solution.py
+++ b/solution.py
@@ -139,8 +139,8 @@
     return jnp.concatenate(lows, axis=0), jnp.concatenate(highs, axis=0)
 
 
-def pack_kernel(l_ref, rhs, acc, perm, cell, remote, mask, trans,
-                top, bottom, a8, kx_first, kx_last, kz, sem):
+def pack_kernel(l_ref, rhs, acc, perm, cell_in, remote_in, mask_in, trans_in,
+                top, bottom, a8, kz, cell, remote, mask, trans, sem):
     tiles = a8.shape[0]
     cx, cy = rhs.shape[0], rhs.shape[1]
     sources = [rhs, acc] + [perm.at[n] for n in range(3)]
@@ -149,10 +149,12 @@
         moves.append(pltpu.make_async_copy(source.at[:, cy - H :, :], top.at[n], sem.at[1 + 2 * n]))
         moves.append(pltpu.make_async_copy(source.at[:, :H, :], bottom.at[n], sem.at[2 + 2 * n]))
     count = 2 * len(sources) + 1
-    moves.append(pltpu.make_async_copy(perm.at[0, 0], kx_first, sem.at[count]))
-    moves.append(pltpu.make_async_copy(perm.at[0, cx - 1], kx_last, sem.at[count + 1]))
-    for move in moves:
+    slots = ((cell_in, cell), (remote_in, remote), (mask_in, mask), (trans_in, trans))
+    lists = [pltpu.make_async_copy(a, b, sem.at[count + n]) for n, (a, b) in enumerate(slots)]
+    for move in lists + moves:
         move.start()
+    for move in lists:
+        move.wait()
     weight = trans[...] * mask[...].astype(f32)
     own, far = cell[...], remote[...]
     column = tiles * 128
@@ -178,22 +180,14 @@
         move.wait()
 
 
-def relay_kernel(l_ref, a8, faces, lists):
+def relay_kernel(l_ref, a8, up, down):
     tiles = a8.shape[0]
-    l = l_ref[0]
-    faces[...] = get_faces(l, a8)
+    faces = get_faces(l_ref[0], a8)
+    up[...] = faces
+    down[0:BOTH_ROWS, :] = faces
     for t in range(tiles):
-        lists[LIST_ROWS * t : LIST_ROWS * (t + 1), :] = a8[t, FACE_ROWS:, :]
-
-
-def join_kernel(faces, lists, kx_low, kx_high, up, down):
-    cy = kx_low.shape[0]
-    base = BOTH_ROWS
-    for out in (up, down):
-        out[0:base, :] = faces[...]
-        out[base : base + cy, :] = kx_low[...]
-        out[base + cy : base + 2 * cy, :] = kx_high[...]
-    down[base + 2 * cy :, :] = lists[...]
+        at = BOTH_ROWS + LIST_ROWS * t
+        down[at : at + LIST_ROWS, :] = a8[t, FACE_ROWS:, :]
 
 
 def emit(l_ref, a8_ref, planes, faces, row_ref, pick_ref, far_x):
@@ -286,49 +280,64 @@
         fault[2 * q + 1] = near_sum(row_ref, q, slot_row(row_ref, q, WEIGHT) * near, cx)
 
 
-def setup_kernel(l_ref, rhs, acc, perm, before, after, below, above, kx_low, kx_high, a8,
-                 inv, z_out, d_out, tx, tym, typ, tzm, tzp, d_first, d_last, a8_out,
-                 row_ref, pick_ref, far_x, planes, fault):
-    cx, cy = rhs.shape[0], rhs.shape[1]
-    ye = cy + 2 * H
+def extended(before, after, n, own, x):
+    return jnp.concatenate([before[n, x], own, after[n, x]], axis=0)
+
+
+def side_faces(ky, kz, faces, x):
+    ye = ky.shape[0]
+    low, high = unpacked(faces, kz, x)
+    return (
+        harmonic(ky, pltpu.roll(ky, 1, 0)),
+        harmonic(ky, pltpu.roll(ky, ye - 1, 0)),
+        harmonic(kz, low),
+        harmonic(kz, high),
+    )
+
+
+def inverse_of(diag):
+    live = diag > 0.0
+    return jnp.where(live, 1.0 / jnp.where(live, diag, 1.0), 0.0)
+
+
+def edge_kernel(l_ref, rhs, acc, perm, before, after, below, above, a8,
+                fault, row_ref, pick_ref, far_x, faces, low_edge, high_edge):
+    cx = rhs.shape[0]
     l = l_ref[0]
     weights(l, a8, above, row_ref, pick_ref, far_x, fault)
     own = get_faces(l, a8)
     left = lane_iota((8, 128)) < 64
-    faces_in = jnp.concatenate(
-        [
-            jnp.where(left, pltpu.roll(below[8:16, :], 64, 1), own[0:8]),
-            own[8:16],
-            jnp.where(left, own[16:24], pltpu.roll(above[8:16, :], 64, 1)),
-        ],
-        axis=0,
-    )
-
-    def ext_face(n, own):
-        at = BOTH_ROWS + n * cy
-        return jnp.concatenate([below[at + cy - H : at + cy, :], own[...], above[at : at + H, :]], axis=0)
-
-    kx_under, kx_over = ext_face(0, kx_low), ext_face(1, kx_high)
-
-    def ext(a, own, x):
-        return jnp.concatenate([before[a, x], own, after[a, x]], axis=0)
+    faces[0:8, :] = jnp.where(left, pltpu.roll(below[8:16, :], 64, 1), own[0:8])
+    faces[8:16, :] = own[8:16]
+    faces[16:24, :] = jnp.where(left, own[16:24], pltpu.roll(above[8:16, :], 64, 1))
+
+    def slab(n, source, x):
+        return extended(before, after, n, source[x], x)
+
+    for edge, x, inner in ((low_edge, 0, 1), (high_edge, cx - 1, cx - 2)):
+        kx, kx_inner = slab(2, perm.at[0], x), slab(2, perm.at[0], inner)
+        sides = side_faces(slab(3, perm.at[1], x), slab(4, perm.at[2], x), faces[...], x)
+        edge[0] = kx
+        edge[1] = with_fault(slab(1, acc, x) + harmonic(kx, kx_inner) + sum(sides), fault, x)
+        edge[2] = slab(0, rhs, x)
+
+
+def setup_kernel(l_ref, rhs, acc, perm, before, after, faces_in, fault, low_edge, high_edge,
+                 row_ref, pick_ref, far_x,
+                 inv, z_out, d_out, tx, tym, typ, tzm, tzp, x_low, x_high, a8_out, planes):
+    cx = rhs.shape[0]
+
+    def ext(n, own, x):
+        return extended(before, after, n, own, x)
 
     def body(x, carry):
         faces, t_low, kx = carry
         nxt = jnp.minimum(x + 1, cx - 1)
-        kx_next = jnp.where(x == cx - 1, kx_over, ext(2, perm[0, nxt], nxt))
-        ky = ext(3, perm[1, x], x)
-        kz = ext(4, perm[2, x], x)
+        kx_next = jnp.where(x == cx - 1, high_edge[0], ext(2, perm[0, nxt], nxt))
         t_high = harmonic(kx, kx_next)
-        ym = harmonic(ky, pltpu.roll(ky, 1, 0))
-        yp = harmonic(ky, pltpu.roll(ky, ye - 1, 0))
-        kz_low, kz_high = unpacked(faces_in, kz, x)
-        zm = harmonic(kz, kz_low)
-        zp = harmonic(kz, kz_high)
+        ym, yp, zm, zp = side_faces(ext(3, perm[1, x], x), ext(4, perm[2, x], x), faces_in[...], x)
         diag = ext(1, acc[x], x) + t_low + t_high + ym + yp + zm + zp
-        diag = with_fault(diag, fault, x)
-        live = diag > 0.0
-        inverse = jnp.where(live, 1.0 / jnp.where(live, diag, 1.0), 0.0)
+        inverse = inverse_of(with_fault(diag, fault, x))
         z = inverse * ext(0, rhs[x], x)
         d = z / theta
         inv[x] = inverse
@@ -344,10 +353,10 @@
         return pack_faces(faces, y_tiles(d), x), t_high, kx_next
 
     kx0 = ext(2, perm[0, 0], 0)
-    init = (no_faces(), harmonic(kx_under, kx0), kx0)
+    init = (no_faces(), harmonic(low_edge[0], kx0), kx0)
     faces, _, _ = lax.fori_loop(0, cx, body, init, unroll=4)
-    d_first[...] = d_out[0]
-    d_last[...] = d_out[cx - 1]
+    for out, edge, at in ((x_low, low_edge, 0), (x_high, high_edge, cx)):
+        out[...] = inverse_of(edge[1] + tx[at]) * edge[2] / theta
     emit(l_ref, a8_out, planes, faces, row_ref, pick_ref, far_x)
 
 
@@ -423,33 +432,25 @@
     flats = [a.reshape(1, slots) for a in (nnc_cell, nnc_remote, nnc_mask, nnc_trans)]
     l, *flats = lax.optimization_barrier((l, *flats))
     halo = struct(5, cx, H, cz)
-    top, bottom, a8, kx_first, kx_last = pl.pallas_call(
+    top, bottom, a8 = pl.pallas_call(
         pack_kernel,
-        out_shape=(halo, halo, struct(tiles, FACE_ROWS + LIST_ROWS, cz), struct(cy, cz), struct(cy, cz)),
-        in_specs=[SMEM] + [HBM] * 3 + [VMEM] * 4,
-        out_specs=(VMEM,) * 5,
-        scratch_shapes=[pltpu.VMEM((cx, cy, cz), f32), pltpu.SemaphoreType.DMA((13,))],
+        out_shape=(halo, halo, struct(tiles, FACE_ROWS + LIST_ROWS, cz)),
+        in_specs=[SMEM] + [HBM] * 7,
+        out_specs=(VMEM,) * 3,
+        scratch_shapes=[pltpu.VMEM((cx, cy, cz), f32)]
+        + [pltpu.VMEM((1, slots), jnp.int32)] * 3
+        + [pltpu.VMEM((1, slots), f32), pltpu.SemaphoreType.DMA((15,))],
     )(l, rhs, accumulation, permeability, *flats)
-    kx_low = lax.ppermute(kx_last, "gx", up_x)
-    kx_high = lax.ppermute(kx_first, "gx", down_x)
     before = lax.ppermute(top, "gy", up_y)
     after = lax.ppermute(bottom, "gy", down_y)
     a8 = lax.all_to_all(a8, "gz", 0, 0, tiled=True)
-    faces, group = pl.pallas_call(
+    below, above = pl.pallas_call(
         relay_kernel,
-        out_shape=(struct(BOTH_ROWS, cz), struct(tiles * LIST_ROWS, cz)),
+        out_shape=(struct(BOTH_ROWS, cz), struct(BOTH_ROWS + tiles * LIST_ROWS, cz)),
         in_specs=[SMEM, VMEM],
         out_specs=(VMEM,) * 2,
         compiler_params=PARAMS,
     )(l, a8)
-    small = BOTH_ROWS + 2 * cy
-    below, above = pl.pallas_call(
-        join_kernel,
-        out_shape=(struct(small, cz), struct(small + tiles * LIST_ROWS, cz)),
-        in_specs=[VMEM] * 4,
-        out_specs=(VMEM,) * 2,
-        compiler_params=PARAMS,
-    )(faces, group, kx_low, kx_high)
     below = lax.ppermute(below, "gy", up_y)
     above = lax.ppermute(above, "gy", down_y)
 
@@ -461,14 +462,23 @@
     scratch = [pltpu.VMEM((4, cx, cz), f32)]
     every = tiles * slots
     lists = (struct(2, 8, slots), struct(2, cz, every, dtype=bf16), struct(2, every))
-    inv, z, d, tx, tym, typ, tzm, tzp, d_first, d_last, a8, row, pick, far_x = pl.pallas_call(
+    fault, row, pick, far_x, faces, low_edge, high_edge = pl.pallas_call(
+        edge_kernel,
+        out_shape=(struct(4, cx, cz),) + lists + (struct(BOTH_ROWS, cz),) + (struct(3, ye, cz),) * 2,
+        in_specs=[SMEM] + [VMEM] * 8,
+        out_specs=(VMEM,) * 7,
+        compiler_params=PARAMS,
+    )(l, rhs, accumulation, permeability, before, after, below, above, a8)
+    low_got = lax.ppermute(high_edge, "gx", up_x)
+    high_got = lax.ppermute(low_edge, "gx", down_x)
+    inv, z, d, tx, tym, typ, tzm, tzp, xlow, xhigh, a8 = pl.pallas_call(
         setup_kernel,
-        out_shape=(big, big, big, tall, big, big, big, big, edge, edge, sent) + lists,
-        in_specs=[SMEM] + [VMEM] * 10,
-        out_specs=(VMEM,) * 14,
-        scratch_shapes=scratch * 2,
+        out_shape=(big, big, big, tall, big, big, big, big, edge, edge, sent),
+        in_specs=[SMEM] + [VMEM] * 12,
+        out_specs=(VMEM,) * 11,
+        scratch_shapes=scratch,
         compiler_params=PARAMS,
-    )(l, rhs, accumulation, permeability, before, after, below, above, kx_low, kx_high, a8)
+    )(l, rhs, accumulation, permeability, before, after, faces, fault, low_got, high_got, row, pick, far_x)
 
     rho = 1.0 / sigma
     corr = None
@@ -477,8 +487,9 @@
         rho_next = 1.0 / (2.0 * sigma - rho)
         c1, c2 = rho_next * rho, 2.0 * rho_next / delta
         rho = rho_next
-        xlow = lax.ppermute(d_last, "gx", up_x)
-        xhigh = lax.ppermute(d_first, "gx", down_x)
+        if not first:
+            xlow = lax.ppermute(d_last, "gx", up_x)
+            xhigh = lax.ppermute(d_first, "gx", down_x)
         a8 = lax.all_to_all(a8, "gz", 0, 0, tiled=True)
         fault = pl.pallas_call(
             fault_kernel,

time: 203 us -> 185 us (0.911)
  blocking collectives: 0 us -> 34.5 us
  starting transfers between devices: 73.1 us -> 48.9 us
  local copies, waits for them, and re-layouts: 55.5 us -> 37 us
  waiting for transfers between devices: 44.1 us -> 35.8 us
    all_to_all x0 -> x2, blocking collectives: none -> 34.5 us  [local(): a8 = lax.all_to_all(a8, 'gz', 0, 0, tiled=True)]
    all_to_all x6 -> x4, starting transfers between devices: 41 us -> 19.8 us  [local(): a8 = lax.all_to_all(a8, 'gz', 0, 0, tiled=True)]
    unnamed x138 -> x106, local copies, waits for them, and re-layouts: 55.5 us -> 37 us
    all_to_all x6 -> x4, waiting for transfers between devices: 41 us -> 28.1 us  [local(): a8 = lax.all_to_all(a8, 'gz', 0, 0, tiled=True)]
    ppermute x2, waiting for transfers between devices: 0.01 us -> 4.95 us  [the longest x1 4.29 us: local(): high_got = lax.ppermute(low_edge, 'gx', down_x)]
    ppermute x5 -> x4, starting transfers between devices: 11.6 us -> 8.63 us  [local(): xlow = lax.ppermute(d_last, 'gx', up_x)]
    ppermute x5 -> x4, starting transfers between devices: 6.46 us -> 5.17 us  [local(): xhigh = lax.ppermute(d_first, 'gx', down_x)]
  transfers between devices with their start and end apart: 22 -> 18, of which waited for: 7 -> 7; matrix products, arithmetic and copies ran while one was open for 0% -> 0% of each run, Pallas kernels for 2% -> 2%
where the time goes in v7:
time: 185 us; the launch traced here: 183 us
  starting transfers between devices  48.9 us (26%)
  local copies, waits for them, and re-layouts  37 us (20%)
  waiting for transfers between devices  35.8 us (19%)
  blocking collectives  34.5 us (19%)
  Pallas kernels  26.8 us (14%)
    unnamed x106, local copies, waits for them, and re-layouts  37 us
    all_to_all x2, blocking collectives, local(): a8 = lax.all_to_all(a8, 'gz', 0, 0, tiled=True)  34.5 us
    all_to_all x4, waiting for transfers between devices, local(): a8 = lax.all_to_all(a8, 'gz', 0, 0, tiled=True)  28.1 us
    all_to_all x4, starting transfers between devices, local(): a8 = lax.all_to_all(a8, 'gz', 0, 0, tiled=True)  19.8 us
    pallas_call x5, Pallas kernels, local(): pl.pallas_call(kernel, out_shape=small if last else (big, big, small, edg...  15 us
    ppermute x4, starting transfers between devices, local(): xlow = lax.ppermute(d_last, 'gx', up_x)  8.63 us
    ppermute x4, starting transfers between devices, local(): xhigh = lax.ppermute(d_first, 'gx', down_x)  5.17 us
    pallas_call x5, Pallas kernels, local(): pl.pallas_call(fault_kernel, out_shape=struct(4, cx, cz), in_specs=[VMEM]...  4.29 us
  transfers between devices with their start and end apart: 18, of which 7 were waited for; matrix products, arithmetic and copies ran while one was open for 0% of the time, Pallas kernels for 2%

profile of v7, /device:TPU:8, one launch (start us, length us, event | category | flops | bytes accessed | tf_op | source)
XLA Modules:
  0.0 183.2 jit_solution(8912338576137609471)
XLA Ops:
  0.0 3.3 %shard_map.73 = (f32[5,32,8,128]{3,2,1,0:T(8,128)}, f32[5,32,8,128]{3,2,1,0:T(8,128)}, f32[8,40,128]{2,1,0:T(8,128)}) custom-call(s32[1]{0:T(128)} %bitcast.l_ref.refs_0_, f32[32,32,128]{2,1,0:T(8,128)} %rhs.5, f32[32,32,128]{2,1,0:T(8,128)} %acc.5, f32[3,32,32,128]{3,2,1,0:T(8,128)} %perm.5, s32[1,512]{1,0:T(1,128)} %bitcast.5, s32[1,512]{1,0:T(1,128)} %bitcast.6, ...), custom_call_target="tpu_custom_call" | custom-call | tf_op jit(solution)/shard_map/pallas_call | solution.py:435
  3.3 1.9 %collective-permute-start = (f32[5,32,8,128]{3,2,1,0:T(8,128)}, f32[5,32,8,128]{3,2,1,0:T(8,128)S(1)}, u32[]{:S(2)}, u32[]{:S(2)}) collective-permute-start(f32[5,32,8,128]{3,2,1,0:T(8,128)} %get-tuple-element.62), channel_id=1, source_target_pairs={{0,8},{8,16},{16,24},{24,32},{32,40},{40,48},{48,56},{1,9},{9,17},... | collective-permute-start | bytes 1966088 | tf_op jit(solution)/shard_map/ppermute | solution.py:444
  5.2 3.6 %collective-permute-start.1 = (f32[5,32,8,128]{3,2,1,0:T(8,128)}, f32[5,32,8,128]{3,2,1,0:T(8,128)S(1)}, u32[]{:S(2)}, u32[]{:S(2)}) collective-permute-start(f32[5,32,8,128]{3,2,1,0:T(8,128)} %get-tuple-element.63), channel_id=1, source_target_pairs={{8,0},{16,8},{24,16},{32,24},{40,32},{48,40},{56,48},{9,1},{17,9},... | collective-permute-start | bytes 1966088 | tf_op jit(solution)/shard_map/ppermute | solution.py:445
  8.8 21.6 %all_to_all.30.a8 = f32[8,40,128]{2,1,0:T(8,128)S(1)} all-to-all(f32[8,40,128]{2,1,0:T(8,128)} %get-tuple-element.64), channel_id=1, replica_groups=mesh['gx'=4,'gy'=8,'gz'=8] {'gz'}, dimensions={0} | all-to-all | bytes 327680 | tf_op jit(solution)/shard_map/all_to_all | solution.py:446
  32.5 2.4 %collective-permute-start.2 = (f32[24,128]{1,0:T(8,128)S(1)}, f32[24,128]{1,0:T(8,128)S(1)}, u32[]{:S(2)}, u32[]{:S(2)}) collective-permute-start(f32[24,128]{1,0:T(8,128)S(1)} %get-tuple-element.65), channel_id=1, source_target_pairs={{0,8},{8,16},{16,24},{24,32},{32,40},{40,48},{48,56},{1,9},{9,17},... | collective-permute-start | bytes 36872 | tf_op jit(solution)/shard_map/ppermute | solution.py:454
  34.9 2.6 %collective-permute-done.2.below = f32[24,128]{1,0:T(8,128)S(1)} collective-permute-done((f32[24,128]{1,0:T(8,128)S(1)}, f32[24,128]{1,0:T(8,128)S(1)}, u32[]{:S(2)}, u32[]{:S(2)}) %collective-permute-start.2) | collective-permute-done | bytes 12320 | tf_op jit(solution)/shard_map/ppermute | solution.py:454
  39.9 4.2 %collective-permute-start.4 = (f32[3,48,128]{2,1,0:T(8,128)S(1)}, f32[3,48,128]{2,1,0:T(8,128)S(1)}, u32[]{:S(2)}, u32[]{:S(2)}) collective-permute-start(f32[3,48,128]{2,1,0:T(8,128)S(1)} %get-tuple-element.69), channel_id=1, source_target_pairs={{0,64},{64,128},{128,192},{1,65},{65,129},{129,193},{2,66},{66,130... | collective-permute-start | bytes 221192 | tf_op jit(solution)/shard_map/ppermute | solution.py:472
  46.0 4.3 %collective-permute-done.5.high_edge = f32[3,48,128]{2,1,0:T(8,128)S(1)} collective-permute-done((f32[3,48,128]{2,1,0:T(8,128)S(1)}, f32[3,48,128]{2,1,0:T(8,128)S(1)}, u32[]{:S(2)}, u32[]{:S(2)}) %collective-permute-start.5) | collective-permute-done | bytes 73760 | tf_op jit(solution)/shard_map/ppermute | solution.py:473
  50.3 3.1 %shard_map.76 = (f32[32,48,128]{2,1,0:T(8,128)S(1)}, f32[32,48,128]{2,1,0:T(8,128)S(1)}, f32[32,48,128]{2,1,0:T(8,128)S(1)}, f32[33,48,128]{2,1,0:T(8,128)S(1)},...) custom-call(s32[1]{0:T(128)} %bitcast.l_ref.refs_0_, ...), custom_call_target="tpu_custom_call" | custom-call | tf_op jit(solution)/shard_map/pallas_call | solution.py:474
  53.5 12.9 %all_to_all.31.a8.refs_5_ = f32[8,32,128]{2,1,0:T(8,128)S(1)} all-to-all(f32[8,32,128]{2,1,0:T(8,128)S(1)} %get-tuple-element.78), channel_id=1, replica_groups=mesh['gx'=4,'gy'=8,'gz'=8] {'gz'}, dimensions={0} | all-to-all | bytes 262144 | tf_op jit(solution)/shard_map/all_to_all | solution.py:493
  67.2 3.3 %shard_map.78 = (f32[32,48,128]{2,1,0:T(8,128)S(1)}, f32[32,48,128]{2,1,0:T(8,128)S(1)}, f32[32,32,128]{2,1,0:T(8,128)S(1)}, f32[48,128]{1,0:T(8,128)S(1)}, f32[...) custom-call(s32[1]{0:T(128)} %bitcast.l_ref.refs_0_, f32[32,48,128]{2,1,0:T(8,128)S(1)} %get-tuple-element.74.refs_1_, ...), custom_call_target="tpu_custom_call" | custom-call | tf_op jit(solution)/shard_map/pallas_call | solution.py:508
  73.2 3.4 %all-to-all-start.2 = ((f32[8,32,128]{2,1,0:T(8,128)}), f32[8,32,128]{2,1,0:T(8,128)S(1)}, u32[]{:S(2)}, u32[]{:S(2)}) async-start(f32[8,32,128]{2,1,0:T(8,128)} %get-tuple-element.90), calls=%async_computation.2 | async-start | bytes 262144 | tf_op jit(solution)/shard_map/all_to_all | solution.py:493
  76.6 2.9 %collective-permute-start.6 = (f32[48,128]{1,0:T(8,128)S(1)}, f32[48,128]{1,0:T(8,128)S(1)}, u32[]{:S(2)}, u32[]{:S(2)}) collective-permute-start(f32[48,128]{1,0:T(8,128)S(1)} %get-tuple-element.88), channel_id=1, source_target_pairs={{0,64},{64,128},{128,192},{1,65},{65,129},{129,193},{2,66},{66,130... | collective-permute-start | bytes 73736 | tf_op jit(solution)/shard_map/ppermute | solution.py:491
  80.8 6.2 %all-to-all-done.2.a8.refs_6_ = f32[8,32,128]{2,1,0:T(8,128)S(1)} async-done(((f32[8,32,128]{2,1,0:T(8,128)}), f32[8,32,128]{2,1,0:T(8,128)S(1)}, u32[]{:S(2)}, u32[]{:S(2)}) %all-to-all-start.2) | async-done | bytes 131104 | tf_op jit(solution)/shard_map/all_to_all | solution.py:493
  94.2 3.2 %shard_map.80 = (f32[32,48,128]{2,1,0:T(8,128)S(1)}, f32[32,48,128]{2,1,0:T(8,128)S(1)}, f32[32,32,128]{2,1,0:T(8,128)S(1)}, f32[48,128]{1,0:T(8,128)S(1)}, f32[...) custom-call(s32[1]{0:T(128)} %bitcast.l_ref.refs_0_, f32[32,48,128]{2,1,0:T(8,128)S(1)} %copy-done.42, ...), custom_call_target="tpu_custom_call" | custom-call | tf_op jit(solution)/shard_map/pallas_call | solution.py:508
  100.1 6.1 %all-to-all-start.3 = ((f32[8,32,128]{2,1,0:T(8,128)}), f32[8,32,128]{2,1,0:T(8,128)S(1)}, u32[]{:S(2)}, u32[]{:S(2)}) async-start(f32[8,32,128]{2,1,0:T(8,128)} %get-tuple-element.96), calls=%async_computation.3 | async-start | bytes 262144 | tf_op jit(solution)/shard_map/all_to_all | solution.py:493
  109.4 7.3 %all-to-all-done.3.a8.refs_6_ = f32[8,32,128]{2,1,0:T(8,128)S(1)} async-done(((f32[8,32,128]{2,1,0:T(8,128)}), f32[8,32,128]{2,1,0:T(8,128)S(1)}, u32[]{:S(2)}, u32[]{:S(2)}) %all-to-all-start.3) | async-done | bytes 131104 | tf_op jit(solution)/shard_map/all_to_all | solution.py:493
  123.9 3.2 %shard_map.82 = (f32[32,48,128]{2,1,0:T(8,128)S(1)}, f32[32,48,128]{2,1,0:T(8,128)S(1)}, f32[32,32,128]{2,1,0:T(8,128)S(1)}, f32[48,128]{1,0:T(8,128)S(1)}, f32[...) custom-call(s32[1]{0:T(128)} %bitcast.l_ref.refs_0_, f32[32,48,128]{2,1,0:T(8,128)S(1)} %copy-done.34, ...), custom_call_target="tpu_custom_call" | custom-call | tf_op jit(solution)/shard_map/pallas_call | solution.py:508
  129.7 5.1 %all-to-all-start.4 = ((f32[8,32,128]{2,1,0:T(8,128)}), f32[8,32,128]{2,1,0:T(8,128)S(1)}, u32[]{:S(2)}, u32[]{:S(2)}) async-start(f32[8,32,128]{2,1,0:T(8,128)} %get-tuple-element.102), calls=%async_computation.4 | async-start | bytes 262144 | tf_op jit(solution)/shard_map/all_to_all | solution.py:493
  138.1 7.3 %all-to-all-done.4.a8.refs_6_ = f32[8,32,128]{2,1,0:T(8,128)S(1)} async-done(((f32[8,32,128]{2,1,0:T(8,128)}), f32[8,32,128]{2,1,0:T(8,128)S(1)}, u32[]{:S(2)}, u32[]{:S(2)}) %all-to-all-start.4) | async-done | bytes 131104 | tf_op jit(solution)/shard_map/all_to_all | solution.py:493
  152.6 3.2 %shard_map.84 = (f32[32,48,128]{2,1,0:T(8,128)S(1)}, f32[32,48,128]{2,1,0:T(8,128)S(1)}, f32[32,32,128]{2,1,0:T(8,128)S(1)}, f32[48,128]{1,0:T(8,128)S(1)}, f32[...) custom-call(s32[1]{0:T(128)} %bitcast.l_ref.refs_0_, f32[32,48,128]{2,1,0:T(8,128)S(1)} %copy-done.38, ...), custom_call_target="tpu_custom_call" | custom-call | tf_op jit(solution)/shard_map/pallas_call | solution.py:508
  158.4 5.1 %all-to-all-start.5 = ((f32[8,32,128]{2,1,0:T(8,128)}), f32[8,32,128]{2,1,0:T(8,128)S(1)}, u32[]{:S(2)}, u32[]{:S(2)}) async-start(f32[8,32,128]{2,1,0:T(8,128)} %get-tuple-element.108), calls=%async_computation.5 | async-start | bytes 262144 | tf_op jit(solution)/shard_map/all_to_all | solution.py:493
  166.7 7.3 %all-to-all-done.5.a8.refs_6_ = f32[8,32,128]{2,1,0:T(8,128)S(1)} async-done(((f32[8,32,128]{2,1,0:T(8,128)}), f32[8,32,128]{2,1,0:T(8,128)S(1)}, u32[]{:S(2)}, u32[]{:S(2)}) %all-to-all-start.5) | async-done | bytes 131104 | tf_op jit(solution)/shard_map/all_to_all | solution.py:493
  181.2 2.0 %shard_map.86 = f32[32,32,128]{2,1,0:T(8,128)} custom-call(s32[1]{0:T(128)} %bitcast.l_ref.refs_0_, f32[32,48,128]{2,1,0:T(8,128)S(1)} %copy-done.30, f32[32,48,128]{2,1,0:T(8,128)S(1)} %copy-done.32, f32[32,32,128]{2,1,0:T(8,128)S(1)} %copy-done.46, f32[48,128]{1,0:T(8,128)S(1)} %collective-permute-done.12.refs_4_, ...), custom_call_target="tpu_custom_call" | custom-call | tf_op jit(solution)/shard_map/pallas_call | solution.py:508
  (134 shorter events, 57.2 us)
Async XLA Ops:
  0.0 37.5 %copy-start.27 = (f32[32,32,128]{2,1,0:T(8,128)S(1)}, f32[32,32,128]{2,1,0:T(8,128)}, u32[]{:S(2)}) copy-start(f32[32,32,128]{2,1,0:T(8,128)} %acc.5) | copy-start | bytes 1572868
  0.0 37.5 %copy-start.26 = (f32[32,32,128]{2,1,0:T(8,128)S(1)}, f32[32,32,128]{2,1,0:T(8,128)}, u32[]{:S(2)}) copy-start(f32[32,32,128]{2,1,0:T(8,128)} %rhs.5) | copy-start | bytes 1572868
  3.3 34.3 %collective-permute-start = (f32[5,32,8,128]{3,2,1,0:T(8,128)}, f32[5,32,8,128]{3,2,1,0:T(8,128)S(1)}, u32[]{:S(2)}, u32[]{:S(2)}) collective-permute-start(f32[5,32,8,128]{3,2,1,0:T(8,128)} %get-tuple-element.62), channel_id=1, source_target_pairs={{0,8},{8,16},{16,24},{24,32},{32,40},{40,48},{48,56},{1,9},{9,17},... | collective-permute-start | bytes 1966088 | tf_op jit(solution)/shard_map/ppermute | solution.py:444
  5.2 32.3 %collective-permute-start.1 = (f32[5,32,8,128]{3,2,1,0:T(8,128)}, f32[5,32,8,128]{3,2,1,0:T(8,128)S(1)}, u32[]{:S(2)}, u32[]{:S(2)}) collective-permute-start(f32[5,32,8,128]{3,2,1,0:T(8,128)} %get-tuple-element.63), channel_id=1, source_target_pairs={{8,0},{16,8},{24,16},{32,24},{40,32},{48,40},{56,48},{9,1},{17,9},... | collective-permute-start | bytes 1966088 | tf_op jit(solution)/shard_map/ppermute | solution.py:445
  30.6 6.9 %collective-permute-start.3 = (f32[216,128]{1,0:T(8,128)S(1)}, f32[216,128]{1,0:T(8,128)S(1)}, u32[]{:S(2)}, u32[]{:S(2)}) collective-permute-start(f32[216,128]{1,0:T(8,128)S(1)} %get-tuple-element.66), channel_id=1, source_target_pairs={{8,0},{16,8},{24,16},{32,24},{40,32},{48,40},{56,48},{9,1},{17,9},... | collective-permute-start | bytes 331784 | tf_op jit(solution)/shard_map/ppermute | solution.py:455
  32.5 5.0 %collective-permute-start.2 = (f32[24,128]{1,0:T(8,128)S(1)}, f32[24,128]{1,0:T(8,128)S(1)}, u32[]{:S(2)}, u32[]{:S(2)}) collective-permute-start(f32[24,128]{1,0:T(8,128)S(1)} %get-tuple-element.65), channel_id=1, source_target_pairs={{0,8},{8,16},{16,24},{24,32},{32,40},{40,48},{48,56},{1,9},{9,17},... | collective-permute-start | bytes 36872 | tf_op jit(solution)/shard_map/ppermute | solution.py:454
  39.9 6.1 %collective-permute-start.4 = (f32[3,48,128]{2,1,0:T(8,128)S(1)}, f32[3,48,128]{2,1,0:T(8,128)S(1)}, u32[]{:S(2)}, u32[]{:S(2)}) collective-permute-start(f32[3,48,128]{2,1,0:T(8,128)S(1)} %get-tuple-element.69), channel_id=1, source_target_pairs={{0,64},{64,128},{128,192},{1,65},{65,129},{129,193},{2,66},{66,130... | collective-permute-start | bytes 221192 | tf_op jit(solution)/shard_map/ppermute | solution.py:472
  44.1 6.2 %collective-permute-start.5 = (f32[3,48,128]{2,1,0:T(8,128)S(1)}, f32[3,48,128]{2,1,0:T(8,128)S(1)}, u32[]{:S(2)}, u32[]{:S(2)}) collective-permute-start(f32[3,48,128]{2,1,0:T(8,128)S(1)} %get-tuple-element.70), channel_id=1, source_target_pairs={{64,0},{128,64},{192,128},{65,1},{129,65},{193,129},{66,2},{130,66... | collective-permute-start | bytes 221192 | tf_op jit(solution)/shard_map/ppermute | solution.py:473
  53.5 17.1 %copy-start = (f32[32,48,128]{2,1,0:T(8,128)}, f32[32,48,128]{2,1,0:T(8,128)S(1)}, u32[]{:S(2)}) copy-start(f32[32,48,128]{2,1,0:T(8,128)S(1)} %get-tuple-element.79.refs_7_.refs_8_) | copy-start | bytes 2359300
  53.5 17.1 %copy-start.5 = (f32[32,48,128]{2,1,0:T(8,128)}, f32[32,48,128]{2,1,0:T(8,128)S(1)}, u32[]{:S(2)}) copy-start(f32[32,48,128]{2,1,0:T(8,128)S(1)} %get-tuple-element.81.refs_9_.refs_10_) | copy-start | bytes 2359300
  53.5 17.1 %copy-start.10 = (f32[32,48,128]{2,1,0:T(8,128)}, f32[32,48,128]{2,1,0:T(8,128)S(1)}, u32[]{:S(2)}) copy-start(f32[32,48,128]{2,1,0:T(8,128)S(1)} %get-tuple-element.82.refs_10_.refs_11_) | copy-start | bytes 2359300
  53.5 17.1 %copy-start.15 = (f32[32,48,128]{2,1,0:T(8,128)}, f32[32,48,128]{2,1,0:T(8,128)S(1)}, u32[]{:S(2)}) copy-start(f32[32,48,128]{2,1,0:T(8,128)S(1)} %get-tuple-element.83.refs_11_.refs_12_) | copy-start | bytes 2359300
  73.2 13.8 %all-to-all-start.2 = ((f32[8,32,128]{2,1,0:T(8,128)}), f32[8,32,128]{2,1,0:T(8,128)S(1)}, u32[]{:S(2)}, u32[]{:S(2)}) async-start(f32[8,32,128]{2,1,0:T(8,128)} %get-tuple-element.90), calls=%async_computation.2 | async-start | bytes 262144 | tf_op jit(solution)/shard_map/all_to_all | solution.py:493
  76.6 11.3 %collective-permute-start.6 = (f32[48,128]{1,0:T(8,128)S(1)}, f32[48,128]{1,0:T(8,128)S(1)}, u32[]{:S(2)}, u32[]{:S(2)}) collective-permute-start(f32[48,128]{1,0:T(8,128)S(1)} %get-tuple-element.88), channel_id=1, source_target_pairs={{0,64},{64,128},{128,192},{1,65},{65,129},{129,193},{2,66},{66,130... | collective-permute-start | bytes 73736 | tf_op jit(solution)/shard_map/ppermute | solution.py:491
  79.5 8.4 %collective-permute-start.7 = (f32[48,128]{1,0:T(8,128)S(1)}, f32[48,128]{1,0:T(8,128)S(1)}, u32[]{:S(2)}, u32[]{:S(2)}) collective-permute-start(f32[48,128]{1,0:T(8,128)S(1)} %get-tuple-element.89), channel_id=1, source_target_pairs={{64,0},{128,64},{192,128},{65,1},{129,65},{193,129},{66,2},{130,66... | collective-permute-start | bytes 73736 | tf_op jit(solution)/shard_map/ppermute | solution.py:492
  100.1 16.6 %all-to-all-start.3 = ((f32[8,32,128]{2,1,0:T(8,128)}), f32[8,32,128]{2,1,0:T(8,128)S(1)}, u32[]{:S(2)}, u32[]{:S(2)}) async-start(f32[8,32,128]{2,1,0:T(8,128)} %get-tuple-element.96), calls=%async_computation.3 | async-start | bytes 262144 | tf_op jit(solution)/shard_map/all_to_all | solution.py:493
  106.2 11.4 %collective-permute-start.8 = (f32[48,128]{1,0:T(8,128)S(1)}, f32[48,128]{1,0:T(8,128)S(1)}, u32[]{:S(2)}, u32[]{:S(2)}) collective-permute-start(f32[48,128]{1,0:T(8,128)S(1)} %get-tuple-element.94), channel_id=1, source_target_pairs={{0,64},{64,128},{128,192},{1,65},{65,129},{129,193},{2,66},{66,130... | collective-permute-start | bytes 73736 | tf_op jit(solution)/shard_map/ppermute | solution.py:491
  108.1 9.5 %collective-permute-start.9 = (f32[48,128]{1,0:T(8,128)S(1)}, f32[48,128]{1,0:T(8,128)S(1)}, u32[]{:S(2)}, u32[]{:S(2)}) collective-permute-start(f32[48,128]{1,0:T(8,128)S(1)} %get-tuple-element.95), channel_id=1, source_target_pairs={{64,0},{128,64},{192,128},{65,1},{129,65},{193,129},{66,2},{130,66... | collective-permute-start | bytes 73736 | tf_op jit(solution)/shard_map/ppermute | solution.py:492
  129.7 15.7 %all-to-all-start.4 = ((f32[8,32,128]{2,1,0:T(8,128)}), f32[8,32,128]{2,1,0:T(8,128)S(1)}, u32[]{:S(2)}, u32[]{:S(2)}) async-start(f32[8,32,128]{2,1,0:T(8,128)} %get-tuple-element.102), calls=%async_computation.4 | async-start | bytes 262144 | tf_op jit(solution)/shard_map/all_to_all | solution.py:493
  134.9 11.4 %collective-permute-start.10 = (f32[48,128]{1,0:T(8,128)S(1)}, f32[48,128]{1,0:T(8,128)S(1)}, u32[]{:S(2)}, u32[]{:S(2)}) collective-permute-start(f32[48,128]{1,0:T(8,128)S(1)} %get-tuple-element.100), channel_id=1, source_target_pairs={{0,64},{64,128},{128,192},{1,65},{65,129},{129,193},{2,66},{66,130... | collective-permute-start | bytes 73736 | tf_op jit(solution)/shard_map/ppermute | solution.py:491
  136.8 9.5 %collective-permute-start.11 = (f32[48,128]{1,0:T(8,128)S(1)}, f32[48,128]{1,0:T(8,128)S(1)}, u32[]{:S(2)}, u32[]{:S(2)}) collective-permute-start(f32[48,128]{1,0:T(8,128)S(1)} %get-tuple-element.101), channel_id=1, source_target_pairs={{64,0},{128,64},{192,128},{65,1},{129,65},{193,129},{66,2},{130,66... | collective-permute-start | bytes 73736 | tf_op jit(solution)/shard_map/ppermute | solution.py:492
  158.4 15.7 %all-to-all-start.5 = ((f32[8,32,128]{2,1,0:T(8,128)}), f32[8,32,128]{2,1,0:T(8,128)S(1)}, u32[]{:S(2)}, u32[]{:S(2)}) async-start(f32[8,32,128]{2,1,0:T(8,128)} %get-tuple-element.108), calls=%async_computation.5 | async-start | bytes 262144 | tf_op jit(solution)/shard_map/all_to_all | solution.py:493
  163.5 11.4 %collective-permute-start.12 = (f32[48,128]{1,0:T(8,128)S(1)}, f32[48,128]{1,0:T(8,128)S(1)}, u32[]{:S(2)}, u32[]{:S(2)}) collective-permute-start(f32[48,128]{1,0:T(8,128)S(1)} %get-tuple-element.106), channel_id=1, source_target_pairs={{0,64},{64,128},{128,192},{1,65},{65,129},{129,193},{2,66},{66,130... | collective-permute-start | bytes 73736 | tf_op jit(solution)/shard_map/ppermute | solution.py:491
  165.4 9.5 %collective-permute-start.13 = (f32[48,128]{1,0:T(8,128)S(1)}, f32[48,128]{1,0:T(8,128)S(1)}, u32[]{:S(2)}, u32[]{:S(2)}) collective-permute-start(f32[48,128]{1,0:T(8,128)S(1)} %get-tuple-element.107), channel_id=1, source_target_pairs={{64,0},{128,64},{192,128},{65,1},{129,65},{193,129},{66,2},{130,66... | collective-permute-start | bytes 73736 | tf_op jit(solution)/shard_map/ppermute | solution.py:492
  (47 other events, 79.0 us)

commit v8 on v7

--- a/solution.py
+++ b/solution.py
@@ -322,9 +322,8 @@
         edge[2] = slab(0, rhs, x)
 
 
-def setup_kernel(l_ref, rhs, acc, perm, before, after, faces_in, fault, low_edge, high_edge,
-                 row_ref, pick_ref, far_x,
-                 inv, z_out, d_out, tx, tym, typ, tzm, tzp, x_low, x_high, a8_out, planes):
+def setup_kernel(rhs, acc, perm, before, after, faces_in, fault,
+                 inv, z_out, d_out, tx, tym, typ, tzm, tzp, faces_out, planes):
     cx = rhs.shape[0]
 
     def ext(n, own, x):
@@ -333,7 +332,7 @@
     def body(x, carry):
         faces, t_low, kx = carry
         nxt = jnp.minimum(x + 1, cx - 1)
-        kx_next = jnp.where(x == cx - 1, high_edge[0], ext(2, perm[0, nxt], nxt))
+        kx_next = ext(2, perm[0, nxt], nxt)
         t_high = harmonic(kx, kx_next)
         ym, yp, zm, zp = side_faces(ext(3, perm[1, x], x), ext(4, perm[2, x], x), faces_in[...], x)
         diag = ext(1, acc[x], x) + t_low + t_high + ym + yp + zm + zp
@@ -353,11 +352,33 @@
         return pack_faces(faces, y_tiles(d), x), t_high, kx_next
 
     kx0 = ext(2, perm[0, 0], 0)
-    init = (no_faces(), harmonic(low_edge[0], kx0), kx0)
-    faces, _, _ = lax.fori_loop(0, cx, body, init, unroll=4)
-    for out, edge, at in ((x_low, low_edge, 0), (x_high, high_edge, cx)):
-        out[...] = inverse_of(edge[1] + tx[at]) * edge[2] / theta
+    faces, _, _ = lax.fori_loop(0, cx, body, (no_faces(), jnp.zeros_like(kx0), kx0), unroll=4)
+    faces_out[...] = jnp.concatenate(faces, axis=0)
+
+
+def finish_kernel(l_ref, low_own, high_own, low_got, high_got, faces_in, planes_in,
+                  row_ref, pick_ref, far_x, *refs):
+    inv, z_out, d_out, tx, x_low, x_high, a8_out, planes, slabs, sem = refs[4:]
+    cx = planes.shape[1]
+    planes[...] = planes_in[...]
+    faces = (faces_in[0:8, :], faces_in[8:16, :], faces_in[16:24, :])
+    moves = []
+    sides = ((low_own, low_got, x_low, 0, 0), (high_own, high_got, x_high, cx - 1, cx))
+    for n, (own, got, out, x, at) in enumerate(sides):
+        t = harmonic(own[0], got[0])
+        inverse = inverse_of(own[1] + t)
+        z = inverse * own[2]
+        d = z / theta
+        out[...] = inverse_of(got[1] + t) * got[2] / theta
+        keep_planes(planes, d, x)
+        faces = pack_faces(faces, y_tiles(d), x)
+        for m, (value, ref, to) in enumerate(((inverse, inv, x), (z, z_out, x), (d, d_out, x), (t, tx, at))):
+            slabs[4 * n + m] = value
+            moves.append(pltpu.make_async_copy(slabs.at[4 * n + m], ref.at[to], sem.at[4 * n + m]))
+            moves[-1].start()
     emit(l_ref, a8_out, planes, faces, row_ref, pick_ref, far_x)
+    for move in moves:
+        move.wait()
 
 
 def sweep_kernel(c1, c2, first, last, l_ref, d_in, z_in, *refs):
@@ -407,6 +428,7 @@
 
 VMEM = pl.BlockSpec(memory_space=pltpu.VMEM)
 SMEM = pl.BlockSpec(memory_space=pltpu.SMEM)
+ANY = pl.BlockSpec(memory_space=pl.ANY)
 HBM = pl.BlockSpec(memory_space=pltpu.HBM)
 PARAMS = pltpu.CompilerParams(vmem_limit_bytes=24 << 20)
 
@@ -471,14 +493,23 @@
     )(l, rhs, accumulation, permeability, before, after, below, above, a8)
     low_got = lax.ppermute(high_edge, "gx", up_x)
     high_got = lax.ppermute(low_edge, "gx", down_x)
-    inv, z, d, tx, tym, typ, tzm, tzp, xlow, xhigh, a8 = pl.pallas_call(
+    inv, z, d, tx, tym, typ, tzm, tzp, faces, planes = pl.pallas_call(
         setup_kernel,
-        out_shape=(big, big, big, tall, big, big, big, big, edge, edge, sent),
-        in_specs=[SMEM] + [VMEM] * 12,
-        out_specs=(VMEM,) * 11,
-        scratch_shapes=scratch,
+        out_shape=(big, big, big, tall, big, big, big, big)
+        + (struct(BOTH_ROWS, cz), struct(4, cx, cz)),
+        in_specs=[VMEM] * 7,
+        out_specs=(VMEM,) * 10,
         compiler_params=PARAMS,
-    )(l, rhs, accumulation, permeability, before, after, faces, fault, low_got, high_got, row, pick, far_x)
+    )(rhs, accumulation, permeability, before, after, faces, fault)
+    inv, z, d, tx, xlow, xhigh, a8 = pl.pallas_call(
+        finish_kernel,
+        out_shape=(big, big, big, tall, edge, edge, sent),
+        in_specs=[SMEM] + [VMEM] * 9 + [ANY] * 4,
+        out_specs=(ANY,) * 4 + (VMEM,) * 3,
+        scratch_shapes=scratch + [pltpu.VMEM((8, ye, cz), f32), pltpu.SemaphoreType.DMA((8,))],
+        input_output_aliases={10: 0, 11: 1, 12: 2, 13: 3},
+        compiler_params=PARAMS,
+    )(l, low_edge, high_edge, low_got, high_got, faces, planes, row, pick, far_x, inv, z, d, tx)
 
     rho = 1.0 / sigma
     corr = None

time: 185 us -> 185 us (level)
  waiting for transfers between devices: 35.8 us -> 27 us
  starting transfers between devices: 48.9 us -> 57.2 us
    ppermute x1, waiting for transfers between devices: 4.29 us -> 0.01 us  [local(): high_got = lax.ppermute(low_edge, 'gx', down_x)]
    ppermute x4, starting transfers between devices: 8.63 us -> 12.5 us  [local(): xlow = lax.ppermute(d_last, 'gx', up_x)]
    all_to_all x4, waiting for transfers between devices: 28.1 us -> 24.3 us  [local(): a8 = lax.all_to_all(a8, 'gz', 0, 0, tiled=True)]
    all_to_all x4, starting transfers between devices: 19.8 us -> 23.6 us  [local(): a8 = lax.all_to_all(a8, 'gz', 0, 0, tiled=True)]
    unnamed x106 -> x108, local copies, waits for them, and re-layouts: 37 us -> 37.1 us
  transfers between devices with their start and end apart: 18 -> 18, of which waited for: 7 -> 5; matrix products, arithmetic and copies ran while one was open for 0% -> 0% of each run, Pallas kernels for 2% -> 3%
where the time goes in v8:
time: 185 us; the launch traced here: 183 us
  starting transfers between devices  57.2 us (31%)
  local copies, waits for them, and re-layouts  37.1 us (20%)
  blocking collectives  34.5 us (19%)
  Pallas kernels  27 us (15%)
  waiting for transfers between devices  27 us (15%)
    unnamed x108, local copies, waits for them, and re-layouts  37.1 us
    all_to_all x2, blocking collectives, local(): a8 = lax.all_to_all(a8, 'gz', 0, 0, tiled=True)  34.5 us
    all_to_all x4, waiting for transfers between devices, local(): a8 = lax.all_to_all(a8, 'gz', 0, 0, tiled=True)  24.3 us
    all_to_all x4, starting transfers between devices, local(): a8 = lax.all_to_all(a8, 'gz', 0, 0, tiled=True)  23.6 us
    pallas_call x5, Pallas kernels, local(): pl.pallas_call(kernel, out_shape=small if last else (big, big, small, edg...  15 us
    ppermute x4, starting transfers between devices, local(): xlow = lax.ppermute(d_last, 'gx', up_x)  12.5 us
    ppermute x4, starting transfers between devices, local(): xhigh = lax.ppermute(d_first, 'gx', down_x)  5.17 us
    ppermute x1, starting transfers between devices, local(): low_got = lax.ppermute(high_edge, 'gx', up_x)  4.78 us
  transfers between devices with their start and end apart: 18, of which 5 were waited for; matrix products, arithmetic and copies ran while one was open for 0% of the time, Pallas kernels for 3%

profile of v8, /device:TPU:8, one launch (start us, length us, event | category | flops | bytes accessed | tf_op | source)
XLA Modules:
  0.0 183.2 jit_solution(4474433791615853936)
XLA Ops:
  0.0 3.2 %shard_map.73 = (f32[5,32,8,128]{3,2,1,0:T(8,128)}, f32[5,32,8,128]{3,2,1,0:T(8,128)}, f32[8,40,128]{2,1,0:T(8,128)}) custom-call(s32[1]{0:T(128)} %bitcast.l_ref.refs_0_, f32[32,32,128]{2,1,0:T(8,128)} %rhs.5, f32[32,32,128]{2,1,0:T(8,128)} %acc.5, f32[3,32,32,128]{3,2,1,0:T(8,128)} %perm.5, s32[1,512]{1,0:T(1,128)} %bitcast.5, s32[1,512]{1,0:T(1,128)} %bitcast.6, ...), custom_call_target="tpu_custom_call" | custom-call | tf_op jit(solution)/shard_map/pallas_call | solution.py:457
  5.2 3.6 %collective-permute-start.1 = (f32[5,32,8,128]{3,2,1,0:T(8,128)}, f32[5,32,8,128]{3,2,1,0:T(8,128)S(1)}, u32[]{:S(2)}, u32[]{:S(2)}) collective-permute-start(f32[5,32,8,128]{3,2,1,0:T(8,128)} %get-tuple-element.69), channel_id=1, source_target_pairs={{8,0},{16,8},{24,16},{32,24},{40,32},{48,40},{56,48},{9,1},{17,9},... | collective-permute-start | bytes 1966088 | tf_op jit(solution)/shard_map/ppermute | solution.py:467
  8.8 21.6 %all_to_all.30.a8 = f32[8,40,128]{2,1,0:T(8,128)S(1)} all-to-all(f32[8,40,128]{2,1,0:T(8,128)} %get-tuple-element.70), channel_id=1, replica_groups=mesh['gx'=4,'gy'=8,'gz'=8] {'gz'}, dimensions={0} | all-to-all | bytes 327680 | tf_op jit(solution)/shard_map/all_to_all | solution.py:468
  32.5 2.4 %collective-permute-start.2 = (f32[24,128]{1,0:T(8,128)S(1)}, f32[24,128]{1,0:T(8,128)S(1)}, u32[]{:S(2)}, u32[]{:S(2)}) collective-permute-start(f32[24,128]{1,0:T(8,128)S(1)} %get-tuple-element.71), channel_id=1, source_target_pairs={{0,8},{8,16},{16,24},{24,32},{32,40},{40,48},{48,56},{1,9},{9,17},... | collective-permute-start | bytes 36872 | tf_op jit(solution)/shard_map/ppermute | solution.py:476
  34.9 2.6 %collective-permute-done.2.below = f32[24,128]{1,0:T(8,128)S(1)} collective-permute-done((f32[24,128]{1,0:T(8,128)S(1)}, f32[24,128]{1,0:T(8,128)S(1)}, u32[]{:S(2)}, u32[]{:S(2)}) %collective-permute-start.2) | collective-permute-done | bytes 12320 | tf_op jit(solution)/shard_map/ppermute | solution.py:476
  41.2 4.8 %collective-permute-start.4 = (f32[3,48,128]{2,1,0:T(8,128)S(1)}, f32[3,48,128]{2,1,0:T(8,128)S(1)}, u32[]{:S(2)}, u32[]{:S(2)}) collective-permute-start(f32[3,48,128]{2,1,0:T(8,128)S(1)} %get-tuple-element.74.high_own), channel_id=1, source_target_pairs={{0,64},{64,128},{128,192},{1,65},{65,129},{129,193},{2,66},{66,130... | collective-permute-start | bytes 221192 | tf_op jit(solution)/shard_map/ppermute | solution.py:494
  46.0 2.3 %shard_map.76 = (f32[32,48,128]{2,1,0:T(8,128)S(1)}, f32[32,48,128]{2,1,0:T(8,128)S(1)}, f32[32,48,128]{2,1,0:T(8,128)S(1)}, f32[33,48,128]{2,1,0:T(8,128)S(1)},...) custom-call(f32[32,32,128]{2,1,0:T(8,128)S(1)} %copy-done.27, ...), custom_call_target="tpu_custom_call" | custom-call | tf_op jit(solution)/shard_map/pallas_call | solution.py:496
  49.6 12.9 %all_to_all.31.a8.refs_5_ = f32[8,32,128]{2,1,0:T(8,128)S(1)} all-to-all(f32[8,32,128]{2,1,0:T(8,128)S(1)} %get-tuple-element.90), channel_id=1, replica_groups=mesh['gx'=4,'gy'=8,'gz'=8] {'gz'}, dimensions={0} | all-to-all | bytes 262144 | tf_op jit(solution)/shard_map/all_to_all | solution.py:524
  63.3 3.3 %shard_map.79 = (f32[32,48,128]{2,1,0:T(8,128)S(1)}, f32[32,48,128]{2,1,0:T(8,128)S(1)}, f32[32,32,128]{2,1,0:T(8,128)S(1)}, f32[48,128]{1,0:T(8,128)S(1)}, f32[...) custom-call(s32[1]{0:T(128)} %bitcast.l_ref.refs_0_, f32[32,48,128]{2,1,0:T(8,128)S(1)} %get-tuple-element.86.refs_1_, ...), custom_call_target="tpu_custom_call" | custom-call | tf_op jit(solution)/shard_map/pallas_call | solution.py:539
  69.3 3.4 %all-to-all-start.2 = ((f32[8,32,128]{2,1,0:T(8,128)}), f32[8,32,128]{2,1,0:T(8,128)S(1)}, u32[]{:S(2)}, u32[]{:S(2)}) async-start(f32[8,32,128]{2,1,0:T(8,128)} %get-tuple-element.102), calls=%async_computation.2 | async-start | bytes 262144 | tf_op jit(solution)/shard_map/all_to_all | solution.py:524
  72.7 3.9 %collective-permute-start.6 = (f32[48,128]{1,0:T(8,128)S(1)}, f32[48,128]{1,0:T(8,128)S(1)}, u32[]{:S(2)}, u32[]{:S(2)}) collective-permute-start(f32[48,128]{1,0:T(8,128)S(1)} %get-tuple-element.100), channel_id=1, source_target_pairs={{0,64},{64,128},{128,192},{1,65},{65,129},{129,193},{2,66},{66,130... | collective-permute-start | bytes 73736 | tf_op jit(solution)/shard_map/ppermute | solution.py:522
  77.9 5.2 %all-to-all-done.2.a8.refs_6_ = f32[8,32,128]{2,1,0:T(8,128)S(1)} async-done(((f32[8,32,128]{2,1,0:T(8,128)}), f32[8,32,128]{2,1,0:T(8,128)S(1)}, u32[]{:S(2)}, u32[]{:S(2)}) %all-to-all-start.2) | async-done | bytes 131104 | tf_op jit(solution)/shard_map/all_to_all | solution.py:524
  90.3 3.2 %shard_map.81 = (f32[32,48,128]{2,1,0:T(8,128)S(1)}, f32[32,48,128]{2,1,0:T(8,128)S(1)}, f32[32,32,128]{2,1,0:T(8,128)S(1)}, f32[48,128]{1,0:T(8,128)S(1)}, f32[...) custom-call(s32[1]{0:T(128)} %bitcast.l_ref.refs_0_, f32[32,48,128]{2,1,0:T(8,128)S(1)} %copy-done.43, ...), custom_call_target="tpu_custom_call" | custom-call | tf_op jit(solution)/shard_map/pallas_call | solution.py:539
  96.1 7.2 %all-to-all-start.3 = ((f32[8,32,128]{2,1,0:T(8,128)}), f32[8,32,128]{2,1,0:T(8,128)S(1)}, u32[]{:S(2)}, u32[]{:S(2)}) async-start(f32[8,32,128]{2,1,0:T(8,128)} %get-tuple-element.108), calls=%async_computation.3 | async-start | bytes 262144 | tf_op jit(solution)/shard_map/all_to_all | solution.py:524
  103.3 3.8 %collective-permute-start.8 = (f32[48,128]{1,0:T(8,128)S(1)}, f32[48,128]{1,0:T(8,128)S(1)}, u32[]{:S(2)}, u32[]{:S(2)}) collective-permute-start(f32[48,128]{1,0:T(8,128)S(1)} %get-tuple-element.106), channel_id=1, source_target_pairs={{0,64},{64,128},{128,192},{1,65},{65,129},{129,193},{2,66},{66,130... | collective-permute-start | bytes 73736 | tf_op jit(solution)/shard_map/ppermute | solution.py:522
  108.4 5.5 %all-to-all-done.3.a8.refs_6_ = f32[8,32,128]{2,1,0:T(8,128)S(1)} async-done(((f32[8,32,128]{2,1,0:T(8,128)}), f32[8,32,128]{2,1,0:T(8,128)S(1)}, u32[]{:S(2)}, u32[]{:S(2)}) %all-to-all-start.3) | async-done | bytes 131104 | tf_op jit(solution)/shard_map/all_to_all | solution.py:524
  121.0 3.2 %shard_map.83 = (f32[32,48,128]{2,1,0:T(8,128)S(1)}, f32[32,48,128]{2,1,0:T(8,128)S(1)}, f32[32,32,128]{2,1,0:T(8,128)S(1)}, f32[48,128]{1,0:T(8,128)S(1)}, f32[...) custom-call(s32[1]{0:T(128)} %bitcast.l_ref.refs_0_, f32[32,48,128]{2,1,0:T(8,128)S(1)} %copy-done.35, ...), custom_call_target="tpu_custom_call" | custom-call | tf_op jit(solution)/shard_map/pallas_call | solution.py:539
  126.9 7.0 %all-to-all-start.4 = ((f32[8,32,128]{2,1,0:T(8,128)}), f32[8,32,128]{2,1,0:T(8,128)S(1)}, u32[]{:S(2)}, u32[]{:S(2)}) async-start(f32[8,32,128]{2,1,0:T(8,128)} %get-tuple-element.114), calls=%async_computation.4 | async-start | bytes 262144 | tf_op jit(solution)/shard_map/all_to_all | solution.py:524
  133.8 2.9 %collective-permute-start.10 = (f32[48,128]{1,0:T(8,128)S(1)}, f32[48,128]{1,0:T(8,128)S(1)}, u32[]{:S(2)}, u32[]{:S(2)}) collective-permute-start(f32[48,128]{1,0:T(8,128)S(1)} %get-tuple-element.112), channel_id=1, source_target_pairs={{0,64},{64,128},{128,192},{1,65},{65,129},{129,193},{2,66},{66,130... | collective-permute-start | bytes 73736 | tf_op jit(solution)/shard_map/ppermute | solution.py:522
  138.0 6.3 %all-to-all-done.4.a8.refs_6_ = f32[8,32,128]{2,1,0:T(8,128)S(1)} async-done(((f32[8,32,128]{2,1,0:T(8,128)}), f32[8,32,128]{2,1,0:T(8,128)S(1)}, u32[]{:S(2)}, u32[]{:S(2)}) %all-to-all-start.4) | async-done | bytes 131104 | tf_op jit(solution)/shard_map/all_to_all | solution.py:524
  151.6 3.2 %shard_map.85 = (f32[32,48,128]{2,1,0:T(8,128)S(1)}, f32[32,48,128]{2,1,0:T(8,128)S(1)}, f32[32,32,128]{2,1,0:T(8,128)S(1)}, f32[48,128]{1,0:T(8,128)S(1)}, f32[...) custom-call(s32[1]{0:T(128)} %bitcast.l_ref.refs_0_, f32[32,48,128]{2,1,0:T(8,128)S(1)} %copy-done.39, ...), custom_call_target="tpu_custom_call" | custom-call | tf_op jit(solution)/shard_map/pallas_call | solution.py:539
  157.4 6.1 %all-to-all-start.5 = ((f32[8,32,128]{2,1,0:T(8,128)}), f32[8,32,128]{2,1,0:T(8,128)S(1)}, u32[]{:S(2)}, u32[]{:S(2)}) async-start(f32[8,32,128]{2,1,0:T(8,128)} %get-tuple-element.120), calls=%async_computation.5 | async-start | bytes 262144 | tf_op jit(solution)/shard_map/all_to_all | solution.py:524
  166.7 7.3 %all-to-all-done.5.a8.refs_6_ = f32[8,32,128]{2,1,0:T(8,128)S(1)} async-done(((f32[8,32,128]{2,1,0:T(8,128)}), f32[8,32,128]{2,1,0:T(8,128)S(1)}, u32[]{:S(2)}, u32[]{:S(2)}) %all-to-all-start.5) | async-done | bytes 131104 | tf_op jit(solution)/shard_map/all_to_all | solution.py:524
  181.2 2.0 %shard_map.87 = f32[32,32,128]{2,1,0:T(8,128)} custom-call(s32[1]{0:T(128)} %bitcast.l_ref.refs_0_, f32[32,48,128]{2,1,0:T(8,128)S(1)} %copy-done.31, f32[32,48,128]{2,1,0:T(8,128)S(1)} %copy-done.33, f32[32,32,128]{2,1,0:T(8,128)S(1)} %copy-done.47, f32[48,128]{1,0:T(8,128)S(1)} %collective-permute-done.12.refs_4_, ...), custom_call_target="tpu_custom_call" | custom-call | tf_op jit(solution)/shard_map/pallas_call | solution.py:539
  (137 shorter events, 55.9 us)
Async XLA Ops:
  0.0 37.5 %copy-start.28 = (f32[32,32,128]{2,1,0:T(8,128)S(1)}, f32[32,32,128]{2,1,0:T(8,128)}, u32[]{:S(2)}) copy-start(f32[32,32,128]{2,1,0:T(8,128)} %acc.5) | copy-start | bytes 1572868
  0.0 37.5 %copy-start.27 = (f32[32,32,128]{2,1,0:T(8,128)S(1)}, f32[32,32,128]{2,1,0:T(8,128)}, u32[]{:S(2)}) copy-start(f32[32,32,128]{2,1,0:T(8,128)} %rhs.5) | copy-start | bytes 1572868
  3.3 34.3 %collective-permute-start = (f32[5,32,8,128]{3,2,1,0:T(8,128)}, f32[5,32,8,128]{3,2,1,0:T(8,128)S(1)}, u32[]{:S(2)}, u32[]{:S(2)}) collective-permute-start(f32[5,32,8,128]{3,2,1,0:T(8,128)} %get-tuple-element.68), channel_id=1, source_target_pairs={{0,8},{8,16},{16,24},{24,32},{32,40},{40,48},{48,56},{1,9},{9,17},... | collective-permute-start | bytes 1966088 | tf_op jit(solution)/shard_map/ppermute | solution.py:466
  5.2 32.3 %collective-permute-start.1 = (f32[5,32,8,128]{3,2,1,0:T(8,128)}, f32[5,32,8,128]{3,2,1,0:T(8,128)S(1)}, u32[]{:S(2)}, u32[]{:S(2)}) collective-permute-start(f32[5,32,8,128]{3,2,1,0:T(8,128)} %get-tuple-element.69), channel_id=1, source_target_pairs={{8,0},{16,8},{24,16},{32,24},{40,32},{48,40},{56,48},{9,1},{17,9},... | collective-permute-start | bytes 1966088 | tf_op jit(solution)/shard_map/ppermute | solution.py:467
  30.6 6.9 %collective-permute-start.3 = (f32[216,128]{1,0:T(8,128)S(1)}, f32[216,128]{1,0:T(8,128)S(1)}, u32[]{:S(2)}, u32[]{:S(2)}) collective-permute-start(f32[216,128]{1,0:T(8,128)S(1)} %get-tuple-element.72), channel_id=1, source_target_pairs={{8,0},{16,8},{24,16},{32,24},{40,32},{48,40},{56,48},{9,1},{17,9},... | collective-permute-start | bytes 331784 | tf_op jit(solution)/shard_map/ppermute | solution.py:477
  32.5 5.0 %collective-permute-start.2 = (f32[24,128]{1,0:T(8,128)S(1)}, f32[24,128]{1,0:T(8,128)S(1)}, u32[]{:S(2)}, u32[]{:S(2)}) collective-permute-start(f32[24,128]{1,0:T(8,128)S(1)} %get-tuple-element.71), channel_id=1, source_target_pairs={{0,8},{8,16},{16,24},{24,32},{32,40},{40,48},{48,56},{1,9},{9,17},... | collective-permute-start | bytes 36872 | tf_op jit(solution)/shard_map/ppermute | solution.py:476
  39.9 8.5 %collective-permute-start.5 = (f32[3,48,128]{2,1,0:T(8,128)S(1)}, f32[3,48,128]{2,1,0:T(8,128)S(1)}, u32[]{:S(2)}, u32[]{:S(2)}) collective-permute-start(f32[3,48,128]{2,1,0:T(8,128)S(1)} %get-tuple-element.73.low_own), channel_id=1, source_target_pairs={{64,0},{128,64},{192,128},{65,1},{129,65},{193,129},{66,2},{130,66... | collective-permute-start | bytes 221192 | tf_op jit(solution)/shard_map/ppermute | solution.py:495
  41.2 7.2 %collective-permute-start.4 = (f32[3,48,128]{2,1,0:T(8,128)S(1)}, f32[3,48,128]{2,1,0:T(8,128)S(1)}, u32[]{:S(2)}, u32[]{:S(2)}) collective-permute-start(f32[3,48,128]{2,1,0:T(8,128)S(1)} %get-tuple-element.74.high_own), channel_id=1, source_target_pairs={{0,64},{64,128},{128,192},{1,65},{65,129},{129,193},{2,66},{66,130... | collective-permute-start | bytes 221192 | tf_op jit(solution)/shard_map/ppermute | solution.py:494
  48.3 15.0 %copy-start.5 = (f32[32,48,128]{2,1,0:T(8,128)}, f32[32,48,128]{2,1,0:T(8,128)S(1)}, u32[]{:S(2)}) copy-start(f32[32,48,128]{2,1,0:T(8,128)S(1)} %get-tuple-element.93.refs_9_.refs_10_) | copy-start | bytes 2359300
  48.4 15.0 %copy-start.10 = (f32[32,48,128]{2,1,0:T(8,128)}, f32[32,48,128]{2,1,0:T(8,128)S(1)}, u32[]{:S(2)}) copy-start(f32[32,48,128]{2,1,0:T(8,128)S(1)} %get-tuple-element.94.refs_10_.refs_11_) | copy-start | bytes 2359300
  48.4 15.0 %copy-start.15 = (f32[32,48,128]{2,1,0:T(8,128)}, f32[32,48,128]{2,1,0:T(8,128)S(1)}, u32[]{:S(2)}) copy-start(f32[32,48,128]{2,1,0:T(8,128)S(1)} %get-tuple-element.95.refs_11_.refs_12_) | copy-start | bytes 2359300
  49.5 17.1 %copy-start = (f32[32,48,128]{2,1,0:T(8,128)}, f32[32,48,128]{2,1,0:T(8,128)S(1)}, u32[]{:S(2)}) copy-start(f32[32,48,128]{2,1,0:T(8,128)S(1)} %get-tuple-element.91.refs_7_.refs_8_) | copy-start | bytes 2359300
  69.3 13.8 %all-to-all-start.2 = ((f32[8,32,128]{2,1,0:T(8,128)}), f32[8,32,128]{2,1,0:T(8,128)S(1)}, u32[]{:S(2)}, u32[]{:S(2)}) async-start(f32[8,32,128]{2,1,0:T(8,128)} %get-tuple-element.102), calls=%async_computation.2 | async-start | bytes 262144 | tf_op jit(solution)/shard_map/all_to_all | solution.py:524
  72.7 11.3 %collective-permute-start.6 = (f32[48,128]{1,0:T(8,128)S(1)}, f32[48,128]{1,0:T(8,128)S(1)}, u32[]{:S(2)}, u32[]{:S(2)}) collective-permute-start(f32[48,128]{1,0:T(8,128)S(1)} %get-tuple-element.100), channel_id=1, source_target_pairs={{0,64},{64,128},{128,192},{1,65},{65,129},{129,193},{2,66},{66,130... | collective-permute-start | bytes 73736 | tf_op jit(solution)/shard_map/ppermute | solution.py:522
  76.6 7.4 %collective-permute-start.7 = (f32[48,128]{1,0:T(8,128)S(1)}, f32[48,128]{1,0:T(8,128)S(1)}, u32[]{:S(2)}, u32[]{:S(2)}) collective-permute-start(f32[48,128]{1,0:T(8,128)S(1)} %get-tuple-element.101), channel_id=1, source_target_pairs={{64,0},{128,64},{192,128},{65,1},{129,65},{193,129},{66,2},{130,66... | collective-permute-start | bytes 73736 | tf_op jit(solution)/shard_map/ppermute | solution.py:523
  96.1 17.7 %all-to-all-start.3 = ((f32[8,32,128]{2,1,0:T(8,128)}), f32[8,32,128]{2,1,0:T(8,128)S(1)}, u32[]{:S(2)}, u32[]{:S(2)}) async-start(f32[8,32,128]{2,1,0:T(8,128)} %get-tuple-element.108), calls=%async_computation.3 | async-start | bytes 262144 | tf_op jit(solution)/shard_map/all_to_all | solution.py:524
  103.3 11.5 %collective-permute-start.8 = (f32[48,128]{1,0:T(8,128)S(1)}, f32[48,128]{1,0:T(8,128)S(1)}, u32[]{:S(2)}, u32[]{:S(2)}) collective-permute-start(f32[48,128]{1,0:T(8,128)S(1)} %get-tuple-element.106), channel_id=1, source_target_pairs={{0,64},{64,128},{128,192},{1,65},{65,129},{129,193},{2,66},{66,130... | collective-permute-start | bytes 73736 | tf_op jit(solution)/shard_map/ppermute | solution.py:522
  107.1 7.7 %collective-permute-start.9 = (f32[48,128]{1,0:T(8,128)S(1)}, f32[48,128]{1,0:T(8,128)S(1)}, u32[]{:S(2)}, u32[]{:S(2)}) collective-permute-start(f32[48,128]{1,0:T(8,128)S(1)} %get-tuple-element.107), channel_id=1, source_target_pairs={{64,0},{128,64},{192,128},{65,1},{129,65},{193,129},{66,2},{130,66... | collective-permute-start | bytes 73736 | tf_op jit(solution)/shard_map/ppermute | solution.py:523
  126.9 17.5 %all-to-all-start.4 = ((f32[8,32,128]{2,1,0:T(8,128)}), f32[8,32,128]{2,1,0:T(8,128)S(1)}, u32[]{:S(2)}, u32[]{:S(2)}) async-start(f32[8,32,128]{2,1,0:T(8,128)} %get-tuple-element.114), calls=%async_computation.4 | async-start | bytes 262144 | tf_op jit(solution)/shard_map/all_to_all | solution.py:524
  133.8 11.4 %collective-permute-start.10 = (f32[48,128]{1,0:T(8,128)S(1)}, f32[48,128]{1,0:T(8,128)S(1)}, u32[]{:S(2)}, u32[]{:S(2)}) collective-permute-start(f32[48,128]{1,0:T(8,128)S(1)} %get-tuple-element.112), channel_id=1, source_target_pairs={{0,64},{64,128},{128,192},{1,65},{65,129},{129,193},{2,66},{66,130... | collective-permute-start | bytes 73736 | tf_op jit(solution)/shard_map/ppermute | solution.py:522
  136.7 8.5 %collective-permute-start.11 = (f32[48,128]{1,0:T(8,128)S(1)}, f32[48,128]{1,0:T(8,128)S(1)}, u32[]{:S(2)}, u32[]{:S(2)}) collective-permute-start(f32[48,128]{1,0:T(8,128)S(1)} %get-tuple-element.113), channel_id=1, source_target_pairs={{64,0},{128,64},{192,128},{65,1},{129,65},{193,129},{66,2},{130,66... | collective-permute-start | bytes 73736 | tf_op jit(solution)/shard_map/ppermute | solution.py:523
  157.4 16.6 %all-to-all-start.5 = ((f32[8,32,128]{2,1,0:T(8,128)}), f32[8,32,128]{2,1,0:T(8,128)S(1)}, u32[]{:S(2)}, u32[]{:S(2)}) async-start(f32[8,32,128]{2,1,0:T(8,128)} %get-tuple-element.120), calls=%async_computation.5 | async-start | bytes 262144 | tf_op jit(solution)/shard_map/all_to_all | solution.py:524
  163.5 11.4 %collective-permute-start.12 = (f32[48,128]{1,0:T(8,128)S(1)}, f32[48,128]{1,0:T(8,128)S(1)}, u32[]{:S(2)}, u32[]{:S(2)}) collective-permute-start(f32[48,128]{1,0:T(8,128)S(1)} %get-tuple-element.118), channel_id=1, source_target_pairs={{0,64},{64,128},{128,192},{1,65},{65,129},{129,193},{2,66},{66,130... | collective-permute-start | bytes 73736 | tf_op jit(solution)/shard_map/ppermute | solution.py:522
  165.4 9.5 %collective-permute-start.13 = (f32[48,128]{1,0:T(8,128)S(1)}, f32[48,128]{1,0:T(8,128)S(1)}, u32[]{:S(2)}, u32[]{:S(2)}) collective-permute-start(f32[48,128]{1,0:T(8,128)S(1)} %get-tuple-element.119), channel_id=1, source_target_pairs={{64,0},{128,64},{192,128},{65,1},{129,65},{193,129},{66,2},{130,66... | collective-permute-start | bytes 73736 | tf_op jit(solution)/shard_map/ppermute | solution.py:523
  (48 other events, 79.7 us)

commit v9 on v8

--- a/solution.py
+++ b/solution.py
@@ -128,10 +128,12 @@
     return jnp.concatenate([first, second, third], axis=0)
 
 
-def unpacked(faces, slab, x):
+def unpacked(faces, slab, x, skip=0):
     lane = lane_iota((8, 128))
     lows, highs = [], []
-    for n, tile in enumerate(y_tiles(slab)):
+    tiles = y_tiles(slab)
+    for n in range(skip, len(tiles) - skip):
+        tile = tiles[n]
         packed = faces[8 * (n % 3) : 8 * (n % 3) + 8]
         outer = pltpu.roll(packed, (127 - 64 * (n // 3) - 2 * x) % 128, 1)
         lows.append(jnp.where(lane == 0, outer, pltpu.roll(tile, 1, 1)))
@@ -190,22 +192,27 @@
         down[at : at + LIST_ROWS, :] = a8[t, FACE_ROWS:, :]
 
 
-def emit(l_ref, a8_ref, planes, faces, row_ref, pick_ref, far_x):
+def emit(l_ref, a8_ref, planes, faces, row_ref, pick_ref, far_x, final=False):
     tiles = a8_ref.shape[0]
     cx = planes.shape[1]
     slots = row_ref.shape[2]
     put_faces(l_ref[0], a8_ref, faces)
+    base = FACE_ROWS
     for q in range(2):
-        base = FACE_ROWS + q * 2 * SLOT_ROWS
-        near = gather(
-            planes[2 * q + 1], picks(slot_row(row_ref, q, NEAR_Z)), rows_hit(slot_row(row_ref, q, NEAR_X), cx)
-        )
-        near = slot_row(row_ref, q, WEIGHT) * near
-        for t in range(tiles):
-            at = slice(t * slots, (t + 1) * slots)
-            far = gather(planes[2 * q], pick_ref[q, :, at], rows_hit(far_x[q : q + 1, at], cx))
-            put_rows(a8_ref, t, base, near)
-            put_rows(a8_ref, t, base + SLOT_ROWS, far)
+        if not final or q == 1:
+            near = gather(
+                planes[2 * q + 1], picks(slot_row(row_ref, q, NEAR_Z)), rows_hit(slot_row(row_ref, q, NEAR_X), cx)
+            )
+            near = slot_row(row_ref, q, WEIGHT) * near
+            for t in range(tiles):
+                put_rows(a8_ref, t, base, near)
+            base = base + SLOT_ROWS
+        if not final or q == 0:
+            for t in range(tiles):
+                at = slice(t * slots, (t + 1) * slots)
+                far = gather(planes[2 * q], pick_ref[q, :, at], rows_hit(far_x[q : q + 1, at], cx))
+                put_rows(a8_ref, t, base, far)
+            base = base + SLOT_ROWS
 
 
 def keep_planes(planes, slab, x):
@@ -214,12 +221,14 @@
         planes[n, pl.ds(x, 1), :] = slab[y : y + 1, :]
 
 
-def with_fault(total, fault, x):
+def with_fault(total, fault, x, first=0):
     tiles = y_tiles(total)
     y = lax.broadcasted_iota(jnp.int32, tiles[0].shape, 0)
-    last = total.shape[0] - H - 1
+    last = total.shape[0] + 2 * first - H - 1
     for n, at in enumerate((H - 1, H, last, last + 1)):
-        tiles[at // 8] += jnp.where(y == at % 8, fault[n, pl.ds(x, 1), :], 0.0)
+        at = at - first
+        if 0 <= at < total.shape[0]:
+            tiles[at // 8] += jnp.where(y == at % 8, fault[n, pl.ds(x, 1), :], 0.0)
     return jnp.concatenate(tiles, axis=0)
 
 
@@ -263,21 +272,26 @@
         fault[2 * q + 1] = near_sum(row_ref, q, slot_row(row_ref, q, WEIGHT), cx)
 
 
-def fault_kernel(a8, row_ref, pick_ref, far_x, fault):
-    tiles, rows = a8.shape[0], a8.shape[1]
+def fault_kernel(final, a8, row_ref, pick_ref, far_x, fault):
+    tiles = a8.shape[0]
     cx = fault.shape[1]
     slots = row_ref.shape[2]
+    base = FACE_ROWS
     for q in range(2):
-        base = rows - (2 - q) * 2 * SLOT_ROWS
-        far = jnp.zeros((cx, 128), f32)
-        near = jnp.zeros((1, slots), f32)
-        for t in range(tiles):
-            at = slice(t * slots, (t + 1) * slots)
-            values = get_rows(a8, t, base, SLOT_ROWS)
-            far = far + scatter(values, pick_ref[q, :, at], rows_hit(far_x[q : q + 1, at], cx))
-            near = near + get_rows(a8, t, base + SLOT_ROWS, SLOT_ROWS)
-        fault[2 * q] = far
-        fault[2 * q + 1] = near_sum(row_ref, q, slot_row(row_ref, q, WEIGHT) * near, cx)
+        if not final or q == 1:
+            far = jnp.zeros((cx, 128), f32)
+            for t in range(tiles):
+                at = slice(t * slots, (t + 1) * slots)
+                values = get_rows(a8, t, base, SLOT_ROWS)
+                far = far + scatter(values, pick_ref[q, :, at], rows_hit(far_x[q : q + 1, at], cx))
+            fault[2 * q] = far
+            base = base + SLOT_ROWS
+        if not final or q == 0:
+            near = jnp.zeros((1, slots), f32)
+            for t in range(tiles):
+                near = near + get_rows(a8, t, base, SLOT_ROWS)
+            fault[2 * q + 1] = near_sum(row_ref, q, slot_row(row_ref, q, WEIGHT) * near, cx)
+            base = base + SLOT_ROWS
 
 
 def extended(before, after, n, own, x):
@@ -381,7 +395,7 @@
         move.wait()
 
 
-def sweep_kernel(c1, c2, first, last, l_ref, d_in, z_in, *refs):
+def sweep_kernel(c1, c2, first, last, final, l_ref, d_in, z_in, *refs):
     refs = list(refs)
     corr_in = None if first else refs.pop(0)
     xlow, xhigh, a8, fault, inv, tx, tym, typ, tzm, tzp = refs[:10]
@@ -402,15 +416,18 @@
         faces, d_prev, d, t_low = carry
         t_high = tx[x + 1]
         d_next = jnp.where(x == cx - 1, xhigh[...], d_in[jnp.minimum(x + 1, cx - 1)])
-        z_low, z_high = unpacked(faces_in, d, x)
-        flow = t_low * d_prev + t_high * d_next
-        flow = flow + (tym[x] * pltpu.roll(d, 1, 0) + typ[x] * pltpu.roll(d, ye - 1, 0))
-        flow = flow + (tzm[x] * z_low + tzp[x] * z_high)
-        flow = with_fault(flow, fault, x)
-        z = z_in[x] - d + inv[x] * flow
-        new = c1 * d + c2 * z
-        before = d[H : H + cy] if first else corr_in[x]
-        corr_out[x] = before + new[H : H + cy]
+        skip = 1 if last else 0
+        rows = slice(8 * skip, ye - 8 * skip)
+        z_low, z_high = unpacked(faces_in, d, x, skip)
+        below, above = pltpu.roll(d, 1, 0)[rows], pltpu.roll(d, ye - 1, 0)[rows]
+        flow = t_low[rows] * d_prev[rows] + t_high[rows] * d_next[rows]
+        flow = flow + (tym[x, rows, :] * below + typ[x, rows, :] * above)
+        flow = flow + (tzm[x, rows, :] * z_low + tzp[x, rows, :] * z_high)
+        flow = with_fault(flow, fault, x, 8 * skip)
+        z = z_in[x, rows, :] - d[rows] + inv[x, rows, :] * flow
+        new = c1 * d[rows] + c2 * z
+        own = slice(H - 8 * skip, H - 8 * skip + cy)
+        corr_out[x] = (d[H : H + cy] if first else corr_in[x]) + new[own]
         if last:
             return faces, d, d_next, t_high
         d_out[x] = new
@@ -423,7 +440,7 @@
     if not last:
         d_first[...] = d_out[0]
         d_last[...] = d_out[cx - 1]
-        emit(l_ref, a8_out, planes, faces, row_ref, pick_ref, far_x)
+        emit(l_ref, a8_out, planes, faces, row_ref, pick_ref, far_x, final)
 
 
 VMEM = pl.BlockSpec(memory_space=pltpu.VMEM)
@@ -522,8 +539,12 @@
             xlow = lax.ppermute(d_last, "gx", up_x)
             xhigh = lax.ppermute(d_first, "gx", down_x)
         a8 = lax.all_to_all(a8, "gz", 0, 0, tiled=True)
+
+        def sums(*refs, final=last):
+            fault_kernel(final, *refs)
+
         fault = pl.pallas_call(
-            fault_kernel,
+            sums,
             out_shape=struct(4, cx, cz),
             in_specs=[VMEM] * 4,
             out_specs=VMEM,
@@ -533,8 +554,12 @@
         args += [xlow, xhigh, a8, fault, inv, tx, tym, typ, tzm, tzp]
         args += [] if last else [row, pick, far_x]
 
-        def kernel(*refs, c1=c1, c2=c2, first=first, last=last):
-            sweep_kernel(c1, c2, first, last, *refs)
+        final = sweep == SWEEPS - 2
+        rows = FACE_ROWS + (2 if final else 4) * SLOT_ROWS
+        sent = struct(tiles, rows, cz)
+
+        def kernel(*refs, c1=c1, c2=c2, first=first, last=last, final=final):
+            sweep_kernel(c1, c2, first, last, final, *refs)
 
         out = pl.pallas_call(
             kernel,

time: 185 us -> 185 us (level)
  no operation moved by 1% of the time
where the time goes in v9:
time: 185 us; the launch traced here: 183 us
  starting transfers between devices  57.2 us (31%)
  local copies, waits for them, and re-layouts  37.5 us (20%)
  blocking collectives  34.5 us (19%)
  waiting for transfers between devices  26.8 us (14%)
  Pallas kernels  26.4 us (14%)
    unnamed x108, local copies, waits for them, and re-layouts  37.5 us
    all_to_all x2, blocking collectives, local(): a8 = lax.all_to_all(a8, 'gz', 0, 0, tiled=True)  34.5 us
    all_to_all x4, waiting for transfers between devices, local(): a8 = lax.all_to_all(a8, 'gz', 0, 0, tiled=True)  24.1 us
    all_to_all x4, starting transfers between devices, local(): a8 = lax.all_to_all(a8, 'gz', 0, 0, tiled=True)  23.6 us
    pallas_call x5, Pallas kernels, local(): pl.pallas_call(kernel, out_shape=small if last else (big, big, small, edg...  14.7 us
    ppermute x4, starting transfers between devices, local(): xlow = lax.ppermute(d_last, 'gx', up_x)  12.5 us
    ppermute x4, starting transfers between devices, local(): xhigh = lax.ppermute(d_first, 'gx', down_x)  5.17 us
    ppermute x1, starting transfers between devices, local(): low_got = lax.ppermute(high_edge, 'gx', up_x)  4.78 us
  transfers between devices with their start and end apart: 18, of which 5 were waited for; matrix products, arithmetic and copies ran while one was open for 0% of the time, Pallas kernels for 3%

profile of v9, /device:TPU:8, one launch (start us, length us, event | category | flops | bytes accessed | tf_op | source)
XLA Modules:
  0.0 182.8 jit_solution(12198352929129508076)
XLA Ops:
  0.0 3.2 %shard_map.73 = (f32[5,32,8,128]{3,2,1,0:T(8,128)}, f32[5,32,8,128]{3,2,1,0:T(8,128)}, f32[8,40,128]{2,1,0:T(8,128)}) custom-call(s32[1]{0:T(128)} %bitcast.l_ref.refs_0_, f32[32,32,128]{2,1,0:T(8,128)} %rhs.5, f32[32,32,128]{2,1,0:T(8,128)} %acc.5, f32[3,32,32,128]{3,2,1,0:T(8,128)} %perm.5, s32[1,512]{1,0:T(1,128)} %bitcast.5, s32[1,512]{1,0:T(1,128)} %bitcast.6, ...), custom_call_target="tpu_custom_call" | custom-call | tf_op jit(solution)/shard_map/pallas_call | solution.py:474
  5.2 3.6 %collective-permute-start.1 = (f32[5,32,8,128]{3,2,1,0:T(8,128)}, f32[5,32,8,128]{3,2,1,0:T(8,128)S(1)}, u32[]{:S(2)}, u32[]{:S(2)}) collective-permute-start(f32[5,32,8,128]{3,2,1,0:T(8,128)} %get-tuple-element.69), channel_id=1, source_target_pairs={{8,0},{16,8},{24,16},{32,24},{40,32},{48,40},{56,48},{9,1},{17,9},... | collective-permute-start | bytes 1966088 | tf_op jit(solution)/shard_map/ppermute | solution.py:484
  8.8 21.6 %all_to_all.30.a8 = f32[8,40,128]{2,1,0:T(8,128)S(1)} all-to-all(f32[8,40,128]{2,1,0:T(8,128)} %get-tuple-element.70), channel_id=1, replica_groups=mesh['gx'=4,'gy'=8,'gz'=8] {'gz'}, dimensions={0} | all-to-all | bytes 327680 | tf_op jit(solution)/shard_map/all_to_all | solution.py:485
  32.5 2.4 %collective-permute-start.2 = (f32[24,128]{1,0:T(8,128)S(1)}, f32[24,128]{1,0:T(8,128)S(1)}, u32[]{:S(2)}, u32[]{:S(2)}) collective-permute-start(f32[24,128]{1,0:T(8,128)S(1)} %get-tuple-element.71), channel_id=1, source_target_pairs={{0,8},{8,16},{16,24},{24,32},{32,40},{40,48},{48,56},{1,9},{9,17},... | collective-permute-start | bytes 36872 | tf_op jit(solution)/shard_map/ppermute | solution.py:493
  34.9 2.6 %collective-permute-done.2.below = f32[24,128]{1,0:T(8,128)S(1)} collective-permute-done((f32[24,128]{1,0:T(8,128)S(1)}, f32[24,128]{1,0:T(8,128)S(1)}, u32[]{:S(2)}, u32[]{:S(2)}) %collective-permute-start.2) | collective-permute-done | bytes 12320 | tf_op jit(solution)/shard_map/ppermute | solution.py:493
  41.2 4.8 %collective-permute-start.4 = (f32[3,48,128]{2,1,0:T(8,128)S(1)}, f32[3,48,128]{2,1,0:T(8,128)S(1)}, u32[]{:S(2)}, u32[]{:S(2)}) collective-permute-start(f32[3,48,128]{2,1,0:T(8,128)S(1)} %get-tuple-element.74.high_own), channel_id=1, source_target_pairs={{0,64},{64,128},{128,192},{1,65},{65,129},{129,193},{2,66},{66,130... | collective-permute-start | bytes 221192 | tf_op jit(solution)/shard_map/ppermute | solution.py:511
  46.0 2.3 %shard_map.76 = (f32[32,48,128]{2,1,0:T(8,128)S(1)}, f32[32,48,128]{2,1,0:T(8,128)S(1)}, f32[32,48,128]{2,1,0:T(8,128)S(1)}, f32[33,48,128]{2,1,0:T(8,128)S(1)},...) custom-call(f32[32,32,128]{2,1,0:T(8,128)S(1)} %copy-done.27, ...), custom_call_target="tpu_custom_call" | custom-call | tf_op jit(solution)/shard_map/pallas_call | solution.py:513
  49.6 12.9 %all_to_all.31.refs_0_.refs_5_ = f32[8,32,128]{2,1,0:T(8,128)S(1)} all-to-all(f32[8,32,128]{2,1,0:T(8,128)S(1)} %get-tuple-element.90), channel_id=1, replica_groups=mesh['gx'=4,'gy'=8,'gz'=8] {'gz'}, dimensions={0} | all-to-all | bytes 262144 | tf_op jit(solution)/shard_map/all_to_all | solution.py:541
  63.3 3.3 %shard_map.79 = (f32[32,48,128]{2,1,0:T(8,128)S(1)}, f32[32,48,128]{2,1,0:T(8,128)S(1)}, f32[32,32,128]{2,1,0:T(8,128)S(1)}, f32[48,128]{1,0:T(8,128)S(1)}, f32[...) custom-call(s32[1]{0:T(128)} %bitcast.l_ref.refs_0_, f32[32,48,128]{2,1,0:T(8,128)S(1)} %get-tuple-element.86.refs_1_, ...), custom_call_target="tpu_custom_call" | custom-call | tf_op jit(solution)/shard_map/pallas_call | solution.py:564
  69.2 3.4 %all-to-all-start.2 = ((f32[8,32,128]{2,1,0:T(8,128)}), f32[8,32,128]{2,1,0:T(8,128)S(1)}, u32[]{:S(2)}, u32[]{:S(2)}) async-start(f32[8,32,128]{2,1,0:T(8,128)} %get-tuple-element.102), calls=%async_computation.2 | async-start | bytes 262144 | tf_op jit(solution)/shard_map/all_to_all | solution.py:541
  72.6 3.9 %collective-permute-start.6 = (f32[48,128]{1,0:T(8,128)S(1)}, f32[48,128]{1,0:T(8,128)S(1)}, u32[]{:S(2)}, u32[]{:S(2)}) collective-permute-start(f32[48,128]{1,0:T(8,128)S(1)} %get-tuple-element.100), channel_id=1, source_target_pairs={{0,64},{64,128},{128,192},{1,65},{65,129},{129,193},{2,66},{66,130... | collective-permute-start | bytes 73736 | tf_op jit(solution)/shard_map/ppermute | solution.py:539
  77.8 5.2 %all-to-all-done.2.refs_0_.refs_6_ = f32[8,32,128]{2,1,0:T(8,128)S(1)} async-done(((f32[8,32,128]{2,1,0:T(8,128)}), f32[8,32,128]{2,1,0:T(8,128)S(1)}, u32[]{:S(2)}, u32[]{:S(2)}) %all-to-all-start.2) | async-done | bytes 131104 | tf_op jit(solution)/shard_map/all_to_all | solution.py:541
  90.2 3.2 %shard_map.81 = (f32[32,48,128]{2,1,0:T(8,128)S(1)}, f32[32,48,128]{2,1,0:T(8,128)S(1)}, f32[32,32,128]{2,1,0:T(8,128)S(1)}, f32[48,128]{1,0:T(8,128)S(1)}, f32[...) custom-call(s32[1]{0:T(128)} %bitcast.l_ref.refs_0_, f32[32,48,128]{2,1,0:T(8,128)S(1)} %copy-done.43, ...), custom_call_target="tpu_custom_call" | custom-call | tf_op jit(solution)/shard_map/pallas_call | solution.py:564
  96.1 7.2 %all-to-all-start.3 = ((f32[8,32,128]{2,1,0:T(8,128)}), f32[8,32,128]{2,1,0:T(8,128)S(1)}, u32[]{:S(2)}, u32[]{:S(2)}) async-start(f32[8,32,128]{2,1,0:T(8,128)} %get-tuple-element.108), calls=%async_computation.3 | async-start | bytes 262144 | tf_op jit(solution)/shard_map/all_to_all | solution.py:541
  103.2 3.8 %collective-permute-start.8 = (f32[48,128]{1,0:T(8,128)S(1)}, f32[48,128]{1,0:T(8,128)S(1)}, u32[]{:S(2)}, u32[]{:S(2)}) collective-permute-start(f32[48,128]{1,0:T(8,128)S(1)} %get-tuple-element.106), channel_id=1, source_target_pairs={{0,64},{64,128},{128,192},{1,65},{65,129},{129,193},{2,66},{66,130... | collective-permute-start | bytes 73736 | tf_op jit(solution)/shard_map/ppermute | solution.py:539
  108.4 5.5 %all-to-all-done.3.refs_0_.refs_6_ = f32[8,32,128]{2,1,0:T(8,128)S(1)} async-done(((f32[8,32,128]{2,1,0:T(8,128)}), f32[8,32,128]{2,1,0:T(8,128)S(1)}, u32[]{:S(2)}, u32[]{:S(2)}) %all-to-all-start.3) | async-done | bytes 131104 | tf_op jit(solution)/shard_map/all_to_all | solution.py:541
  121.0 3.2 %shard_map.83 = (f32[32,48,128]{2,1,0:T(8,128)S(1)}, f32[32,48,128]{2,1,0:T(8,128)S(1)}, f32[32,32,128]{2,1,0:T(8,128)S(1)}, f32[48,128]{1,0:T(8,128)S(1)}, f32[...) custom-call(s32[1]{0:T(128)} %bitcast.l_ref.refs_0_, f32[32,48,128]{2,1,0:T(8,128)S(1)} %copy-done.35, ...), custom_call_target="tpu_custom_call" | custom-call | tf_op jit(solution)/shard_map/pallas_call | solution.py:564
  126.9 7.0 %all-to-all-start.4 = ((f32[8,32,128]{2,1,0:T(8,128)}), f32[8,32,128]{2,1,0:T(8,128)S(1)}, u32[]{:S(2)}, u32[]{:S(2)}) async-start(f32[8,32,128]{2,1,0:T(8,128)} %get-tuple-element.114), calls=%async_computation.4 | async-start | bytes 262144 | tf_op jit(solution)/shard_map/all_to_all | solution.py:541
  133.8 2.9 %collective-permute-start.10 = (f32[48,128]{1,0:T(8,128)S(1)}, f32[48,128]{1,0:T(8,128)S(1)}, u32[]{:S(2)}, u32[]{:S(2)}) collective-permute-start(f32[48,128]{1,0:T(8,128)S(1)} %get-tuple-element.112), channel_id=1, source_target_pairs={{0,64},{64,128},{128,192},{1,65},{65,129},{129,193},{2,66},{66,130... | collective-permute-start | bytes 73736 | tf_op jit(solution)/shard_map/ppermute | solution.py:539
  138.0 6.3 %all-to-all-done.4.refs_0_.refs_6_ = f32[8,32,128]{2,1,0:T(8,128)S(1)} async-done(((f32[8,32,128]{2,1,0:T(8,128)}), f32[8,32,128]{2,1,0:T(8,128)S(1)}, u32[]{:S(2)}, u32[]{:S(2)}) %all-to-all-start.4) | async-done | bytes 131104 | tf_op jit(solution)/shard_map/all_to_all | solution.py:541
  151.5 3.0 %shard_map.85 = (f32[32,48,128]{2,1,0:T(8,128)S(1)}, f32[32,48,128]{2,1,0:T(8,128)S(1)}, f32[32,32,128]{2,1,0:T(8,128)S(1)}, f32[48,128]{1,0:T(8,128)S(1)}, f32[...) custom-call(s32[1]{0:T(128)} %bitcast.l_ref.refs_0_, f32[32,48,128]{2,1,0:T(8,128)S(1)} %copy-done.39, ...), custom_call_target="tpu_custom_call" | custom-call | tf_op jit(solution)/shard_map/pallas_call | solution.py:564
  157.2 6.1 %all-to-all-start.5 = ((f32[8,24,128]{2,1,0:T(8,128)}), f32[8,24,128]{2,1,0:T(8,128)S(1)}, u32[]{:S(2)}, u32[]{:S(2)}) async-start(f32[8,24,128]{2,1,0:T(8,128)} %get-tuple-element.120), calls=%async_computation.5 | async-start | bytes 196608 | tf_op jit(solution)/shard_map/all_to_all | solution.py:541
  166.5 7.1 %all-to-all-done.5.refs_0_.refs_6_ = f32[8,24,128]{2,1,0:T(8,128)S(1)} async-done(((f32[8,24,128]{2,1,0:T(8,128)}), f32[8,24,128]{2,1,0:T(8,128)S(1)}, u32[]{:S(2)}, u32[]{:S(2)}) %all-to-all-start.5) | async-done | bytes 98336 | tf_op jit(solution)/shard_map/all_to_all | solution.py:541
  180.8 2.0 %shard_map.87 = f32[32,32,128]{2,1,0:T(8,128)} custom-call(s32[1]{0:T(128)} %bitcast.l_ref.refs_0_, f32[32,48,128]{2,1,0:T(8,128)S(1)} %copy-done.31, f32[32,48,128]{2,1,0:T(8,128)S(1)} %copy-done.33, f32[32,32,128]{2,1,0:T(8,128)S(1)} %copy-done.47, f32[48,128]{1,0:T(8,128)S(1)} %collective-permute-done.12.refs_4_, ...), custom_call_target="tpu_custom_call" | custom-call | tf_op jit(solution)/shard_map/pallas_call | solution.py:564
  (137 shorter events, 55.9 us)
Async XLA Ops:
  0.0 37.5 %copy-start.28 = (f32[32,32,128]{2,1,0:T(8,128)S(1)}, f32[32,32,128]{2,1,0:T(8,128)}, u32[]{:S(2)}) copy-start(f32[32,32,128]{2,1,0:T(8,128)} %acc.5) | copy-start | bytes 1572868
  0.0 37.5 %copy-start.27 = (f32[32,32,128]{2,1,0:T(8,128)S(1)}, f32[32,32,128]{2,1,0:T(8,128)}, u32[]{:S(2)}) copy-start(f32[32,32,128]{2,1,0:T(8,128)} %rhs.5) | copy-start | bytes 1572868
  3.3 34.3 %collective-permute-start = (f32[5,32,8,128]{3,2,1,0:T(8,128)}, f32[5,32,8,128]{3,2,1,0:T(8,128)S(1)}, u32[]{:S(2)}, u32[]{:S(2)}) collective-permute-start(f32[5,32,8,128]{3,2,1,0:T(8,128)} %get-tuple-element.68), channel_id=1, source_target_pairs={{0,8},{8,16},{16,24},{24,32},{32,40},{40,48},{48,56},{1,9},{9,17},... | collective-permute-start | bytes 1966088 | tf_op jit(solution)/shard_map/ppermute | solution.py:483
  5.2 32.3 %collective-permute-start.1 = (f32[5,32,8,128]{3,2,1,0:T(8,128)}, f32[5,32,8,128]{3,2,1,0:T(8,128)S(1)}, u32[]{:S(2)}, u32[]{:S(2)}) collective-permute-start(f32[5,32,8,128]{3,2,1,0:T(8,128)} %get-tuple-element.69), channel_id=1, source_target_pairs={{8,0},{16,8},{24,16},{32,24},{40,32},{48,40},{56,48},{9,1},{17,9},... | collective-permute-start | bytes 1966088 | tf_op jit(solution)/shard_map/ppermute | solution.py:484
  30.6 6.9 %collective-permute-start.3 = (f32[216,128]{1,0:T(8,128)S(1)}, f32[216,128]{1,0:T(8,128)S(1)}, u32[]{:S(2)}, u32[]{:S(2)}) collective-permute-start(f32[216,128]{1,0:T(8,128)S(1)} %get-tuple-element.72), channel_id=1, source_target_pairs={{8,0},{16,8},{24,16},{32,24},{40,32},{48,40},{56,48},{9,1},{17,9},... | collective-permute-start | bytes 331784 | tf_op jit(solution)/shard_map/ppermute | solution.py:494
  32.5 5.0 %collective-permute-start.2 = (f32[24,128]{1,0:T(8,128)S(1)}, f32[24,128]{1,0:T(8,128)S(1)}, u32[]{:S(2)}, u32[]{:S(2)}) collective-permute-start(f32[24,128]{1,0:T(8,128)S(1)} %get-tuple-element.71), channel_id=1, source_target_pairs={{0,8},{8,16},{16,24},{24,32},{32,40},{40,48},{48,56},{1,9},{9,17},... | collective-permute-start | bytes 36872 | tf_op jit(solution)/shard_map/ppermute | solution.py:493
  39.9 8.5 %collective-permute-start.5 = (f32[3,48,128]{2,1,0:T(8,128)S(1)}, f32[3,48,128]{2,1,0:T(8,128)S(1)}, u32[]{:S(2)}, u32[]{:S(2)}) collective-permute-start(f32[3,48,128]{2,1,0:T(8,128)S(1)} %get-tuple-element.73.low_own), channel_id=1, source_target_pairs={{64,0},{128,64},{192,128},{65,1},{129,65},{193,129},{66,2},{130,66... | collective-permute-start | bytes 221192 | tf_op jit(solution)/shard_map/ppermute | solution.py:512
  41.2 7.2 %collective-permute-start.4 = (f32[3,48,128]{2,1,0:T(8,128)S(1)}, f32[3,48,128]{2,1,0:T(8,128)S(1)}, u32[]{:S(2)}, u32[]{:S(2)}) collective-permute-start(f32[3,48,128]{2,1,0:T(8,128)S(1)} %get-tuple-element.74.high_own), channel_id=1, source_target_pairs={{0,64},{64,128},{128,192},{1,65},{65,129},{129,193},{2,66},{66,130... | collective-permute-start | bytes 221192 | tf_op jit(solution)/shard_map/ppermute | solution.py:511
  48.3 15.0 %copy-start.5 = (f32[32,48,128]{2,1,0:T(8,128)}, f32[32,48,128]{2,1,0:T(8,128)S(1)}, u32[]{:S(2)}) copy-start(f32[32,48,128]{2,1,0:T(8,128)S(1)} %get-tuple-element.93.refs_9_.refs_10_) | copy-start | bytes 2359300
  48.4 15.0 %copy-start.10 = (f32[32,48,128]{2,1,0:T(8,128)}, f32[32,48,128]{2,1,0:T(8,128)S(1)}, u32[]{:S(2)}) copy-start(f32[32,48,128]{2,1,0:T(8,128)S(1)} %get-tuple-element.94.refs_10_.refs_11_) | copy-start | bytes 2359300
  48.4 15.0 %copy-start.15 = (f32[32,48,128]{2,1,0:T(8,128)}, f32[32,48,128]{2,1,0:T(8,128)S(1)}, u32[]{:S(2)}) copy-start(f32[32,48,128]{2,1,0:T(8,128)S(1)} %get-tuple-element.95.refs_11_.refs_12_) | copy-start | bytes 2359300
  49.5 17.1 %copy-start = (f32[32,48,128]{2,1,0:T(8,128)}, f32[32,48,128]{2,1,0:T(8,128)S(1)}, u32[]{:S(2)}) copy-start(f32[32,48,128]{2,1,0:T(8,128)S(1)} %get-tuple-element.91.refs_7_.refs_8_) | copy-start | bytes 2359300
  69.2 13.8 %all-to-all-start.2 = ((f32[8,32,128]{2,1,0:T(8,128)}), f32[8,32,128]{2,1,0:T(8,128)S(1)}, u32[]{:S(2)}, u32[]{:S(2)}) async-start(f32[8,32,128]{2,1,0:T(8,128)} %get-tuple-element.102), calls=%async_computation.2 | async-start | bytes 262144 | tf_op jit(solution)/shard_map/all_to_all | solution.py:541
  72.6 11.3 %collective-permute-start.6 = (f32[48,128]{1,0:T(8,128)S(1)}, f32[48,128]{1,0:T(8,128)S(1)}, u32[]{:S(2)}, u32[]{:S(2)}) collective-permute-start(f32[48,128]{1,0:T(8,128)S(1)} %get-tuple-element.100), channel_id=1, source_target_pairs={{0,64},{64,128},{128,192},{1,65},{65,129},{129,193},{2,66},{66,130... | collective-permute-start | bytes 73736 | tf_op jit(solution)/shard_map/ppermute | solution.py:539
  76.5 7.4 %collective-permute-start.7 = (f32[48,128]{1,0:T(8,128)S(1)}, f32[48,128]{1,0:T(8,128)S(1)}, u32[]{:S(2)}, u32[]{:S(2)}) collective-permute-start(f32[48,128]{1,0:T(8,128)S(1)} %get-tuple-element.101), channel_id=1, source_target_pairs={{64,0},{128,64},{192,128},{65,1},{129,65},{193,129},{66,2},{130,66... | collective-permute-start | bytes 73736 | tf_op jit(solution)/shard_map/ppermute | solution.py:540
  96.1 17.7 %all-to-all-start.3 = ((f32[8,32,128]{2,1,0:T(8,128)}), f32[8,32,128]{2,1,0:T(8,128)S(1)}, u32[]{:S(2)}, u32[]{:S(2)}) async-start(f32[8,32,128]{2,1,0:T(8,128)} %get-tuple-element.108), calls=%async_computation.3 | async-start | bytes 262144 | tf_op jit(solution)/shard_map/all_to_all | solution.py:541
  103.2 11.5 %collective-permute-start.8 = (f32[48,128]{1,0:T(8,128)S(1)}, f32[48,128]{1,0:T(8,128)S(1)}, u32[]{:S(2)}, u32[]{:S(2)}) collective-permute-start(f32[48,128]{1,0:T(8,128)S(1)} %get-tuple-element.106), channel_id=1, source_target_pairs={{0,64},{64,128},{128,192},{1,65},{65,129},{129,193},{2,66},{66,130... | collective-permute-start | bytes 73736 | tf_op jit(solution)/shard_map/ppermute | solution.py:539
  107.1 7.7 %collective-permute-start.9 = (f32[48,128]{1,0:T(8,128)S(1)}, f32[48,128]{1,0:T(8,128)S(1)}, u32[]{:S(2)}, u32[]{:S(2)}) collective-permute-start(f32[48,128]{1,0:T(8,128)S(1)} %get-tuple-element.107), channel_id=1, source_target_pairs={{64,0},{128,64},{192,128},{65,1},{129,65},{193,129},{66,2},{130,66... | collective-permute-start | bytes 73736 | tf_op jit(solution)/shard_map/ppermute | solution.py:540
  126.9 17.5 %all-to-all-start.4 = ((f32[8,32,128]{2,1,0:T(8,128)}), f32[8,32,128]{2,1,0:T(8,128)S(1)}, u32[]{:S(2)}, u32[]{:S(2)}) async-start(f32[8,32,128]{2,1,0:T(8,128)} %get-tuple-element.114), calls=%async_computation.4 | async-start | bytes 262144 | tf_op jit(solution)/shard_map/all_to_all | solution.py:541
  133.8 11.4 %collective-permute-start.10 = (f32[48,128]{1,0:T(8,128)S(1)}, f32[48,128]{1,0:T(8,128)S(1)}, u32[]{:S(2)}, u32[]{:S(2)}) collective-permute-start(f32[48,128]{1,0:T(8,128)S(1)} %get-tuple-element.112), channel_id=1, source_target_pairs={{0,64},{64,128},{128,192},{1,65},{65,129},{129,193},{2,66},{66,130... | collective-permute-start | bytes 73736 | tf_op jit(solution)/shard_map/ppermute | solution.py:539
  136.7 8.5 %collective-permute-start.11 = (f32[48,128]{1,0:T(8,128)S(1)}, f32[48,128]{1,0:T(8,128)S(1)}, u32[]{:S(2)}, u32[]{:S(2)}) collective-permute-start(f32[48,128]{1,0:T(8,128)S(1)} %get-tuple-element.113), channel_id=1, source_target_pairs={{64,0},{128,64},{192,128},{65,1},{129,65},{193,129},{66,2},{130,66... | collective-permute-start | bytes 73736 | tf_op jit(solution)/shard_map/ppermute | solution.py:540
  157.2 16.5 %all-to-all-start.5 = ((f32[8,24,128]{2,1,0:T(8,128)}), f32[8,24,128]{2,1,0:T(8,128)S(1)}, u32[]{:S(2)}, u32[]{:S(2)}) async-start(f32[8,24,128]{2,1,0:T(8,128)} %get-tuple-element.120), calls=%async_computation.5 | async-start | bytes 196608 | tf_op jit(solution)/shard_map/all_to_all | solution.py:541
  163.3 10.9 %collective-permute-start.12 = (f32[48,128]{1,0:T(8,128)S(1)}, f32[48,128]{1,0:T(8,128)S(1)}, u32[]{:S(2)}, u32[]{:S(2)}) collective-permute-start(f32[48,128]{1,0:T(8,128)S(1)} %get-tuple-element.118), channel_id=1, source_target_pairs={{0,64},{64,128},{128,192},{1,65},{65,129},{129,193},{2,66},{66,130... | collective-permute-start | bytes 73736 | tf_op jit(solution)/shard_map/ppermute | solution.py:539
  165.2 9.0 %collective-permute-start.13 = (f32[48,128]{1,0:T(8,128)S(1)}, f32[48,128]{1,0:T(8,128)S(1)}, u32[]{:S(2)}, u32[]{:S(2)}) collective-permute-start(f32[48,128]{1,0:T(8,128)S(1)} %get-tuple-element.119), channel_id=1, source_target_pairs={{64,0},{128,64},{192,128},{65,1},{129,65},{193,129},{66,2},{130,66... | collective-permute-start | bytes 73736 | tf_op jit(solution)/shard_map/ppermute | solution.py:540
  (48 other events, 79.7 us)

commit v10 on v9

--- a/solution.py
+++ b/solution.py
@@ -187,9 +187,21 @@
     faces = get_faces(l_ref[0], a8)
     up[...] = faces
     down[0:BOTH_ROWS, :] = faces
+    here = l_ref[0].astype(f32)
+
+    def part(t, which):
+        at = FACE_ROWS + which * SLOT_ROWS
+        return a8[t, at : at + SLOT_ROWS, :]
+
+    at = BOTH_ROWS
     for t in range(tiles):
-        at = BOTH_ROWS + LIST_ROWS * t
-        down[at : at + LIST_ROWS, :] = a8[t, FACE_ROWS:, :]
+        x = jnp.where(part(t, FAR_TILE) == here, part(t, FAR_X), -1.0)
+        for values in (x, part(t, FAR_Z), part(t, WEIGHT)):
+            down[at : at + SLOT_ROWS, :] = values
+            at = at + SLOT_ROWS
+    for which in (NEAR_Z, NEAR_X, WEIGHT):
+        down[at : at + SLOT_ROWS, :] = part(l_ref[0], which)
+        at = at + SLOT_ROWS
 
 
 def emit(l_ref, a8_ref, planes, faces, row_ref, pick_ref, far_x, final=False):
@@ -242,32 +254,36 @@
     tiles = a8.shape[0]
     cx = fault.shape[1]
     slots = row_ref.shape[2]
-    first = above.shape[0] - tiles * LIST_ROWS
+    here = l.astype(f32)
 
     def codes(block):
-        parts = [block[n : n + 1] for n in range(LIST_ROWS)]
+        parts = [block[n : n + 1] for n in range(block.shape[0])]
+        count = len(parts) // SLOT_ROWS
         return [
-            jnp.concatenate(parts[SLOT_ROWS * n : SLOT_ROWS * (n + 1)], axis=1) for n in range(6)
+            jnp.concatenate(parts[SLOT_ROWS * n : SLOT_ROWS * (n + 1)], axis=1) for n in range(count)
         ]
 
-    def block(q, t):
-        if q == 0:
-            return a8[t, FACE_ROWS : FACE_ROWS + LIST_ROWS, :]
-        return above[pl.ds(pl.multiple_of(first + t * LIST_ROWS, 8), LIST_ROWS), :]
+    def relayed(t):
+        at = BOTH_ROWS + 3 * SLOT_ROWS * t
+        return codes(above[at : at + 3 * SLOT_ROWS, :])
 
     for q in range(2):
-        mine = codes(block(q, l))
+        mine = relayed(tiles) if q else codes(a8[l, FACE_ROWS : FACE_ROWS + LIST_ROWS, :])
         for n in range(3):
             row_ref[q, n : n + 1, :] = mine[n]
         far = jnp.zeros((cx, 128), f32)
         for t in range(tiles):
             at = slice(t * slots, (t + 1) * slots)
-            table = codes(block(q, t))
-            x = jnp.where(table[FAR_TILE] == l.astype(f32), table[FAR_X], -1.0)
-            pick = picks(table[FAR_Z])
+            if q:
+                x, z, weight = relayed(t)
+            else:
+                table = codes(a8[t, FACE_ROWS : FACE_ROWS + LIST_ROWS, :])
+                x = jnp.where(table[FAR_TILE] == here, table[FAR_X], -1.0)
+                z, weight = table[FAR_Z], table[WEIGHT]
+            pick = picks(z)
             pick_ref[q, :, at] = pick
             far_x[q : q + 1, at] = x
-            far = far + scatter(table[WEIGHT], pick, rows_hit(x, cx))
+            far = far + scatter(weight, pick, rows_hit(x, cx))
         fault[2 * q] = far
         fault[2 * q + 1] = near_sum(row_ref, q, slot_row(row_ref, q, WEIGHT), cx)
 
@@ -485,7 +501,7 @@
     a8 = lax.all_to_all(a8, "gz", 0, 0, tiled=True)
     below, above = pl.pallas_call(
         relay_kernel,
-        out_shape=(struct(BOTH_ROWS, cz), struct(BOTH_ROWS + tiles * LIST_ROWS, cz)),
+        out_shape=(struct(BOTH_ROWS, cz), struct(BOTH_ROWS + 3 * SLOT_ROWS * (tiles + 1), cz)),
         in_specs=[SMEM, VMEM],
         out_specs=(VMEM,) * 2,
         compiler_params=PARAMS,

time: 185 us -> 185 us (level)
  no operation moved by 1% of the time
where the time goes in v10:
time: 185 us; the launch traced here: 183 us
  starting transfers between devices  57.2 us (31%)
  local copies, waits for them, and re-layouts  37.5 us (20%)
  blocking collectives  34.5 us (19%)
  waiting for transfers between devices  26.8 us (14%)
  Pallas kernels  26.4 us (14%)
    unnamed x108, local copies, waits for them, and re-layouts  37.5 us
    all_to_all x2, blocking collectives, local(): a8 = lax.all_to_all(a8, 'gz', 0, 0, tiled=True)  34.5 us
    all_to_all x4, waiting for transfers between devices, local(): a8 = lax.all_to_all(a8, 'gz', 0, 0, tiled=True)  24.1 us
    all_to_all x4, starting transfers between devices, local(): a8 = lax.all_to_all(a8, 'gz', 0, 0, tiled=True)  23.6 us
    pallas_call x5, Pallas kernels, local(): pl.pallas_call(kernel, out_shape=small if last else (big, big, small, edg...  14.7 us
    ppermute x4, starting transfers between devices, local(): xlow = lax.ppermute(d_last, 'gx', up_x)  12.5 us
    ppermute x4, starting transfers between devices, local(): xhigh = lax.ppermute(d_first, 'gx', down_x)  5.17 us
    ppermute x1, starting transfers between devices, local(): low_got = lax.ppermute(high_edge, 'gx', up_x)  4.78 us
  transfers between devices with their start and end apart: 18, of which 5 were waited for; matrix products, arithmetic and copies ran while one was open for 0% of the time, Pallas kernels for 3%

profile of v10, /device:TPU:8, one launch (start us, length us, event | category | flops | bytes accessed | tf_op | source)
XLA Modules:
  0.0 182.8 jit_solution(16572267216150108948)
XLA Ops:
  0.0 3.2 %shard_map.73 = (f32[5,32,8,128]{3,2,1,0:T(8,128)}, f32[5,32,8,128]{3,2,1,0:T(8,128)}, f32[8,40,128]{2,1,0:T(8,128)}) custom-call(s32[1]{0:T(128)} %bitcast.l_ref.refs_0_, f32[32,32,128]{2,1,0:T(8,128)} %rhs.5, f32[32,32,128]{2,1,0:T(8,128)} %acc.5, f32[3,32,32,128]{3,2,1,0:T(8,128)} %perm.5, s32[1,512]{1,0:T(1,128)} %bitcast.5, s32[1,512]{1,0:T(1,128)} %bitcast.6, ...), custom_call_target="tpu_custom_call" | custom-call | tf_op jit(solution)/shard_map/pallas_call | solution.py:490
  5.2 3.6 %collective-permute-start.1 = (f32[5,32,8,128]{3,2,1,0:T(8,128)}, f32[5,32,8,128]{3,2,1,0:T(8,128)S(1)}, u32[]{:S(2)}, u32[]{:S(2)}) collective-permute-start(f32[5,32,8,128]{3,2,1,0:T(8,128)} %get-tuple-element.69), channel_id=1, source_target_pairs={{8,0},{16,8},{24,16},{32,24},{40,32},{48,40},{56,48},{9,1},{17,9},... | collective-permute-start | bytes 1966088 | tf_op jit(solution)/shard_map/ppermute | solution.py:500
  8.8 21.6 %all_to_all.30.a8 = f32[8,40,128]{2,1,0:T(8,128)S(1)} all-to-all(f32[8,40,128]{2,1,0:T(8,128)} %get-tuple-element.70), channel_id=1, replica_groups=mesh['gx'=4,'gy'=8,'gz'=8] {'gz'}, dimensions={0} | all-to-all | bytes 327680 | tf_op jit(solution)/shard_map/all_to_all | solution.py:501
  32.5 2.4 %collective-permute-start.2 = (f32[24,128]{1,0:T(8,128)S(1)}, f32[24,128]{1,0:T(8,128)S(1)}, u32[]{:S(2)}, u32[]{:S(2)}) collective-permute-start(f32[24,128]{1,0:T(8,128)S(1)} %get-tuple-element.71), channel_id=1, source_target_pairs={{0,8},{8,16},{16,24},{24,32},{32,40},{40,48},{48,56},{1,9},{9,17},... | collective-permute-start | bytes 36872 | tf_op jit(solution)/shard_map/ppermute | solution.py:509
  34.9 2.6 %collective-permute-done.2.below = f32[24,128]{1,0:T(8,128)S(1)} collective-permute-done((f32[24,128]{1,0:T(8,128)S(1)}, f32[24,128]{1,0:T(8,128)S(1)}, u32[]{:S(2)}, u32[]{:S(2)}) %collective-permute-start.2) | collective-permute-done | bytes 12320 | tf_op jit(solution)/shard_map/ppermute | solution.py:509
  41.2 4.8 %collective-permute-start.4 = (f32[3,48,128]{2,1,0:T(8,128)S(1)}, f32[3,48,128]{2,1,0:T(8,128)S(1)}, u32[]{:S(2)}, u32[]{:S(2)}) collective-permute-start(f32[3,48,128]{2,1,0:T(8,128)S(1)} %get-tuple-element.74.high_own), channel_id=1, source_target_pairs={{0,64},{64,128},{128,192},{1,65},{65,129},{129,193},{2,66},{66,130... | collective-permute-start | bytes 221192 | tf_op jit(solution)/shard_map/ppermute | solution.py:527
  46.0 2.3 %shard_map.76 = (f32[32,48,128]{2,1,0:T(8,128)S(1)}, f32[32,48,128]{2,1,0:T(8,128)S(1)}, f32[32,48,128]{2,1,0:T(8,128)S(1)}, f32[33,48,128]{2,1,0:T(8,128)S(1)},...) custom-call(f32[32,32,128]{2,1,0:T(8,128)S(1)} %copy-done.27, ...), custom_call_target="tpu_custom_call" | custom-call | tf_op jit(solution)/shard_map/pallas_call | solution.py:529
  49.6 12.9 %all_to_all.31.refs_0_.refs_5_ = f32[8,32,128]{2,1,0:T(8,128)S(1)} all-to-all(f32[8,32,128]{2,1,0:T(8,128)S(1)} %get-tuple-element.90), channel_id=1, replica_groups=mesh['gx'=4,'gy'=8,'gz'=8] {'gz'}, dimensions={0} | all-to-all | bytes 262144 | tf_op jit(solution)/shard_map/all_to_all | solution.py:557
  63.3 3.3 %shard_map.79 = (f32[32,48,128]{2,1,0:T(8,128)S(1)}, f32[32,48,128]{2,1,0:T(8,128)S(1)}, f32[32,32,128]{2,1,0:T(8,128)S(1)}, f32[48,128]{1,0:T(8,128)S(1)}, f32[...) custom-call(s32[1]{0:T(128)} %bitcast.l_ref.refs_0_, f32[32,48,128]{2,1,0:T(8,128)S(1)} %get-tuple-element.86.refs_1_, ...), custom_call_target="tpu_custom_call" | custom-call | tf_op jit(solution)/shard_map/pallas_call | solution.py:580
  69.2 3.4 %all-to-all-start.2 = ((f32[8,32,128]{2,1,0:T(8,128)}), f32[8,32,128]{2,1,0:T(8,128)S(1)}, u32[]{:S(2)}, u32[]{:S(2)}) async-start(f32[8,32,128]{2,1,0:T(8,128)} %get-tuple-element.102), calls=%async_computation.2 | async-start | bytes 262144 | tf_op jit(solution)/shard_map/all_to_all | solution.py:557
  72.6 3.9 %collective-permute-start.6 = (f32[48,128]{1,0:T(8,128)S(1)}, f32[48,128]{1,0:T(8,128)S(1)}, u32[]{:S(2)}, u32[]{:S(2)}) collective-permute-start(f32[48,128]{1,0:T(8,128)S(1)} %get-tuple-element.100), channel_id=1, source_target_pairs={{0,64},{64,128},{128,192},{1,65},{65,129},{129,193},{2,66},{66,130... | collective-permute-start | bytes 73736 | tf_op jit(solution)/shard_map/ppermute | solution.py:555
  77.9 5.2 %all-to-all-done.2.refs_0_.refs_6_ = f32[8,32,128]{2,1,0:T(8,128)S(1)} async-done(((f32[8,32,128]{2,1,0:T(8,128)}), f32[8,32,128]{2,1,0:T(8,128)S(1)}, u32[]{:S(2)}, u32[]{:S(2)}) %all-to-all-start.2) | async-done | bytes 131104 | tf_op jit(solution)/shard_map/all_to_all | solution.py:557
  90.2 3.2 %shard_map.81 = (f32[32,48,128]{2,1,0:T(8,128)S(1)}, f32[32,48,128]{2,1,0:T(8,128)S(1)}, f32[32,32,128]{2,1,0:T(8,128)S(1)}, f32[48,128]{1,0:T(8,128)S(1)}, f32[...) custom-call(s32[1]{0:T(128)} %bitcast.l_ref.refs_0_, f32[32,48,128]{2,1,0:T(8,128)S(1)} %copy-done.43, ...), custom_call_target="tpu_custom_call" | custom-call | tf_op jit(solution)/shard_map/pallas_call | solution.py:580
  96.1 7.2 %all-to-all-start.3 = ((f32[8,32,128]{2,1,0:T(8,128)}), f32[8,32,128]{2,1,0:T(8,128)S(1)}, u32[]{:S(2)}, u32[]{:S(2)}) async-start(f32[8,32,128]{2,1,0:T(8,128)} %get-tuple-element.108), calls=%async_computation.3 | async-start | bytes 262144 | tf_op jit(solution)/shard_map/all_to_all | solution.py:557
  103.2 3.8 %collective-permute-start.8 = (f32[48,128]{1,0:T(8,128)S(1)}, f32[48,128]{1,0:T(8,128)S(1)}, u32[]{:S(2)}, u32[]{:S(2)}) collective-permute-start(f32[48,128]{1,0:T(8,128)S(1)} %get-tuple-element.106), channel_id=1, source_target_pairs={{0,64},{64,128},{128,192},{1,65},{65,129},{129,193},{2,66},{66,130... | collective-permute-start | bytes 73736 | tf_op jit(solution)/shard_map/ppermute | solution.py:555
  108.4 5.5 %all-to-all-done.3.refs_0_.refs_6_ = f32[8,32,128]{2,1,0:T(8,128)S(1)} async-done(((f32[8,32,128]{2,1,0:T(8,128)}), f32[8,32,128]{2,1,0:T(8,128)S(1)}, u32[]{:S(2)}, u32[]{:S(2)}) %all-to-all-start.3) | async-done | bytes 131104 | tf_op jit(solution)/shard_map/all_to_all | solution.py:557
  121.0 3.2 %shard_map.83 = (f32[32,48,128]{2,1,0:T(8,128)S(1)}, f32[32,48,128]{2,1,0:T(8,128)S(1)}, f32[32,32,128]{2,1,0:T(8,128)S(1)}, f32[48,128]{1,0:T(8,128)S(1)}, f32[...) custom-call(s32[1]{0:T(128)} %bitcast.l_ref.refs_0_, f32[32,48,128]{2,1,0:T(8,128)S(1)} %copy-done.35, ...), custom_call_target="tpu_custom_call" | custom-call | tf_op jit(solution)/shard_map/pallas_call | solution.py:580
  126.9 7.0 %all-to-all-start.4 = ((f32[8,32,128]{2,1,0:T(8,128)}), f32[8,32,128]{2,1,0:T(8,128)S(1)}, u32[]{:S(2)}, u32[]{:S(2)}) async-start(f32[8,32,128]{2,1,0:T(8,128)} %get-tuple-element.114), calls=%async_computation.4 | async-start | bytes 262144 | tf_op jit(solution)/shard_map/all_to_all | solution.py:557
  133.8 2.9 %collective-permute-start.10 = (f32[48,128]{1,0:T(8,128)S(1)}, f32[48,128]{1,0:T(8,128)S(1)}, u32[]{:S(2)}, u32[]{:S(2)}) collective-permute-start(f32[48,128]{1,0:T(8,128)S(1)} %get-tuple-element.112), channel_id=1, source_target_pairs={{0,64},{64,128},{128,192},{1,65},{65,129},{129,193},{2,66},{66,130... | collective-permute-start | bytes 73736 | tf_op jit(solution)/shard_map/ppermute | solution.py:555
  138.0 6.3 %all-to-all-done.4.refs_0_.refs_6_ = f32[8,32,128]{2,1,0:T(8,128)S(1)} async-done(((f32[8,32,128]{2,1,0:T(8,128)}), f32[8,32,128]{2,1,0:T(8,128)S(1)}, u32[]{:S(2)}, u32[]{:S(2)}) %all-to-all-start.4) | async-done | bytes 131104 | tf_op jit(solution)/shard_map/all_to_all | solution.py:557
  151.5 3.0 %shard_map.85 = (f32[32,48,128]{2,1,0:T(8,128)S(1)}, f32[32,48,128]{2,1,0:T(8,128)S(1)}, f32[32,32,128]{2,1,0:T(8,128)S(1)}, f32[48,128]{1,0:T(8,128)S(1)}, f32[...) custom-call(s32[1]{0:T(128)} %bitcast.l_ref.refs_0_, f32[32,48,128]{2,1,0:T(8,128)S(1)} %copy-done.39, ...), custom_call_target="tpu_custom_call" | custom-call | tf_op jit(solution)/shard_map/pallas_call | solution.py:580
  157.2 6.1 %all-to-all-start.5 = ((f32[8,24,128]{2,1,0:T(8,128)}), f32[8,24,128]{2,1,0:T(8,128)S(1)}, u32[]{:S(2)}, u32[]{:S(2)}) async-start(f32[8,24,128]{2,1,0:T(8,128)} %get-tuple-element.120), calls=%async_computation.5 | async-start | bytes 196608 | tf_op jit(solution)/shard_map/all_to_all | solution.py:557
  166.5 7.1 %all-to-all-done.5.refs_0_.refs_6_ = f32[8,24,128]{2,1,0:T(8,128)S(1)} async-done(((f32[8,24,128]{2,1,0:T(8,128)}), f32[8,24,128]{2,1,0:T(8,128)S(1)}, u32[]{:S(2)}, u32[]{:S(2)}) %all-to-all-start.5) | async-done | bytes 98336 | tf_op jit(solution)/shard_map/all_to_all | solution.py:557
  180.8 2.0 %shard_map.87 = f32[32,32,128]{2,1,0:T(8,128)} custom-call(s32[1]{0:T(128)} %bitcast.l_ref.refs_0_, f32[32,48,128]{2,1,0:T(8,128)S(1)} %copy-done.31, f32[32,48,128]{2,1,0:T(8,128)S(1)} %copy-done.33, f32[32,32,128]{2,1,0:T(8,128)S(1)} %copy-done.47, f32[48,128]{1,0:T(8,128)S(1)} %collective-permute-done.12.refs_4_, ...), custom_call_target="tpu_custom_call" | custom-call | tf_op jit(solution)/shard_map/pallas_call | solution.py:580
  (137 shorter events, 55.9 us)
Async XLA Ops:
  0.0 37.5 %copy-start.28 = (f32[32,32,128]{2,1,0:T(8,128)S(1)}, f32[32,32,128]{2,1,0:T(8,128)}, u32[]{:S(2)}) copy-start(f32[32,32,128]{2,1,0:T(8,128)} %acc.5) | copy-start | bytes 1572868
  0.0 37.5 %copy-start.27 = (f32[32,32,128]{2,1,0:T(8,128)S(1)}, f32[32,32,128]{2,1,0:T(8,128)}, u32[]{:S(2)}) copy-start(f32[32,32,128]{2,1,0:T(8,128)} %rhs.5) | copy-start | bytes 1572868
  3.3 34.3 %collective-permute-start = (f32[5,32,8,128]{3,2,1,0:T(8,128)}, f32[5,32,8,128]{3,2,1,0:T(8,128)S(1)}, u32[]{:S(2)}, u32[]{:S(2)}) collective-permute-start(f32[5,32,8,128]{3,2,1,0:T(8,128)} %get-tuple-element.68), channel_id=1, source_target_pairs={{0,8},{8,16},{16,24},{24,32},{32,40},{40,48},{48,56},{1,9},{9,17},... | collective-permute-start | bytes 1966088 | tf_op jit(solution)/shard_map/ppermute | solution.py:499
  5.2 32.3 %collective-permute-start.1 = (f32[5,32,8,128]{3,2,1,0:T(8,128)}, f32[5,32,8,128]{3,2,1,0:T(8,128)S(1)}, u32[]{:S(2)}, u32[]{:S(2)}) collective-permute-start(f32[5,32,8,128]{3,2,1,0:T(8,128)} %get-tuple-element.69), channel_id=1, source_target_pairs={{8,0},{16,8},{24,16},{32,24},{40,32},{48,40},{56,48},{9,1},{17,9},... | collective-permute-start | bytes 1966088 | tf_op jit(solution)/shard_map/ppermute | solution.py:500
  30.6 6.9 %collective-permute-start.3 = (f32[132,128]{1,0:T(8,128)S(1)}, f32[132,128]{1,0:T(8,128)S(1)}, u32[]{:S(2)}, u32[]{:S(2)}) collective-permute-start(f32[132,128]{1,0:T(8,128)S(1)} %get-tuple-element.72), channel_id=1, source_target_pairs={{8,0},{16,8},{24,16},{32,24},{40,32},{48,40},{56,48},{9,1},{17,9},... | collective-permute-start | bytes 202760 | tf_op jit(solution)/shard_map/ppermute | solution.py:510
  32.5 5.0 %collective-permute-start.2 = (f32[24,128]{1,0:T(8,128)S(1)}, f32[24,128]{1,0:T(8,128)S(1)}, u32[]{:S(2)}, u32[]{:S(2)}) collective-permute-start(f32[24,128]{1,0:T(8,128)S(1)} %get-tuple-element.71), channel_id=1, source_target_pairs={{0,8},{8,16},{16,24},{24,32},{32,40},{40,48},{48,56},{1,9},{9,17},... | collective-permute-start | bytes 36872 | tf_op jit(solution)/shard_map/ppermute | solution.py:509
  39.9 8.5 %collective-permute-start.5 = (f32[3,48,128]{2,1,0:T(8,128)S(1)}, f32[3,48,128]{2,1,0:T(8,128)S(1)}, u32[]{:S(2)}, u32[]{:S(2)}) collective-permute-start(f32[3,48,128]{2,1,0:T(8,128)S(1)} %get-tuple-element.73.low_own), channel_id=1, source_target_pairs={{64,0},{128,64},{192,128},{65,1},{129,65},{193,129},{66,2},{130,66... | collective-permute-start | bytes 221192 | tf_op jit(solution)/shard_map/ppermute | solution.py:528
  41.2 7.2 %collective-permute-start.4 = (f32[3,48,128]{2,1,0:T(8,128)S(1)}, f32[3,48,128]{2,1,0:T(8,128)S(1)}, u32[]{:S(2)}, u32[]{:S(2)}) collective-permute-start(f32[3,48,128]{2,1,0:T(8,128)S(1)} %get-tuple-element.74.high_own), channel_id=1, source_target_pairs={{0,64},{64,128},{128,192},{1,65},{65,129},{129,193},{2,66},{66,130... | collective-permute-start | bytes 221192 | tf_op jit(solution)/shard_map/ppermute | solution.py:527
  48.3 15.0 %copy-start.5 = (f32[32,48,128]{2,1,0:T(8,128)}, f32[32,48,128]{2,1,0:T(8,128)S(1)}, u32[]{:S(2)}) copy-start(f32[32,48,128]{2,1,0:T(8,128)S(1)} %get-tuple-element.93.refs_9_.refs_10_) | copy-start | bytes 2359300
  48.4 15.0 %copy-start.10 = (f32[32,48,128]{2,1,0:T(8,128)}, f32[32,48,128]{2,1,0:T(8,128)S(1)}, u32[]{:S(2)}) copy-start(f32[32,48,128]{2,1,0:T(8,128)S(1)} %get-tuple-element.94.refs_10_.refs_11_) | copy-start | bytes 2359300
  48.4 15.0 %copy-start.15 = (f32[32,48,128]{2,1,0:T(8,128)}, f32[32,48,128]{2,1,0:T(8,128)S(1)}, u32[]{:S(2)}) copy-start(f32[32,48,128]{2,1,0:T(8,128)S(1)} %get-tuple-element.95.refs_11_.refs_12_) | copy-start | bytes 2359300
  49.5 17.1 %copy-start = (f32[32,48,128]{2,1,0:T(8,128)}, f32[32,48,128]{2,1,0:T(8,128)S(1)}, u32[]{:S(2)}) copy-start(f32[32,48,128]{2,1,0:T(8,128)S(1)} %get-tuple-element.91.refs_7_.refs_8_) | copy-start | bytes 2359300
  69.2 13.8 %all-to-all-start.2 = ((f32[8,32,128]{2,1,0:T(8,128)}), f32[8,32,128]{2,1,0:T(8,128)S(1)}, u32[]{:S(2)}, u32[]{:S(2)}) async-start(f32[8,32,128]{2,1,0:T(8,128)} %get-tuple-element.102), calls=%async_computation.2 | async-start | bytes 262144 | tf_op jit(solution)/shard_map/all_to_all | solution.py:557
  72.6 11.3 %collective-permute-start.6 = (f32[48,128]{1,0:T(8,128)S(1)}, f32[48,128]{1,0:T(8,128)S(1)}, u32[]{:S(2)}, u32[]{:S(2)}) collective-permute-start(f32[48,128]{1,0:T(8,128)S(1)} %get-tuple-element.100), channel_id=1, source_target_pairs={{0,64},{64,128},{128,192},{1,65},{65,129},{129,193},{2,66},{66,130... | collective-permute-start | bytes 73736 | tf_op jit(solution)/shard_map/ppermute | solution.py:555
  76.6 7.4 %collective-permute-start.7 = (f32[48,128]{1,0:T(8,128)S(1)}, f32[48,128]{1,0:T(8,128)S(1)}, u32[]{:S(2)}, u32[]{:S(2)}) collective-permute-start(f32[48,128]{1,0:T(8,128)S(1)} %get-tuple-element.101), channel_id=1, source_target_pairs={{64,0},{128,64},{192,128},{65,1},{129,65},{193,129},{66,2},{130,66... | collective-permute-start | bytes 73736 | tf_op jit(solution)/shard_map/ppermute | solution.py:556
  96.1 17.7 %all-to-all-start.3 = ((f32[8,32,128]{2,1,0:T(8,128)}), f32[8,32,128]{2,1,0:T(8,128)S(1)}, u32[]{:S(2)}, u32[]{:S(2)}) async-start(f32[8,32,128]{2,1,0:T(8,128)} %get-tuple-element.108), calls=%async_computation.3 | async-start | bytes 262144 | tf_op jit(solution)/shard_map/all_to_all | solution.py:557
  103.2 11.5 %collective-permute-start.8 = (f32[48,128]{1,0:T(8,128)S(1)}, f32[48,128]{1,0:T(8,128)S(1)}, u32[]{:S(2)}, u32[]{:S(2)}) collective-permute-start(f32[48,128]{1,0:T(8,128)S(1)} %get-tuple-element.106), channel_id=1, source_target_pairs={{0,64},{64,128},{128,192},{1,65},{65,129},{129,193},{2,66},{66,130... | collective-permute-start | bytes 73736 | tf_op jit(solution)/shard_map/ppermute | solution.py:555
  107.1 7.7 %collective-permute-start.9 = (f32[48,128]{1,0:T(8,128)S(1)}, f32[48,128]{1,0:T(8,128)S(1)}, u32[]{:S(2)}, u32[]{:S(2)}) collective-permute-start(f32[48,128]{1,0:T(8,128)S(1)} %get-tuple-element.107), channel_id=1, source_target_pairs={{64,0},{128,64},{192,128},{65,1},{129,65},{193,129},{66,2},{130,66... | collective-permute-start | bytes 73736 | tf_op jit(solution)/shard_map/ppermute | solution.py:556
  126.9 17.5 %all-to-all-start.4 = ((f32[8,32,128]{2,1,0:T(8,128)}), f32[8,32,128]{2,1,0:T(8,128)S(1)}, u32[]{:S(2)}, u32[]{:S(2)}) async-start(f32[8,32,128]{2,1,0:T(8,128)} %get-tuple-element.114), calls=%async_computation.4 | async-start | bytes 262144 | tf_op jit(solution)/shard_map/all_to_all | solution.py:557
  133.8 11.4 %collective-permute-start.10 = (f32[48,128]{1,0:T(8,128)S(1)}, f32[48,128]{1,0:T(8,128)S(1)}, u32[]{:S(2)}, u32[]{:S(2)}) collective-permute-start(f32[48,128]{1,0:T(8,128)S(1)} %get-tuple-element.112), channel_id=1, source_target_pairs={{0,64},{64,128},{128,192},{1,65},{65,129},{129,193},{2,66},{66,130... | collective-permute-start | bytes 73736 | tf_op jit(solution)/shard_map/ppermute | solution.py:555
  136.7 8.5 %collective-permute-start.11 = (f32[48,128]{1,0:T(8,128)S(1)}, f32[48,128]{1,0:T(8,128)S(1)}, u32[]{:S(2)}, u32[]{:S(2)}) collective-permute-start(f32[48,128]{1,0:T(8,128)S(1)} %get-tuple-element.113), channel_id=1, source_target_pairs={{64,0},{128,64},{192,128},{65,1},{129,65},{193,129},{66,2},{130,66... | collective-permute-start | bytes 73736 | tf_op jit(solution)/shard_map/ppermute | solution.py:556
  157.2 16.5 %all-to-all-start.5 = ((f32[8,24,128]{2,1,0:T(8,128)}), f32[8,24,128]{2,1,0:T(8,128)S(1)}, u32[]{:S(2)}, u32[]{:S(2)}) async-start(f32[8,24,128]{2,1,0:T(8,128)} %get-tuple-element.120), calls=%async_computation.5 | async-start | bytes 196608 | tf_op jit(solution)/shard_map/all_to_all | solution.py:557
  163.3 10.9 %collective-permute-start.12 = (f32[48,128]{1,0:T(8,128)S(1)}, f32[48,128]{1,0:T(8,128)S(1)}, u32[]{:S(2)}, u32[]{:S(2)}) collective-permute-start(f32[48,128]{1,0:T(8,128)S(1)} %get-tuple-element.118), channel_id=1, source_target_pairs={{0,64},{64,128},{128,192},{1,65},{65,129},{129,193},{2,66},{66,130... | collective-permute-start | bytes 73736 | tf_op jit(solution)/shard_map/ppermute | solution.py:555
  165.2 9.0 %collective-permute-start.13 = (f32[48,128]{1,0:T(8,128)S(1)}, f32[48,128]{1,0:T(8,128)S(1)}, u32[]{:S(2)}, u32[]{:S(2)}) collective-permute-start(f32[48,128]{1,0:T(8,128)S(1)} %get-tuple-element.119), channel_id=1, source_target_pairs={{64,0},{128,64},{192,128},{65,1},{129,65},{193,129},{66,2},{130,66... | collective-permute-start | bytes 73736 | tf_op jit(solution)/shard_map/ppermute | solution.py:556
  (48 other events, 79.7 us)
